TPU v7x, 256 devices: a whole 4x4x8 slice. The times are simulated.
256 devices in a mesh: rows: 64 (over z, x, core), cols: 4 (over y).
Axes of the slice: x: 4, y: 4, z: 8, core: 2. Of those that a mesh axis runs over, the one named last changes fastest.
Arguments:
- tables: float32 [4, 32768, 512], P(None, 'rows', 'cols'), may hold values from -1.5 to 1.5
- dense_features: float32 [2048, 512], P('rows', 'cols'), may hold values from -6 to 6
- slot_rows: int32 [64, 64, 4, 64], P('rows'), may hold values from 0 to 511, as said below
- slot_examples: int32 [64, 64, 4, 64], P('rows'), may hold values from 0 to 31, as said below
- slot_counts: int32 [64, 64, 4], P('rows'), may hold values from 21 to 64, as said below
Outputs:
- pooled: float32 [2048, 4, 512], P('rows', None, 'cols')
- interactions: float32 [2048, 10], P('rows')
Inputs may be any that keep to these rules, and one draw needn't show every extreme that they name: slot_rows[s, o, t, c] names row o * 512 + value of table t. `slot_examples`: an example of the source device s. `slot_counts`: slots 0 to count - 1 of a bucket are live, the others unused; some bucket of every draw is full.
All inputs are finite; a program needn't handle non-finite values.
Results may differ from a plain program's by a relative error of at most 0.0003.
Values sent between devices are 32-bit elements; how exact they have to be, the bound alone decides.
No kernel may reach another device: no remote copies, remote signals or barrier semaphores. Data moves between devices by JAX's collectives and lax.ppermute only.
A program may use at most 64 MiB of HBM per device.

v0:
```python
import math

import jax
import jax.numpy as jnp
from jax import lax
from jax.sharding import Mesh
from jax.sharding import PartitionSpec as P

E = 512
ROWS = ("rows_0", "rows_1", "rows_2")


def in_one_piece(arrays, axis, split_dim, concat_dim, along):
    widths = [math.prod(a.shape[along:]) for a in arrays]
    both = jnp.concatenate(
        [a.reshape(*a.shape[:along], w) for a, w in zip(arrays, widths)], axis=along
    )
    filled = lax.all_to_all(both, axis, split_axis=split_dim, concat_axis=concat_dim, tiled=True)
    tiles = jnp.split(filled, [sum(widths[:k]) for k in range(1, len(widths))], axis=along)
    return tuple(
        (b.reshape(*filled.shape[:along], *a.shape[along:]) for a, b in zip(arrays, tiles))
    )


def in_blocks(x, dim, size):
    before, after = (x.shape[:dim], x.shape[dim + 1 :])
    return jnp.moveaxis(x.reshape(*before, size, -1, *after), dim, 0)


def sent_and_summed(x, axis, dim):
    size = lax.axis_size(axis)
    tiles = lax.all_to_all(in_blocks(x, dim, size), axis, 0, 0, tiled=True)
    return jnp.sum(tiles, axis=0)


def sum_by_axis(x, axes, dim):
    far, near = axes
    tiles = in_blocks(x, dim, lax.axis_size(far))
    nearer = sent_and_summed(tiles, near, dim + 1)
    arrived = lax.all_to_all(nearer, far, split_axis=0, concat_axis=0, tiled=True)
    return arrived.sum(axis=0)


def copy_for_each(x, axis):
    copies = jnp.broadcast_to(x, (lax.axis_size(axis), *x.shape))
    return lax.all_to_all(copies, axis, split_axis=0, concat_axis=0, tiled=True)


def over_copies(x, axis):
    return copy_for_each(x, axis).sum(axis=0)


def lookup(got_rows, tables):
    range_rows = tables.shape[1]
    row_ids = jnp.arange(range_rows, dtype=jnp.int32)

    def one_table(pieces):
        rows_table, table_slice = pieces
        selector = (rows_table[:, :, None] == row_ids[None, None, :]).astype(jnp.float32)
        return jnp.einsum("scr,re->sce", selector, table_slice, precision=lax.Precision.HIGHEST)

    picked = lax.map(one_table, (jnp.moveaxis(got_rows, 1, 0), tables))
    return jnp.moveaxis(picked, 0, 1)


def upper_pairs(gram_matrix, count):
    pieces = [gram_matrix[:, first, first + 1 :] for first in range(count - 1)]
    return jnp.concatenate(pieces, axis=1)


def body(tables, dense_features, slot_rows, slot_examples, slot_counts):
    table_count = tables.shape[0]
    width = tables.shape[2]
    capacity = slot_rows.shape[3]
    examples_here = dense_features.shape[0]
    slot_index = jnp.arange(capacity, dtype=jnp.int32)
    example_ids = jnp.arange(examples_here, dtype=jnp.int32)
    got_rows, got_examples, got_counts = in_one_piece(
        (slot_rows, slot_examples, slot_counts), ROWS, 1, 0, 3
    )
    looked = lookup(got_rows[:, 0], tables)
    owner_examples = got_examples[:, 0]
    owner_live = slot_index[None, None, :] < got_counts[:, 0, :, None]
    source_count = examples_here * lax.axis_size(ROWS) // examples_here
    onehot = (
        (owner_examples[:, :, :, None] == example_ids[None, None, None, :])
        & owner_live[:, :, :, None]
    ).astype(jnp.float32)
    summed = jnp.einsum("stcb,stce->sbte", onehot, looked, precision=lax.Precision.HIGHEST)
    pooled = sum_by_axis(
        summed.reshape(source_count * examples_here, table_count, width),
        (("rows_0", "rows_1"), "rows_2"),
        0,
    )
    vectors = jnp.concatenate([dense_features[:, None, :], pooled], axis=1)
    gram_matrix = jnp.einsum("bie,bje->bij", vectors, vectors, precision=lax.Precision.HIGHEST)
    interactions = over_copies(upper_pairs(gram_matrix, table_count + 1) * E ** (-0.5), "cols")
    return (pooled, interactions)


def solution(mesh):
    torus = Mesh(
        mesh.devices.reshape(8, 4, 2, mesh.shape["cols"]), ("rows_0", "rows_1", "rows_2", "cols")
    )
    return jax.shard_map(
        body,
        mesh=torus,
        in_specs=(
            P(None, ROWS, "cols"),
            P(ROWS, "cols"),
            P(ROWS, None, None, None),
            P(ROWS, None, None, None),
            P(ROWS, None, None),
        ),
        out_specs=(P(ROWS, None, "cols"), P(ROWS, None)),
        check_vma=False,
    )
```

profile of v0, /device:TPU:24, one launch (start us, length us, event | category | flops | bytes accessed | tf_op | source)
XLA Modules:
  0.0 139.6 jit_solution(16277469829711478321)
XLA Ops:
  0.6 0.8 copy.40
  1.4 1.9 %pad_add_fusion = s32[1,64,4,129]{3,2,0,1:T(4,128)} fusion(s32[1,64,4,1]{3,2,0,1:T(4,128)S(1)} %copy.40, s32[1,64,4,64]{3,2,0,1:T(4,128)} %bitcast.50, s32[1,64,4,64]{3,2,0,1:T(4,128)} %bitcast.51), kind=kLoop, calls=%fused_computation.16 | loop fusion | flops 66048 | bytes 264192 | tf_op jit(solution)/shard_map/concatenate | solution.py:15
  3.3 11.9 %all-to-all-start = ((s32[1,64,4,129]{3,2,0,1:T(4,128)}), s32[1,64,4,129]{3,2,0,1:T(4,128)S(1)}, u32[]{:S(2)}, u32[]{:S(2)}) async-start(s32[1,64,4,129]{3,2,0,1:T(4,128)} %pad_add_fusion), calls=%async_computation | async-start | bytes 524288 | tf_op jit(solution)/shard_map/all_to_all | solution.py:18
  15.3 12.9 %all-to-all-done = s32[1,64,4,129]{3,2,0,1:T(4,128)S(1)} async-done(((s32[1,64,4,129]{3,2,0,1:T(4,128)}), s32[1,64,4,129]{3,2,0,1:T(4,128)S(1)}, u32[]{:S(2)}, u32[]{:S(2)}) %all-to-all-start) | async-done | bytes 132128 | tf_op jit(solution)/shard_map/all_to_all | solution.py:18
  28.2 0.1 slice_bitcast_fusion
  28.3 0.1 copy.42
  28.4 0.1 copy.43
  28.5 0.2 iota_compare_fusion.5
  28.7 23.8 %while.11 = (s32[]{:T(128)}, f32[4,64,64,128]{3,2,1,0:T(8,128)}, s32[4,64,64]{2,0,1:T(4,128)S(1)}, f32[4,512,128]{2,1,0:T(8,128)}, s32[]{:T(128)}) while((s32[]{:T(128)}, f32[4,64,64,128]{3,2,1,0:T(8,128)}, s32[4,64,64]{2,0,1:T(4,128)S(1)}, f32[4,512,128]{2,1,0:T(8,128)}, s32[]{:T(128)}) %tuple.29), condition=%wide.region_1.2_spmd.clone, body=%wide.region_0.1_spmd.clone.sunk | while | flops 3223322624 | bytes 2409545 | solution.py:62
  28.7 5.9 %bitcast_dynamic-update-slice_fusion.2 = f32[4,64,64,128]{3,2,1,0:T(8,128)} fusion(f32[4,64,64,128]{3,2,1,0:T(8,128)} %get-tuple-element.91, s32[]{:T(128)S(6)} %copy.61, s32[64,64]{1,0:T(8,128)S(1)} %bitcast.49, f32[4,512,128]{2,1,0:T(8,128)} %get-tuple-element.98), kind=kOutput, calls=%fused_computation.4.clone.1 | convolution fusion | flops 3223322624 | bytes 2376704 | tf_op jit(solution)/shard_map/while/body/eval_jaxpr/scr,re->sce/dot_general | solution.py:60
  34.7 5.9 %bitcast_dynamic-update-slice_fusion.2 = f32[4,64,64,128]{3,2,1,0:T(8,128)} fusion(f32[4,64,64,128]{3,2,1,0:T(8,128)} %get-tuple-element.91, s32[]{:T(128)S(6)} %copy.61, s32[64,64]{1,0:T(8,128)S(1)} %bitcast.49, f32[4,512,128]{2,1,0:T(8,128)} %get-tuple-element.98), kind=kOutput, calls=%fused_computation.4.clone.1 | convolution fusion | flops 3223322624 | bytes 2376704 | tf_op jit(solution)/shard_map/while/body/eval_jaxpr/scr,re->sce/dot_general | solution.py:60
  40.6 5.9 %bitcast_dynamic-update-slice_fusion.2 = f32[4,64,64,128]{3,2,1,0:T(8,128)} fusion(f32[4,64,64,128]{3,2,1,0:T(8,128)} %get-tuple-element.91, s32[]{:T(128)S(6)} %copy.61, s32[64,64]{1,0:T(8,128)S(1)} %bitcast.49, f32[4,512,128]{2,1,0:T(8,128)} %get-tuple-element.98), kind=kOutput, calls=%fused_computation.4.clone.1 | convolution fusion | flops 3223322624 | bytes 2376704 | tf_op jit(solution)/shard_map/while/body/eval_jaxpr/scr,re->sce/dot_general | solution.py:60
  46.6 5.9 %bitcast_dynamic-update-slice_fusion.2 = f32[4,64,64,128]{3,2,1,0:T(8,128)} fusion(f32[4,64,64,128]{3,2,1,0:T(8,128)} %get-tuple-element.91, s32[]{:T(128)S(6)} %copy.61, s32[64,64]{1,0:T(8,128)S(1)} %bitcast.49, f32[4,512,128]{2,1,0:T(8,128)} %get-tuple-element.98), kind=kOutput, calls=%fused_computation.4.clone.1 | convolution fusion | flops 3223322624 | bytes 2376704 | tf_op jit(solution)/shard_map/while/body/eval_jaxpr/scr,re->sce/dot_general | solution.py:60
  52.5 7.3 %fusion.7 = f32[64,4,128,32]{2,3,1,0:T(8,128)S(1)} fusion(s32[64,4,64]{2,1,0:T(4,128)S(1)} %get-tuple-element.58, pred[64,4,64]{2,1,0:T(4,128)(4,1)S(1)} %iota_compare_fusion.5, f32[4,64,64,128]{3,2,1,0:T(8,128)} %get-tuple-element.29), kind=kOutput, calls=%fused_computation.9 | convolution fusion | flops 806354944 | bytes 12664832 | tf_op jit(solution)/shard_map/stcb,stce->sbte/dot_general | solution.py:89
  59.7 0.8 copy.57
  60.6 8.2 %all_to_all.27 = f32[2,32,32,4,128]{4,2,3,1,0:T(8,128)} all-to-all(f32[2,32,32,4,128]{4,2,3,1,0:T(8,128)S(1)} %bitcast.46), channel_id=1, replica_groups=mesh['rows_0'=8,'rows_1'=4,'rows_2'=2,'cols'=4] {'rows_2'}, dimensions={0} | all-to-all | bytes 8388608 | tf_op jit(solution)/shard_map/all_to_all | solution.py:32
  68.7 2.9 %reduce_sum.27 = f32[32,32,4,128]{3,1,2,0:T(8,128)S(1)} reduce(f32[2,32,32,4,128]{4,2,3,1,0:T(8,128)} %all_to_all.27, f32[]{:T(128)} %constant.3.clone.1), dimensions={0}, to_apply=%region_2.3 | reduce | flops 524288 | bytes 6291460 | tf_op jit(solution)/shard_map/reduce_sum | solution.py:33
  71.6 55.1 %all_to_all.28 = f32[32,32,4,128]{3,1,2,0:T(8,128)} all-to-all(f32[32,32,4,128]{3,1,2,0:T(8,128)S(1)} %reduce_sum.27), channel_id=1, replica_groups=mesh['rows_0'=8,'rows_1'=4,'rows_2'=2,'cols'=4] {'rows_0','rows_1'}, dimensions={0} | all-to-all | bytes 4194304 | tf_op jit(solution)/shard_map/all_to_all | solution.py:40
  126.7 1.7 %reduce_sum.28 = f32[32,4,128]{2,0,1:T(8,128)S(1)} reduce(f32[32,32,4,128]{3,1,2,0:T(8,128)} %all_to_all.28, f32[]{:T(128)} %constant.3.clone.1), dimensions={0}, to_apply=%region_3.4 | reduce | flops 507904 | bytes 2162692 | tf_op jit(solution)/shard_map/reduce_sum | solution.py:41
  128.5 0.3 fusion.13
  128.8 0.5 slice_reduce_fusion
  129.3 0.1 slice.18
  129.4 0.1 slice.17
  129.5 0.1 slice.16
  129.7 0.1 copy.50
  129.8 0.1 copy.48
  129.9 0.1 reshape.21
  130.0 7.7 %all_to_all.29 = f32[4,1,320]{2,1,0:T(1,128)S(1)} all-to-all(f32[4,1,320]{2,1,0:T(1,128)S(1)} %reshape.21), channel_id=1, replica_groups=mesh['rows_0'=8,'rows_1'=4,'rows_2'=2,'cols'=4] {'cols'}, dimensions={0} | all-to-all | bytes 10240 | tf_op jit(solution)/shard_map/all_to_all | solution.py:46
  137.7 0.5 broadcast.7
  138.2 0.7 reduce.2
  138.9 0.1 reshape.22
  139.0 0.6 bitcast_reduce_fusion
  (14 shorter events, 0.3 us)
Async XLA Ops:
  3.3 24.8 %all-to-all-start = ((s32[1,64,4,129]{3,2,0,1:T(4,128)}), s32[1,64,4,129]{3,2,0,1:T(4,128)S(1)}, u32[]{:S(2)}, u32[]{:S(2)}) async-start(s32[1,64,4,129]{3,2,0,1:T(4,128)} %pad_add_fusion), calls=%async_computation | async-start | bytes 524288 | tf_op jit(solution)/shard_map/all_to_all | solution.py:18
  68.7 59.8 %copy-start.1 = (f32[32,128]{1,0:T(8,128)S(1)}, f32[32,128]{1,0:T(8,128)}, u32[]{:S(2)}) copy-start(f32[32,128]{1,0:T(8,128)} %param.8) | copy-start | bytes 49156
  128.5 11.1 %copy-start = (f32[32,4,128]{2,1,0:T(4,128)}, f32[32,4,128]{2,1,0:T(4,128)S(1)}, u32[]{:S(2)}) copy-start(f32[32,4,128]{2,1,0:T(4,128)S(1)} %copy.51) | copy-start | bytes 196612
where the time goes:
time: 142 us; the launch traced here: 140 us
  blocking collectives  71 us (50%)
  matrix products  31.3 us (22%)
  waiting for transfers between devices  12.9 us (9%)
  starting transfers between devices  11.9 us (8%)
  other arithmetic  7.95 us (6%)
  local copies, waits for them, and re-layouts  3.82 us (3%)
    all_to_all x1, blocking collectives, sum_by_axis(): lax.all_to_all(nearer, far, split_axis=0, concat_axis=0, tiled=True)  55.1 us
    dot_general x4, matrix products, one_table(): jnp.einsum('scr,re->sce', selector, table_slice, precision=lax.Precision....  23.6 us
    all_to_all x1, waiting for transfers between devices, in_one_piece(): lax.all_to_all(both, axis, split_axis=split_dim, concat_axis=concat_dim,...  12.9 us
    all_to_all x1, starting transfers between devices, in_one_piece(): lax.all_to_all(both, axis, split_axis=split_dim, concat_axis=concat_dim,...  11.9 us
    all_to_all x1, blocking collectives, sent_and_summed(): tiles = lax.all_to_all(in_blocks(x, dim, size), axis, 0, 0, tiled=True)  8.17 us
    all_to_all x1, blocking collectives, copy_for_each(): return lax.all_to_all(copies, axis, split_axis=0, concat_axis=0, tiled=True)  7.71 us
    dot_general x1, matrix products, body(): jnp.einsum('stcb,stce->sbte', onehot, looked, precision=lax.Precision.HIG...  7.26 us
    reduce_sum x1, other arithmetic, sent_and_summed(): return jnp.sum(tiles, axis=0)  2.88 us
  transfers between devices with their start and end apart: 1, of which 1 were waited for; matrix products, arithmetic and copies ran while one was open for 0% of the time, Pallas kernels for 0%

commit v1 on v0

v1 whole, which is shorter than its diff:
```python
import functools

import jax
import jax.numpy as jnp
from jax import lax
from jax.experimental import pallas as pl
from jax.experimental.pallas import tpu as pltpu
from jax.sharding import Mesh
from jax.sharding import PartitionSpec as P

ROWS = ("z", "x", "c")
DEAD = 1 << 20


def shifted(value, axis, by):
    size = lax.axis_size(axis)
    return lax.ppermute(value, axis, [(i, (i + by) % size) for i in range(size)])


def split_kernel(own_ref, other_ref, out_ref):
    for place, ref in enumerate((own_ref, other_ref)):
        full = ref[...]
        high = full.astype(jnp.bfloat16)
        low = (full - high.astype(jnp.float32)).astype(jnp.bfloat16)
        out_ref[place, :, :, :128] = high
        out_ref[place, :, :, 128:] = low


def split_tables(own, other):
    tables, rows, width = own.shape
    return pl.pallas_call(
        split_kernel,
        grid=(tables,),
        in_specs=[pl.BlockSpec((1, rows, width), lambda t: (t, 0, 0))] * 2,
        out_specs=pl.BlockSpec((2, 1, rows, 2 * width), lambda t: (0, t, 0, 0)),
        out_shape=jax.ShapeDtypeStruct((2, tables, rows, 2 * width), jnp.bfloat16),
        cost_estimate=pl.CostEstimate(flops=3000000, bytes_accessed=4 << 20, transcendentals=0),
    )(own, other)


def bags_kernel(me_ref, ids_ref, tables_ref, out_ref, *, examples):
    sources = ids_ref.shape[0]
    owners, tables, rows, wide = tables_ref.shape
    slots = ids_ref.shape[3] // 2
    group = 4
    core = me_ref[1]
    row_iota = lax.broadcasted_iota(jnp.int32, (slots, rows), 1)
    key_iota = lax.broadcasted_iota(jnp.int32, (group * examples, group * slots), 0)

    def one_hot(mask):
        return jnp.where(mask, 1.0, 0.0).astype(jnp.bfloat16)

    for t in range(tables):
        total = [None] * (sources // group)
        for o in range(owners):
            ids = ids_ref[:, 0, o * tables + t, :]
            columns = jnp.swapaxes(ids, 0, 1)
            table = tables_ref[o ^ core, t]
            for g in range(sources // group):
                picks = jnp.concatenate(
                    [
                        one_hot(columns[:slots, s : s + 1] == row_iota)
                        for s in range(g * group, (g + 1) * group)
                    ],
                    axis=0,
                )
                looked = jnp.dot(picks, table, preferred_element_type=jnp.float32)
                keys = jnp.concatenate(
                    [
                        ids[g * group + s : g * group + s + 1, slots:] + s * examples
                        for s in range(group)
                    ],
                    axis=1,
                )
                into = one_hot(keys == key_iota)
                part = jnp.dot(into, looked.astype(jnp.bfloat16), preferred_element_type=jnp.float32)
                total[g] = part if total[g] is None else total[g] + part
        for g in range(sources // group):
            summed = total[g][:, : wide // 2] + total[g][:, wide // 2 :]
            out_ref[0, g * group : (g + 1) * group, t * examples : (t + 1) * examples, :] = (
                summed.reshape(group, examples, wide // 2)
            )


def bags(me, ids, tables, offsets, examples):
    sources, ring = ids.shape[0], ids.shape[1]
    owners, count, rows, wide = tables.shape
    first = offsets[0]
    step = (offsets[1] - offsets[0]) if len(offsets) > 1 else 0
    flops = 2 * len(offsets) * sources * owners * count * 64 * wide * (rows + 128)
    return pl.pallas_call(
        functools.partial(bags_kernel, examples=examples),
        grid_spec=pltpu.PrefetchScalarGridSpec(
            num_scalar_prefetch=1,
            grid=(len(offsets),),
            in_specs=[
                pl.BlockSpec(
                    (sources, 1) + ids.shape[2:],
                    lambda k, me: (0, lax.rem(me[0] + first + k * step, ring), 0, 0),
                ),
                pl.BlockSpec(tables.shape, lambda k, me: (0, 0, 0, 0)),
            ],
            out_specs=pl.BlockSpec(
                (1, sources, count * examples, wide // 2), lambda k, me: (k, 0, 0, 0)
            ),
        ),
        out_shape=jax.ShapeDtypeStruct(
            (len(offsets), sources, count * examples, wide // 2), jnp.float32
        ),
        cost_estimate=pl.CostEstimate(flops=flops, bytes_accessed=4 << 20, transcendentals=0),
    )(me, ids, tables)


def close_kernel(parts_ref, dense_ref, pooled_ref, pairs_ref, *, examples):
    pooled = parts_ref[0]
    for k in range(1, parts_ref.shape[0]):
        pooled = pooled + parts_ref[k]
    tables = pooled.shape[0] // examples
    vectors = [dense_ref[...]]
    for t in range(tables):
        one = pooled[t * examples : (t + 1) * examples]
        pooled_ref[:, t, :] = one
        vectors.append(one)
    lane = lax.broadcasted_iota(jnp.int32, pairs_ref.shape, 1)
    pairs = jnp.zeros(pairs_ref.shape, jnp.float32)
    place = 0
    for i in range(tables + 1):
        for j in range(i + 1, tables + 1):
            product = jnp.sum(vectors[i] * vectors[j], axis=1, keepdims=True)
            pairs = jnp.where(lane == place, product, pairs)
            place += 1
    pairs_ref[...] = pairs


def close(parts, dense, tables):
    examples, width = dense.shape
    return pl.pallas_call(
        functools.partial(close_kernel, examples=examples),
        out_shape=(
            jax.ShapeDtypeStruct((examples, tables, width), jnp.float32),
            jax.ShapeDtypeStruct((examples, 128), jnp.float32),
        ),
    )(parts, dense)


def body(embedding, tables, dense_features, slot_rows, slot_examples, slot_counts):
    count = tables.shape[0]
    examples = dense_features.shape[0]
    capacity = slot_rows.shape[3]
    z, x, c = (lax.axis_size(a) for a in ROWS)
    other = shifted(tables, "c", 1)
    live = jnp.arange(capacity, dtype=jnp.int32) < slot_counts[0, :, :, None]
    ids = jnp.concatenate([slot_rows[0], jnp.where(live, slot_examples[0], DEAD)], axis=2)
    ids = ids.reshape(z * x, c * count, 2 * capacity)
    ids = lax.all_to_all(ids, ("z", "x"), 0, 0, tiled=True)
    ids = ids.reshape(z, x, c * count, 2 * capacity)
    split = split_tables(tables, other)
    me = jnp.stack([lax.axis_index("x"), lax.axis_index("c")]).astype(jnp.int32)

    far = bags(me, ids, split, (2,), examples)[0]
    half = far.shape[1] // 2
    from_left = shifted(far[:, :half], "x", 1)
    from_right = shifted(far[:, half:], "x", -1)
    near = bags(me, ids, split, (1, 3), examples)
    to_right = jnp.concatenate([near[0, :, :half] + from_left, near[0, :, half:]], axis=1)
    to_left = jnp.concatenate([near[1, :, :half], near[1, :, half:] + from_right], axis=1)
    right = shifted(to_right, "x", 1)
    left = shifted(to_left, "x", -1)
    mine = bags(me, ids, split, (0,), examples)[0]
    parts = lax.all_to_all(mine + right + left, "z", 0, 0, tiled=True)
    pooled, pairs = close(parts, dense_features, count)
    opposite = shifted(pairs, "y", 2)
    beside = shifted(pairs, "y", 1) + shifted(pairs, "y", -1)
    total = ((pairs + opposite) + beside) * embedding**-0.5
    return pooled, total[:, : count * (count + 1) // 2]


def solution(mesh):
    torus = Mesh(mesh.devices.reshape(8, 4, 2, mesh.shape["cols"]), ROWS + ("y",))
    return jax.shard_map(
        functools.partial(body, 512),
        mesh=torus,
        in_specs=(
            P(None, ROWS, "y"),
            P(ROWS, "y"),
            P(ROWS, None, None, None),
            P(ROWS, None, None, None),
            P(ROWS, None, None),
        ),
        out_specs=(P(ROWS, None, "y"), P(ROWS, None)),
        check_vma=False,
    )
```

time: 142 us -> 97.3 us (0.69); the launches traced: 140 us -> 96.7 us
  blocking collectives: 71 us -> 19.2 us
  matrix products: 31.3 us -> 0 us
  Pallas kernels: 0 us -> 28.9 us
  starting transfers between devices: 11.9 us -> 20.3 us
  waiting for transfers between devices: 12.9 us -> 16 us
  other arithmetic: 7.95 us -> 6.26 us
  local copies, waits for them, and re-layouts: 3.82 us -> 5.28 us
    all_to_all x3 -> x1, blocking collectives: 71 us -> 19.2 us  [body(): parts = lax.all_to_all(mine + right + left, 'z', 0, 0, tiled=True)]
    dot_general x6 -> x0, matrix products: 31.3 us -> none  [the longest x4 23.6 us: one_table(): jnp.einsum('scr,re->sce', selector, table_slice, precision=lax.Precision....]
    pallas_call x0 -> x5, Pallas kernels: none -> 28.9 us  [the longest x3 23.2 us: bags(): pl.pallas_call(functools.partial(bags_kernel, examples=examples), grid_sp...]
    ppermute x0 -> x8, waiting for transfers between devices: none -> 10.4 us  [shifted(): lax.ppermute(value, axis, [(i, (i + by) % size) for i in range(size)])]
    ppermute x0 -> x8, starting transfers between devices: none -> 9.02 us  [shifted(): lax.ppermute(value, axis, [(i, (i + by) % size) for i in range(size)])]
    all_to_all x1, waiting for transfers between devices: 12.9 us -> 5.6 us  [body(): ids = lax.all_to_all(ids, ('z', 'x'), 0, 0, tiled=True)]
    reduce_sum x3 -> x0, other arithmetic: 5.22 us -> none  [the longest x1 2.88 us: sent_and_summed(): return jnp.sum(tiles, axis=0)]
    unnamed x8 -> x6, local copies, waits for them, and re-layouts: 0.23 us -> 3.07 us
  transfers between devices with their start and end apart: 1 -> 9, of which waited for: 1 -> 5; matrix products, arithmetic and copies ran while one was open for 0% -> 5% of each run, Pallas kernels for 0% -> 21%
where the time goes in v1:
time: 97.3 us; the launch traced here: 96.7 us
  Pallas kernels  28.9 us (30%)
  starting transfers between devices  20.3 us (21%)
  blocking collectives  19.2 us (20%)
  waiting for transfers between devices  16 us (16%)
  other arithmetic  6.26 us (6%)
  local copies, waits for them, and re-layouts  5.28 us (5%)
    pallas_call x3, Pallas kernels, bags(): pl.pallas_call(functools.partial(bags_kernel, examples=examples), grid_sp...  23.2 us
    all_to_all x1, blocking collectives, body(): parts = lax.all_to_all(mine + right + left, 'z', 0, 0, tiled=True)  19.2 us
    all_to_all x1, starting transfers between devices, body(): ids = lax.all_to_all(ids, ('z', 'x'), 0, 0, tiled=True)  11.3 us
    ppermute x8, waiting for transfers between devices, shifted(): lax.ppermute(value, axis, [(i, (i + by) % size) for i in range(size)])  10.4 us
    ppermute x8, starting transfers between devices, shifted(): lax.ppermute(value, axis, [(i, (i + by) % size) for i in range(size)])  9.02 us
    all_to_all x1, waiting for transfers between devices, body(): ids = lax.all_to_all(ids, ('z', 'x'), 0, 0, tiled=True)  5.6 us
    pallas_call x1, Pallas kernels, split_tables(): pl.pallas_call(split_kernel, grid=(tables,), in_specs=[pl.BlockSpec((1, r...  3.9 us
    unnamed x6, local copies, waits for them, and re-layouts  3.07 us
  transfers between devices with their start and end apart: 9, of which 5 were waited for; matrix products, arithmetic and copies ran while one was open for 5% of the time, Pallas kernels for 21%

profile of v1, /device:TPU:24, one launch (start us, length us, event | category | flops | bytes accessed | tf_op | source)
XLA Modules:
  0.0 96.7 jit_solution(7629503561530317213)
XLA Ops:
  0.6 0.1 collective-permute-start
  0.7 0.8 copy.8
  1.5 0.1 lt.17
  1.6 1.0 %fusion.3 = s32[32,8,64]{2,1,0:T(8,128)S(1)} fusion(s32[32,8,64]{2,1,0:T(8,128)} %bitcast.24, s32[32,8]{1,0:T(8,128)S(1)} %lt.17), kind=kLoop, calls=%fused_computation.12 | loop fusion | flops 32768 | bytes 132096 | tf_op jit(solution)/shard_map/jit(_where)/select_n | solution.py:153
  2.6 1.7 %pad_add_fusion = s32[32,8,128]{2,1,0:T(8,128)} fusion(s32[32,8,64]{2,1,0:T(8,128)S(1)} %fusion.3, s32[32,8,64]{2,1,0:T(8,128)} %bitcast.23), kind=kLoop, calls=%fused_computation.10 | loop fusion | flops 32768 | bytes 262144 | tf_op jit(solution)/shard_map/concatenate | solution.py:153
  4.3 11.3 %all-to-all-start = ((s32[32,8,128]{2,1,0:T(8,128)}), s32[32,8,128]{2,1,0:T(8,128)S(1)}, u32[]{:S(2)}, u32[]{:S(2)}) async-start(s32[32,8,128]{2,1,0:T(8,128)} %pad_add_fusion), calls=%async_computation | async-start | bytes 262144 | tf_op jit(solution)/shard_map/all_to_all | solution.py:155
  15.6 0.6 pad_add_fusion.1.me_ref
  16.2 1.0 %copy-done = f32[4,512,128]{2,1,0:T(8,128)} copy-done((f32[4,512,128]{2,1,0:T(8,128)}, f32[4,512,128]{2,1,0:T(8,128)S(1)}, u32[]{:S(2)}) %copy-start) | copy-done | bytes 1048600
  17.1 3.9 %shard_map.68.tables_ref = bf16[2,4,512,256]{3,2,1,0:T(8,128)(2,1)} custom-call(f32[4,512,128]{2,1,0:T(8,128)} %own_ref.1, f32[4,512,128]{2,1,0:T(8,128)} %copy-done), custom_call_target="tpu_custom_call" | custom-call | flops 3000000 | bytes 4194304 | tf_op jit(solution)/shard_map/pallas_call | solution.py:31
  21.0 5.6 %all-to-all-done = s32[32,8,128]{2,1,0:T(8,128)S(1)} async-done(((s32[32,8,128]{2,1,0:T(8,128)}), s32[32,8,128]{2,1,0:T(8,128)S(1)}, u32[]{:S(2)}, u32[]{:S(2)}) %all-to-all-start) | async-done | bytes 131104 | tf_op jit(solution)/shard_map/all_to_all | solution.py:155
  26.6 0.7 copy-done.1
  27.3 6.5 %shard_map.71 = f32[1,8,128,128]{3,2,1,0:T(8,128)} custom-call(s32[2]{0:T(128)} %pad_add_fusion.1.me_ref, s32[8,4,8,128]{3,2,1,0:T(8,128)} %bitcast.25, bf16[2,4,512,256]{3,2,1,0:T(8,128)(2,1)} %shard_map.68.tables_ref), custom_call_target="tpu_custom_call" | custom-call | flops 1342177280 | bytes 4194304 | tf_op jit(solution)/shard_map/pallas_call | solution.py:91
  33.8 1.1 %fusion.6 = (f32[8,64,128]{2,1,0:T(8,128)S(1)}, f32[8,64,128]{2,1,0:T(8,128)S(1)}) fusion(f32[8,128,128]{2,1,0:T(8,128)} %bitcast.22), kind=kLoop, calls=%fused_computation.18 | loop fusion | bytes 1048576 | tf_op jit(solution)/shard_map/slice | solution.py:162
  34.9 0.1 collective-permute-start.1
  35.0 3.2 %collective-permute-start.3 = (f32[8,64,128]{2,1,0:T(8,128)S(1)}, f32[8,64,128]{2,1,0:T(8,128)S(1)}, u32[]{:S(2)}, u32[]{:S(2)}) collective-permute-start(f32[8,64,128]{2,1,0:T(8,128)S(1)} %get-tuple-element.15), channel_id=1, source_target_pairs={{0,24},{8,0},{16,8},{24,16},{1,25},{9,1},{17,9},{25,17},{2,26},{10... | collective-permute-start | bytes 786440 | tf_op jit(solution)/shard_map/ppermute | solution.py:17
  38.2 10.1 %shard_map.70 = f32[2,8,128,128]{3,2,1,0:T(8,128)} custom-call(s32[2]{0:T(128)} %pad_add_fusion.1.me_ref, s32[8,4,8,128]{3,2,1,0:T(8,128)} %bitcast.26, bf16[2,4,512,256]{3,2,1,0:T(8,128)(2,1)} %shard_map.68.tables_ref), custom_call_target="tpu_custom_call" | custom-call | flops 2684354560 | bytes 4194304 | tf_op jit(solution)/shard_map/pallas_call | solution.py:91
  48.3 1.1 %slice_bitcast_fusion.2 = (f32[8,64,128]{2,1,0:T(8,128)S(1)}, f32[8,64,128]{2,1,0:T(8,128)S(1)}) fusion(f32[2,8,128,128]{3,2,1,0:T(8,128)} %shard_map.70), kind=kLoop, calls=%fused_computation.7 | loop fusion | bytes 1048576 | tf_op jit(solution)/shard_map/squeeze | solution.py:165
  49.4 1.1 %fusion.2 = (f32[8,64,128]{2,1,0:T(8,128)S(1)}, f32[8,64,128]{2,1,0:T(8,128)S(1)}) fusion(f32[8,64,128]{2,1,0:T(8,128)S(1)} %collective-permute-done.1, f32[2,8,128,128]{3,2,1,0:T(8,128)} %shard_map.70, f32[8,64,128]{2,1,0:T(8,128)S(1)} %collective-permute-done.3), kind=kLoop, calls=%fused_computation.9 | loop fusion | flops 131072 | bytes 1572864 | tf_op jit(solution)/shard_map/add | solution.py:165
  50.5 0.3 collective-permute-start.4
  50.9 2.1 %collective-permute-start.2 = (f32[8,128,128]{2,1,0:T(8,128)S(1)}, f32[8,128,128]{2,1,0:T(8,128)S(1)}, u32[]{:S(2)}, u32[]{:S(2)}) collective-permute-start(f32[8,128,128]{2,1,0:T(8,128)S(1)} %pad_maximum_fusion), channel_id=1, source_target_pairs={{0,8},{8,16},{16,24},{24,0},{1,9},{9,17},{17,25},{25,1},{2,10},{10... | collective-permute-start | bytes 1572872 | tf_op jit(solution)/shard_map/ppermute | solution.py:17
  52.9 6.5 %shard_map.69 = f32[1,8,128,128]{3,2,1,0:T(8,128)} custom-call(s32[2]{0:T(128)} %pad_add_fusion.1.me_ref, s32[8,4,8,128]{3,2,1,0:T(8,128)} %bitcast.27, bf16[2,4,512,256]{3,2,1,0:T(8,128)(2,1)} %shard_map.68.tables_ref), custom_call_target="tpu_custom_call" | custom-call | flops 1342177280 | bytes 4194304 | tf_op jit(solution)/shard_map/pallas_call | solution.py:91
  59.5 3.5 %collective-permute-done.4 = f32[8,128,128]{2,1,0:T(8,128)S(1)} collective-permute-done((f32[8,128,128]{2,1,0:T(8,128)S(1)}, f32[8,128,128]{2,1,0:T(8,128)S(1)}, u32[]{:S(2)}, u32[]{:S(2)}) %collective-permute-start.4) | collective-permute-done | bytes 524320 | tf_op jit(solution)/shard_map/ppermute | solution.py:17
  63.0 1.5 %collective-permute-done.2 = f32[8,128,128]{2,1,0:T(8,128)S(1)} collective-permute-done((f32[8,128,128]{2,1,0:T(8,128)S(1)}, f32[8,128,128]{2,1,0:T(8,128)S(1)}, u32[]{:S(2)}, u32[]{:S(2)}) %collective-permute-start.2) | collective-permute-done | bytes 524320 | tf_op jit(solution)/shard_map/ppermute | solution.py:17
  64.5 1.1 %fusion = f32[8,128,128]{2,1,0:T(8,128)S(1)} fusion(f32[8,128,128]{2,1,0:T(8,128)S(1)} %collective-permute-done.4, f32[8,128,128]{2,1,0:T(8,128)S(1)} %collective-permute-done.2, f32[1,8,128,128]{3,2,1,0:T(8,128)} %shard_map.69), kind=kLoop, calls=%fused_computation.3 | loop fusion | flops 262144 | bytes 2097152 | tf_op jit(solution)/shard_map/add | solution.py:170
  65.6 19.2 %all_to_all.10.parts_ref = f32[8,128,128]{2,1,0:T(8,128)} all-to-all(f32[8,128,128]{2,1,0:T(8,128)S(1)} %fusion), channel_id=1, replica_groups=mesh['z'=8,'x'=4,'c'=2,'y'=4] {'z'}, dimensions={0} | all-to-all | bytes 1048576 | tf_op jit(solution)/shard_map/all_to_all | solution.py:170
  84.8 1.8 %shard_map.72 = (f32[32,4,128]{2,1,0:T(4,128)}, f32[32,128]{1,0:T(8,128)}) custom-call(f32[8,128,128]{2,1,0:T(8,128)} %all_to_all.10.parts_ref, f32[32,128]{1,0:T(8,128)} %dense_ref.1), custom_call_target="tpu_custom_call" | custom-call | tf_op jit(solution)/shard_map/pallas_call | solution.py:137
  86.6 0.7 collective-permute-start.7
  87.4 2.5 %collective-permute-start.6 = (f32[32,128]{1,0:T(8,128)}, f32[32,128]{1,0:T(8,128)S(1)}, u32[]{:S(2)}, u32[]{:S(2)}) collective-permute-start(f32[32,128]{1,0:T(8,128)} %get-tuple-element.5), channel_id=1, source_target_pairs={{0,1},{1,2},{2,3},{3,0},{4,5},{5,6},{6,7},{7,4},{8,9},{9,10},{10,1... | collective-permute-start | bytes 49160 | tf_op jit(solution)/shard_map/ppermute | solution.py:17
  89.9 1.9 %collective-permute-done.7 = f32[32,128]{1,0:T(8,128)S(1)} collective-permute-done((f32[32,128]{1,0:T(8,128)}, f32[32,128]{1,0:T(8,128)S(1)}, u32[]{:S(2)}, u32[]{:S(2)}) %collective-permute-start.7) | collective-permute-done | bytes 16416 | tf_op jit(solution)/shard_map/ppermute | solution.py:17
  91.8 3.5 %collective-permute-done.5 = f32[32,128]{1,0:T(8,128)S(1)} collective-permute-done((f32[32,128]{1,0:T(8,128)}, f32[32,128]{1,0:T(8,128)S(1)}, u32[]{:S(2)}, u32[]{:S(2)}) %collective-permute-start.5) | collective-permute-done | bytes 16416 | tf_op jit(solution)/shard_map/ppermute | solution.py:17
  95.3 0.7 fusion.5
  96.0 0.7 copy.9
  (9 shorter events, 0.1 us)
Async XLA Ops:
  0.6 15.5 %collective-permute-start = (f32[4,512,128]{2,1,0:T(8,128)}, f32[4,512,128]{2,1,0:T(8,128)S(1)}, u32[]{:S(2)}, u32[]{:S(2)}) collective-permute-start(f32[4,512,128]{2,1,0:T(8,128)} %own_ref.1), channel_id=1, source_target_pairs={{0,4},{4,0},{1,5},{5,1},{2,6},{6,2},{3,7},{7,3},{8,12},{12,8},{9,1... | collective-permute-start | bytes 3145736 | tf_op jit(solution)/shard_map/ppermute | solution.py:17
  4.3 22.4 %all-to-all-start = ((s32[32,8,128]{2,1,0:T(8,128)}), s32[32,8,128]{2,1,0:T(8,128)S(1)}, u32[]{:S(2)}, u32[]{:S(2)}) async-start(s32[32,8,128]{2,1,0:T(8,128)} %pad_add_fusion), calls=%async_computation | async-start | bytes 262144 | tf_op jit(solution)/shard_map/all_to_all | solution.py:155
  16.2 1.0 %copy-start = (f32[4,512,128]{2,1,0:T(8,128)}, f32[4,512,128]{2,1,0:T(8,128)S(1)}, u32[]{:S(2)}) copy-start(f32[4,512,128]{2,1,0:T(8,128)S(1)} %collective-permute-done.other_ref) | copy-start | bytes 3145732
  26.6 0.7 copy-start.1
  34.9 14.5 %collective-permute-start.1 = (f32[8,64,128]{2,1,0:T(8,128)S(1)}, f32[8,64,128]{2,1,0:T(8,128)S(1)}, u32[]{:S(2)}, u32[]{:S(2)}) collective-permute-start(f32[8,64,128]{2,1,0:T(8,128)S(1)} %get-tuple-element.14), channel_id=1, source_target_pairs={{0,8},{8,16},{16,24},{24,0},{1,9},{9,17},{17,25},{25,1},{2,10},{10... | collective-permute-start | bytes 786440 | tf_op jit(solution)/shard_map/ppermute | solution.py:17
  35.0 14.4 %collective-permute-start.3 = (f32[8,64,128]{2,1,0:T(8,128)S(1)}, f32[8,64,128]{2,1,0:T(8,128)S(1)}, u32[]{:S(2)}, u32[]{:S(2)}) collective-permute-start(f32[8,64,128]{2,1,0:T(8,128)S(1)} %get-tuple-element.15), channel_id=1, source_target_pairs={{0,24},{8,0},{16,8},{24,16},{1,25},{9,1},{17,9},{25,17},{2,26},{10... | collective-permute-start | bytes 786440 | tf_op jit(solution)/shard_map/ppermute | solution.py:17
  50.5 12.4 %collective-permute-start.4 = (f32[8,128,128]{2,1,0:T(8,128)S(1)}, f32[8,128,128]{2,1,0:T(8,128)S(1)}, u32[]{:S(2)}, u32[]{:S(2)}) collective-permute-start(f32[8,128,128]{2,1,0:T(8,128)S(1)} %pad_maximum_fusion.1), channel_id=1, source_target_pairs={{0,24},{8,0},{16,8},{24,16},{1,25},{9,1},{17,9},{25,17},{2,26},{10... | collective-permute-start | bytes 1572872 | tf_op jit(solution)/shard_map/ppermute | solution.py:17
  50.9 13.6 %collective-permute-start.2 = (f32[8,128,128]{2,1,0:T(8,128)S(1)}, f32[8,128,128]{2,1,0:T(8,128)S(1)}, u32[]{:S(2)}, u32[]{:S(2)}) collective-permute-start(f32[8,128,128]{2,1,0:T(8,128)S(1)} %pad_maximum_fusion), channel_id=1, source_target_pairs={{0,8},{8,16},{16,24},{24,0},{1,9},{9,17},{17,25},{25,1},{2,10},{10... | collective-permute-start | bytes 1572872 | tf_op jit(solution)/shard_map/ppermute | solution.py:17
  86.6 5.2 %collective-permute-start.7 = (f32[32,128]{1,0:T(8,128)}, f32[32,128]{1,0:T(8,128)S(1)}, u32[]{:S(2)}, u32[]{:S(2)}) collective-permute-start(f32[32,128]{1,0:T(8,128)} %get-tuple-element.5), channel_id=1, source_target_pairs={{0,3},{1,0},{2,1},{3,2},{4,7},{5,4},{6,5},{7,6},{8,11},{9,8},{10,9... | collective-permute-start | bytes 49160 | tf_op jit(solution)/shard_map/ppermute | solution.py:17
  87.4 4.4 %collective-permute-start.6 = (f32[32,128]{1,0:T(8,128)}, f32[32,128]{1,0:T(8,128)S(1)}, u32[]{:S(2)}, u32[]{:S(2)}) collective-permute-start(f32[32,128]{1,0:T(8,128)} %get-tuple-element.5), channel_id=1, source_target_pairs={{0,1},{1,2},{2,3},{3,0},{4,5},{5,6},{6,7},{7,4},{8,9},{9,10},{10,1... | collective-permute-start | bytes 49160 | tf_op jit(solution)/shard_map/ppermute | solution.py:17
  89.9 5.5 %collective-permute-start.5 = (f32[32,128]{1,0:T(8,128)}, f32[32,128]{1,0:T(8,128)S(1)}, u32[]{:S(2)}, u32[]{:S(2)}) collective-permute-start(f32[32,128]{1,0:T(8,128)} %get-tuple-element.5), channel_id=1, source_target_pairs={{0,2},{1,3},{2,0},{3,1},{4,6},{5,7},{6,4},{7,5},{8,10},{9,11},{10,... | collective-permute-start | bytes 49160 | tf_op jit(solution)/shard_map/ppermute | solution.py:17

commit v2 on v1

v2 whole, which is shorter than its diff:
```python
import functools

import jax
import jax.numpy as jnp
from jax import lax
from jax.experimental import pallas as pl
from jax.experimental.pallas import tpu as pltpu
from jax.sharding import Mesh
from jax.sharding import PartitionSpec as P

ROWS = ("z", "x", "c")
DEAD = 1 << 20
VMEM = pl.BlockSpec(memory_space=pltpu.VMEM)


def shifted(value, axis, by):
    size = lax.axis_size(axis)
    return lax.ppermute(value, axis, [(i, (i + by) % size) for i in range(size)])


def local_kernel(kernel, out_shape, operands, flops=1 << 20, vmem=12 << 20):
    single = not isinstance(out_shape, tuple)
    return pl.pallas_call(
        kernel,
        in_specs=[VMEM] * len(operands),
        out_specs=VMEM if single else (VMEM,) * len(out_shape),
        out_shape=out_shape,
        compiler_params=pltpu.CompilerParams(vmem_limit_bytes=vmem),
        cost_estimate=pl.CostEstimate(flops=flops, bytes_accessed=1 << 20, transcendentals=0),
    )(*operands)


def prepare_kernel(rows_ref, examples_ref, counts_ref, out_ref):
    buckets, capacity = rows_ref.shape
    tables, owners = counts_ref.shape
    bucket = lax.broadcasted_iota(jnp.int32, (buckets, owners), 0)
    owner = lax.broadcasted_iota(jnp.int32, (buckets, owners), 1)
    spread = jnp.where(bucket // tables == owner, 1.0, 0.0).astype(jnp.bfloat16)
    counts = counts_ref[...].astype(jnp.float32).astype(jnp.bfloat16)
    by_table = lax.dot_general(
        spread, counts, (((1,), (1,)), ((), ())), preferred_element_type=jnp.float32
    )
    table = lax.broadcasted_iota(jnp.int32, (buckets, tables), 1)
    own = lax.broadcasted_iota(jnp.int32, (buckets, tables), 0) % tables
    count = jnp.sum(jnp.where(table == own, by_table, 0.0), axis=1, keepdims=True)
    slot = lax.broadcasted_iota(jnp.int32, (buckets, capacity), 1).astype(jnp.float32)
    out_ref[:, :capacity] = rows_ref[...]
    out_ref[:, capacity:] = jnp.where(slot < count, examples_ref[...], DEAD)


def split_kernel(own_ref, other_ref, out_ref):
    width = own_ref.shape[2]
    for place, ref in enumerate((own_ref, other_ref)):
        for t in range(ref.shape[0]):
            full = ref[t]
            high = full.astype(jnp.bfloat16)
            out_ref[place, t, :, :width] = high
            out_ref[place, t, :, width:] = (full - high.astype(jnp.float32)).astype(jnp.bfloat16)


def one_hot(mask):
    return jnp.where(mask, 1.0, 0.0).astype(jnp.bfloat16)


def bags_kernel(ids_ref, tables_ref, *out_refs, items, examples):
    sources, ring = ids_ref.shape[:2]
    owners, count, rows, wide = tables_ref.shape
    slots = ids_ref.shape[3] // 2
    group = 4
    core = lax.axis_index("c")
    me = lax.axis_index("x")
    row_iota = lax.broadcasted_iota(jnp.int32, (slots, rows), 1)
    key_iota = lax.broadcasted_iota(jnp.int32, (group * examples, group * slots), 0)
    for (away, tables), out_ref in zip(items, out_refs):
        column = lax.rem(me + away, ring)
        for place, t in enumerate(tables):
            total = [None] * (sources // group)
            for o in range(owners):
                ids = ids_ref[:, column, o * count + t, :]
                columns = jnp.swapaxes(ids, 0, 1)
                table = tables_ref[o ^ core, t]
                for g in range(sources // group):
                    first = g * group
                    picks = jnp.concatenate(
                        [
                            one_hot(columns[:slots, s : s + 1] == row_iota)
                            for s in range(first, first + group)
                        ],
                        axis=0,
                    )
                    looked = jnp.dot(picks, table, preferred_element_type=jnp.float32)
                    keys = jnp.concatenate(
                        [
                            ids[first + s : first + s + 1, slots:] + s * examples
                            for s in range(group)
                        ],
                        axis=1,
                    )
                    part = jnp.dot(
                        one_hot(keys == key_iota),
                        looked.astype(jnp.bfloat16),
                        preferred_element_type=jnp.float32,
                    )
                    total[g] = part if total[g] is None else total[g] + part
            for g in range(sources // group):
                summed = total[g][:, : wide // 2] + total[g][:, wide // 2 :]
                out_ref[
                    g * group : (g + 1) * group, place * examples : (place + 1) * examples, :
                ] = summed.reshape(group, examples, wide // 2)


def bags(ids, tables, items, examples):
    sources = ids.shape[0]
    owners, count, rows, wide = tables.shape
    tasks = sum(len(t) for _, t in items)
    out = tuple(
        jax.ShapeDtypeStruct((sources, len(t) * examples, wide // 2), jnp.float32)
        for _, t in items
    )
    return local_kernel(
        functools.partial(bags_kernel, items=items, examples=examples),
        out,
        (ids, tables),
        flops=2 * tasks * sources * owners * 64 * wide * (rows + 128),
    )


def add_kernel(left_ref, left_part_ref, right_ref, right_part_ref, a_ref, b_ref):
    a_ref[...] = left_ref[...] + left_part_ref[...]
    b_ref[...] = right_ref[...] + right_part_ref[...]


def join_kernel(*refs):
    out_ref = refs[-1]
    half = refs[0].shape[1]
    for place in range(2):
        one, two, three = refs[3 * place : 3 * place + 3]
        out_ref[:, place * half : (place + 1) * half, :] = one[...] + two[...] + three[...]


def close_kernel(parts_ref, dense_ref, pooled_ref, pairs_ref, *, examples):
    pooled = parts_ref[0]
    for k in range(1, parts_ref.shape[0]):
        pooled = pooled + parts_ref[k]
    tables = pooled.shape[0] // examples
    vectors = [dense_ref[...]]
    for t in range(tables):
        one = pooled[t * examples : (t + 1) * examples]
        pooled_ref[:, t, :] = one
        vectors.append(one)
    lane = lax.broadcasted_iota(jnp.int32, dense_ref.shape, 1)
    pairs = jnp.zeros(dense_ref.shape, jnp.float32)
    place = 0
    for i in range(tables + 1):
        for j in range(i + 1, tables + 1):
            product = jnp.sum(vectors[i] * vectors[j], axis=1, keepdims=True)
            pairs = jnp.where(lane == place, product, pairs)
            place += 1
    pairs_ref[...] = jnp.swapaxes(pairs, 0, 1)[: pairs_ref.shape[0]]


def body(embedding, tables, dense_features, slot_rows, slot_examples, slot_counts):
    count = tables.shape[0]
    examples, width = dense_features.shape
    capacity = slot_rows.shape[3]
    z, x, c = (lax.axis_size(a) for a in ROWS)
    owners = z * x * c
    other = shifted(tables, "c", 1)
    ids = local_kernel(
        prepare_kernel,
        jax.ShapeDtypeStruct((owners * count, 2 * capacity), jnp.int32),
        (
            slot_rows.reshape(owners * count, capacity),
            slot_examples.reshape(owners * count, capacity),
            slot_counts[0].T,
        ),
    )
    ids = ids.reshape(z * x, c * count, 2 * capacity)
    ids = lax.all_to_all(ids, ("z", "x"), 0, 0, tiled=True)
    ids = ids.reshape(z, x, c * count, 2 * capacity)
    split = local_kernel(
        split_kernel,
        jax.ShapeDtypeStruct((2,) + tables.shape[:2] + (2 * width,), jnp.bfloat16),
        (tables, other),
        flops=4 << 20,
    )
    low, high = tuple(range(count // 2)), tuple(range(count // 2, count))

    far_low, far_high = bags(ids, split, ((2, low), (2, high)), examples)
    from_left = shifted(far_low, "x", 1)
    from_right = shifted(far_high, "x", -1)
    right_high, left_low = bags(ids, split, ((1, high), (3, low)), examples)
    right_high = shifted(right_high, "x", 1)
    left_low = shifted(left_low, "x", -1)
    right_low, left_high = bags(ids, split, ((1, low), (3, high)), examples)
    half = jax.ShapeDtypeStruct(right_low.shape, jnp.float32)
    right_low, left_high = local_kernel(
        add_kernel, (half, half), (right_low, from_left, left_high, from_right)
    )
    right_low = shifted(right_low, "x", 1)
    left_high = shifted(left_high, "x", -1)
    mine_low, mine_high = bags(ids, split, ((0, low), (0, high)), examples)
    parts = local_kernel(
        join_kernel,
        jax.ShapeDtypeStruct((z, count * examples, width), jnp.float32),
        (mine_low, right_low, left_low, mine_high, right_high, left_high),
    )
    parts = lax.all_to_all(parts, "z", 0, 0, tiled=True)
    pairs = count * (count + 1) // 2
    pooled, products = local_kernel(
        functools.partial(close_kernel, examples=examples),
        (
            jax.ShapeDtypeStruct((examples, count, width), jnp.float32),
            jax.ShapeDtypeStruct((pairs, examples), jnp.float32),
        ),
        (parts, dense_features),
    )
    opposite = shifted(products, "y", 2)
    beside = shifted(products, "y", 1) + shifted(products, "y", -1)
    total = ((products + opposite) + beside) * embedding**-0.5
    return pooled, total.T


def solution(mesh):
    torus = Mesh(mesh.devices.reshape(8, 4, 2, mesh.shape["cols"]), ROWS + ("y",))
    return jax.shard_map(
        functools.partial(body, 512),
        mesh=torus,
        in_specs=(
            P(None, ROWS, "y"),
            P(ROWS, "y"),
            P(ROWS, None, None, None),
            P(ROWS, None, None, None),
            P(ROWS, None, None),
        ),
        out_specs=(P(ROWS, None, "y"), P(ROWS, None)),
        check_vma=False,
    )
```

time: 97.3 us -> 79 us (0.81)
  Pallas kernels: 28.9 us -> 16.1 us
  other arithmetic: 6.26 us -> 0.6 us
  starting transfers between devices: 20.3 us -> 23.5 us
  local copies, waits for them, and re-layouts: 5.28 us -> 3.71 us
    pallas_call x5 -> x9, Pallas kernels: 28.9 us -> 16.1 us  [local_kernel(): pl.pallas_call(kernel, in_specs=[VMEM] * len(operands), out_specs=VMEM if...]
    ppermute x8 -> x10, waiting for transfers between devices: 10.4 us -> 6.28 us  [shifted(): lax.ppermute(value, axis, [(i, (i + by) % size) for i in range(size)])]
    all_to_all x1, waiting for transfers between devices: 5.6 us -> 9.38 us  [body(): ids = lax.all_to_all(ids, ('z', 'x'), 0, 0, tiled=True)]
    ppermute x8 -> x10, starting transfers between devices: 9.02 us -> 12.2 us  [shifted(): lax.ppermute(value, axis, [(i, (i + by) % size) for i in range(size)])]
    add x2 -> x0, other arithmetic: 2.22 us -> none  [the longest x1 1.12 us: body(): parts = lax.all_to_all(mine + right + left, 'z', 0, 0, tiled=True)]
    concatenate x3 -> x0, other arithmetic: 1.74 us -> none  [the longest x1 1.67 us: body(): jnp.concatenate([slot_rows[0], jnp.where(live, slot_examples[0], DEAD)],...]
    slice x1 -> x0, local copies, waits for them, and re-layouts: 1.07 us -> none  [body(): from_left = shifted(far[:, :half], 'x', 1)]
    squeeze x1 -> x0, local copies, waits for them, and re-layouts: 1.07 us -> none  [body(): near[0, :, half:]]
  transfers between devices with their start and end apart: 9 -> 11, of which waited for: 5 -> 4; matrix products, arithmetic and copies ran while one was open for 5% -> 0% of each run, Pallas kernels for 21% -> 15%
where the time goes in v2:
time: 79 us; the launch traced here: 78.7 us
  starting transfers between devices  23.5 us (30%)
  blocking collectives  18.3 us (23%)
  Pallas kernels  16.1 us (20%)
  waiting for transfers between devices  15.7 us (20%)
  local copies, waits for them, and re-layouts  3.71 us (5%)
  between operations  0.79 us (1%)
    all_to_all x1, blocking collectives, body(): parts = lax.all_to_all(parts, 'z', 0, 0, tiled=True)  18.3 us
    pallas_call x9, Pallas kernels, local_kernel(): pl.pallas_call(kernel, in_specs=[VMEM] * len(operands), out_specs=VMEM if...  16.1 us
    ppermute x10, starting transfers between devices, shifted(): lax.ppermute(value, axis, [(i, (i + by) % size) for i in range(size)])  12.2 us
    all_to_all x1, starting transfers between devices, body(): ids = lax.all_to_all(ids, ('z', 'x'), 0, 0, tiled=True)  11.3 us
    all_to_all x1, waiting for transfers between devices, body(): ids = lax.all_to_all(ids, ('z', 'x'), 0, 0, tiled=True)  9.38 us
    ppermute x10, waiting for transfers between devices, shifted(): lax.ppermute(value, axis, [(i, (i + by) % size) for i in range(size)])  6.28 us
    unnamed x10, local copies, waits for them, and re-layouts  3.71 us
  transfers between devices with their start and end apart: 11, of which 4 were waited for; matrix products, arithmetic and copies ran while one was open for 0% of the time, Pallas kernels for 15%

profile of v2, /device:TPU:24, one launch (start us, length us, event | category | flops | bytes accessed | tf_op | source)
XLA Modules:
  0.0 78.7 jit_solution(15723484193379519948)
XLA Ops:
  0.6 0.1 collective-permute-start
  0.7 0.9 %copy-done.1 = s32[1,64,4,64]{3,2,1,0:T(4,128)S(1)} copy-done((s32[1,64,4,64]{3,2,1,0:T(4,128)S(1)}, s32[1,64,4,64]{3,2,1,0:T(4,128)}, u32[]{:S(2)}) %copy-start.1) | copy-done | bytes 65560
  1.6 0.9 %copy-done.2 = s32[1,64,4,64]{3,2,1,0:T(4,128)S(1)} copy-done((s32[1,64,4,64]{3,2,1,0:T(4,128)S(1)}, s32[1,64,4,64]{3,2,1,0:T(4,128)}, u32[]{:S(2)}) %copy-start.2) | copy-done | bytes 65560
  2.5 0.7 copy-done.4
  3.2 1.0 %shard_map.68 = s32[256,128]{1,0:T(8,128)} custom-call(s32[256,64]{1,0:T(8,128)S(1)} %bitcast.9, s32[256,64]{1,0:T(8,128)S(1)} %bitcast.10, s32[4,64]{1,0:T(4,128)S(1)} %bitcast.15), custom_call_target="tpu_custom_call" | custom-call | flops 1048576 | bytes 1048576 | tf_op jit(solution)/shard_map/pallas_call | solution.py:23
  4.2 11.3 %all-to-all-start = ((s32[32,8,128]{2,1,0:T(8,128)}), s32[32,8,128]{2,1,0:T(8,128)S(1)}, u32[]{:S(2)}, u32[]{:S(2)}) async-start(s32[32,8,128]{2,1,0:T(8,128)} %bitcast.4), calls=%async_computation | async-start | bytes 262144 | tf_op jit(solution)/shard_map/all_to_all | solution.py:179
  15.5 0.0 collective-permute-done.other_ref
  15.5 0.0 copy-start
  15.5 1.2 %copy-done = f32[4,512,128]{2,1,0:T(8,128)S(1)} copy-done((f32[4,512,128]{2,1,0:T(8,128)S(1)}, f32[4,512,128]{2,1,0:T(8,128)}, u32[]{:S(2)}) %copy-start) | copy-done | bytes 1048600
  16.7 0.4 shard_map.69.tables_ref
  17.2 9.4 %all-to-all-done = s32[32,8,128]{2,1,0:T(8,128)S(1)} async-done(((s32[32,8,128]{2,1,0:T(8,128)}), s32[32,8,128]{2,1,0:T(8,128)S(1)}, u32[]{:S(2)}, u32[]{:S(2)}) %all-to-all-start) | async-done | bytes 131104 | tf_op jit(solution)/shard_map/all_to_all | solution.py:179
  26.6 3.5 %shard_map.72 = (f32[8,64,128]{2,1,0:T(8,128)S(1)}, f32[8,64,128]{2,1,0:T(8,128)S(1)}) custom-call(s32[8,4,8,128]{3,2,1,0:T(8,128)S(1)} %bitcast.11, bf16[2,4,512,256]{3,2,1,0:T(8,128)(2,1)S(1)} %shard_map.69.tables_ref), custom_call_target="tpu_custom_call" | custom-call | flops 1342177280 | bytes 1048576 | tf_op jit(solution)/shard_map/pallas_call | solution.py:23
  30.0 0.1 collective-permute-start.1
  30.1 3.2 %collective-permute-start.2 = (f32[8,64,128]{2,1,0:T(8,128)S(1)}, f32[8,64,128]{2,1,0:T(8,128)S(1)}, u32[]{:S(2)}, u32[]{:S(2)}) collective-permute-start(f32[8,64,128]{2,1,0:T(8,128)S(1)} %get-tuple-element.18), channel_id=1, source_target_pairs={{0,24},{8,0},{16,8},{24,16},{1,25},{9,1},{17,9},{25,17},{2,26},{10... | collective-permute-start | bytes 786440 | tf_op jit(solution)/shard_map/ppermute | solution.py:18
  33.4 3.5 %shard_map.74 = (f32[8,64,128]{2,1,0:T(8,128)S(1)}, f32[8,64,128]{2,1,0:T(8,128)S(1)}) custom-call(s32[8,4,8,128]{3,2,1,0:T(8,128)S(1)} %bitcast.12, bf16[2,4,512,256]{3,2,1,0:T(8,128)(2,1)S(1)} %shard_map.69.tables_ref), custom_call_target="tpu_custom_call" | custom-call | flops 1342177280 | bytes 1048576 | tf_op jit(solution)/shard_map/pallas_call | solution.py:23
  36.8 0.3 collective-permute-start.4
  37.1 1.8 %collective-permute-start.5 = (f32[8,64,128]{2,1,0:T(8,128)S(1)}, f32[8,64,128]{2,1,0:T(8,128)S(1)}, u32[]{:S(2)}, u32[]{:S(2)}) collective-permute-start(f32[8,64,128]{2,1,0:T(8,128)S(1)} %get-tuple-element.22), channel_id=1, source_target_pairs={{0,8},{8,16},{16,24},{24,0},{1,9},{9,17},{17,25},{25,1},{2,10},{10... | collective-permute-start | bytes 786440 | tf_op jit(solution)/shard_map/ppermute | solution.py:18
  38.9 3.5 %shard_map.71 = (f32[8,64,128]{2,1,0:T(8,128)S(1)}, f32[8,64,128]{2,1,0:T(8,128)S(1)}) custom-call(s32[8,4,8,128]{3,2,1,0:T(8,128)S(1)} %bitcast.13, bf16[2,4,512,256]{3,2,1,0:T(8,128)(2,1)S(1)} %shard_map.69.tables_ref), custom_call_target="tpu_custom_call" | custom-call | flops 1342177280 | bytes 1048576 | tf_op jit(solution)/shard_map/pallas_call | solution.py:23
  42.4 0.1 shard_map.73
  42.5 0.1 collective-permute-start.3
  42.6 3.2 %collective-permute-start.6 = (f32[8,64,128]{2,1,0:T(8,128)S(1)}, f32[8,64,128]{2,1,0:T(8,128)S(1)}, u32[]{:S(2)}, u32[]{:S(2)}) collective-permute-start(f32[8,64,128]{2,1,0:T(8,128)S(1)} %get-tuple-element.23), channel_id=1, source_target_pairs={{0,24},{8,0},{16,8},{24,16},{1,25},{9,1},{17,9},{25,17},{2,26},{10... | collective-permute-start | bytes 786440 | tf_op jit(solution)/shard_map/ppermute | solution.py:18
  45.8 3.5 %shard_map.70 = (f32[8,64,128]{2,1,0:T(8,128)S(1)}, f32[8,64,128]{2,1,0:T(8,128)S(1)}) custom-call(s32[8,4,8,128]{3,2,1,0:T(8,128)S(1)} %bitcast.14, bf16[2,4,512,256]{3,2,1,0:T(8,128)(2,1)S(1)} %shard_map.69.tables_ref), custom_call_target="tpu_custom_call" | custom-call | flops 1342177280 | bytes 1048576 | tf_op jit(solution)/shard_map/pallas_call | solution.py:23
  49.3 0.0 copy-start.3
  49.3 1.4 %collective-permute-done.3.refs_1_ = f32[8,64,128]{2,1,0:T(8,128)S(1)} collective-permute-done((f32[8,64,128]{2,1,0:T(8,128)S(1)}, f32[8,64,128]{2,1,0:T(8,128)S(1)}, u32[]{:S(2)}, u32[]{:S(2)}) %collective-permute-start.3) | collective-permute-done | bytes 262176 | tf_op jit(solution)/shard_map/ppermute | solution.py:18
  50.7 0.1 shard_map.75
  50.8 18.3 %all_to_all.10.parts_ref = f32[8,128,128]{2,1,0:T(8,128)S(1)} all-to-all(f32[8,128,128]{2,1,0:T(8,128)S(1)} %shard_map.75), channel_id=1, replica_groups=mesh['z'=8,'x'=4,'c'=2,'y'=4] {'z'}, dimensions={0} | all-to-all | bytes 1048576 | tf_op jit(solution)/shard_map/all_to_all | solution.py:208
  69.2 0.7 shard_map.76
  69.9 1.2 %collective-permute-start.7 = (f32[10,32]{1,0:T(8,128)S(1)}, f32[10,32]{1,0:T(8,128)S(1)}, u32[]{:S(2)}, u32[]{:S(2)}) collective-permute-start(f32[10,32]{1,0:T(8,128)S(1)} %get-tuple-element.25), channel_id=1, source_target_pairs={{0,2},{1,3},{2,0},{3,1},{4,6},{5,7},{6,4},{7,5},{8,10},{9,11},{10,... | collective-permute-start | bytes 3848 | tf_op jit(solution)/shard_map/ppermute | solution.py:18
  71.1 2.2 %collective-permute-start.8 = (f32[10,32]{1,0:T(8,128)S(1)}, f32[10,32]{1,0:T(8,128)S(1)}, u32[]{:S(2)}, u32[]{:S(2)}) collective-permute-start(f32[10,32]{1,0:T(8,128)S(1)} %get-tuple-element.25), channel_id=1, source_target_pairs={{0,1},{1,2},{2,3},{3,0},{4,5},{5,6},{6,7},{7,4},{8,9},{9,10},{10,1... | collective-permute-start | bytes 3848 | tf_op jit(solution)/shard_map/ppermute | solution.py:18
  73.3 1.7 %collective-permute-done.7 = f32[10,32]{1,0:T(8,128)S(1)} collective-permute-done((f32[10,32]{1,0:T(8,128)S(1)}, f32[10,32]{1,0:T(8,128)S(1)}, u32[]{:S(2)}, u32[]{:S(2)}) %collective-permute-start.7) | collective-permute-done | bytes 1312 | tf_op jit(solution)/shard_map/ppermute | solution.py:18
  75.0 3.1 %collective-permute-done.9 = f32[10,32]{1,0:T(8,128)S(1)} collective-permute-done((f32[10,32]{1,0:T(8,128)S(1)}, f32[10,32]{1,0:T(8,128)S(1)}, u32[]{:S(2)}, u32[]{:S(2)}) %collective-permute-start.9) | collective-permute-done | bytes 1312 | tf_op jit(solution)/shard_map/ppermute | solution.py:18
  78.1 0.6 multiply_bitcast_fusion
  (11 shorter events, 0.0 us)
Async XLA Ops:
  0.6 14.9 %collective-permute-start = (f32[4,512,128]{2,1,0:T(8,128)}, f32[4,512,128]{2,1,0:T(8,128)S(1)}, u32[]{:S(2)}, u32[]{:S(2)}) collective-permute-start(f32[4,512,128]{2,1,0:T(8,128)} %own_ref.1), channel_id=1, source_target_pairs={{0,4},{4,0},{1,5},{5,1},{2,6},{6,2},{3,7},{7,3},{8,12},{12,8},{9,1... | collective-permute-start | bytes 3145736 | tf_op jit(solution)/shard_map/ppermute | solution.py:18
  0.7 0.9 %copy-start.1 = (s32[1,64,4,64]{3,2,1,0:T(4,128)S(1)}, s32[1,64,4,64]{3,2,1,0:T(4,128)}, u32[]{:S(2)}) copy-start(s32[1,64,4,64]{3,2,1,0:T(4,128)} %param.7) | copy-start | bytes 196612
  1.6 0.9 %copy-start.2 = (s32[1,64,4,64]{3,2,1,0:T(4,128)S(1)}, s32[1,64,4,64]{3,2,1,0:T(4,128)}, u32[]{:S(2)}) copy-start(s32[1,64,4,64]{3,2,1,0:T(4,128)} %param.8) | copy-start | bytes 196612
  2.5 0.7 copy-start.4
  4.2 22.4 %all-to-all-start = ((s32[32,8,128]{2,1,0:T(8,128)}), s32[32,8,128]{2,1,0:T(8,128)S(1)}, u32[]{:S(2)}, u32[]{:S(2)}) async-start(s32[32,8,128]{2,1,0:T(8,128)} %bitcast.4), calls=%async_computation | async-start | bytes 262144 | tf_op jit(solution)/shard_map/all_to_all | solution.py:179
  15.5 1.2 %copy-start = (f32[4,512,128]{2,1,0:T(8,128)S(1)}, f32[4,512,128]{2,1,0:T(8,128)}, u32[]{:S(2)}) copy-start(f32[4,512,128]{2,1,0:T(8,128)} %own_ref.1) | copy-start | bytes 3145732
  30.0 12.4 %collective-permute-start.1 = (f32[8,64,128]{2,1,0:T(8,128)S(1)}, f32[8,64,128]{2,1,0:T(8,128)S(1)}, u32[]{:S(2)}, u32[]{:S(2)}) collective-permute-start(f32[8,64,128]{2,1,0:T(8,128)S(1)} %get-tuple-element.16), channel_id=1, source_target_pairs={{0,8},{8,16},{16,24},{24,0},{1,9},{9,17},{17,25},{25,1},{2,10},{10... | collective-permute-start | bytes 786440 | tf_op jit(solution)/shard_map/ppermute | solution.py:18
  30.1 12.3 %collective-permute-start.2 = (f32[8,64,128]{2,1,0:T(8,128)S(1)}, f32[8,64,128]{2,1,0:T(8,128)S(1)}, u32[]{:S(2)}, u32[]{:S(2)}) collective-permute-start(f32[8,64,128]{2,1,0:T(8,128)S(1)} %get-tuple-element.18), channel_id=1, source_target_pairs={{0,24},{8,0},{16,8},{24,16},{1,25},{9,1},{17,9},{25,17},{2,26},{10... | collective-permute-start | bytes 786440 | tf_op jit(solution)/shard_map/ppermute | solution.py:18
  36.8 12.5 %collective-permute-start.4 = (f32[8,64,128]{2,1,0:T(8,128)S(1)}, f32[8,64,128]{2,1,0:T(8,128)S(1)}, u32[]{:S(2)}, u32[]{:S(2)}) collective-permute-start(f32[8,64,128]{2,1,0:T(8,128)S(1)} %get-tuple-element.20), channel_id=1, source_target_pairs={{0,24},{8,0},{16,8},{24,16},{1,25},{9,1},{17,9},{25,17},{2,26},{10... | collective-permute-start | bytes 786440 | tf_op jit(solution)/shard_map/ppermute | solution.py:18
  37.1 12.2 %collective-permute-start.5 = (f32[8,64,128]{2,1,0:T(8,128)S(1)}, f32[8,64,128]{2,1,0:T(8,128)S(1)}, u32[]{:S(2)}, u32[]{:S(2)}) collective-permute-start(f32[8,64,128]{2,1,0:T(8,128)S(1)} %get-tuple-element.22), channel_id=1, source_target_pairs={{0,8},{8,16},{16,24},{24,0},{1,9},{9,17},{17,25},{25,1},{2,10},{10... | collective-permute-start | bytes 786440 | tf_op jit(solution)/shard_map/ppermute | solution.py:18
  42.5 8.2 %collective-permute-start.3 = (f32[8,64,128]{2,1,0:T(8,128)S(1)}, f32[8,64,128]{2,1,0:T(8,128)S(1)}, u32[]{:S(2)}, u32[]{:S(2)}) collective-permute-start(f32[8,64,128]{2,1,0:T(8,128)S(1)} %get-tuple-element.19), channel_id=1, source_target_pairs={{0,8},{8,16},{16,24},{24,0},{1,9},{9,17},{17,25},{25,1},{2,10},{10... | collective-permute-start | bytes 786440 | tf_op jit(solution)/shard_map/ppermute | solution.py:18
  42.6 8.1 %collective-permute-start.6 = (f32[8,64,128]{2,1,0:T(8,128)S(1)}, f32[8,64,128]{2,1,0:T(8,128)S(1)}, u32[]{:S(2)}, u32[]{:S(2)}) collective-permute-start(f32[8,64,128]{2,1,0:T(8,128)S(1)} %get-tuple-element.23), channel_id=1, source_target_pairs={{0,24},{8,0},{16,8},{24,16},{1,25},{9,1},{17,9},{25,17},{2,26},{10... | collective-permute-start | bytes 786440 | tf_op jit(solution)/shard_map/ppermute | solution.py:18
  49.3 19.9 %copy-start.3 = (f32[32,128]{1,0:T(8,128)S(1)}, f32[32,128]{1,0:T(8,128)}, u32[]{:S(2)}) copy-start(f32[32,128]{1,0:T(8,128)} %dense_ref.1) | copy-start | bytes 49156
  69.9 5.2 %collective-permute-start.7 = (f32[10,32]{1,0:T(8,128)S(1)}, f32[10,32]{1,0:T(8,128)S(1)}, u32[]{:S(2)}, u32[]{:S(2)}) collective-permute-start(f32[10,32]{1,0:T(8,128)S(1)} %get-tuple-element.25), channel_id=1, source_target_pairs={{0,2},{1,3},{2,0},{3,1},{4,6},{5,7},{6,4},{7,5},{8,10},{9,11},{10,... | collective-permute-start | bytes 3848 | tf_op jit(solution)/shard_map/ppermute | solution.py:18
  71.1 3.9 %collective-permute-start.8 = (f32[10,32]{1,0:T(8,128)S(1)}, f32[10,32]{1,0:T(8,128)S(1)}, u32[]{:S(2)}, u32[]{:S(2)}) collective-permute-start(f32[10,32]{1,0:T(8,128)S(1)} %get-tuple-element.25), channel_id=1, source_target_pairs={{0,1},{1,2},{2,3},{3,0},{4,5},{5,6},{6,7},{7,4},{8,9},{9,10},{10,1... | collective-permute-start | bytes 3848 | tf_op jit(solution)/shard_map/ppermute | solution.py:18
  73.3 4.9 %collective-permute-start.9 = (f32[10,32]{1,0:T(8,128)S(1)}, f32[10,32]{1,0:T(8,128)S(1)}, u32[]{:S(2)}, u32[]{:S(2)}) collective-permute-start(f32[10,32]{1,0:T(8,128)S(1)} %get-tuple-element.25), channel_id=1, source_target_pairs={{0,3},{1,0},{2,1},{3,2},{4,7},{5,4},{6,5},{7,6},{8,11},{9,8},{10,9... | collective-permute-start | bytes 3848 | tf_op jit(solution)/shard_map/ppermute | solution.py:18

commit v3 on v2

v3 whole, which is shorter than its diff:
```python
import functools

import jax
import jax.numpy as jnp
from jax import lax
from jax.experimental import pallas as pl
from jax.experimental.pallas import tpu as pltpu
from jax.sharding import Mesh
from jax.sharding import PartitionSpec as P


Z = ("zq", "zp")
ROWS = Z + ("x", "c")
DEAD = 1 << 20
VMEM = pl.BlockSpec(memory_space=pltpu.VMEM)


def shifted(value, axis, by):
    size = lax.axis_size(axis)
    return lax.ppermute(value, axis, [(i, (i + by) % size) for i in range(size)])


def local_kernel(kernel, out_shape, operands, flops=1 << 20, vmem=12 << 20, scratch=()):
    single = not isinstance(out_shape, tuple)
    return pl.pallas_call(
        kernel,
        in_specs=[VMEM] * len(operands),
        out_specs=VMEM if single else (VMEM,) * len(out_shape),
        out_shape=out_shape,
        scratch_shapes=scratch,
        compiler_params=pltpu.CompilerParams(vmem_limit_bytes=vmem),
        cost_estimate=pl.CostEstimate(flops=flops, bytes_accessed=1 << 20, transcendentals=0),
    )(*operands)


def prepare_kernel(rows_ref, examples_ref, counts_ref, out_ref, live_ref):
    depth, across, under, capacity = rows_ref.shape
    tables, owners = counts_ref.shape
    buckets = owners * tables
    bucket = lax.broadcasted_iota(jnp.int32, (buckets, owners), 0)
    owner = lax.broadcasted_iota(jnp.int32, (buckets, owners), 1)
    spread = jnp.where(bucket // tables == owner, 1.0, 0.0).astype(jnp.bfloat16)
    table = lax.broadcasted_iota(jnp.int32, (buckets, tables), 1)
    own = lax.broadcasted_iota(jnp.int32, (buckets, tables), 0) % tables
    slot = lax.broadcasted_iota(jnp.int32, (buckets, capacity), 1).astype(jnp.float32)
    counts = counts_ref[...].astype(jnp.float32).astype(jnp.bfloat16)
    by_table = lax.dot_general(
        spread, counts, (((1,), (1,)), ((), ())), preferred_element_type=jnp.float32
    )
    count = jnp.sum(jnp.where(table == own, by_table, 0.0), axis=1, keepdims=True)
    live = jnp.where(slot < count, examples_ref[...].reshape(buckets, capacity), DEAD)
    live_ref[...] = live.reshape(live_ref.shape)
    odd = lax.axis_index("zp")
    early = lax.broadcasted_iota(jnp.int32, (across, under, capacity), 1) % tables < tables // 2
    for q in range(depth // 2):
        here = 2 * q + odd
        first = 2 * q + 1 - odd
        second = lax.rem(2 * q + depth - 1 + 3 * odd, depth)
        for ref, lanes in ((rows_ref, slice(0, capacity)), (live_ref, slice(capacity, None))):
            out_ref[q, :, :under, lanes] = ref[here]
            out_ref[q, :, under:, lanes] = jnp.where(early, ref[first], ref[second])


def split_kernel(*refs):
    out_ref = refs[-1]
    width = out_ref.shape[3] // 2
    sides = (refs[:1], refs[1:2]) if len(refs) == 3 else (refs[:2], refs[2:4])
    for place, pieces in enumerate(sides):
        t = 0
        for ref in pieces:
            for k in range(ref.shape[0]):
                full = ref[k]
                high = full.astype(jnp.bfloat16)
                out_ref[place, t, :, :width] = high
                out_ref[place, t, :, width:] = (full - high.astype(jnp.float32)).astype(
                    jnp.bfloat16
                )
                t += 1


def split_tables(pieces, count, rows, width):
    return local_kernel(
        split_kernel,
        jax.ShapeDtypeStruct((2, count, rows, 2 * width), jnp.bfloat16),
        pieces,
        flops=4 << 20,
    )


def one_hot(mask):
    return jnp.where(mask, 1.0, 0.0).astype(jnp.bfloat16)


def bags_kernel(ids_ref, near_ref, partner_ref, out_ref, looked_ref, *, away, examples):
    group, ring, messages, lanes = ids_ref.shape
    cores, count, rows, wide = near_ref.shape
    slots = lanes // 2
    core = lax.axis_index("c")
    column = lax.rem(lax.axis_index("x") + away, ring)
    depth = lax.axis_index("zq")
    row_iota = lax.broadcasted_iota(jnp.int32, (slots, rows), 1)
    key_iota = lax.broadcasted_iota(jnp.int32, (group * examples, group * slots), 0)
    ids = [ids_ref[lax.rem(depth + j, group), column] for j in range(group)]
    columns = jnp.swapaxes(jnp.concatenate(ids, axis=0), 0, 1)
    keys = jnp.concatenate([ids[j][:, slots:] + j * examples for j in range(group)], axis=1)
    for t in range(count):
        into = []
        for block, tables_ref in enumerate((near_ref, partner_ref)):
            for o in range(cores):
                message = (block * cores + o) * count + t
                picks = jnp.concatenate(
                    [
                        one_hot(
                            columns[:slots, j * messages + message : j * messages + message + 1]
                            == row_iota
                        )
                        for j in range(group)
                    ],
                    axis=0,
                )
                looked = jnp.dot(
                    picks, tables_ref[o ^ core, t], preferred_element_type=jnp.float32
                )
                place = (block * cores + o) * group * slots
                looked_ref[t, place : place + group * slots, :] = looked.astype(jnp.bfloat16)
                into.append(one_hot(keys[message : message + 1] == key_iota))
        total = jnp.dot(
            jnp.concatenate(into, axis=1), looked_ref[t], preferred_element_type=jnp.float32
        )
        summed = total[:, : wide // 2] + total[:, wide // 2 :]
        out_ref[:, t * examples : (t + 1) * examples, :] = summed.reshape(
            group, examples, wide // 2
        )


def bags(ids, near, partner, away, examples):
    group, _, _, lanes = ids.shape
    cores, count, rows, wide = near.shape
    work = 2 * cores * count * group * lanes // 2
    return local_kernel(
        functools.partial(bags_kernel, away=away, examples=examples),
        jax.ShapeDtypeStruct((group, count * examples, wide // 2), jnp.float32),
        (ids, near, partner),
        flops=2 * work * wide * (rows + group * examples),
        vmem=16 << 20,
        scratch=[pltpu.VMEM((count, 2 * cores * group * lanes // 2, wide), jnp.bfloat16)],
    )


def join_kernel(*refs):
    ins, outs = refs[:4], refs[4:]
    for j, out_ref in enumerate(outs):
        out_ref[...] = ins[0][j] + ins[1][j] + ins[2][j] + ins[3][j]


def close_kernel(own_ref, one_ref, two_ref, three_ref, dense_ref, pooled_ref, pairs_ref):
    examples = dense_ref.shape[0]
    pooled = own_ref[...] + one_ref[...] + two_ref[...] + three_ref[...]
    tables = pooled.shape[0] // examples
    vectors = [dense_ref[...]]
    for t in range(tables):
        one = pooled[t * examples : (t + 1) * examples]
        pooled_ref[:, t, :] = one
        vectors.append(one)
    lane = lax.broadcasted_iota(jnp.int32, dense_ref.shape, 1)
    pairs = jnp.zeros(dense_ref.shape, jnp.float32)
    place = 0
    for i in range(tables + 1):
        for j in range(i + 1, tables + 1):
            product = jnp.sum(vectors[i] * vectors[j], axis=1, keepdims=True)
            pairs = jnp.where(lane == place, product, pairs)
            place += 1
    pairs_ref[...] = jnp.swapaxes(pairs, 0, 1)[: pairs_ref.shape[0]]


def body(embedding, tables, dense_features, slot_rows, slot_examples, slot_counts):
    count, rows, width = tables.shape
    examples = dense_features.shape[0]
    capacity = slot_rows.shape[3]
    group, parities, ring, cores = (lax.axis_size(a) for a in ROWS)
    depth = group * parities
    half = count // 2

    other = shifted(tables, "c", 1)
    low = lax.ppermute(tables[:half], Z, [(i, i ^ 1) for i in range(depth)])
    high = lax.ppermute(
        tables[half:], Z, [(i, (i + (1 if i % 2 else -1)) % depth) for i in range(depth)]
    )
    split_ids = (depth, ring, cores * count, capacity)
    ids = local_kernel(
        prepare_kernel,
        jax.ShapeDtypeStruct((group, ring, 2 * cores * count, 2 * capacity), jnp.int32),
        (slot_rows.reshape(split_ids), slot_examples.reshape(split_ids), slot_counts[0].T),
        scratch=[pltpu.VMEM(split_ids, jnp.int32)],
    )
    ids = ids.reshape((group * ring,) + ids.shape[2:])
    ids = lax.all_to_all(ids, ("zq", "x"), 0, 0, tiled=True)
    ids = ids.reshape((group, ring) + ids.shape[1:])
    other_low = shifted(low, "c", 1)
    other_high = shifted(high, "c", 1)
    near = split_tables((tables, other), count, rows, width)
    partner = split_tables((low, high, other_low, other_high), count, rows, width)

    far = bags(ids, near, partner, 2, examples)
    far = shifted(far, "x", 2)
    right = bags(ids, near, partner, 1, examples)
    right = shifted(right, "x", 1)
    left = bags(ids, near, partner, 3, examples)
    left = shifted(left, "x", -1)
    own = bags(ids, near, partner, 0, examples)
    block = jax.ShapeDtypeStruct(own.shape[1:], jnp.float32)
    here, up, over, down = local_kernel(join_kernel, (block,) * group, (own, far, right, left))
    over, up, down = (
        lax.ppermute(piece, Z, [(i, (i + parities * by) % depth) for i in range(depth)])
        for piece, by in ((over, 2), (up, 1), (down, 3))
    )
    pairs = count * (count + 1) // 2
    pooled, products = local_kernel(
        close_kernel,
        (
            jax.ShapeDtypeStruct((examples, count, width), jnp.float32),
            jax.ShapeDtypeStruct((pairs, examples), jnp.float32),
        ),
        (here, over, up, down, dense_features),
    )
    opposite = shifted(products, "y", 2)
    beside = shifted(products, "y", 1) + shifted(products, "y", -1)
    total = ((products + opposite) + beside) * embedding**-0.5
    return pooled, total.T


def solution(mesh):
    torus = Mesh(mesh.devices.reshape(4, 2, 4, 2, mesh.shape["cols"]), ROWS + ("y",))

    def layer(*args):
        return body(512, *args)

    return jax.shard_map(
        layer,
        mesh=torus,
        in_specs=(
            P(None, ROWS, "y"),
            P(ROWS, "y"),
            P(ROWS, None, None, None),
            P(ROWS, None, None, None),
            P(ROWS, None, None),
        ),
        out_specs=(P(ROWS, None, "y"), P(ROWS, None)),
        check_vma=False,
    )
```

time: 79 us -> 83.8 us (1.061)
  waiting for transfers between devices: 15.7 us -> 35.7 us
  blocking collectives: 18.3 us -> 0 us
  starting transfers between devices: 23.5 us -> 27.7 us
  Pallas kernels: 16.1 us -> 12.2 us
  local copies, waits for them, and re-layouts: 3.71 us -> 6.53 us
    ppermute x0 -> x5, waiting for transfers between devices: none -> 18.9 us  [the longest x1 12.6 us: body(): lax.ppermute(tables[half:], Z, [(i, (i + (1 if i % 2 else -1)) % depth) f...]
    all_to_all x1 -> x0, blocking collectives: 18.3 us -> none  [body(): parts = lax.all_to_all(parts, 'z', 0, 0, tiled=True)]
    ppermute x0 -> x5, starting transfers between devices: none -> 12.3 us  [the longest x3 6.34 us: body(): lax.ppermute(piece, Z, [(i, (i + parities * by) % depth) for i in range(d...]
    ppermute x10 -> x9, waiting for transfers between devices: 6.28 us -> 12.4 us  [shifted(): lax.ppermute(value, axis, [(i, (i + by) % size) for i in range(size)])]
    all_to_all x1, waiting for transfers between devices: 9.38 us -> 4.47 us  [body(): ids = lax.all_to_all(ids, ('zq', 'x'), 0, 0, tiled=True)]
    all_to_all x1, starting transfers between devices: 11.3 us -> 7.17 us  [body(): ids = lax.all_to_all(ids, ('zq', 'x'), 0, 0, tiled=True)]
    ppermute x10 -> x9, starting transfers between devices: 12.2 us -> 8.23 us  [shifted(): lax.ppermute(value, axis, [(i, (i + by) % size) for i in range(size)])]
    pallas_call x9, Pallas kernels: 16.1 us -> 12.2 us  [local_kernel(): pl.pallas_call(kernel, in_specs=[VMEM] * len(operands), out_specs=VMEM if...]
  transfers between devices with their start and end apart: 11 -> 15, of which waited for: 4 -> 9; matrix products, arithmetic and copies ran while one was open for 0% -> 2% of each run, Pallas kernels for 15% -> 6%
where the time goes in v3:
time: 83.8 us; the launch traced here: 83.5 us
  waiting for transfers between devices  35.7 us (43%)
  starting transfers between devices  27.7 us (33%)
  Pallas kernels  12.2 us (15%)
  local copies, waits for them, and re-layouts  6.53 us (8%)
    ppermute x1, waiting for transfers between devices, body(): lax.ppermute(tables[half:], Z, [(i, (i + (1 if i % 2 else -1)) % depth) f...  12.6 us
    ppermute x9, waiting for transfers between devices, shifted(): lax.ppermute(value, axis, [(i, (i + by) % size) for i in range(size)])  12.4 us
    pallas_call x9, Pallas kernels, local_kernel(): pl.pallas_call(kernel, in_specs=[VMEM] * len(operands), out_specs=VMEM if...  12.2 us
    ppermute x9, starting transfers between devices, shifted(): lax.ppermute(value, axis, [(i, (i + by) % size) for i in range(size)])  8.23 us
    all_to_all x1, starting transfers between devices, body(): ids = lax.all_to_all(ids, ('zq', 'x'), 0, 0, tiled=True)  7.17 us
    ppermute x3, starting transfers between devices, body(): lax.ppermute(piece, Z, [(i, (i + parities * by) % depth) for i in range(d...  6.34 us
    ppermute x1, starting transfers between devices, body(): lax.ppermute(tables[half:], Z, [(i, (i + (1 if i % 2 else -1)) % depth) f...  5.94 us
    unnamed x18, local copies, waits for them, and re-layouts  5.17 us
  transfers between devices with their start and end apart: 15, of which 9 were waited for; matrix products, arithmetic and copies ran while one was open for 2% of the time, Pallas kernels for 6%

profile of v3, /device:TPU:24, one launch (start us, length us, event | category | flops | bytes accessed | tf_op | source)
XLA Modules:
  0.0 83.5 jit_solution(14245158041221879139)
XLA Ops:
  0.8 1.4 %fusion = (f32[2,512,128]{2,1,0:T(8,128)S(1)}, f32[2,512,128]{2,1,0:T(8,128)S(1)}) fusion(f32[4,512,128]{2,1,0:T(8,128)} %refs_0_.1), kind=kLoop, calls=%fused_computation.1 | loop fusion | bytes 2097152 | tf_op jit(solution)/shard_map/slice | solution.py:187
  2.1 5.9 %collective-permute-start.2 = (f32[2,512,128]{2,1,0:T(8,128)S(1)}, f32[2,512,128]{2,1,0:T(8,128)}, u32[]{:S(2)}, u32[]{:S(2)}) collective-permute-start(f32[2,512,128]{2,1,0:T(8,128)S(1)} %get-tuple-element.14), channel_id=1, source_target_pairs={{0,224},{32,64},{64,32},{96,128},{128,96},{160,192},{192,160},{224... | collective-permute-start | bytes 1572872 | tf_op jit(solution)/shard_map/ppermute | solution.py:186
  8.1 12.6 %collective-permute-done.2.refs_1_ = f32[2,512,128]{2,1,0:T(8,128)} collective-permute-done((f32[2,512,128]{2,1,0:T(8,128)S(1)}, f32[2,512,128]{2,1,0:T(8,128)}, u32[]{:S(2)}, u32[]{:S(2)}) %collective-permute-start.2) | collective-permute-done | bytes 524320 | tf_op jit(solution)/shard_map/ppermute | solution.py:186
  20.7 1.5 %collective-permute-done.1.refs_0_ = f32[2,512,128]{2,1,0:T(8,128)} collective-permute-done((f32[2,512,128]{2,1,0:T(8,128)S(1)}, f32[2,512,128]{2,1,0:T(8,128)}, u32[]{:S(2)}, u32[]{:S(2)}) %collective-permute-start.1) | collective-permute-done | bytes 524320 | tf_op jit(solution)/shard_map/ppermute | solution.py:185
  22.2 1.0 %shard_map.68 = s32[4,4,16,128]{3,2,1,0:T(8,128)} custom-call(s32[8,4,8,64]{3,2,1,0:T(8,128)S(1)} %bitcast.9, s32[8,4,8,64]{3,2,1,0:T(8,128)S(1)} %bitcast.10, s32[4,64]{1,0:T(4,128)S(1)} %bitcast.15), custom_call_target="tpu_custom_call" | custom-call | flops 1048576 | bytes 1048576 | tf_op jit(solution)/shard_map/pallas_call | solution.py:25
  23.2 7.2 %all-to-all-start = ((s32[16,16,128]{2,1,0:T(8,128)}), s32[16,16,128]{2,1,0:T(8,128)S(1)}, u32[]{:S(2)}, u32[]{:S(2)}) async-start(s32[16,16,128]{2,1,0:T(8,128)} %bitcast.4), calls=%async_computation | async-start | bytes 262144 | tf_op jit(solution)/shard_map/all_to_all | solution.py:197
  30.3 1.0 %copy-done.3 = f32[4,512,128]{2,1,0:T(8,128)} copy-done((f32[4,512,128]{2,1,0:T(8,128)}, f32[4,512,128]{2,1,0:T(8,128)S(1)}, u32[]{:S(2)}) %copy-start.3) | copy-done | bytes 1048600
  31.4 1.2 %copy-done.4 = f32[4,512,128]{2,1,0:T(8,128)S(1)} copy-done((f32[4,512,128]{2,1,0:T(8,128)S(1)}, f32[4,512,128]{2,1,0:T(8,128)}, u32[]{:S(2)}) %copy-start.4) | copy-done | bytes 1048600
  33.0 1.9 %shard_map.70.partner_ref = bf16[2,4,512,256]{3,2,1,0:T(8,128)(2,1)S(1)} custom-call(f32[2,512,128]{2,1,0:T(8,128)} %collective-permute-done.1.refs_0_, f32[2,512,128]{2,1,0:T(8,128)} %collective-permute-done.2.refs_1_, f32[2,512,128]{2,1,0:T(8,128)} %collective-permute-done.3.refs_2_, f32[2,512,128]{2,1,0:T(8,128)} %collective-permute-done.4.refs_3_), custom_call_target="tpu_custom_call" | custom-call | flops 4194304 | bytes 1048576 | tf_op jit(solution)/shard_map/pallas_call | solution.py:25
  35.0 1.3 %copy-done.1 = bf16[2,4,512,256]{3,2,1,0:T(8,128)(2,1)} copy-done((bf16[2,4,512,256]{3,2,1,0:T(8,128)(2,1)}, bf16[2,4,512,256]{3,2,1,0:T(8,128)(2,1)S(1)}, u32[]{:S(2)}) %copy-start.1) | copy-done | bytes 2097176
  36.3 4.5 %all-to-all-done = s32[16,16,128]{2,1,0:T(8,128)S(1)} async-done(((s32[16,16,128]{2,1,0:T(8,128)}), s32[16,16,128]{2,1,0:T(8,128)S(1)}, u32[]{:S(2)}, u32[]{:S(2)}) %all-to-all-start) | async-done | bytes 131104 | tf_op jit(solution)/shard_map/all_to_all | solution.py:197
  40.8 1.6 %copy-done.2 = bf16[2,4,512,256]{3,2,1,0:T(8,128)(2,1)S(1)} copy-done((bf16[2,4,512,256]{3,2,1,0:T(8,128)(2,1)S(1)}, bf16[2,4,512,256]{3,2,1,0:T(8,128)(2,1)}, u32[]{:S(2)}) %copy-start.2) | copy-done | bytes 2097176
  42.4 2.0 %shard_map.74 = f32[4,128,128]{2,1,0:T(8,128)S(1)} custom-call(s32[4,4,16,128]{3,2,1,0:T(8,128)S(1)} %bitcast.11, bf16[2,4,512,256]{3,2,1,0:T(8,128)(2,1)S(1)} %shard_map.69.near_ref, bf16[2,4,512,256]{3,2,1,0:T(8,128)(2,1)S(1)} %copy-done.2), custom_call_target="tpu_custom_call" | custom-call | flops 1342177280 | bytes 1048576 | tf_op jit(solution)/shard_map/pallas_call | solution.py:25
  44.4 2.0 %shard_map.73 = f32[4,128,128]{2,1,0:T(8,128)S(1)} custom-call(s32[4,4,16,128]{3,2,1,0:T(8,128)S(1)} %bitcast.12, bf16[2,4,512,256]{3,2,1,0:T(8,128)(2,1)S(1)} %shard_map.69.near_ref, bf16[2,4,512,256]{3,2,1,0:T(8,128)(2,1)S(1)} %copy-done.2), custom_call_target="tpu_custom_call" | custom-call | flops 1342177280 | bytes 1048576 | tf_op jit(solution)/shard_map/pallas_call | solution.py:25
  46.4 2.0 %shard_map.72 = f32[4,128,128]{2,1,0:T(8,128)S(1)} custom-call(s32[4,4,16,128]{3,2,1,0:T(8,128)S(1)} %bitcast.13, bf16[2,4,512,256]{3,2,1,0:T(8,128)(2,1)S(1)} %shard_map.69.near_ref, bf16[2,4,512,256]{3,2,1,0:T(8,128)(2,1)S(1)} %copy-done.2), custom_call_target="tpu_custom_call" | custom-call | flops 1342177280 | bytes 1048576 | tf_op jit(solution)/shard_map/pallas_call | solution.py:25
  48.5 1.6 %collective-permute-start.5 = (f32[4,128,128]{2,1,0:T(8,128)S(1)}, f32[4,128,128]{2,1,0:T(8,128)S(1)}, u32[]{:S(2)}, u32[]{:S(2)}) collective-permute-start(f32[4,128,128]{2,1,0:T(8,128)S(1)} %shard_map.72), channel_id=1, source_target_pairs={{0,16},{8,24},{16,0},{24,8},{1,17},{9,25},{17,1},{25,9},{2,18},{10... | collective-permute-start | bytes 786440 | tf_op jit(solution)/shard_map/ppermute | solution.py:20
  50.1 0.5 collective-permute-start.6
  50.6 2.8 %collective-permute-start.7 = (f32[4,128,128]{2,1,0:T(8,128)S(1)}, f32[4,128,128]{2,1,0:T(8,128)S(1)}, u32[]{:S(2)}, u32[]{:S(2)}) collective-permute-start(f32[4,128,128]{2,1,0:T(8,128)S(1)} %shard_map.74), channel_id=1, source_target_pairs={{0,24},{8,0},{16,8},{24,16},{1,25},{9,1},{17,9},{25,17},{2,26},{10... | collective-permute-start | bytes 786440 | tf_op jit(solution)/shard_map/ppermute | solution.py:20
  53.4 2.0 %shard_map.71.refs_0_ = f32[4,128,128]{2,1,0:T(8,128)S(1)} custom-call(s32[4,4,16,128]{3,2,1,0:T(8,128)S(1)} %bitcast.14, bf16[2,4,512,256]{3,2,1,0:T(8,128)(2,1)S(1)} %shard_map.69.near_ref, bf16[2,4,512,256]{3,2,1,0:T(8,128)(2,1)S(1)} %copy-done.2), custom_call_target="tpu_custom_call" | custom-call | flops 1342177280 | bytes 1048576 | tf_op jit(solution)/shard_map/pallas_call | solution.py:25
  55.4 3.9 %collective-permute-done.5.refs_1_ = f32[4,128,128]{2,1,0:T(8,128)S(1)} collective-permute-done((f32[4,128,128]{2,1,0:T(8,128)S(1)}, f32[4,128,128]{2,1,0:T(8,128)S(1)}, u32[]{:S(2)}, u32[]{:S(2)}) %collective-permute-start.5) | collective-permute-done | bytes 262176 | tf_op jit(solution)/shard_map/ppermute | solution.py:20
  59.3 3.3 %collective-permute-done.6.refs_2_ = f32[4,128,128]{2,1,0:T(8,128)S(1)} collective-permute-done((f32[4,128,128]{2,1,0:T(8,128)S(1)}, f32[4,128,128]{2,1,0:T(8,128)S(1)}, u32[]{:S(2)}, u32[]{:S(2)}) %collective-permute-start.6) | collective-permute-done | bytes 262176 | tf_op jit(solution)/shard_map/ppermute | solution.py:20
  62.7 2.2 %collective-permute-start.8 = (f32[128,128]{1,0:T(8,128)S(1)}, f32[128,128]{1,0:T(8,128)S(1)}, u32[]{:S(2)}, u32[]{:S(2)}) collective-permute-start(f32[128,128]{1,0:T(8,128)S(1)} %get-tuple-element.9), channel_id=1, source_target_pairs={{0,128},{32,160},{64,192},{96,224},{128,0},{160,32},{192,64},{224,... | collective-permute-start | bytes 196616 | tf_op jit(solution)/shard_map/ppermute | solution.py:214
  64.9 1.9 %collective-permute-start.9 = (f32[128,128]{1,0:T(8,128)S(1)}, f32[128,128]{1,0:T(8,128)S(1)}, u32[]{:S(2)}, u32[]{:S(2)}) collective-permute-start(f32[128,128]{1,0:T(8,128)S(1)} %get-tuple-element.10), channel_id=1, source_target_pairs={{0,64},{32,96},{64,128},{96,160},{128,192},{160,224},{192,0},{224,... | collective-permute-start | bytes 196616 | tf_op jit(solution)/shard_map/ppermute | solution.py:214
  66.7 2.3 %collective-permute-start.10 = (f32[128,128]{1,0:T(8,128)S(1)}, f32[128,128]{1,0:T(8,128)S(1)}, u32[]{:S(2)}, u32[]{:S(2)}) collective-permute-start(f32[128,128]{1,0:T(8,128)S(1)} %get-tuple-element.11), channel_id=1, source_target_pairs={{0,192},{32,224},{64,0},{96,32},{128,64},{160,96},{192,128},{224,1... | collective-permute-start | bytes 196616 | tf_op jit(solution)/shard_map/ppermute | solution.py:214
  69.0 2.6 %collective-permute-done.8.one_ref = f32[128,128]{1,0:T(8,128)S(1)} collective-permute-done((f32[128,128]{1,0:T(8,128)S(1)}, f32[128,128]{1,0:T(8,128)S(1)}, u32[]{:S(2)}, u32[]{:S(2)}) %collective-permute-start.8) | collective-permute-done | bytes 65568 | tf_op jit(solution)/shard_map/ppermute | solution.py:214
  71.6 2.2 %collective-permute-done.9.two_ref = f32[128,128]{1,0:T(8,128)S(1)} collective-permute-done((f32[128,128]{1,0:T(8,128)S(1)}, f32[128,128]{1,0:T(8,128)S(1)}, u32[]{:S(2)}, u32[]{:S(2)}) %collective-permute-start.9) | collective-permute-done | bytes 65568 | tf_op jit(solution)/shard_map/ppermute | solution.py:214
  73.8 0.7 shard_map.76
  74.5 0.7 collective-permute-start.13
  75.3 2.5 %collective-permute-start.12 = (f32[10,32]{1,0:T(8,128)S(1)}, f32[10,32]{1,0:T(8,128)S(1)}, u32[]{:S(2)}, u32[]{:S(2)}) collective-permute-start(f32[10,32]{1,0:T(8,128)S(1)} %get-tuple-element.13), channel_id=1, source_target_pairs={{0,1},{1,2},{2,3},{3,0},{4,5},{5,6},{6,7},{7,4},{8,9},{9,10},{10,1... | collective-permute-start | bytes 3848 | tf_op jit(solution)/shard_map/ppermute | solution.py:20
  77.8 1.6 %collective-permute-done.13 = f32[10,32]{1,0:T(8,128)S(1)} collective-permute-done((f32[10,32]{1,0:T(8,128)S(1)}, f32[10,32]{1,0:T(8,128)S(1)}, u32[]{:S(2)}, u32[]{:S(2)}) %collective-permute-start.13) | collective-permute-done | bytes 1312 | tf_op jit(solution)/shard_map/ppermute | solution.py:20
  79.4 3.5 %collective-permute-done.11 = f32[10,32]{1,0:T(8,128)S(1)} collective-permute-done((f32[10,32]{1,0:T(8,128)S(1)}, f32[10,32]{1,0:T(8,128)S(1)}, u32[]{:S(2)}, u32[]{:S(2)}) %collective-permute-start.11) | collective-permute-done | bytes 1312 | tf_op jit(solution)/shard_map/ppermute | solution.py:20
  82.9 0.6 multiply_bitcast_fusion
  (27 shorter events, 0.6 us)
Async XLA Ops:
  0.6 30.7 %copy-start = (f32[4,512,128]{2,1,0:T(8,128)S(1)}, f32[4,512,128]{2,1,0:T(8,128)}, u32[]{:S(2)}) copy-start(f32[4,512,128]{2,1,0:T(8,128)} %refs_0_.1) | copy-start | bytes 3145732
  0.6 21.5 %copy-start.8 = (s32[1,64,4]{1,2,0:T(4,128)S(1)}, s32[1,64,4]{1,2,0:T(4,128)}, u32[]{:S(2)}) copy-start(s32[1,64,4]{1,2,0:T(4,128)} %param.9) | copy-start | bytes 3076
  0.7 21.5 %copy-start.6 = (s32[1,64,4,64]{3,2,1,0:T(4,128)S(1)}, s32[1,64,4,64]{3,2,1,0:T(4,128)}, u32[]{:S(2)}) copy-start(s32[1,64,4,64]{3,2,1,0:T(4,128)} %param.8) | copy-start | bytes 196612
  0.7 21.5 %copy-start.5 = (s32[1,64,4,64]{3,2,1,0:T(4,128)S(1)}, s32[1,64,4,64]{3,2,1,0:T(4,128)}, u32[]{:S(2)}) copy-start(s32[1,64,4,64]{3,2,1,0:T(4,128)} %param.7) | copy-start | bytes 196612
  0.7 29.7 %collective-permute-start = (f32[4,512,128]{2,1,0:T(8,128)}, f32[4,512,128]{2,1,0:T(8,128)S(1)}, u32[]{:S(2)}, u32[]{:S(2)}) collective-permute-start(f32[4,512,128]{2,1,0:T(8,128)} %refs_0_.1), channel_id=1, source_target_pairs={{0,4},{4,0},{1,5},{5,1},{2,6},{6,2},{3,7},{7,3},{8,12},{12,8},{9,1... | collective-permute-start | bytes 3145736 | tf_op jit(solution)/shard_map/ppermute | solution.py:20
  2.1 18.5 %collective-permute-start.2 = (f32[2,512,128]{2,1,0:T(8,128)S(1)}, f32[2,512,128]{2,1,0:T(8,128)}, u32[]{:S(2)}, u32[]{:S(2)}) collective-permute-start(f32[2,512,128]{2,1,0:T(8,128)S(1)} %get-tuple-element.14), channel_id=1, source_target_pairs={{0,224},{32,64},{64,32},{96,128},{128,96},{160,192},{192,160},{224... | collective-permute-start | bytes 1572872 | tf_op jit(solution)/shard_map/ppermute | solution.py:186
  8.1 14.1 %collective-permute-start.1 = (f32[2,512,128]{2,1,0:T(8,128)S(1)}, f32[2,512,128]{2,1,0:T(8,128)}, u32[]{:S(2)}, u32[]{:S(2)}) collective-permute-start(f32[2,512,128]{2,1,0:T(8,128)S(1)} %get-tuple-element.15), channel_id=1, source_target_pairs={{0,32},{32,0},{64,96},{96,64},{128,160},{160,128},{192,224},{224,1... | collective-permute-start | bytes 1572872 | tf_op jit(solution)/shard_map/ppermute | solution.py:185
  20.7 12.3 %collective-permute-start.4 = (f32[2,512,128]{2,1,0:T(8,128)}, f32[2,512,128]{2,1,0:T(8,128)}, u32[]{:S(2)}, u32[]{:S(2)}) collective-permute-start(f32[2,512,128]{2,1,0:T(8,128)} %collective-permute-done.2.refs_1_), channel_id=1, source_target_pairs={{0,4},{4,0},{1,5},{5,1},{2,6},{6,2},{3,7},{7,3},{8,12},{12,8},{9,1... | collective-permute-start | bytes 1572872 | tf_op jit(solution)/shard_map/ppermute | solution.py:20
  22.1 10.9 %collective-permute-start.3 = (f32[2,512,128]{2,1,0:T(8,128)}, f32[2,512,128]{2,1,0:T(8,128)}, u32[]{:S(2)}, u32[]{:S(2)}) collective-permute-start(f32[2,512,128]{2,1,0:T(8,128)} %collective-permute-done.1.refs_0_), channel_id=1, source_target_pairs={{0,4},{4,0},{1,5},{5,1},{2,6},{6,2},{3,7},{7,3},{8,12},{12,8},{9,1... | collective-permute-start | bytes 1572872 | tf_op jit(solution)/shard_map/ppermute | solution.py:20
  23.2 17.6 %all-to-all-start = ((s32[16,16,128]{2,1,0:T(8,128)}), s32[16,16,128]{2,1,0:T(8,128)S(1)}, u32[]{:S(2)}, u32[]{:S(2)}) async-start(s32[16,16,128]{2,1,0:T(8,128)} %bitcast.4), calls=%async_computation | async-start | bytes 262144 | tf_op jit(solution)/shard_map/all_to_all | solution.py:197
  30.3 1.0 %copy-start.3 = (f32[4,512,128]{2,1,0:T(8,128)}, f32[4,512,128]{2,1,0:T(8,128)S(1)}, u32[]{:S(2)}) copy-start(f32[4,512,128]{2,1,0:T(8,128)S(1)} %collective-permute-done.refs_1_) | copy-start | bytes 3145732
  31.4 1.2 %copy-start.4 = (f32[4,512,128]{2,1,0:T(8,128)S(1)}, f32[4,512,128]{2,1,0:T(8,128)}, u32[]{:S(2)}) copy-start(f32[4,512,128]{2,1,0:T(8,128)} %copy-done.3) | copy-start | bytes 3145732
  35.0 1.3 %copy-start.1 = (bf16[2,4,512,256]{3,2,1,0:T(8,128)(2,1)}, bf16[2,4,512,256]{3,2,1,0:T(8,128)(2,1)S(1)}, u32[]{:S(2)}) copy-start(bf16[2,4,512,256]{3,2,1,0:T(8,128)(2,1)S(1)} %shard_map.70.partner_ref) | copy-start | bytes 6291460
  40.8 1.6 %copy-start.2 = (bf16[2,4,512,256]{3,2,1,0:T(8,128)(2,1)S(1)}, bf16[2,4,512,256]{3,2,1,0:T(8,128)(2,1)}, u32[]{:S(2)}) copy-start(bf16[2,4,512,256]{3,2,1,0:T(8,128)(2,1)} %copy-done.1) | copy-start | bytes 6291460
  48.5 25.4 %copy-start.7 = (f32[32,128]{1,0:T(8,128)S(1)}, f32[32,128]{1,0:T(8,128)}, u32[]{:S(2)}) copy-start(f32[32,128]{1,0:T(8,128)} %dense_ref.1) | copy-start | bytes 49156
  48.5 10.8 %collective-permute-start.5 = (f32[4,128,128]{2,1,0:T(8,128)S(1)}, f32[4,128,128]{2,1,0:T(8,128)S(1)}, u32[]{:S(2)}, u32[]{:S(2)}) collective-permute-start(f32[4,128,128]{2,1,0:T(8,128)S(1)} %shard_map.72), channel_id=1, source_target_pairs={{0,16},{8,24},{16,0},{24,8},{1,17},{9,25},{17,1},{25,9},{2,18},{10... | collective-permute-start | bytes 786440 | tf_op jit(solution)/shard_map/ppermute | solution.py:20
  50.1 12.5 %collective-permute-start.6 = (f32[4,128,128]{2,1,0:T(8,128)S(1)}, f32[4,128,128]{2,1,0:T(8,128)S(1)}, u32[]{:S(2)}, u32[]{:S(2)}) collective-permute-start(f32[4,128,128]{2,1,0:T(8,128)S(1)} %shard_map.73), channel_id=1, source_target_pairs={{0,8},{8,16},{16,24},{24,0},{1,9},{9,17},{17,25},{25,1},{2,10},{10... | collective-permute-start | bytes 786440 | tf_op jit(solution)/shard_map/ppermute | solution.py:20
  50.6 12.0 %collective-permute-start.7 = (f32[4,128,128]{2,1,0:T(8,128)S(1)}, f32[4,128,128]{2,1,0:T(8,128)S(1)}, u32[]{:S(2)}, u32[]{:S(2)}) collective-permute-start(f32[4,128,128]{2,1,0:T(8,128)S(1)} %shard_map.74), channel_id=1, source_target_pairs={{0,24},{8,0},{16,8},{24,16},{1,25},{9,1},{17,9},{25,17},{2,26},{10... | collective-permute-start | bytes 786440 | tf_op jit(solution)/shard_map/ppermute | solution.py:20
  62.7 9.0 %collective-permute-start.8 = (f32[128,128]{1,0:T(8,128)S(1)}, f32[128,128]{1,0:T(8,128)S(1)}, u32[]{:S(2)}, u32[]{:S(2)}) collective-permute-start(f32[128,128]{1,0:T(8,128)S(1)} %get-tuple-element.9), channel_id=1, source_target_pairs={{0,128},{32,160},{64,192},{96,224},{128,0},{160,32},{192,64},{224,... | collective-permute-start | bytes 196616 | tf_op jit(solution)/shard_map/ppermute | solution.py:214
  64.9 9.0 %collective-permute-start.9 = (f32[128,128]{1,0:T(8,128)S(1)}, f32[128,128]{1,0:T(8,128)S(1)}, u32[]{:S(2)}, u32[]{:S(2)}) collective-permute-start(f32[128,128]{1,0:T(8,128)S(1)} %get-tuple-element.10), channel_id=1, source_target_pairs={{0,64},{32,96},{64,128},{96,160},{128,192},{160,224},{192,0},{224,... | collective-permute-start | bytes 196616 | tf_op jit(solution)/shard_map/ppermute | solution.py:214
  66.7 7.1 %collective-permute-start.10 = (f32[128,128]{1,0:T(8,128)S(1)}, f32[128,128]{1,0:T(8,128)S(1)}, u32[]{:S(2)}, u32[]{:S(2)}) collective-permute-start(f32[128,128]{1,0:T(8,128)S(1)} %get-tuple-element.11), channel_id=1, source_target_pairs={{0,192},{32,224},{64,0},{96,32},{128,64},{160,96},{192,128},{224,1... | collective-permute-start | bytes 196616 | tf_op jit(solution)/shard_map/ppermute | solution.py:214
  74.5 4.9 %collective-permute-start.13 = (f32[10,32]{1,0:T(8,128)S(1)}, f32[10,32]{1,0:T(8,128)S(1)}, u32[]{:S(2)}, u32[]{:S(2)}) collective-permute-start(f32[10,32]{1,0:T(8,128)S(1)} %get-tuple-element.13), channel_id=1, source_target_pairs={{0,3},{1,0},{2,1},{3,2},{4,7},{5,4},{6,5},{7,6},{8,11},{9,8},{10,9... | collective-permute-start | bytes 3848 | tf_op jit(solution)/shard_map/ppermute | solution.py:20
  75.3 4.1 %collective-permute-start.12 = (f32[10,32]{1,0:T(8,128)S(1)}, f32[10,32]{1,0:T(8,128)S(1)}, u32[]{:S(2)}, u32[]{:S(2)}) collective-permute-start(f32[10,32]{1,0:T(8,128)S(1)} %get-tuple-element.13), channel_id=1, source_target_pairs={{0,1},{1,2},{2,3},{3,0},{4,5},{5,6},{6,7},{7,4},{8,9},{9,10},{10,1... | collective-permute-start | bytes 3848 | tf_op jit(solution)/shard_map/ppermute | solution.py:20
  77.8 5.2 %collective-permute-start.11 = (f32[10,32]{1,0:T(8,128)S(1)}, f32[10,32]{1,0:T(8,128)S(1)}, u32[]{:S(2)}, u32[]{:S(2)}) collective-permute-start(f32[10,32]{1,0:T(8,128)S(1)} %get-tuple-element.13), channel_id=1, source_target_pairs={{0,2},{1,3},{2,0},{3,1},{4,6},{5,7},{6,4},{7,5},{8,10},{9,11},{10,... | collective-permute-start | bytes 3848 | tf_op jit(solution)/shard_map/ppermute | solution.py:20

commit v4 on v3

--- a/solution.py
+++ b/solution.py
@@ -13,6 +13,7 @@
 ROWS = Z + ("x", "c")
 DEAD = 1 << 20
 VMEM = pl.BlockSpec(memory_space=pltpu.VMEM)
+HBM = pl.BlockSpec(memory_space=pltpu.HBM)
 
 
 def shifted(value, axis, by):
@@ -20,17 +21,24 @@
     return lax.ppermute(value, axis, [(i, (i + by) % size) for i in range(size)])
 
 
-def local_kernel(kernel, out_shape, operands, flops=1 << 20, vmem=12 << 20, scratch=()):
+def local_kernel(kernel, out_shape, operands, flops=1 << 20, vmem=12 << 20, scratch=(), in_hbm=()):
     single = not isinstance(out_shape, tuple)
     return pl.pallas_call(
         kernel,
-        in_specs=[VMEM] * len(operands),
+        in_specs=[HBM if k in in_hbm else VMEM for k in range(len(operands))],
         out_specs=VMEM if single else (VMEM,) * len(out_shape),
         out_shape=out_shape,
         scratch_shapes=scratch,
         compiler_params=pltpu.CompilerParams(vmem_limit_bytes=vmem),
         cost_estimate=pl.CostEstimate(flops=flops, bytes_accessed=1 << 20, transcendentals=0),
     )(*operands)
+
+
+def started(pairs, sems):
+    copies = [pltpu.make_async_copy(a, b, sems.at[k]) for k, (a, b) in enumerate(pairs)]
+    for copy in copies:
+        copy.start()
+    return copies
 
 
 def prepare_kernel(rows_ref, examples_ref, counts_ref, out_ref, live_ref):
@@ -61,69 +69,71 @@
             out_ref[q, :, under:, lanes] = jnp.where(early, ref[first], ref[second])
 
 
-def split_kernel(*refs):
-    out_ref = refs[-1]
-    width = out_ref.shape[3] // 2
-    sides = (refs[:1], refs[1:2]) if len(refs) == 3 else (refs[:2], refs[2:4])
-    for place, pieces in enumerate(sides):
-        t = 0
-        for ref in pieces:
-            for k in range(ref.shape[0]):
-                full = ref[k]
-                high = full.astype(jnp.bfloat16)
-                out_ref[place, t, :, :width] = high
-                out_ref[place, t, :, width:] = (full - high.astype(jnp.float32)).astype(
-                    jnp.bfloat16
-                )
-                t += 1
-
-
-def split_tables(pieces, count, rows, width):
-    return local_kernel(
-        split_kernel,
-        jax.ShapeDtypeStruct((2, count, rows, 2 * width), jnp.bfloat16),
-        pieces,
-        flops=4 << 20,
-    )
+def split_into(out_ref, place, t, full):
+    width = full.shape[1]
+    high = full.astype(jnp.bfloat16)
+    out_ref[place, t, :, :width] = high
+    out_ref[place, t, :, width:] = (full - high.astype(jnp.float32)).astype(jnp.bfloat16)
+
+
+def split_kernel(own_ref, other_ref, out_ref):
+    for place, ref in enumerate((own_ref, other_ref)):
+        for t in range(ref.shape[0]):
+            split_into(out_ref, place, t, ref[t])
 
 
 def one_hot(mask):
     return jnp.where(mask, 1.0, 0.0).astype(jnp.bfloat16)
 
 
-def bags_kernel(ids_ref, near_ref, partner_ref, out_ref, looked_ref, *, away, examples):
+def bags_kernel(*refs, away, examples):
+    if len(refs) == 11:
+        ids_ref, near_ref, *raw, out_ref, partner_ref, looked_ref, full_ref, sems = refs
+        half = raw[0].shape[0]
+        copies = started(
+            [
+                (ref, full_ref.at[k // 2, half * (k % 2) : half * (k % 2) + half])
+                for k, ref in enumerate(raw)
+            ],
+            sems,
+        )
+    else:
+        ids_ref, near_ref, partner_ref, out_ref, looked_ref = refs
+        copies = []
     group, ring, messages, lanes = ids_ref.shape
     cores, count, rows, wide = near_ref.shape
     slots = lanes // 2
     core = lax.axis_index("c")
-    column = lax.rem(lax.axis_index("x") + away, ring)
+    chosen = away[0] + core * (away[1] - away[0])
+    column = lax.rem(lax.axis_index("x") + chosen, ring)
     depth = lax.axis_index("zq")
     row_iota = lax.broadcasted_iota(jnp.int32, (slots, rows), 1)
     key_iota = lax.broadcasted_iota(jnp.int32, (group * examples, group * slots), 0)
     ids = [ids_ref[lax.rem(depth + j, group), column] for j in range(group)]
     columns = jnp.swapaxes(jnp.concatenate(ids, axis=0), 0, 1)
     keys = jnp.concatenate([ids[j][:, slots:] + j * examples for j in range(group)], axis=1)
-    for t in range(count):
-        into = []
-        for block, tables_ref in enumerate((near_ref, partner_ref)):
-            for o in range(cores):
-                message = (block * cores + o) * count + t
-                picks = jnp.concatenate(
-                    [
-                        one_hot(
-                            columns[:slots, j * messages + message : j * messages + message + 1]
-                            == row_iota
-                        )
-                        for j in range(group)
-                    ],
-                    axis=0,
-                )
-                looked = jnp.dot(
-                    picks, tables_ref[o ^ core, t], preferred_element_type=jnp.float32
-                )
-                place = (block * cores + o) * group * slots
-                looked_ref[t, place : place + group * slots, :] = looked.astype(jnp.bfloat16)
-                into.append(one_hot(keys[message : message + 1] == key_iota))
+
+    def look(block, tables_ref, t):
+        for o in range(cores):
+            message = (block * cores + o) * count + t
+            picks = jnp.concatenate(
+                [
+                    one_hot(
+                        columns[:slots, j * messages + message : j * messages + message + 1]
+                        == row_iota
+                    )
+                    for j in range(group)
+                ],
+                axis=0,
+            )
+            looked = jnp.dot(picks, tables_ref[o ^ core, t], preferred_element_type=jnp.float32)
+            place = (block * cores + o) * group * slots
+            looked_ref[t, place : place + group * slots, :] = looked.astype(jnp.bfloat16)
+
+    def pool(t):
+        into = [
+            one_hot(keys[b * count + t : b * count + t + 1] == key_iota) for b in range(2 * cores)
+        ]
         total = jnp.dot(
             jnp.concatenate(into, axis=1), looked_ref[t], preferred_element_type=jnp.float32
         )
@@ -132,25 +142,62 @@
             group, examples, wide // 2
         )
 
+    if copies:
+        for t in range(count):
+            look(0, near_ref, t)
+        for copy in copies:
+            copy.wait()
+        for t in range(count):
+            for place in range(cores):
+                split_into(partner_ref, place, t, full_ref[place, t])
+            look(1, partner_ref, t)
+            pool(t)
+    else:
+        for t in range(count):
+            look(0, near_ref, t)
+            look(1, partner_ref, t)
+            pool(t)
+
 
 def bags(ids, near, partner, away, examples):
     group, _, _, lanes = ids.shape
     cores, count, rows, wide = near.shape
     work = 2 * cores * count * group * lanes // 2
+    out = jax.ShapeDtypeStruct((group, count * examples, wide // 2), jnp.float32)
+    scratch = [pltpu.VMEM((count, 2 * cores * group * lanes // 2, wide), jnp.bfloat16)]
+    raw = isinstance(partner, tuple)
+    if raw:
+        out = (out, jax.ShapeDtypeStruct(near.shape, near.dtype))
+        scratch += [
+            pltpu.VMEM((cores, count, rows, wide // 2), jnp.float32),
+            pltpu.SemaphoreType.DMA((len(partner),)),
+        ]
     return local_kernel(
         functools.partial(bags_kernel, away=away, examples=examples),
-        jax.ShapeDtypeStruct((group, count * examples, wide // 2), jnp.float32),
-        (ids, near, partner),
+        out,
+        (ids, near) + (partner if raw else (partner,)),
         flops=2 * work * wide * (rows + group * examples),
         vmem=16 << 20,
-        scratch=[pltpu.VMEM((count, 2 * cores * group * lanes // 2, wide), jnp.bfloat16)],
-    )
+        scratch=scratch,
+        in_hbm=range(2, 6) if raw else (),
+    )
+
+
+def by_core(value, by, ring):
+    pairs = [
+        (2 * i + c, 2 * ((i + by * (1 - 2 * c)) % ring) + c) for i in range(ring) for c in range(2)
+    ]
+    return lax.ppermute(value, ("x", "c"), pairs)
+
+
+def add_kernel(one_ref, two_ref, out_ref):
+    out_ref[...] = one_ref[...] + two_ref[...]
 
 
 def join_kernel(*refs):
-    ins, outs = refs[:4], refs[4:]
+    ins, outs = refs[:3], refs[3:]
     for j, out_ref in enumerate(outs):
-        out_ref[...] = ins[0][j] + ins[1][j] + ins[2][j] + ins[3][j]
+        out_ref[...] = ins[0][j] + ins[1][j] + ins[2][j]
 
 
 def close_kernel(own_ref, one_ref, two_ref, three_ref, dense_ref, pooled_ref, pairs_ref):
@@ -174,7 +221,7 @@
 
 
 def body(embedding, tables, dense_features, slot_rows, slot_examples, slot_counts):
-    count, rows, width = tables.shape
+    count, _, width = tables.shape
     examples = dense_features.shape[0]
     capacity = slot_rows.shape[3]
     group, parities, ring, cores = (lax.axis_size(a) for a in ROWS)
@@ -198,18 +245,22 @@
     ids = ids.reshape((group, ring) + ids.shape[1:])
     other_low = shifted(low, "c", 1)
     other_high = shifted(high, "c", 1)
-    near = split_tables((tables, other), count, rows, width)
-    partner = split_tables((low, high, other_low, other_high), count, rows, width)
-
-    far = bags(ids, near, partner, 2, examples)
-    far = shifted(far, "x", 2)
-    right = bags(ids, near, partner, 1, examples)
-    right = shifted(right, "x", 1)
-    left = bags(ids, near, partner, 3, examples)
-    left = shifted(left, "x", -1)
-    own = bags(ids, near, partner, 0, examples)
+    near = local_kernel(
+        split_kernel,
+        jax.ShapeDtypeStruct((cores,) + tables.shape[:2] + (2 * width,), jnp.bfloat16),
+        (tables, other),
+    )
+
+    far, partner = bags(ids, near, (low, high, other_low, other_high), (2, 2), examples)
+    far = by_core(far, 1, ring)
+    soon = bags(ids, near, partner, (3, 1), examples)
+    soon = by_core(soon, -1, ring)
+    late = bags(ids, near, partner, (1, 3), examples)
+    late = local_kernel(add_kernel, jax.ShapeDtypeStruct(late.shape, late.dtype), (late, far))
+    late = by_core(late, 1, ring)
+    own = bags(ids, near, partner, (0, 0), examples)
     block = jax.ShapeDtypeStruct(own.shape[1:], jnp.float32)
-    here, up, over, down = local_kernel(join_kernel, (block,) * group, (own, far, right, left))
+    here, up, over, down = local_kernel(join_kernel, (block,) * group, (own, soon, late))
     over, up, down = (
         lax.ppermute(piece, Z, [(i, (i + parities * by) % depth) for i in range(depth)])
         for piece, by in ((over, 2), (up, 1), (down, 3))

time: 83.8 us -> 83 us (level)
  waiting for transfers between devices: 35.7 us -> 40.7 us
  local copies, waits for them, and re-layouts: 6.53 us -> 3.62 us
  starting transfers between devices: 27.7 us -> 24.8 us
    ppermute x0 -> x3, waiting for transfers between devices: none -> 7.97 us  [by_core(): return lax.ppermute(value, ('x', 'c'), pairs)]
    ppermute x9 -> x6, waiting for transfers between devices: 12.4 us -> 5.14 us  [shifted(): lax.ppermute(value, axis, [(i, (i + by) % size) for i in range(size)])]
    ppermute x9 -> x6, starting transfers between devices: 8.23 us -> 3.36 us  [shifted(): lax.ppermute(value, axis, [(i, (i + by) % size) for i in range(size)])]
    ppermute x0 -> x3, starting transfers between devices: none -> 3.65 us  [by_core(): return lax.ppermute(value, ('x', 'c'), pairs)]
    all_to_all x1, waiting for transfers between devices: 4.47 us -> 7.77 us  [body(): ids = lax.all_to_all(ids, ('zq', 'x'), 0, 0, tiled=True)]
    unnamed x18 -> x14, local copies, waits for them, and re-layouts: 5.17 us -> 2.26 us
    ppermute x3, starting transfers between devices: 6.34 us -> 4.68 us  [body(): lax.ppermute(piece, Z, [(i, (i + parities * by) % depth) for i in range(d...]
    ppermute x3, waiting for transfers between devices: 4.83 us -> 5.74 us  [body(): lax.ppermute(piece, Z, [(i, (i + parities * by) % depth) for i in range(d...]
  transfers between devices with their start and end apart: 15 -> 15, of which waited for: 9 -> 9; matrix products, arithmetic and copies ran while one was open for 2% -> 2% of each run, Pallas kernels for 6% -> 9%
where the time goes in v4:
time: 83 us; the launch traced here: 82.8 us
  waiting for transfers between devices  40.7 us (49%)
  starting transfers between devices  24.8 us (30%)
  Pallas kernels  12.3 us (15%)
  local copies, waits for them, and re-layouts  3.62 us (4%)
    ppermute x1, waiting for transfers between devices, body(): lax.ppermute(tables[half:], Z, [(i, (i + (1 if i % 2 else -1)) % depth) f...  12.6 us
    pallas_call x9, Pallas kernels, local_kernel(): pl.pallas_call(kernel, in_specs=[HBM if k in in_hbm else VMEM for k in ra...  12.3 us
    ppermute x3, waiting for transfers between devices, by_core(): return lax.ppermute(value, ('x', 'c'), pairs)  7.97 us
    all_to_all x1, waiting for transfers between devices, body(): ids = lax.all_to_all(ids, ('zq', 'x'), 0, 0, tiled=True)  7.77 us
    all_to_all x1, starting transfers between devices, body(): ids = lax.all_to_all(ids, ('zq', 'x'), 0, 0, tiled=True)  7.17 us
    ppermute x1, starting transfers between devices, body(): lax.ppermute(tables[half:], Z, [(i, (i + (1 if i % 2 else -1)) % depth) f...  5.94 us
    ppermute x3, waiting for transfers between devices, body(): lax.ppermute(piece, Z, [(i, (i + parities * by) % depth) for i in range(d...  5.74 us
    ppermute x6, waiting for transfers between devices, shifted(): lax.ppermute(value, axis, [(i, (i + by) % size) for i in range(size)])  5.14 us
  transfers between devices with their start and end apart: 15, of which 9 were waited for; matrix products, arithmetic and copies ran while one was open for 2% of the time, Pallas kernels for 9%

profile of v4, /device:TPU:24, one launch (start us, length us, event | category | flops | bytes accessed | tf_op | source)
XLA Modules:
  0.0 82.8 jit_solution(15520375484220999527)
XLA Ops:
  0.7 0.1 collective-permute-start
  0.8 1.4 %fusion = (f32[2,512,128]{2,1,0:T(8,128)S(1)}, f32[2,512,128]{2,1,0:T(8,128)S(1)}) fusion(f32[4,512,128]{2,1,0:T(8,128)} %own_ref.1), kind=kLoop, calls=%fused_computation.1 | loop fusion | bytes 2097152 | tf_op jit(solution)/shard_map/slice | solution.py:234
  2.1 5.9 %collective-permute-start.2 = (f32[2,512,128]{2,1,0:T(8,128)S(1)}, f32[2,512,128]{2,1,0:T(8,128)}, u32[]{:S(2)}, u32[]{:S(2)}) collective-permute-start(f32[2,512,128]{2,1,0:T(8,128)S(1)} %get-tuple-element.18), channel_id=1, source_target_pairs={{0,224},{32,64},{64,32},{96,128},{128,96},{160,192},{192,160},{224... | collective-permute-start | bytes 1572872 | tf_op jit(solution)/shard_map/ppermute | solution.py:233
  8.1 12.6 %collective-permute-done.2.refs_3_ = f32[2,512,128]{2,1,0:T(8,128)} collective-permute-done((f32[2,512,128]{2,1,0:T(8,128)S(1)}, f32[2,512,128]{2,1,0:T(8,128)}, u32[]{:S(2)}, u32[]{:S(2)}) %collective-permute-start.2) | collective-permute-done | bytes 524320 | tf_op jit(solution)/shard_map/ppermute | solution.py:233
  20.7 1.5 %collective-permute-done.1.refs_2_ = f32[2,512,128]{2,1,0:T(8,128)} collective-permute-done((f32[2,512,128]{2,1,0:T(8,128)S(1)}, f32[2,512,128]{2,1,0:T(8,128)}, u32[]{:S(2)}, u32[]{:S(2)}) %collective-permute-start.1) | collective-permute-done | bytes 524320 | tf_op jit(solution)/shard_map/ppermute | solution.py:232
  22.2 1.0 %shard_map.68 = s32[4,4,16,128]{3,2,1,0:T(8,128)} custom-call(s32[8,4,8,64]{3,2,1,0:T(8,128)S(1)} %bitcast.9, s32[8,4,8,64]{3,2,1,0:T(8,128)S(1)} %bitcast.10, s32[4,64]{1,0:T(4,128)S(1)} %bitcast.15), custom_call_target="tpu_custom_call" | custom-call | flops 1048576 | bytes 1048576 | tf_op jit(solution)/shard_map/pallas_call | solution.py:26
  23.2 7.2 %all-to-all-start = ((s32[16,16,128]{2,1,0:T(8,128)}), s32[16,16,128]{2,1,0:T(8,128)S(1)}, u32[]{:S(2)}, u32[]{:S(2)}) async-start(s32[16,16,128]{2,1,0:T(8,128)} %bitcast.4), calls=%async_computation | async-start | bytes 262144 | tf_op jit(solution)/shard_map/all_to_all | solution.py:244
  30.4 1.0 %copy-done.1 = f32[4,512,128]{2,1,0:T(8,128)} copy-done((f32[4,512,128]{2,1,0:T(8,128)}, f32[4,512,128]{2,1,0:T(8,128)S(1)}, u32[]{:S(2)}) %copy-start.1) | copy-done | bytes 1048600
  31.4 1.2 %copy-done.2 = f32[4,512,128]{2,1,0:T(8,128)S(1)} copy-done((f32[4,512,128]{2,1,0:T(8,128)S(1)}, f32[4,512,128]{2,1,0:T(8,128)}, u32[]{:S(2)}) %copy-start.2) | copy-done | bytes 1048600
  32.6 0.4 shard_map.69.refs_1_
  33.0 7.8 %all-to-all-done = s32[16,16,128]{2,1,0:T(8,128)S(1)} async-done(((s32[16,16,128]{2,1,0:T(8,128)}), s32[16,16,128]{2,1,0:T(8,128)S(1)}, u32[]{:S(2)}, u32[]{:S(2)}) %all-to-all-start) | async-done | bytes 131104 | tf_op jit(solution)/shard_map/all_to_all | solution.py:244
  40.8 4.0 %shard_map.70 = (f32[4,128,128]{2,1,0:T(8,128)S(1)}, bf16[2,4,512,256]{3,2,1,0:T(8,128)(2,1)S(1)}) custom-call(s32[4,4,16,128]{3,2,1,0:T(8,128)S(1)} %bitcast.11, bf16[2,4,512,256]{3,2,1,0:T(8,128)(2,1)S(1)} %shard_map.69.refs_1_, f32[2,512,128]{2,1,0:T(8,128)} %collective-permute-done.1.refs_2_, f32[2,512,128]{2,1,0:T(8,128)} %collective-permute-done.2.refs_3_, ...), custom_call_target="tpu_custom_call" | custom-call | flops 1342177280 | bytes 1048576 | tf_op jit(solution)/shard_map/pallas_call | solution.py:26
  44.8 0.4 collective-permute-start.6
  45.3 2.0 %shard_map.72 = f32[4,128,128]{2,1,0:T(8,128)S(1)} custom-call(s32[4,4,16,128]{3,2,1,0:T(8,128)S(1)} %bitcast.12, bf16[2,4,512,256]{3,2,1,0:T(8,128)(2,1)S(1)} %shard_map.69.refs_1_, bf16[2,4,512,256]{3,2,1,0:T(8,128)(2,1)S(1)} %get-tuple-element.10.refs_2_), custom_call_target="tpu_custom_call" | custom-call | flops 1342177280 | bytes 1048576 | tf_op jit(solution)/shard_map/pallas_call | solution.py:26
  47.3 3.0 %collective-permute-start.5 = (f32[4,128,128]{2,1,0:T(8,128)S(1)}, f32[4,128,128]{2,1,0:T(8,128)S(1)}, u32[]{:S(2)}, u32[]{:S(2)}) collective-permute-start(f32[4,128,128]{2,1,0:T(8,128)S(1)} %shard_map.72), channel_id=1, source_target_pairs={{0,24},{4,12},{8,0},{12,20},{16,8},{20,28},{24,16},{28,4},{1,25},{... | collective-permute-start | bytes 786440 | tf_op jit(solution)/shard_map/ppermute | solution.py:190
  50.3 2.0 %shard_map.73.one_ref = f32[4,128,128]{2,1,0:T(8,128)S(1)} custom-call(s32[4,4,16,128]{3,2,1,0:T(8,128)S(1)} %bitcast.13, bf16[2,4,512,256]{3,2,1,0:T(8,128)(2,1)S(1)} %shard_map.69.refs_1_, bf16[2,4,512,256]{3,2,1,0:T(8,128)(2,1)S(1)} %get-tuple-element.10.refs_2_), custom_call_target="tpu_custom_call" | custom-call | flops 1342177280 | bytes 1048576 | tf_op jit(solution)/shard_map/pallas_call | solution.py:26
  52.3 2.4 %collective-permute-done.6.two_ref = f32[4,128,128]{2,1,0:T(8,128)S(1)} collective-permute-done((f32[4,128,128]{2,1,0:T(8,128)S(1)}, f32[4,128,128]{2,1,0:T(8,128)S(1)}, u32[]{:S(2)}, u32[]{:S(2)}) %collective-permute-start.6) | collective-permute-done | bytes 262176 | tf_op jit(solution)/shard_map/ppermute | solution.py:190
  54.8 0.3 collective-permute-start.7
  55.0 2.0 %shard_map.71.refs_0_ = f32[4,128,128]{2,1,0:T(8,128)S(1)} custom-call(s32[4,4,16,128]{3,2,1,0:T(8,128)S(1)} %bitcast.14, bf16[2,4,512,256]{3,2,1,0:T(8,128)(2,1)S(1)} %shard_map.69.refs_1_, bf16[2,4,512,256]{3,2,1,0:T(8,128)(2,1)S(1)} %get-tuple-element.10.refs_2_), custom_call_target="tpu_custom_call" | custom-call | flops 1342177280 | bytes 1048576 | tf_op jit(solution)/shard_map/pallas_call | solution.py:26
  57.1 5.5 %collective-permute-done.7.refs_2_ = f32[4,128,128]{2,1,0:T(8,128)S(1)} collective-permute-done((f32[4,128,128]{2,1,0:T(8,128)S(1)}, f32[4,128,128]{2,1,0:T(8,128)S(1)}, u32[]{:S(2)}, u32[]{:S(2)}) %collective-permute-start.7) | collective-permute-done | bytes 262176 | tf_op jit(solution)/shard_map/ppermute | solution.py:190
  62.6 0.5 collective-permute-start.8
  63.2 3.3 %collective-permute-start.9 = (f32[128,128]{1,0:T(8,128)S(1)}, f32[128,128]{1,0:T(8,128)S(1)}, u32[]{:S(2)}, u32[]{:S(2)}) collective-permute-start(f32[128,128]{1,0:T(8,128)S(1)} %get-tuple-element.14), channel_id=1, source_target_pairs={{0,64},{32,96},{64,128},{96,160},{128,192},{160,224},{192,0},{224,... | collective-permute-start | bytes 196616 | tf_op jit(solution)/shard_map/ppermute | solution.py:265
  66.5 0.8 %collective-permute-start.10 = (f32[128,128]{1,0:T(8,128)S(1)}, f32[128,128]{1,0:T(8,128)S(1)}, u32[]{:S(2)}, u32[]{:S(2)}) collective-permute-start(f32[128,128]{1,0:T(8,128)S(1)} %get-tuple-element.15), channel_id=1, source_target_pairs={{0,192},{32,224},{64,0},{96,32},{128,64},{160,96},{192,128},{224,1... | collective-permute-start | bytes 196616 | tf_op jit(solution)/shard_map/ppermute | solution.py:265
  67.3 3.6 %collective-permute-done.8.one_ref = f32[128,128]{1,0:T(8,128)S(1)} collective-permute-done((f32[128,128]{1,0:T(8,128)S(1)}, f32[128,128]{1,0:T(8,128)S(1)}, u32[]{:S(2)}, u32[]{:S(2)}) %collective-permute-start.8) | collective-permute-done | bytes 65568 | tf_op jit(solution)/shard_map/ppermute | solution.py:265
  71.0 2.1 %collective-permute-done.10.three_ref = f32[128,128]{1,0:T(8,128)S(1)} collective-permute-done((f32[128,128]{1,0:T(8,128)S(1)}, f32[128,128]{1,0:T(8,128)S(1)}, u32[]{:S(2)}, u32[]{:S(2)}) %collective-permute-start.10) | collective-permute-done | bytes 65568 | tf_op jit(solution)/shard_map/ppermute | solution.py:265
  73.1 0.7 shard_map.76
  73.8 0.7 collective-permute-start.13
  74.5 2.5 %collective-permute-start.12 = (f32[10,32]{1,0:T(8,128)S(1)}, f32[10,32]{1,0:T(8,128)S(1)}, u32[]{:S(2)}, u32[]{:S(2)}) collective-permute-start(f32[10,32]{1,0:T(8,128)S(1)} %get-tuple-element.17), channel_id=1, source_target_pairs={{0,1},{1,2},{2,3},{3,0},{4,5},{5,6},{6,7},{7,4},{8,9},{9,10},{10,1... | collective-permute-start | bytes 3848 | tf_op jit(solution)/shard_map/ppermute | solution.py:21
  77.0 0.0 collective-permute-start.11
  77.0 1.6 %collective-permute-done.13 = f32[10,32]{1,0:T(8,128)S(1)} collective-permute-done((f32[10,32]{1,0:T(8,128)S(1)}, f32[10,32]{1,0:T(8,128)S(1)}, u32[]{:S(2)}, u32[]{:S(2)}) %collective-permute-start.13) | collective-permute-done | bytes 1312 | tf_op jit(solution)/shard_map/ppermute | solution.py:21
  78.6 3.5 %collective-permute-done.11 = f32[10,32]{1,0:T(8,128)S(1)} collective-permute-done((f32[10,32]{1,0:T(8,128)S(1)}, f32[10,32]{1,0:T(8,128)S(1)}, u32[]{:S(2)}, u32[]{:S(2)}) %collective-permute-start.11) | collective-permute-done | bytes 1312 | tf_op jit(solution)/shard_map/ppermute | solution.py:21
  82.2 0.6 multiply_bitcast_fusion
  (23 shorter events, 0.1 us)
Async XLA Ops:
  0.6 30.7 %copy-start = (f32[4,512,128]{2,1,0:T(8,128)S(1)}, f32[4,512,128]{2,1,0:T(8,128)}, u32[]{:S(2)}) copy-start(f32[4,512,128]{2,1,0:T(8,128)} %own_ref.1) | copy-start | bytes 3145732
  0.6 21.5 %copy-start.6 = (s32[1,64,4]{1,2,0:T(4,128)S(1)}, s32[1,64,4]{1,2,0:T(4,128)}, u32[]{:S(2)}) copy-start(s32[1,64,4]{1,2,0:T(4,128)} %param.9) | copy-start | bytes 3076
  0.7 21.5 %copy-start.4 = (s32[1,64,4,64]{3,2,1,0:T(4,128)S(1)}, s32[1,64,4,64]{3,2,1,0:T(4,128)}, u32[]{:S(2)}) copy-start(s32[1,64,4,64]{3,2,1,0:T(4,128)} %param.8) | copy-start | bytes 196612
  0.7 21.5 %copy-start.3 = (s32[1,64,4,64]{3,2,1,0:T(4,128)S(1)}, s32[1,64,4,64]{3,2,1,0:T(4,128)}, u32[]{:S(2)}) copy-start(s32[1,64,4,64]{3,2,1,0:T(4,128)} %param.7) | copy-start | bytes 196612
  0.7 29.7 %collective-permute-start = (f32[4,512,128]{2,1,0:T(8,128)}, f32[4,512,128]{2,1,0:T(8,128)S(1)}, u32[]{:S(2)}, u32[]{:S(2)}) collective-permute-start(f32[4,512,128]{2,1,0:T(8,128)} %own_ref.1), channel_id=1, source_target_pairs={{0,4},{4,0},{1,5},{5,1},{2,6},{6,2},{3,7},{7,3},{8,12},{12,8},{9,1... | collective-permute-start | bytes 3145736 | tf_op jit(solution)/shard_map/ppermute | solution.py:21
  2.1 18.5 %collective-permute-start.2 = (f32[2,512,128]{2,1,0:T(8,128)S(1)}, f32[2,512,128]{2,1,0:T(8,128)}, u32[]{:S(2)}, u32[]{:S(2)}) collective-permute-start(f32[2,512,128]{2,1,0:T(8,128)S(1)} %get-tuple-element.18), channel_id=1, source_target_pairs={{0,224},{32,64},{64,32},{96,128},{128,96},{160,192},{192,160},{224... | collective-permute-start | bytes 1572872 | tf_op jit(solution)/shard_map/ppermute | solution.py:233
  8.1 14.1 %collective-permute-start.1 = (f32[2,512,128]{2,1,0:T(8,128)S(1)}, f32[2,512,128]{2,1,0:T(8,128)}, u32[]{:S(2)}, u32[]{:S(2)}) collective-permute-start(f32[2,512,128]{2,1,0:T(8,128)S(1)} %get-tuple-element.19), channel_id=1, source_target_pairs={{0,32},{32,0},{64,96},{96,64},{128,160},{160,128},{192,224},{224,1... | collective-permute-start | bytes 1572872 | tf_op jit(solution)/shard_map/ppermute | solution.py:232
  20.7 20.1 %collective-permute-start.4 = (f32[2,512,128]{2,1,0:T(8,128)}, f32[2,512,128]{2,1,0:T(8,128)}, u32[]{:S(2)}, u32[]{:S(2)}) collective-permute-start(f32[2,512,128]{2,1,0:T(8,128)} %collective-permute-done.2.refs_3_), channel_id=1, source_target_pairs={{0,4},{4,0},{1,5},{5,1},{2,6},{6,2},{3,7},{7,3},{8,12},{12,8},{9,1... | collective-permute-start | bytes 1572872 | tf_op jit(solution)/shard_map/ppermute | solution.py:21
  22.1 18.7 %collective-permute-start.3 = (f32[2,512,128]{2,1,0:T(8,128)}, f32[2,512,128]{2,1,0:T(8,128)}, u32[]{:S(2)}, u32[]{:S(2)}) collective-permute-start(f32[2,512,128]{2,1,0:T(8,128)} %collective-permute-done.1.refs_2_), channel_id=1, source_target_pairs={{0,4},{4,0},{1,5},{5,1},{2,6},{6,2},{3,7},{7,3},{8,12},{12,8},{9,1... | collective-permute-start | bytes 1572872 | tf_op jit(solution)/shard_map/ppermute | solution.py:21
  23.2 17.6 %all-to-all-start = ((s32[16,16,128]{2,1,0:T(8,128)}), s32[16,16,128]{2,1,0:T(8,128)S(1)}, u32[]{:S(2)}, u32[]{:S(2)}) async-start(s32[16,16,128]{2,1,0:T(8,128)} %bitcast.4), calls=%async_computation | async-start | bytes 262144 | tf_op jit(solution)/shard_map/all_to_all | solution.py:244
  30.3 1.0 %copy-start.1 = (f32[4,512,128]{2,1,0:T(8,128)}, f32[4,512,128]{2,1,0:T(8,128)S(1)}, u32[]{:S(2)}) copy-start(f32[4,512,128]{2,1,0:T(8,128)S(1)} %collective-permute-done.other_ref) | copy-start | bytes 3145732
  31.4 1.2 %copy-start.2 = (f32[4,512,128]{2,1,0:T(8,128)S(1)}, f32[4,512,128]{2,1,0:T(8,128)}, u32[]{:S(2)}) copy-start(f32[4,512,128]{2,1,0:T(8,128)} %copy-done.1) | copy-start | bytes 3145732
  44.8 9.9 %collective-permute-start.6 = (f32[4,128,128]{2,1,0:T(8,128)S(1)}, f32[4,128,128]{2,1,0:T(8,128)S(1)}, u32[]{:S(2)}, u32[]{:S(2)}) collective-permute-start(f32[4,128,128]{2,1,0:T(8,128)S(1)} %get-tuple-element.11), channel_id=1, source_target_pairs={{0,8},{4,28},{8,16},{12,4},{16,24},{20,12},{24,0},{28,20},{1,9},{5... | collective-permute-start | bytes 786440 | tf_op jit(solution)/shard_map/ppermute | solution.py:190
  47.3 9.8 %collective-permute-start.5 = (f32[4,128,128]{2,1,0:T(8,128)S(1)}, f32[4,128,128]{2,1,0:T(8,128)S(1)}, u32[]{:S(2)}, u32[]{:S(2)}) collective-permute-start(f32[4,128,128]{2,1,0:T(8,128)S(1)} %shard_map.72), channel_id=1, source_target_pairs={{0,24},{4,12},{8,0},{12,20},{16,8},{20,28},{24,16},{28,4},{1,25},{... | collective-permute-start | bytes 786440 | tf_op jit(solution)/shard_map/ppermute | solution.py:190
  54.8 18.3 %copy-start.5 = (f32[32,128]{1,0:T(8,128)S(1)}, f32[32,128]{1,0:T(8,128)}, u32[]{:S(2)}) copy-start(f32[32,128]{1,0:T(8,128)} %dense_ref.1) | copy-start | bytes 49156
  54.8 7.8 %collective-permute-start.7 = (f32[4,128,128]{2,1,0:T(8,128)S(1)}, f32[4,128,128]{2,1,0:T(8,128)S(1)}, u32[]{:S(2)}, u32[]{:S(2)}) collective-permute-start(f32[4,128,128]{2,1,0:T(8,128)S(1)} %shard_map.74), channel_id=1, source_target_pairs={{0,8},{4,28},{8,16},{12,4},{16,24},{20,12},{24,0},{28,20},{1,9},{5... | collective-permute-start | bytes 786440 | tf_op jit(solution)/shard_map/ppermute | solution.py:190
  62.6 8.3 %collective-permute-start.8 = (f32[128,128]{1,0:T(8,128)S(1)}, f32[128,128]{1,0:T(8,128)S(1)}, u32[]{:S(2)}, u32[]{:S(2)}) collective-permute-start(f32[128,128]{1,0:T(8,128)S(1)} %get-tuple-element.13), channel_id=1, source_target_pairs={{0,128},{32,160},{64,192},{96,224},{128,0},{160,32},{192,64},{224,... | collective-permute-start | bytes 196616 | tf_op jit(solution)/shard_map/ppermute | solution.py:265
  63.2 7.8 %collective-permute-start.9 = (f32[128,128]{1,0:T(8,128)S(1)}, f32[128,128]{1,0:T(8,128)S(1)}, u32[]{:S(2)}, u32[]{:S(2)}) collective-permute-start(f32[128,128]{1,0:T(8,128)S(1)} %get-tuple-element.14), channel_id=1, source_target_pairs={{0,64},{32,96},{64,128},{96,160},{128,192},{160,224},{192,0},{224,... | collective-permute-start | bytes 196616 | tf_op jit(solution)/shard_map/ppermute | solution.py:265
  66.5 6.6 %collective-permute-start.10 = (f32[128,128]{1,0:T(8,128)S(1)}, f32[128,128]{1,0:T(8,128)S(1)}, u32[]{:S(2)}, u32[]{:S(2)}) collective-permute-start(f32[128,128]{1,0:T(8,128)S(1)} %get-tuple-element.15), channel_id=1, source_target_pairs={{0,192},{32,224},{64,0},{96,32},{128,64},{160,96},{192,128},{224,1... | collective-permute-start | bytes 196616 | tf_op jit(solution)/shard_map/ppermute | solution.py:265
  73.8 4.9 %collective-permute-start.13 = (f32[10,32]{1,0:T(8,128)S(1)}, f32[10,32]{1,0:T(8,128)S(1)}, u32[]{:S(2)}, u32[]{:S(2)}) collective-permute-start(f32[10,32]{1,0:T(8,128)S(1)} %get-tuple-element.17), channel_id=1, source_target_pairs={{0,3},{1,0},{2,1},{3,2},{4,7},{5,4},{6,5},{7,6},{8,11},{9,8},{10,9... | collective-permute-start | bytes 3848 | tf_op jit(solution)/shard_map/ppermute | solution.py:21
  74.5 4.1 %collective-permute-start.12 = (f32[10,32]{1,0:T(8,128)S(1)}, f32[10,32]{1,0:T(8,128)S(1)}, u32[]{:S(2)}, u32[]{:S(2)}) collective-permute-start(f32[10,32]{1,0:T(8,128)S(1)} %get-tuple-element.17), channel_id=1, source_target_pairs={{0,1},{1,2},{2,3},{3,0},{4,5},{5,6},{6,7},{7,4},{8,9},{9,10},{10,1... | collective-permute-start | bytes 3848 | tf_op jit(solution)/shard_map/ppermute | solution.py:21
  77.0 5.2 %collective-permute-start.11 = (f32[10,32]{1,0:T(8,128)S(1)}, f32[10,32]{1,0:T(8,128)S(1)}, u32[]{:S(2)}, u32[]{:S(2)}) collective-permute-start(f32[10,32]{1,0:T(8,128)S(1)} %get-tuple-element.17), channel_id=1, source_target_pairs={{0,2},{1,3},{2,0},{3,1},{4,6},{5,7},{6,4},{7,5},{8,10},{9,11},{10,... | collective-permute-start | bytes 3848 | tf_op jit(solution)/shard_map/ppermute | solution.py:21

commit v5 on v4

v5 whole, which is shorter than its diff:
```python
import functools

import jax
import jax.numpy as jnp
from jax import lax
from jax.experimental import pallas as pl
from jax.experimental.pallas import tpu as pltpu
from jax.sharding import Mesh
from jax.sharding import PartitionSpec as P


Z = ("zq", "zp")
ROWS = Z + ("x", "c")
DEAD = 1 << 20
VMEM = pl.BlockSpec(memory_space=pltpu.VMEM)
HBM = pl.BlockSpec(memory_space=pltpu.HBM)


def shifted(value, axis, by):
    size = lax.axis_size(axis)
    return lax.ppermute(value, axis, [(i, (i + by) % size) for i in range(size)])


def local_kernel(kernel, out_shape, operands, flops=1 << 20, vmem=12 << 20, scratch=(), in_hbm=()):
    single = not isinstance(out_shape, tuple)
    return pl.pallas_call(
        kernel,
        in_specs=[HBM if k in in_hbm else VMEM for k in range(len(operands))],
        out_specs=VMEM if single else (VMEM,) * len(out_shape),
        out_shape=out_shape,
        scratch_shapes=scratch,
        compiler_params=pltpu.CompilerParams(vmem_limit_bytes=vmem),
        cost_estimate=pl.CostEstimate(flops=flops, bytes_accessed=1 << 20, transcendentals=0),
    )(*operands)


def prepare_kernel(
    counts_hbm, examples_hbm, rows_hbm, out_ref, counts_ref, examples_ref, rows_ref, live_ref, sems
):
    copies = [
        pltpu.make_async_copy(source, target, sems.at[k])
        for k, (source, target) in enumerate(
            ((counts_hbm, counts_ref), (examples_hbm, examples_ref), (rows_hbm, rows_ref))
        )
    ]
    for copy in copies:
        copy.start()
    depth, across, under, capacity = rows_ref.shape
    tables, owners = counts_ref.shape
    buckets = owners * tables
    bucket = lax.broadcasted_iota(jnp.int32, (buckets, owners), 0)
    owner = lax.broadcasted_iota(jnp.int32, (buckets, owners), 1)
    spread = jnp.where(bucket // tables == owner, 1.0, 0.0).astype(jnp.bfloat16)
    table = lax.broadcasted_iota(jnp.int32, (buckets, tables), 1)
    own = lax.broadcasted_iota(jnp.int32, (buckets, tables), 0) % tables
    slot = lax.broadcasted_iota(jnp.int32, (buckets, capacity), 1).astype(jnp.float32)
    copies[0].wait()
    counts = counts_ref[...].astype(jnp.float32).astype(jnp.bfloat16)
    by_table = lax.dot_general(
        spread, counts, (((1,), (1,)), ((), ())), preferred_element_type=jnp.float32
    )
    count = jnp.sum(jnp.where(table == own, by_table, 0.0), axis=1, keepdims=True)
    copies[1].wait()
    live = jnp.where(slot < count, examples_ref[...].reshape(buckets, capacity), DEAD)
    live_ref[...] = live.reshape(live_ref.shape)
    copies[2].wait()
    odd = lax.axis_index("zp")
    core = lax.axis_index("c")
    mine = lax.broadcasted_iota(jnp.int32, (across, under, capacity), 1) < tables

    def core_first(value):
        swapped = jnp.concatenate([value[:, tables:], value[:, :tables]], axis=1)
        return jnp.where(core == 0, value, swapped)

    for q in range(depth // 2):
        here = 2 * q + odd
        even_pair = 2 * q + 1 - odd
        odd_pair = lax.rem(2 * q + depth - 1 + 3 * odd, depth)
        first = jnp.where(core == 0, even_pair, odd_pair)
        second = jnp.where(core == 0, odd_pair, even_pair)
        for ref, lanes in ((rows_ref, slice(0, capacity)), (live_ref, slice(capacity, None))):
            out_ref[q, :, :under, lanes] = core_first(ref[here])
            out_ref[q, :, under:, lanes] = core_first(jnp.where(
                mine == (core == 0), ref[first], ref[second]
            ))


def split_into(out_ref, place, full):
    width = full.shape[1]
    high = full.astype(jnp.bfloat16)
    out_ref[place, :, :width] = high
    out_ref[place, :, width:] = (full - high.astype(jnp.float32)).astype(jnp.bfloat16)


def split_kernel(*refs):
    out_ref = refs[-1]
    count = refs[0].shape[0]
    for place, ref in enumerate(refs[:-1]):
        for t in range(count):
            split_into(out_ref, place * count + t, ref[t])


def split_tables(*tables):
    count, rows, width = tables[0].shape
    return local_kernel(
        split_kernel,
        jax.ShapeDtypeStruct((len(tables) * count, rows, 2 * width), jnp.bfloat16),
        tables,
    )


def one_hot(mask):
    return jnp.where(mask, 1.0, 0.0).astype(jnp.bfloat16)


def bags_kernel(*refs, away, examples, count, raw):
    ids_ref, near_ref, part_ref, shared_ref, out_ref, *refs = refs
    if raw:
        full_hbm = shared_ref
        shared_ref, looked_ref, full_ref, sem = refs
        copy = pltpu.make_async_copy(full_hbm, full_ref, sem)
        copy.start()
    else:
        (looked_ref,) = refs
    group, ring, messages, lanes = ids_ref.shape
    rows, wide = near_ref.shape[1:]
    owners = messages // count
    slots = lanes // 2
    core = lax.axis_index("c")
    chosen = away[0] + core * (away[1] - away[0])
    column = lax.rem(lax.axis_index("x") + chosen, ring)
    depth = lax.axis_index("zq")
    row_iota = lax.broadcasted_iota(jnp.int32, (slots, rows), 1)
    key_iota = lax.broadcasted_iota(jnp.int32, (group * examples, group * slots), 0)
    ids = [ids_ref[lax.rem(depth + j, group), column] for j in range(group)]
    columns = jnp.swapaxes(jnp.concatenate(ids, axis=0), 0, 1)
    keys = jnp.concatenate([ids[j][:, slots:] + j * examples for j in range(group)], axis=1)

    def look(o, t):
        ref, place = ((near_ref, t), (near_ref, count + t), (part_ref, t), (shared_ref, t))[o]
        message = o * count + t
        picks = jnp.concatenate(
            [
                one_hot(
                    columns[:slots, j * messages + message : j * messages + message + 1] == row_iota
                )
                for j in range(group)
            ],
            axis=0,
        )
        looked = jnp.dot(picks, ref[place], preferred_element_type=jnp.float32)
        looked_ref[t, o * group * slots : (o + 1) * group * slots, :] = looked.astype(jnp.bfloat16)

    def pool(t):
        into = [one_hot(keys[o * count + t : o * count + t + 1] == key_iota) for o in range(owners)]
        total = jnp.dot(
            jnp.concatenate(into, axis=1), looked_ref[t], preferred_element_type=jnp.float32
        )
        summed = total[:, : wide // 2] + total[:, wide // 2 :]
        out_ref[:, t * examples : (t + 1) * examples, :] = summed.reshape(
            group, examples, wide // 2
        )

    early = owners - 1 if raw else 0
    for t in range(count):
        for o in range(early):
            look(o, t)
    if raw:
        copy.wait()
    for t in range(count):
        if raw:
            split_into(shared_ref, t, full_ref[t])
        for o in range(early, owners):
            look(o, t)
        pool(t)


def bags(ids, near, part, shared, away, examples, raw=False):
    group, _, messages, lanes = ids.shape
    count, rows, wide = part.shape
    work = messages * group * lanes // 2
    out = jax.ShapeDtypeStruct((group, count * examples, wide // 2), jnp.float32)
    scratch = [pltpu.VMEM((count, messages // count * group * lanes // 2, wide), jnp.bfloat16)]
    if raw:
        out = (out, jax.ShapeDtypeStruct(part.shape, part.dtype))
        scratch += [pltpu.VMEM(shared.shape, jnp.float32), pltpu.SemaphoreType.DMA]
    return local_kernel(
        functools.partial(bags_kernel, away=away, examples=examples, count=count, raw=raw),
        out,
        (ids, near, part, shared),
        flops=2 * work * wide * (rows + group * examples),
        vmem=16 << 20,
        scratch=scratch,
        in_hbm=(3,) if raw else (),
    )


def by_core(value, by, ring):
    pairs = [
        (2 * i + c, 2 * ((i + by * (1 - 2 * c)) % ring) + c) for i in range(ring) for c in range(2)
    ]
    return lax.ppermute(value, ("x", "c"), pairs)


def add_kernel(one_ref, two_ref, out_ref):
    out_ref[...] = one_ref[...] + two_ref[...]


def join_kernel(*refs):
    ins, outs = refs[:3], refs[3:]
    for j, out_ref in enumerate(outs):
        out_ref[...] = ins[0][j] + ins[1][j] + ins[2][j]


def close_kernel(own_ref, one_ref, two_ref, three_ref, dense_ref, pooled_ref, pairs_ref):
    examples = dense_ref.shape[0]
    pooled = own_ref[...] + one_ref[...] + two_ref[...] + three_ref[...]
    tables = pooled.shape[0] // examples
    vectors = [dense_ref[...]]
    for t in range(tables):
        one = pooled[t * examples : (t + 1) * examples]
        pooled_ref[:, t, :] = one
        vectors.append(one)
    lane = lax.broadcasted_iota(jnp.int32, dense_ref.shape, 1)
    pairs = jnp.zeros(dense_ref.shape, jnp.float32)
    place = 0
    for i in range(tables + 1):
        for j in range(i + 1, tables + 1):
            product = jnp.sum(vectors[i] * vectors[j], axis=1, keepdims=True)
            pairs = jnp.where(lane == place, product, pairs)
            place += 1
    pairs_ref[...] = jnp.swapaxes(pairs, 0, 1)[: pairs_ref.shape[0]]


def body(embedding, tables, dense_features, slot_rows, slot_examples, slot_counts):
    count, _, width = tables.shape
    examples = dense_features.shape[0]
    capacity = slot_rows.shape[3]
    group, parities, ring, cores = (lax.axis_size(a) for a in ROWS)
    depth = group * parities

    pairs = [
        (2 * i + k, 2 * (i ^ 1 if k == 0 else (i + (1 if i % 2 else -1)) % depth) + k)
        for i in range(depth)
        for k in range(cores)
    ]
    part = lax.ppermute(tables, Z + ("c",), pairs)
    other = shifted(tables, "c", 1)
    split_ids = (depth, ring, cores * count, capacity)
    ids = local_kernel(
        prepare_kernel,
        jax.ShapeDtypeStruct((group, ring, 2 * cores * count, 2 * capacity), jnp.int32),
        (slot_counts[0].T, slot_examples.reshape(split_ids), slot_rows.reshape(split_ids)),
        vmem=67043328,
        scratch=[
            pltpu.VMEM(slot_counts.shape[:0:-1], jnp.int32),
            pltpu.VMEM(split_ids, jnp.int32),
            pltpu.VMEM(split_ids, jnp.int32),
            pltpu.VMEM(split_ids, jnp.int32),
            pltpu.SemaphoreType.DMA((3,)),
        ],
        in_hbm=range(3),
    )
    ids = ids.reshape((group * ring,) + ids.shape[2:])
    ids = lax.all_to_all(ids, ("zq", "x"), 0, 0, tiled=True)
    ids = ids.reshape((group, ring) + ids.shape[1:])
    shared = shifted(part, "c", 1)
    near = split_tables(tables, other)
    part = split_tables(part)

    far, shared = bags(ids, near, part, shared, (2, 2), examples, raw=True)
    far = by_core(far, 1, ring)
    soon = bags(ids, near, part, shared, (3, 1), examples)
    soon = by_core(soon, -1, ring)
    late = bags(ids, near, part, shared, (1, 3), examples)
    late = local_kernel(add_kernel, jax.ShapeDtypeStruct(late.shape, late.dtype), (late, far))
    late = by_core(late, 1, ring)
    own = bags(ids, near, part, shared, (0, 0), examples)
    block = jax.ShapeDtypeStruct(own.shape[1:], jnp.float32)
    here, up, over, down = local_kernel(join_kernel, (block,) * group, (own, soon, late))
    over, up, down = (
        lax.ppermute(piece, Z, [(i, (i + parities * by) % depth) for i in range(depth)])
        for piece, by in ((over, 2), (up, 1), (down, 3))
    )
    pairs = count * (count + 1) // 2
    pooled, products = local_kernel(
        close_kernel,
        (
            jax.ShapeDtypeStruct((examples, count, width), jnp.float32),
            jax.ShapeDtypeStruct((pairs, examples), jnp.float32),
        ),
        (here, over, up, down, dense_features),
    )
    opposite = shifted(products, "y", 2)
    beside = shifted(products, "y", 1) + shifted(products, "y", -1)
    total = ((products + opposite) + beside) * embedding**-0.5
    return pooled, total.T


def solution(mesh):
    torus = Mesh(mesh.devices.reshape(4, 2, 4, 2, mesh.shape["cols"]), ROWS + ("y",))

    def layer(*args):
        return body(512, *args)

    return jax.shard_map(
        layer,
        mesh=torus,
        in_specs=(
            P(None, ROWS, "y"),
            P(ROWS, "y"),
            P(ROWS, None, None, None),
            P(ROWS, None, None, None),
            P(ROWS, None, None),
        ),
        out_specs=(P(ROWS, None, "y"), P(ROWS, None)),
        check_vma=False,
    )
```

time: 83 us -> 81 us (0.976)
  waiting for transfers between devices: 40.7 us -> 35.3 us
  starting transfers between devices: 24.8 us -> 28.9 us
  local copies, waits for them, and re-layouts: 3.62 us -> 0.01 us
  Pallas kernels: 12.3 us -> 15 us
    ppermute x6 -> x5, starting transfers between devices: 3.36 us -> 9.56 us  [shifted(): lax.ppermute(value, axis, [(i, (i + by) % size) for i in range(size)])]
    ppermute x2 -> x1, waiting for transfers between devices: 14 us -> 9.7 us  [body(): part = lax.ppermute(tables, Z + ('c',), pairs)]
    ppermute x2 -> x1, starting transfers between devices: 5.95 us -> 2 us  [body(): part = lax.ppermute(tables, Z + ('c',), pairs)]
    pallas_call x9 -> x10, Pallas kernels: 12.3 us -> 15 us  [local_kernel(): pl.pallas_call(kernel, in_specs=[HBM if k in in_hbm else VMEM for k in ra...]
    unnamed x14 -> x4, local copies, waits for them, and re-layouts: 2.26 us -> 0.01 us
    slice x1 -> x0, local copies, waits for them, and re-layouts: 1.37 us -> none  [body(): tables[half:]]
    all_to_all x1, starting transfers between devices: 7.17 us -> 8.24 us  [body(): ids = lax.all_to_all(ids, ('zq', 'x'), 0, 0, tiled=True)]
    ppermute x3, waiting for transfers between devices: 5.74 us -> 4.76 us  [body(): lax.ppermute(piece, Z, [(i, (i + parities * by) % depth) for i in range(d...]
  transfers between devices with their start and end apart: 15 -> 13, of which waited for: 9 -> 8; matrix products, arithmetic and copies ran while one was open for 2% -> 0% of each run, Pallas kernels for 9% -> 14%
where the time goes in v5:
time: 81 us; the launch traced here: 80.6 us
  waiting for transfers between devices  35.3 us (44%)
  starting transfers between devices  28.9 us (36%)
  Pallas kernels  15 us (19%)
    pallas_call x10, Pallas kernels, local_kernel(): pl.pallas_call(kernel, in_specs=[HBM if k in in_hbm else VMEM for k in ra...  15 us
    ppermute x1, waiting for transfers between devices, body(): part = lax.ppermute(tables, Z + ('c',), pairs)  9.7 us
    ppermute x5, starting transfers between devices, shifted(): lax.ppermute(value, axis, [(i, (i + by) % size) for i in range(size)])  9.56 us
    all_to_all x1, starting transfers between devices, body(): ids = lax.all_to_all(ids, ('zq', 'x'), 0, 0, tiled=True)  8.24 us
    ppermute x3, waiting for transfers between devices, by_core(): return lax.ppermute(value, ('x', 'c'), pairs)  7.87 us
    all_to_all x1, waiting for transfers between devices, body(): ids = lax.all_to_all(ids, ('zq', 'x'), 0, 0, tiled=True)  7.83 us
    ppermute x3, starting transfers between devices, body(): lax.ppermute(piece, Z, [(i, (i + parities * by) % depth) for i in range(d...  5.47 us
    ppermute x5, waiting for transfers between devices, shifted(): lax.ppermute(value, axis, [(i, (i + by) % size) for i in range(size)])  5.13 us
  transfers between devices with their start and end apart: 13, of which 8 were waited for; matrix products, arithmetic and copies ran while one was open for 0% of the time, Pallas kernels for 14%

profile of v5, /device:TPU:24, one launch (start us, length us, event | category | flops | bytes accessed | tf_op | source)
XLA Modules:
  0.0 80.6 jit_solution(16037074334314272143)
XLA Ops:
  0.6 2.0 %collective-permute-start.1 = (f32[4,512,128]{2,1,0:T(8,128)}, f32[4,512,128]{2,1,0:T(8,128)}, u32[]{:S(2)}, u32[]{:S(2)}) collective-permute-start(f32[4,512,128]{2,1,0:T(8,128)} %refs_0_.1), channel_id=1, source_target_pairs={{0,32},{4,228},{32,0},{36,68},{64,96},{68,36},{96,64},{100,132},{1... | collective-permute-start | bytes 3145736 | tf_op jit(solution)/shard_map/ppermute | solution.py:247
  2.6 3.5 %collective-permute-start = (f32[4,512,128]{2,1,0:T(8,128)}, f32[4,512,128]{2,1,0:T(8,128)}, u32[]{:S(2)}, u32[]{:S(2)}) collective-permute-start(f32[4,512,128]{2,1,0:T(8,128)} %refs_0_.1), channel_id=1, source_target_pairs={{0,4},{4,0},{1,5},{5,1},{2,6},{6,2},{3,7},{7,3},{8,12},{12,8},{9,1... | collective-permute-start | bytes 3145736 | tf_op jit(solution)/shard_map/ppermute | solution.py:21
  6.1 9.7 %collective-permute-done.1.refs_0_ = f32[4,512,128]{2,1,0:T(8,128)} collective-permute-done((f32[4,512,128]{2,1,0:T(8,128)}, f32[4,512,128]{2,1,0:T(8,128)}, u32[]{:S(2)}, u32[]{:S(2)}) %collective-permute-start.1) | collective-permute-done | bytes 1048608 | tf_op jit(solution)/shard_map/ppermute | solution.py:247
  15.8 2.8 %collective-permute-start.2 = (f32[4,512,128]{2,1,0:T(8,128)}, f32[4,512,128]{2,1,0:T(8,128)}, u32[]{:S(2)}, u32[]{:S(2)}) collective-permute-start(f32[4,512,128]{2,1,0:T(8,128)} %collective-permute-done.1.refs_0_), channel_id=1, source_target_pairs={{0,4},{4,0},{1,5},{5,1},{2,6},{6,2},{3,7},{7,3},{8,12},{12,8},{9,1... | collective-permute-start | bytes 3145736 | tf_op jit(solution)/shard_map/ppermute | solution.py:21
  18.6 1.8 %shard_map.68 = s32[4,4,16,128]{3,2,1,0:T(8,128)} custom-call(s32[4,64]{1,0:T(4,128)} %bitcast.16, s32[8,4,8,64]{3,2,1,0:T(8,128)} %bitcast.14, s32[8,4,8,64]{3,2,1,0:T(8,128)} %bitcast.15), custom_call_target="tpu_custom_call" | custom-call | flops 1048576 | bytes 1048576 | tf_op jit(solution)/shard_map/pallas_call | solution.py:26
  20.4 8.2 %all-to-all-start = ((s32[16,16,128]{2,1,0:T(8,128)}), s32[16,16,128]{2,1,0:T(8,128)S(1)}, u32[]{:S(2)}, u32[]{:S(2)}) async-start(s32[16,16,128]{2,1,0:T(8,128)} %bitcast.13), calls=%async_computation | async-start | bytes 262144 | tf_op jit(solution)/shard_map/all_to_all | solution.py:265
  28.7 0.0 copy-start
  28.7 1.5 %shard_map.70.refs_2_ = bf16[4,512,256]{2,1,0:T(8,128)(2,1)S(1)} custom-call(f32[4,512,128]{2,1,0:T(8,128)} %collective-permute-done.1.refs_0_), custom_call_target="tpu_custom_call" | custom-call | flops 1048576 | bytes 1048576 | tf_op jit(solution)/shard_map/pallas_call | solution.py:26
  30.2 1.7 %shard_map.69.refs_1_ = bf16[8,512,256]{2,1,0:T(8,128)(2,1)S(1)} custom-call(f32[4,512,128]{2,1,0:T(8,128)S(1)} %copy-done, f32[4,512,128]{2,1,0:T(8,128)} %collective-permute-done.refs_1_), custom_call_target="tpu_custom_call" | custom-call | flops 1048576 | bytes 1048576 | tf_op jit(solution)/shard_map/pallas_call | solution.py:26
  31.9 7.8 %all-to-all-done = s32[16,16,128]{2,1,0:T(8,128)S(1)} async-done(((s32[16,16,128]{2,1,0:T(8,128)}), s32[16,16,128]{2,1,0:T(8,128)S(1)}, u32[]{:S(2)}, u32[]{:S(2)}) %all-to-all-start) | async-done | bytes 131104 | tf_op jit(solution)/shard_map/all_to_all | solution.py:265
  39.7 3.2 %shard_map.71 = (f32[4,128,128]{2,1,0:T(8,128)S(1)}, bf16[4,512,256]{2,1,0:T(8,128)(2,1)S(1)}) custom-call(s32[4,4,16,128]{3,2,1,0:T(8,128)S(1)} %bitcast.9, bf16[8,512,256]{2,1,0:T(8,128)(2,1)S(1)} %shard_map.69.refs_1_, bf16[4,512,256]{2,1,0:T(8,128)(2,1)S(1)} %shard_map.70.refs_2_, f32[4,512,128]{2,1,0:T(8,128)} %collective-permute-done.2.refs_3_), custom_call_target="tpu_custom_call" | custom-call | flops 1342177280 | bytes 1048576 | tf_op jit(solution)/shard_map/pallas_call | solution.py:26
  42.9 0.3 collective-permute-start.4
  43.3 2.0 %shard_map.73 = f32[4,128,128]{2,1,0:T(8,128)S(1)} custom-call(s32[4,4,16,128]{3,2,1,0:T(8,128)S(1)} %bitcast.10, bf16[8,512,256]{2,1,0:T(8,128)(2,1)S(1)} %shard_map.69.refs_1_, bf16[4,512,256]{2,1,0:T(8,128)(2,1)S(1)} %shard_map.70.refs_2_, bf16[4,512,256]{2,1,0:T(8,128)(2,1)S(1)} %get-tuple-element.10.refs_3_), custom_call_target="tpu_custom_call" | custom-call | flops 1342177280 | bytes 1048576 | tf_op jit(solution)/shard_map/pallas_call | solution.py:26
  45.3 3.1 %collective-permute-start.3 = (f32[4,128,128]{2,1,0:T(8,128)S(1)}, f32[4,128,128]{2,1,0:T(8,128)S(1)}, u32[]{:S(2)}, u32[]{:S(2)}) collective-permute-start(f32[4,128,128]{2,1,0:T(8,128)S(1)} %shard_map.73), channel_id=1, source_target_pairs={{0,24},{4,12},{8,0},{12,20},{16,8},{20,28},{24,16},{28,4},{1,25},{... | collective-permute-start | bytes 786440 | tf_op jit(solution)/shard_map/ppermute | solution.py:202
  48.4 2.0 %shard_map.74.one_ref = f32[4,128,128]{2,1,0:T(8,128)S(1)} custom-call(s32[4,4,16,128]{3,2,1,0:T(8,128)S(1)} %bitcast.11, bf16[8,512,256]{2,1,0:T(8,128)(2,1)S(1)} %shard_map.69.refs_1_, bf16[4,512,256]{2,1,0:T(8,128)(2,1)S(1)} %shard_map.70.refs_2_, bf16[4,512,256]{2,1,0:T(8,128)(2,1)S(1)} %get-tuple-element.10.refs_3_), custom_call_target="tpu_custom_call" | custom-call | flops 1342177280 | bytes 1048576 | tf_op jit(solution)/shard_map/pallas_call | solution.py:26
  50.4 2.3 %collective-permute-done.4.two_ref = f32[4,128,128]{2,1,0:T(8,128)S(1)} collective-permute-done((f32[4,128,128]{2,1,0:T(8,128)S(1)}, f32[4,128,128]{2,1,0:T(8,128)S(1)}, u32[]{:S(2)}, u32[]{:S(2)}) %collective-permute-start.4) | collective-permute-done | bytes 262176 | tf_op jit(solution)/shard_map/ppermute | solution.py:202
  52.8 0.0 copy-start.1
  52.8 0.3 collective-permute-start.5
  53.1 2.0 %shard_map.72.refs_0_ = f32[4,128,128]{2,1,0:T(8,128)S(1)} custom-call(s32[4,4,16,128]{3,2,1,0:T(8,128)S(1)} %bitcast.12, bf16[8,512,256]{2,1,0:T(8,128)(2,1)S(1)} %shard_map.69.refs_1_, bf16[4,512,256]{2,1,0:T(8,128)(2,1)S(1)} %shard_map.70.refs_2_, bf16[4,512,256]{2,1,0:T(8,128)(2,1)S(1)} %get-tuple-element.10.refs_3_), custom_call_target="tpu_custom_call" | custom-call | flops 1342177280 | bytes 1048576 | tf_op jit(solution)/shard_map/pallas_call | solution.py:26
  55.1 5.5 %collective-permute-done.5.refs_2_ = f32[4,128,128]{2,1,0:T(8,128)S(1)} collective-permute-done((f32[4,128,128]{2,1,0:T(8,128)S(1)}, f32[4,128,128]{2,1,0:T(8,128)S(1)}, u32[]{:S(2)}, u32[]{:S(2)}) %collective-permute-start.5) | collective-permute-done | bytes 262176 | tf_op jit(solution)/shard_map/ppermute | solution.py:202
  60.7 1.3 %collective-permute-start.6 = (f32[128,128]{1,0:T(8,128)S(1)}, f32[128,128]{1,0:T(8,128)S(1)}, u32[]{:S(2)}, u32[]{:S(2)}) collective-permute-start(f32[128,128]{1,0:T(8,128)S(1)} %get-tuple-element.13), channel_id=1, source_target_pairs={{0,128},{32,160},{64,192},{96,224},{128,0},{160,32},{192,64},{224,... | collective-permute-start | bytes 196616 | tf_op jit(solution)/shard_map/ppermute | solution.py:282
  62.0 2.0 %collective-permute-start.7 = (f32[128,128]{1,0:T(8,128)S(1)}, f32[128,128]{1,0:T(8,128)S(1)}, u32[]{:S(2)}, u32[]{:S(2)}) collective-permute-start(f32[128,128]{1,0:T(8,128)S(1)} %get-tuple-element.14), channel_id=1, source_target_pairs={{0,64},{32,96},{64,128},{96,160},{128,192},{160,224},{192,0},{224,... | collective-permute-start | bytes 196616 | tf_op jit(solution)/shard_map/ppermute | solution.py:282
  64.0 2.2 %collective-permute-start.8 = (f32[128,128]{1,0:T(8,128)S(1)}, f32[128,128]{1,0:T(8,128)S(1)}, u32[]{:S(2)}, u32[]{:S(2)}) collective-permute-start(f32[128,128]{1,0:T(8,128)S(1)} %get-tuple-element.15), channel_id=1, source_target_pairs={{0,192},{32,224},{64,0},{96,32},{128,64},{160,96},{192,128},{224,1... | collective-permute-start | bytes 196616 | tf_op jit(solution)/shard_map/ppermute | solution.py:282
  66.1 3.4 %collective-permute-done.6.one_ref = f32[128,128]{1,0:T(8,128)S(1)} collective-permute-done((f32[128,128]{1,0:T(8,128)S(1)}, f32[128,128]{1,0:T(8,128)S(1)}, u32[]{:S(2)}, u32[]{:S(2)}) %collective-permute-start.6) | collective-permute-done | bytes 65568 | tf_op jit(solution)/shard_map/ppermute | solution.py:282
  69.5 1.4 %collective-permute-done.8.three_ref = f32[128,128]{1,0:T(8,128)S(1)} collective-permute-done((f32[128,128]{1,0:T(8,128)S(1)}, f32[128,128]{1,0:T(8,128)S(1)}, u32[]{:S(2)}, u32[]{:S(2)}) %collective-permute-start.8) | collective-permute-done | bytes 65568 | tf_op jit(solution)/shard_map/ppermute | solution.py:282
  70.9 0.7 shard_map.77
  71.6 0.7 collective-permute-start.11
  72.3 2.5 %collective-permute-start.10 = (f32[10,32]{1,0:T(8,128)S(1)}, f32[10,32]{1,0:T(8,128)S(1)}, u32[]{:S(2)}, u32[]{:S(2)}) collective-permute-start(f32[10,32]{1,0:T(8,128)S(1)} %get-tuple-element.17), channel_id=1, source_target_pairs={{0,1},{1,2},{2,3},{3,0},{4,5},{5,6},{6,7},{7,4},{8,9},{9,10},{10,1... | collective-permute-start | bytes 3848 | tf_op jit(solution)/shard_map/ppermute | solution.py:21
  74.8 0.0 collective-permute-start.9
  74.8 1.6 %collective-permute-done.11 = f32[10,32]{1,0:T(8,128)S(1)} collective-permute-done((f32[10,32]{1,0:T(8,128)S(1)}, f32[10,32]{1,0:T(8,128)S(1)}, u32[]{:S(2)}, u32[]{:S(2)}) %collective-permute-start.11) | collective-permute-done | bytes 1312 | tf_op jit(solution)/shard_map/ppermute | solution.py:21
  76.4 3.5 %collective-permute-done.9 = f32[10,32]{1,0:T(8,128)S(1)} collective-permute-done((f32[10,32]{1,0:T(8,128)S(1)}, f32[10,32]{1,0:T(8,128)S(1)}, u32[]{:S(2)}, u32[]{:S(2)}) %collective-permute-start.9) | collective-permute-done | bytes 1312 | tf_op jit(solution)/shard_map/ppermute | solution.py:21
  80.0 0.6 multiply_bitcast_fusion
  (9 shorter events, 0.1 us)
Async XLA Ops:
  0.6 15.2 %collective-permute-start.1 = (f32[4,512,128]{2,1,0:T(8,128)}, f32[4,512,128]{2,1,0:T(8,128)}, u32[]{:S(2)}, u32[]{:S(2)}) collective-permute-start(f32[4,512,128]{2,1,0:T(8,128)} %refs_0_.1), channel_id=1, source_target_pairs={{0,32},{4,228},{32,0},{36,68},{64,96},{68,36},{96,64},{100,132},{1... | collective-permute-start | bytes 3145736 | tf_op jit(solution)/shard_map/ppermute | solution.py:247
  2.6 27.6 %collective-permute-start = (f32[4,512,128]{2,1,0:T(8,128)}, f32[4,512,128]{2,1,0:T(8,128)}, u32[]{:S(2)}, u32[]{:S(2)}) collective-permute-start(f32[4,512,128]{2,1,0:T(8,128)} %refs_0_.1), channel_id=1, source_target_pairs={{0,4},{4,0},{1,5},{5,1},{2,6},{6,2},{3,7},{7,3},{8,12},{12,8},{9,1... | collective-permute-start | bytes 3145736 | tf_op jit(solution)/shard_map/ppermute | solution.py:21
  15.8 23.9 %collective-permute-start.2 = (f32[4,512,128]{2,1,0:T(8,128)}, f32[4,512,128]{2,1,0:T(8,128)}, u32[]{:S(2)}, u32[]{:S(2)}) collective-permute-start(f32[4,512,128]{2,1,0:T(8,128)} %collective-permute-done.1.refs_0_), channel_id=1, source_target_pairs={{0,4},{4,0},{1,5},{5,1},{2,6},{6,2},{3,7},{7,3},{8,12},{12,8},{9,1... | collective-permute-start | bytes 3145736 | tf_op jit(solution)/shard_map/ppermute | solution.py:21
  20.4 19.3 %all-to-all-start = ((s32[16,16,128]{2,1,0:T(8,128)}), s32[16,16,128]{2,1,0:T(8,128)S(1)}, u32[]{:S(2)}, u32[]{:S(2)}) async-start(s32[16,16,128]{2,1,0:T(8,128)} %bitcast.13), calls=%async_computation | async-start | bytes 262144 | tf_op jit(solution)/shard_map/all_to_all | solution.py:265
  28.7 1.6 %copy-start = (f32[4,512,128]{2,1,0:T(8,128)S(1)}, f32[4,512,128]{2,1,0:T(8,128)}, u32[]{:S(2)}) copy-start(f32[4,512,128]{2,1,0:T(8,128)} %refs_0_.1) | copy-start | bytes 3145732
  42.9 9.8 %collective-permute-start.4 = (f32[4,128,128]{2,1,0:T(8,128)S(1)}, f32[4,128,128]{2,1,0:T(8,128)S(1)}, u32[]{:S(2)}, u32[]{:S(2)}) collective-permute-start(f32[4,128,128]{2,1,0:T(8,128)S(1)} %get-tuple-element.11), channel_id=1, source_target_pairs={{0,8},{4,28},{8,16},{12,4},{16,24},{20,12},{24,0},{28,20},{1,9},{5... | collective-permute-start | bytes 786440 | tf_op jit(solution)/shard_map/ppermute | solution.py:202
  45.3 9.8 %collective-permute-start.3 = (f32[4,128,128]{2,1,0:T(8,128)S(1)}, f32[4,128,128]{2,1,0:T(8,128)S(1)}, u32[]{:S(2)}, u32[]{:S(2)}) collective-permute-start(f32[4,128,128]{2,1,0:T(8,128)S(1)} %shard_map.73), channel_id=1, source_target_pairs={{0,24},{4,12},{8,0},{12,20},{16,8},{20,28},{24,16},{28,4},{1,25},{... | collective-permute-start | bytes 786440 | tf_op jit(solution)/shard_map/ppermute | solution.py:202
  52.8 18.1 %copy-start.1 = (f32[32,128]{1,0:T(8,128)S(1)}, f32[32,128]{1,0:T(8,128)}, u32[]{:S(2)}) copy-start(f32[32,128]{1,0:T(8,128)} %dense_ref.1) | copy-start | bytes 49156
  52.8 7.8 %collective-permute-start.5 = (f32[4,128,128]{2,1,0:T(8,128)S(1)}, f32[4,128,128]{2,1,0:T(8,128)S(1)}, u32[]{:S(2)}, u32[]{:S(2)}) collective-permute-start(f32[4,128,128]{2,1,0:T(8,128)S(1)} %shard_map.75), channel_id=1, source_target_pairs={{0,8},{4,28},{8,16},{12,4},{16,24},{20,12},{24,0},{28,20},{1,9},{5... | collective-permute-start | bytes 786440 | tf_op jit(solution)/shard_map/ppermute | solution.py:202
  60.7 8.8 %collective-permute-start.6 = (f32[128,128]{1,0:T(8,128)S(1)}, f32[128,128]{1,0:T(8,128)S(1)}, u32[]{:S(2)}, u32[]{:S(2)}) collective-permute-start(f32[128,128]{1,0:T(8,128)S(1)} %get-tuple-element.13), channel_id=1, source_target_pairs={{0,128},{32,160},{64,192},{96,224},{128,0},{160,32},{192,64},{224,... | collective-permute-start | bytes 196616 | tf_op jit(solution)/shard_map/ppermute | solution.py:282
  62.0 7.5 %collective-permute-start.7 = (f32[128,128]{1,0:T(8,128)S(1)}, f32[128,128]{1,0:T(8,128)S(1)}, u32[]{:S(2)}, u32[]{:S(2)}) collective-permute-start(f32[128,128]{1,0:T(8,128)S(1)} %get-tuple-element.14), channel_id=1, source_target_pairs={{0,64},{32,96},{64,128},{96,160},{128,192},{160,224},{192,0},{224,... | collective-permute-start | bytes 196616 | tf_op jit(solution)/shard_map/ppermute | solution.py:282
  64.0 6.9 %collective-permute-start.8 = (f32[128,128]{1,0:T(8,128)S(1)}, f32[128,128]{1,0:T(8,128)S(1)}, u32[]{:S(2)}, u32[]{:S(2)}) collective-permute-start(f32[128,128]{1,0:T(8,128)S(1)} %get-tuple-element.15), channel_id=1, source_target_pairs={{0,192},{32,224},{64,0},{96,32},{128,64},{160,96},{192,128},{224,1... | collective-permute-start | bytes 196616 | tf_op jit(solution)/shard_map/ppermute | solution.py:282
  71.6 4.9 %collective-permute-start.11 = (f32[10,32]{1,0:T(8,128)S(1)}, f32[10,32]{1,0:T(8,128)S(1)}, u32[]{:S(2)}, u32[]{:S(2)}) collective-permute-start(f32[10,32]{1,0:T(8,128)S(1)} %get-tuple-element.17), channel_id=1, source_target_pairs={{0,3},{1,0},{2,1},{3,2},{4,7},{5,4},{6,5},{7,6},{8,11},{9,8},{10,9... | collective-permute-start | bytes 3848 | tf_op jit(solution)/shard_map/ppermute | solution.py:21
  72.3 4.1 %collective-permute-start.10 = (f32[10,32]{1,0:T(8,128)S(1)}, f32[10,32]{1,0:T(8,128)S(1)}, u32[]{:S(2)}, u32[]{:S(2)}) collective-permute-start(f32[10,32]{1,0:T(8,128)S(1)} %get-tuple-element.17), channel_id=1, source_target_pairs={{0,1},{1,2},{2,3},{3,0},{4,5},{5,6},{6,7},{7,4},{8,9},{9,10},{10,1... | collective-permute-start | bytes 3848 | tf_op jit(solution)/shard_map/ppermute | solution.py:21
  74.8 5.2 %collective-permute-start.9 = (f32[10,32]{1,0:T(8,128)S(1)}, f32[10,32]{1,0:T(8,128)S(1)}, u32[]{:S(2)}, u32[]{:S(2)}) collective-permute-start(f32[10,32]{1,0:T(8,128)S(1)} %get-tuple-element.17), channel_id=1, source_target_pairs={{0,2},{1,3},{2,0},{3,1},{4,6},{5,7},{6,4},{7,5},{8,10},{9,11},{10,... | collective-permute-start | bytes 3848 | tf_op jit(solution)/shard_map/ppermute | solution.py:21

commit v6 on v5

--- a/solution.py
+++ b/solution.py
@@ -114,14 +114,15 @@
 
 
 def bags_kernel(*refs, away, examples, count, raw):
-    ids_ref, near_ref, part_ref, shared_ref, out_ref, *refs = refs
     if raw:
-        full_hbm = shared_ref
-        shared_ref, looked_ref, full_ref, sem = refs
-        copy = pltpu.make_async_copy(full_hbm, full_ref, sem)
-        copy.start()
+        ids_ref, near_ref, part_hbm, shared_ref, out_ref, moved_ref, looked_ref, full_ref, sems = refs
+        copies = [
+            pltpu.make_async_copy(part_hbm.at[t], full_ref.at[t], sems.at[t]) for t in range(count)
+        ]
+        for copy in copies:
+            copy.start()
     else:
-        (looked_ref,) = refs
+        ids_ref, near_ref, moved_ref, out_ref, looked_ref = refs
     group, ring, messages, lanes = ids_ref.shape
     rows, wide = near_ref.shape[1:]
     owners = messages // count
@@ -137,7 +138,12 @@
     keys = jnp.concatenate([ids[j][:, slots:] + j * examples for j in range(group)], axis=1)
 
     def look(o, t):
-        ref, place = ((near_ref, t), (near_ref, count + t), (part_ref, t), (shared_ref, t))[o]
+        ref, place = (near_ref, moved_ref)[o // 2], o % 2 * count + t
+        if raw and o == 2:
+            copies[t].wait()
+            split_into(ref, place, full_ref[t])
+        if raw and o == 3:
+            split_into(ref, place, shared_ref[t])
         message = o * count + t
         picks = jnp.concatenate(
             [
@@ -161,37 +167,37 @@
             group, examples, wide // 2
         )
 
-    early = owners - 1 if raw else 0
+    if raw:
+        for o in (0, 1, 3):
+            for t in range(count):
+                look(o, t)
     for t in range(count):
-        for o in range(early):
-            look(o, t)
-    if raw:
-        copy.wait()
-    for t in range(count):
-        if raw:
-            split_into(shared_ref, t, full_ref[t])
-        for o in range(early, owners):
+        for o in (2,) if raw else range(owners):
             look(o, t)
         pool(t)
 
 
-def bags(ids, near, part, shared, away, examples, raw=False):
+def bags(ids, near, moved, away, examples, raw=False):
     group, _, messages, lanes = ids.shape
-    count, rows, wide = part.shape
+    rows, wide = near.shape[1:]
+    count = near.shape[0] // 2
     work = messages * group * lanes // 2
     out = jax.ShapeDtypeStruct((group, count * examples, wide // 2), jnp.float32)
     scratch = [pltpu.VMEM((count, messages // count * group * lanes // 2, wide), jnp.bfloat16)]
     if raw:
-        out = (out, jax.ShapeDtypeStruct(part.shape, part.dtype))
-        scratch += [pltpu.VMEM(shared.shape, jnp.float32), pltpu.SemaphoreType.DMA]
+        out = (out, jax.ShapeDtypeStruct(near.shape, near.dtype))
+        scratch += [
+            pltpu.VMEM((count, rows, wide // 2), jnp.float32),
+            pltpu.SemaphoreType.DMA((count,)),
+        ]
     return local_kernel(
         functools.partial(bags_kernel, away=away, examples=examples, count=count, raw=raw),
         out,
-        (ids, near, part, shared),
+        (ids, near) + (moved if raw else (moved,)),
         flops=2 * work * wide * (rows + group * examples),
         vmem=16 << 20,
         scratch=scratch,
-        in_hbm=(3,) if raw else (),
+        in_hbm=(2,) if raw else (),
     )
 
 
@@ -266,16 +272,14 @@
     ids = ids.reshape((group, ring) + ids.shape[1:])
     shared = shifted(part, "c", 1)
     near = split_tables(tables, other)
-    part = split_tables(part)
-
-    far, shared = bags(ids, near, part, shared, (2, 2), examples, raw=True)
+    far, moved = bags(ids, near, (part, shared), (2, 2), examples, raw=True)
     far = by_core(far, 1, ring)
-    soon = bags(ids, near, part, shared, (3, 1), examples)
+    soon = bags(ids, near, moved, (3, 1), examples)
     soon = by_core(soon, -1, ring)
-    late = bags(ids, near, part, shared, (1, 3), examples)
+    late = bags(ids, near, moved, (1, 3), examples)
     late = local_kernel(add_kernel, jax.ShapeDtypeStruct(late.shape, late.dtype), (late, far))
     late = by_core(late, 1, ring)
-    own = bags(ids, near, part, shared, (0, 0), examples)
+    own = bags(ids, near, moved, (0, 0), examples)
     block = jax.ShapeDtypeStruct(own.shape[1:], jnp.float32)
     here, up, over, down = local_kernel(join_kernel, (block,) * group, (own, soon, late))
     over, up, down = (
@@ -292,8 +296,9 @@
         (here, over, up, down, dense_features),
     )
     opposite = shifted(products, "y", 2)
-    beside = shifted(products, "y", 1) + shifted(products, "y", -1)
-    total = ((products + opposite) + beside) * embedding**-0.5
+    after = shifted(products, "y", 1)
+    before = shifted(products, "y", -1)
+    total = ((products + opposite) + (after + before)) * embedding**-0.5
     return pooled, total.T
 
 

time: 81 us -> 83.2 us (1.027)
  local copies, waits for them, and re-layouts: 0.01 us -> 1.23 us
    unnamed x4, local copies, waits for them, and re-layouts: 0.01 us -> 1.23 us
    pallas_call x10 -> x9, Pallas kernels: 15 us -> 15.6 us  [local_kernel(): pl.pallas_call(kernel, in_specs=[HBM if k in in_hbm else VMEM for k in ra...]
  transfers between devices with their start and end apart: 13 -> 13, of which waited for: 8 -> 8; matrix products, arithmetic and copies ran while one was open for 0% -> 0% of each run, Pallas kernels for 14% -> 12%
where the time goes in v6:
time: 83.2 us; the launch traced here: 82.7 us
  waiting for transfers between devices  35.6 us (43%)
  starting transfers between devices  28.9 us (35%)
  Pallas kernels  15.6 us (19%)
  local copies, waits for them, and re-layouts  1.23 us (1%)
    pallas_call x9, Pallas kernels, local_kernel(): pl.pallas_call(kernel, in_specs=[HBM if k in in_hbm else VMEM for k in ra...  15.6 us
    ppermute x1, waiting for transfers between devices, body(): part = lax.ppermute(tables, Z + ('c',), pairs)  9.7 us
    ppermute x5, starting transfers between devices, shifted(): lax.ppermute(value, axis, [(i, (i + by) % size) for i in range(size)])  9.56 us
    all_to_all x1, starting transfers between devices, body(): ids = lax.all_to_all(ids, ('zq', 'x'), 0, 0, tiled=True)  8.24 us
    all_to_all x1, waiting for transfers between devices, body(): ids = lax.all_to_all(ids, ('zq', 'x'), 0, 0, tiled=True)  8.15 us
    ppermute x3, waiting for transfers between devices, by_core(): return lax.ppermute(value, ('x', 'c'), pairs)  7.87 us
    ppermute x3, starting transfers between devices, body(): lax.ppermute(piece, Z, [(i, (i + parities * by) % depth) for i in range(d...  5.46 us
    ppermute x5, waiting for transfers between devices, shifted(): lax.ppermute(value, axis, [(i, (i + by) % size) for i in range(size)])  5.14 us
  transfers between devices with their start and end apart: 13, of which 8 were waited for; matrix products, arithmetic and copies ran while one was open for 0% of the time, Pallas kernels for 12%

profile of v6, /device:TPU:24, one launch (start us, length us, event | category | flops | bytes accessed | tf_op | source)
XLA Modules:
  0.0 82.7 jit_solution(13179965323030820846)
XLA Ops:
  0.6 2.0 %collective-permute-start.1 = (f32[4,512,128]{2,1,0:T(8,128)}, f32[4,512,128]{2,1,0:T(8,128)}, u32[]{:S(2)}, u32[]{:S(2)}) collective-permute-start(f32[4,512,128]{2,1,0:T(8,128)} %refs_0_.1), channel_id=1, source_target_pairs={{0,32},{4,228},{32,0},{36,68},{64,96},{68,36},{96,64},{100,132},{1... | collective-permute-start | bytes 3145736 | tf_op jit(solution)/shard_map/ppermute | solution.py:253
  2.6 3.5 %collective-permute-start = (f32[4,512,128]{2,1,0:T(8,128)}, f32[4,512,128]{2,1,0:T(8,128)}, u32[]{:S(2)}, u32[]{:S(2)}) collective-permute-start(f32[4,512,128]{2,1,0:T(8,128)} %refs_0_.1), channel_id=1, source_target_pairs={{0,4},{4,0},{1,5},{5,1},{2,6},{6,2},{3,7},{7,3},{8,12},{12,8},{9,1... | collective-permute-start | bytes 3145736 | tf_op jit(solution)/shard_map/ppermute | solution.py:21
  6.1 9.7 %collective-permute-done.1.refs_2_ = f32[4,512,128]{2,1,0:T(8,128)} collective-permute-done((f32[4,512,128]{2,1,0:T(8,128)}, f32[4,512,128]{2,1,0:T(8,128)}, u32[]{:S(2)}, u32[]{:S(2)}) %collective-permute-start.1) | collective-permute-done | bytes 1048608 | tf_op jit(solution)/shard_map/ppermute | solution.py:253
  15.8 2.8 %collective-permute-start.2 = (f32[4,512,128]{2,1,0:T(8,128)}, f32[4,512,128]{2,1,0:T(8,128)}, u32[]{:S(2)}, u32[]{:S(2)}) collective-permute-start(f32[4,512,128]{2,1,0:T(8,128)} %collective-permute-done.1.refs_2_), channel_id=1, source_target_pairs={{0,4},{4,0},{1,5},{5,1},{2,6},{6,2},{3,7},{7,3},{8,12},{12,8},{9,1... | collective-permute-start | bytes 3145736 | tf_op jit(solution)/shard_map/ppermute | solution.py:21
  18.6 1.8 %shard_map.68 = s32[4,4,16,128]{3,2,1,0:T(8,128)} custom-call(s32[4,64]{1,0:T(4,128)} %bitcast.16, s32[8,4,8,64]{3,2,1,0:T(8,128)} %bitcast.14, s32[8,4,8,64]{3,2,1,0:T(8,128)} %bitcast.15), custom_call_target="tpu_custom_call" | custom-call | flops 1048576 | bytes 1048576 | tf_op jit(solution)/shard_map/pallas_call | solution.py:26
  20.4 8.2 %all-to-all-start = ((s32[16,16,128]{2,1,0:T(8,128)}), s32[16,16,128]{2,1,0:T(8,128)S(1)}, u32[]{:S(2)}, u32[]{:S(2)}) async-start(s32[16,16,128]{2,1,0:T(8,128)} %bitcast.13), calls=%async_computation | async-start | bytes 262144 | tf_op jit(solution)/shard_map/all_to_all | solution.py:271
  28.7 0.0 copy-start
  28.7 1.2 %copy-done = f32[4,512,128]{2,1,0:T(8,128)S(1)} copy-done((f32[4,512,128]{2,1,0:T(8,128)S(1)}, f32[4,512,128]{2,1,0:T(8,128)}, u32[]{:S(2)}) %copy-start) | copy-done | bytes 1048600
  29.9 1.7 %shard_map.69.refs_1_ = bf16[8,512,256]{2,1,0:T(8,128)(2,1)S(1)} custom-call(f32[4,512,128]{2,1,0:T(8,128)S(1)} %copy-done, f32[4,512,128]{2,1,0:T(8,128)} %collective-permute-done.refs_1_), custom_call_target="tpu_custom_call" | custom-call | flops 1048576 | bytes 1048576 | tf_op jit(solution)/shard_map/pallas_call | solution.py:26
  31.6 8.2 %all-to-all-done = s32[16,16,128]{2,1,0:T(8,128)S(1)} async-done(((s32[16,16,128]{2,1,0:T(8,128)}), s32[16,16,128]{2,1,0:T(8,128)S(1)}, u32[]{:S(2)}, u32[]{:S(2)}) %all-to-all-start) | async-done | bytes 131104 | tf_op jit(solution)/shard_map/all_to_all | solution.py:271
  39.7 5.3 %shard_map.70 = (f32[4,128,128]{2,1,0:T(8,128)S(1)}, bf16[8,512,256]{2,1,0:T(8,128)(2,1)S(1)}) custom-call(s32[4,4,16,128]{3,2,1,0:T(8,128)S(1)} %bitcast.9, bf16[8,512,256]{2,1,0:T(8,128)(2,1)S(1)} %shard_map.69.refs_1_, f32[4,512,128]{2,1,0:T(8,128)} %collective-permute-done.1.refs_2_, f32[4,512,128]{2,1,0:T(8,128)} %collective-permute-done.2.refs_3_), custom_call_target="tpu_custom_call" | custom-call | flops 1342177280 | bytes 1048576 | tf_op jit(solution)/shard_map/pallas_call | solution.py:26
  45.1 0.3 collective-permute-start.4
  45.4 2.0 %shard_map.72 = f32[4,128,128]{2,1,0:T(8,128)S(1)} custom-call(s32[4,4,16,128]{3,2,1,0:T(8,128)S(1)} %bitcast.10, bf16[8,512,256]{2,1,0:T(8,128)(2,1)S(1)} %shard_map.69.refs_1_, bf16[8,512,256]{2,1,0:T(8,128)(2,1)S(1)} %get-tuple-element.10.refs_2_), custom_call_target="tpu_custom_call" | custom-call | flops 1342177280 | bytes 1048576 | tf_op jit(solution)/shard_map/pallas_call | solution.py:26
  47.4 3.1 %collective-permute-start.3 = (f32[4,128,128]{2,1,0:T(8,128)S(1)}, f32[4,128,128]{2,1,0:T(8,128)S(1)}, u32[]{:S(2)}, u32[]{:S(2)}) collective-permute-start(f32[4,128,128]{2,1,0:T(8,128)S(1)} %shard_map.72), channel_id=1, source_target_pairs={{0,24},{4,12},{8,0},{12,20},{16,8},{20,28},{24,16},{28,4},{1,25},{... | collective-permute-start | bytes 786440 | tf_op jit(solution)/shard_map/ppermute | solution.py:208
  50.5 2.0 %shard_map.73.one_ref = f32[4,128,128]{2,1,0:T(8,128)S(1)} custom-call(s32[4,4,16,128]{3,2,1,0:T(8,128)S(1)} %bitcast.11, bf16[8,512,256]{2,1,0:T(8,128)(2,1)S(1)} %shard_map.69.refs_1_, bf16[8,512,256]{2,1,0:T(8,128)(2,1)S(1)} %get-tuple-element.10.refs_2_), custom_call_target="tpu_custom_call" | custom-call | flops 1342177280 | bytes 1048576 | tf_op jit(solution)/shard_map/pallas_call | solution.py:26
  52.5 2.3 %collective-permute-done.4.two_ref = f32[4,128,128]{2,1,0:T(8,128)S(1)} collective-permute-done((f32[4,128,128]{2,1,0:T(8,128)S(1)}, f32[4,128,128]{2,1,0:T(8,128)S(1)}, u32[]{:S(2)}, u32[]{:S(2)}) %collective-permute-start.4) | collective-permute-done | bytes 262176 | tf_op jit(solution)/shard_map/ppermute | solution.py:208
  54.9 0.0 copy-start.1
  54.9 0.3 collective-permute-start.5
  55.2 2.0 %shard_map.71.refs_0_ = f32[4,128,128]{2,1,0:T(8,128)S(1)} custom-call(s32[4,4,16,128]{3,2,1,0:T(8,128)S(1)} %bitcast.12, bf16[8,512,256]{2,1,0:T(8,128)(2,1)S(1)} %shard_map.69.refs_1_, bf16[8,512,256]{2,1,0:T(8,128)(2,1)S(1)} %get-tuple-element.10.refs_2_), custom_call_target="tpu_custom_call" | custom-call | flops 1342177280 | bytes 1048576 | tf_op jit(solution)/shard_map/pallas_call | solution.py:26
  57.2 5.5 %collective-permute-done.5.refs_2_ = f32[4,128,128]{2,1,0:T(8,128)S(1)} collective-permute-done((f32[4,128,128]{2,1,0:T(8,128)S(1)}, f32[4,128,128]{2,1,0:T(8,128)S(1)}, u32[]{:S(2)}, u32[]{:S(2)}) %collective-permute-start.5) | collective-permute-done | bytes 262176 | tf_op jit(solution)/shard_map/ppermute | solution.py:208
  62.8 1.3 %collective-permute-start.6 = (f32[128,128]{1,0:T(8,128)S(1)}, f32[128,128]{1,0:T(8,128)S(1)}, u32[]{:S(2)}, u32[]{:S(2)}) collective-permute-start(f32[128,128]{1,0:T(8,128)S(1)} %get-tuple-element.13), channel_id=1, source_target_pairs={{0,128},{32,160},{64,192},{96,224},{128,0},{160,32},{192,64},{224,... | collective-permute-start | bytes 196616 | tf_op jit(solution)/shard_map/ppermute | solution.py:286
  64.1 2.0 %collective-permute-start.7 = (f32[128,128]{1,0:T(8,128)S(1)}, f32[128,128]{1,0:T(8,128)S(1)}, u32[]{:S(2)}, u32[]{:S(2)}) collective-permute-start(f32[128,128]{1,0:T(8,128)S(1)} %get-tuple-element.14), channel_id=1, source_target_pairs={{0,64},{32,96},{64,128},{96,160},{128,192},{160,224},{192,0},{224,... | collective-permute-start | bytes 196616 | tf_op jit(solution)/shard_map/ppermute | solution.py:286
  66.1 2.2 %collective-permute-start.8 = (f32[128,128]{1,0:T(8,128)S(1)}, f32[128,128]{1,0:T(8,128)S(1)}, u32[]{:S(2)}, u32[]{:S(2)}) collective-permute-start(f32[128,128]{1,0:T(8,128)S(1)} %get-tuple-element.15), channel_id=1, source_target_pairs={{0,192},{32,224},{64,0},{96,32},{128,64},{160,96},{192,128},{224,1... | collective-permute-start | bytes 196616 | tf_op jit(solution)/shard_map/ppermute | solution.py:286
  68.3 3.4 %collective-permute-done.6.one_ref = f32[128,128]{1,0:T(8,128)S(1)} collective-permute-done((f32[128,128]{1,0:T(8,128)S(1)}, f32[128,128]{1,0:T(8,128)S(1)}, u32[]{:S(2)}, u32[]{:S(2)}) %collective-permute-start.6) | collective-permute-done | bytes 65568 | tf_op jit(solution)/shard_map/ppermute | solution.py:286
  71.6 1.4 %collective-permute-done.8.three_ref = f32[128,128]{1,0:T(8,128)S(1)} collective-permute-done((f32[128,128]{1,0:T(8,128)S(1)}, f32[128,128]{1,0:T(8,128)S(1)}, u32[]{:S(2)}, u32[]{:S(2)}) %collective-permute-start.8) | collective-permute-done | bytes 65568 | tf_op jit(solution)/shard_map/ppermute | solution.py:286
  73.0 0.7 shard_map.76
  73.7 0.7 collective-permute-start.11
  74.4 2.5 %collective-permute-start.10 = (f32[10,32]{1,0:T(8,128)S(1)}, f32[10,32]{1,0:T(8,128)S(1)}, u32[]{:S(2)}, u32[]{:S(2)}) collective-permute-start(f32[10,32]{1,0:T(8,128)S(1)} %get-tuple-element.17), channel_id=1, source_target_pairs={{0,1},{1,2},{2,3},{3,0},{4,5},{5,6},{6,7},{7,4},{8,9},{9,10},{10,1... | collective-permute-start | bytes 3848 | tf_op jit(solution)/shard_map/ppermute | solution.py:21
  76.9 0.0 collective-permute-start.9
  77.0 1.6 %collective-permute-done.11 = f32[10,32]{1,0:T(8,128)S(1)} collective-permute-done((f32[10,32]{1,0:T(8,128)S(1)}, f32[10,32]{1,0:T(8,128)S(1)}, u32[]{:S(2)}, u32[]{:S(2)}) %collective-permute-start.11) | collective-permute-done | bytes 1312 | tf_op jit(solution)/shard_map/ppermute | solution.py:21
  78.6 3.5 %collective-permute-done.9 = f32[10,32]{1,0:T(8,128)S(1)} collective-permute-done((f32[10,32]{1,0:T(8,128)S(1)}, f32[10,32]{1,0:T(8,128)S(1)}, u32[]{:S(2)}, u32[]{:S(2)}) %collective-permute-start.9) | collective-permute-done | bytes 1312 | tf_op jit(solution)/shard_map/ppermute | solution.py:21
  82.1 0.6 multiply_bitcast_fusion
  (8 shorter events, 0.1 us)
Async XLA Ops:
  0.6 15.2 %collective-permute-start.1 = (f32[4,512,128]{2,1,0:T(8,128)}, f32[4,512,128]{2,1,0:T(8,128)}, u32[]{:S(2)}, u32[]{:S(2)}) collective-permute-start(f32[4,512,128]{2,1,0:T(8,128)} %refs_0_.1), channel_id=1, source_target_pairs={{0,32},{4,228},{32,0},{36,68},{64,96},{68,36},{96,64},{100,132},{1... | collective-permute-start | bytes 3145736 | tf_op jit(solution)/shard_map/ppermute | solution.py:253
  2.6 26.0 %collective-permute-start = (f32[4,512,128]{2,1,0:T(8,128)}, f32[4,512,128]{2,1,0:T(8,128)}, u32[]{:S(2)}, u32[]{:S(2)}) collective-permute-start(f32[4,512,128]{2,1,0:T(8,128)} %refs_0_.1), channel_id=1, source_target_pairs={{0,4},{4,0},{1,5},{5,1},{2,6},{6,2},{3,7},{7,3},{8,12},{12,8},{9,1... | collective-permute-start | bytes 3145736 | tf_op jit(solution)/shard_map/ppermute | solution.py:21
  15.8 23.9 %collective-permute-start.2 = (f32[4,512,128]{2,1,0:T(8,128)}, f32[4,512,128]{2,1,0:T(8,128)}, u32[]{:S(2)}, u32[]{:S(2)}) collective-permute-start(f32[4,512,128]{2,1,0:T(8,128)} %collective-permute-done.1.refs_2_), channel_id=1, source_target_pairs={{0,4},{4,0},{1,5},{5,1},{2,6},{6,2},{3,7},{7,3},{8,12},{12,8},{9,1... | collective-permute-start | bytes 3145736 | tf_op jit(solution)/shard_map/ppermute | solution.py:21
  20.4 19.3 %all-to-all-start = ((s32[16,16,128]{2,1,0:T(8,128)}), s32[16,16,128]{2,1,0:T(8,128)S(1)}, u32[]{:S(2)}, u32[]{:S(2)}) async-start(s32[16,16,128]{2,1,0:T(8,128)} %bitcast.13), calls=%async_computation | async-start | bytes 262144 | tf_op jit(solution)/shard_map/all_to_all | solution.py:271
  28.7 1.2 %copy-start = (f32[4,512,128]{2,1,0:T(8,128)S(1)}, f32[4,512,128]{2,1,0:T(8,128)}, u32[]{:S(2)}) copy-start(f32[4,512,128]{2,1,0:T(8,128)} %refs_0_.1) | copy-start | bytes 3145732
  45.1 9.8 %collective-permute-start.4 = (f32[4,128,128]{2,1,0:T(8,128)S(1)}, f32[4,128,128]{2,1,0:T(8,128)S(1)}, u32[]{:S(2)}, u32[]{:S(2)}) collective-permute-start(f32[4,128,128]{2,1,0:T(8,128)S(1)} %get-tuple-element.11), channel_id=1, source_target_pairs={{0,8},{4,28},{8,16},{12,4},{16,24},{20,12},{24,0},{28,20},{1,9},{5... | collective-permute-start | bytes 786440 | tf_op jit(solution)/shard_map/ppermute | solution.py:208
  47.4 9.8 %collective-permute-start.3 = (f32[4,128,128]{2,1,0:T(8,128)S(1)}, f32[4,128,128]{2,1,0:T(8,128)S(1)}, u32[]{:S(2)}, u32[]{:S(2)}) collective-permute-start(f32[4,128,128]{2,1,0:T(8,128)S(1)} %shard_map.72), channel_id=1, source_target_pairs={{0,24},{4,12},{8,0},{12,20},{16,8},{20,28},{24,16},{28,4},{1,25},{... | collective-permute-start | bytes 786440 | tf_op jit(solution)/shard_map/ppermute | solution.py:208
  54.9 18.1 %copy-start.1 = (f32[32,128]{1,0:T(8,128)S(1)}, f32[32,128]{1,0:T(8,128)}, u32[]{:S(2)}) copy-start(f32[32,128]{1,0:T(8,128)} %dense_ref.1) | copy-start | bytes 49156
  54.9 7.8 %collective-permute-start.5 = (f32[4,128,128]{2,1,0:T(8,128)S(1)}, f32[4,128,128]{2,1,0:T(8,128)S(1)}, u32[]{:S(2)}, u32[]{:S(2)}) collective-permute-start(f32[4,128,128]{2,1,0:T(8,128)S(1)} %shard_map.74), channel_id=1, source_target_pairs={{0,8},{4,28},{8,16},{12,4},{16,24},{20,12},{24,0},{28,20},{1,9},{5... | collective-permute-start | bytes 786440 | tf_op jit(solution)/shard_map/ppermute | solution.py:208
  62.8 8.8 %collective-permute-start.6 = (f32[128,128]{1,0:T(8,128)S(1)}, f32[128,128]{1,0:T(8,128)S(1)}, u32[]{:S(2)}, u32[]{:S(2)}) collective-permute-start(f32[128,128]{1,0:T(8,128)S(1)} %get-tuple-element.13), channel_id=1, source_target_pairs={{0,128},{32,160},{64,192},{96,224},{128,0},{160,32},{192,64},{224,... | collective-permute-start | bytes 196616 | tf_op jit(solution)/shard_map/ppermute | solution.py:286
  64.1 7.5 %collective-permute-start.7 = (f32[128,128]{1,0:T(8,128)S(1)}, f32[128,128]{1,0:T(8,128)S(1)}, u32[]{:S(2)}, u32[]{:S(2)}) collective-permute-start(f32[128,128]{1,0:T(8,128)S(1)} %get-tuple-element.14), channel_id=1, source_target_pairs={{0,64},{32,96},{64,128},{96,160},{128,192},{160,224},{192,0},{224,... | collective-permute-start | bytes 196616 | tf_op jit(solution)/shard_map/ppermute | solution.py:286
  66.1 6.9 %collective-permute-start.8 = (f32[128,128]{1,0:T(8,128)S(1)}, f32[128,128]{1,0:T(8,128)S(1)}, u32[]{:S(2)}, u32[]{:S(2)}) collective-permute-start(f32[128,128]{1,0:T(8,128)S(1)} %get-tuple-element.15), channel_id=1, source_target_pairs={{0,192},{32,224},{64,0},{96,32},{128,64},{160,96},{192,128},{224,1... | collective-permute-start | bytes 196616 | tf_op jit(solution)/shard_map/ppermute | solution.py:286
  73.7 4.9 %collective-permute-start.11 = (f32[10,32]{1,0:T(8,128)S(1)}, f32[10,32]{1,0:T(8,128)S(1)}, u32[]{:S(2)}, u32[]{:S(2)}) collective-permute-start(f32[10,32]{1,0:T(8,128)S(1)} %get-tuple-element.17), channel_id=1, source_target_pairs={{0,3},{1,0},{2,1},{3,2},{4,7},{5,4},{6,5},{7,6},{8,11},{9,8},{10,9... | collective-permute-start | bytes 3848 | tf_op jit(solution)/shard_map/ppermute | solution.py:21
  74.4 4.1 %collective-permute-start.10 = (f32[10,32]{1,0:T(8,128)S(1)}, f32[10,32]{1,0:T(8,128)S(1)}, u32[]{:S(2)}, u32[]{:S(2)}) collective-permute-start(f32[10,32]{1,0:T(8,128)S(1)} %get-tuple-element.17), channel_id=1, source_target_pairs={{0,1},{1,2},{2,3},{3,0},{4,5},{5,6},{6,7},{7,4},{8,9},{9,10},{10,1... | collective-permute-start | bytes 3848 | tf_op jit(solution)/shard_map/ppermute | solution.py:21
  76.9 5.2 %collective-permute-start.9 = (f32[10,32]{1,0:T(8,128)S(1)}, f32[10,32]{1,0:T(8,128)S(1)}, u32[]{:S(2)}, u32[]{:S(2)}) collective-permute-start(f32[10,32]{1,0:T(8,128)S(1)} %get-tuple-element.17), channel_id=1, source_target_pairs={{0,2},{1,3},{2,0},{3,1},{4,6},{5,7},{6,4},{7,5},{8,10},{9,11},{10,... | collective-permute-start | bytes 3848 | tf_op jit(solution)/shard_map/ppermute | solution.py:21

commit v7 on v5

--- a/solution.py
+++ b/solution.py
@@ -116,10 +116,14 @@
 def bags_kernel(*refs, away, examples, count, raw):
     ids_ref, near_ref, part_ref, shared_ref, out_ref, *refs = refs
     if raw:
-        full_hbm = shared_ref
-        shared_ref, looked_ref, full_ref, sem = refs
-        copy = pltpu.make_async_copy(full_hbm, full_ref, sem)
-        copy.start()
+        shared_hbm = shared_ref
+        shared_ref, looked_ref, full_ref, sems = refs
+        copies = [
+            pltpu.make_async_copy(shared_hbm.at[t], full_ref.at[t], sems.at[t])
+            for t in range(count)
+        ]
+        for copy in copies:
+            copy.start()
     else:
         (looked_ref,) = refs
     group, ring, messages, lanes = ids_ref.shape
@@ -138,6 +142,9 @@
 
     def look(o, t):
         ref, place = ((near_ref, t), (near_ref, count + t), (part_ref, t), (shared_ref, t))[o]
+        if raw and o == owners - 1:
+            copies[t].wait()
+            split_into(ref, t, full_ref[t])
         message = o * count + t
         picks = jnp.concatenate(
             [
@@ -162,14 +169,10 @@
         )
 
     early = owners - 1 if raw else 0
+    for o in range(early):
+        for t in range(count):
+            look(o, t)
     for t in range(count):
-        for o in range(early):
-            look(o, t)
-    if raw:
-        copy.wait()
-    for t in range(count):
-        if raw:
-            split_into(shared_ref, t, full_ref[t])
         for o in range(early, owners):
             look(o, t)
         pool(t)
@@ -183,7 +186,7 @@
     scratch = [pltpu.VMEM((count, messages // count * group * lanes // 2, wide), jnp.bfloat16)]
     if raw:
         out = (out, jax.ShapeDtypeStruct(part.shape, part.dtype))
-        scratch += [pltpu.VMEM(shared.shape, jnp.float32), pltpu.SemaphoreType.DMA]
+        scratch += [pltpu.VMEM(shared.shape, jnp.float32), pltpu.SemaphoreType.DMA((count,))]
     return local_kernel(
         functools.partial(bags_kernel, away=away, examples=examples, count=count, raw=raw),
         out,
@@ -292,8 +295,9 @@
         (here, over, up, down, dense_features),
     )
     opposite = shifted(products, "y", 2)
-    beside = shifted(products, "y", 1) + shifted(products, "y", -1)
-    total = ((products + opposite) + beside) * embedding**-0.5
+    after = shifted(products, "y", 1)
+    before = shifted(products, "y", -1)
+    total = ((products + opposite) + (after + before)) * embedding**-0.5
     return pooled, total.T
 
 

time: 81 us -> 81.7 us (level)
  no operation moved by 1% of the time
where the time goes in v7:
time: 81.7 us; the launch traced here: 81.3 us
  waiting for transfers between devices  35.3 us (43%)
  starting transfers between devices  28.9 us (35%)
  Pallas kernels  15.7 us (19%)
    pallas_call x10, Pallas kernels, local_kernel(): pl.pallas_call(kernel, in_specs=[HBM if k in in_hbm else VMEM for k in ra...  15.7 us
    ppermute x1, waiting for transfers between devices, body(): part = lax.ppermute(tables, Z + ('c',), pairs)  9.7 us
    ppermute x5, starting transfers between devices, shifted(): lax.ppermute(value, axis, [(i, (i + by) % size) for i in range(size)])  9.55 us
    all_to_all x1, starting transfers between devices, body(): ids = lax.all_to_all(ids, ('zq', 'x'), 0, 0, tiled=True)  8.24 us
    ppermute x3, waiting for transfers between devices, by_core(): return lax.ppermute(value, ('x', 'c'), pairs)  7.88 us
    all_to_all x1, waiting for transfers between devices, body(): ids = lax.all_to_all(ids, ('zq', 'x'), 0, 0, tiled=True)  7.83 us
    ppermute x3, starting transfers between devices, body(): lax.ppermute(piece, Z, [(i, (i + parities * by) % depth) for i in range(d...  5.47 us
    ppermute x5, waiting for transfers between devices, shifted(): lax.ppermute(value, axis, [(i, (i + by) % size) for i in range(size)])  5.14 us
  transfers between devices with their start and end apart: 13, of which 8 were waited for; matrix products, arithmetic and copies ran while one was open for 0% of the time, Pallas kernels for 14%

profile of v7, /device:TPU:24, one launch (start us, length us, event | category | flops | bytes accessed | tf_op | source)
XLA Modules:
  0.0 81.3 jit_solution(7194518865429107142)
XLA Ops:
  0.6 2.0 %collective-permute-start.1 = (f32[4,512,128]{2,1,0:T(8,128)}, f32[4,512,128]{2,1,0:T(8,128)}, u32[]{:S(2)}, u32[]{:S(2)}) collective-permute-start(f32[4,512,128]{2,1,0:T(8,128)} %refs_0_.1), channel_id=1, source_target_pairs={{0,32},{4,228},{32,0},{36,68},{64,96},{68,36},{96,64},{100,132},{1... | collective-permute-start | bytes 3145736 | tf_op jit(solution)/shard_map/ppermute | solution.py:250
  2.6 3.5 %collective-permute-start = (f32[4,512,128]{2,1,0:T(8,128)}, f32[4,512,128]{2,1,0:T(8,128)}, u32[]{:S(2)}, u32[]{:S(2)}) collective-permute-start(f32[4,512,128]{2,1,0:T(8,128)} %refs_0_.1), channel_id=1, source_target_pairs={{0,4},{4,0},{1,5},{5,1},{2,6},{6,2},{3,7},{7,3},{8,12},{12,8},{9,1... | collective-permute-start | bytes 3145736 | tf_op jit(solution)/shard_map/ppermute | solution.py:21
  6.1 9.7 %collective-permute-done.1.refs_0_ = f32[4,512,128]{2,1,0:T(8,128)} collective-permute-done((f32[4,512,128]{2,1,0:T(8,128)}, f32[4,512,128]{2,1,0:T(8,128)}, u32[]{:S(2)}, u32[]{:S(2)}) %collective-permute-start.1) | collective-permute-done | bytes 1048608 | tf_op jit(solution)/shard_map/ppermute | solution.py:250
  15.8 2.8 %collective-permute-start.2 = (f32[4,512,128]{2,1,0:T(8,128)}, f32[4,512,128]{2,1,0:T(8,128)}, u32[]{:S(2)}, u32[]{:S(2)}) collective-permute-start(f32[4,512,128]{2,1,0:T(8,128)} %collective-permute-done.1.refs_0_), channel_id=1, source_target_pairs={{0,4},{4,0},{1,5},{5,1},{2,6},{6,2},{3,7},{7,3},{8,12},{12,8},{9,1... | collective-permute-start | bytes 3145736 | tf_op jit(solution)/shard_map/ppermute | solution.py:21
  18.6 1.8 %shard_map.68 = s32[4,4,16,128]{3,2,1,0:T(8,128)} custom-call(s32[4,64]{1,0:T(4,128)} %bitcast.16, s32[8,4,8,64]{3,2,1,0:T(8,128)} %bitcast.14, s32[8,4,8,64]{3,2,1,0:T(8,128)} %bitcast.15), custom_call_target="tpu_custom_call" | custom-call | flops 1048576 | bytes 1048576 | tf_op jit(solution)/shard_map/pallas_call | solution.py:26
  20.4 8.2 %all-to-all-start = ((s32[16,16,128]{2,1,0:T(8,128)}), s32[16,16,128]{2,1,0:T(8,128)S(1)}, u32[]{:S(2)}, u32[]{:S(2)}) async-start(s32[16,16,128]{2,1,0:T(8,128)} %bitcast.13), calls=%async_computation | async-start | bytes 262144 | tf_op jit(solution)/shard_map/all_to_all | solution.py:268
  28.7 0.0 copy-start
  28.7 1.5 %shard_map.70.refs_2_ = bf16[4,512,256]{2,1,0:T(8,128)(2,1)S(1)} custom-call(f32[4,512,128]{2,1,0:T(8,128)} %collective-permute-done.1.refs_0_), custom_call_target="tpu_custom_call" | custom-call | flops 1048576 | bytes 1048576 | tf_op jit(solution)/shard_map/pallas_call | solution.py:26
  30.2 1.7 %shard_map.69.refs_1_ = bf16[8,512,256]{2,1,0:T(8,128)(2,1)S(1)} custom-call(f32[4,512,128]{2,1,0:T(8,128)S(1)} %copy-done, f32[4,512,128]{2,1,0:T(8,128)} %collective-permute-done.refs_1_), custom_call_target="tpu_custom_call" | custom-call | flops 1048576 | bytes 1048576 | tf_op jit(solution)/shard_map/pallas_call | solution.py:26
  31.9 7.8 %all-to-all-done = s32[16,16,128]{2,1,0:T(8,128)S(1)} async-done(((s32[16,16,128]{2,1,0:T(8,128)}), s32[16,16,128]{2,1,0:T(8,128)S(1)}, u32[]{:S(2)}, u32[]{:S(2)}) %all-to-all-start) | async-done | bytes 131104 | tf_op jit(solution)/shard_map/all_to_all | solution.py:268
  39.7 3.9 %shard_map.71 = (f32[4,128,128]{2,1,0:T(8,128)S(1)}, bf16[4,512,256]{2,1,0:T(8,128)(2,1)S(1)}) custom-call(s32[4,4,16,128]{3,2,1,0:T(8,128)S(1)} %bitcast.9, bf16[8,512,256]{2,1,0:T(8,128)(2,1)S(1)} %shard_map.69.refs_1_, bf16[4,512,256]{2,1,0:T(8,128)(2,1)S(1)} %shard_map.70.refs_2_, f32[4,512,128]{2,1,0:T(8,128)} %collective-permute-done.2.refs_3_), custom_call_target="tpu_custom_call" | custom-call | flops 1342177280 | bytes 1048576 | tf_op jit(solution)/shard_map/pallas_call | solution.py:26
  43.6 0.3 collective-permute-start.4
  43.9 2.0 %shard_map.73 = f32[4,128,128]{2,1,0:T(8,128)S(1)} custom-call(s32[4,4,16,128]{3,2,1,0:T(8,128)S(1)} %bitcast.10, bf16[8,512,256]{2,1,0:T(8,128)(2,1)S(1)} %shard_map.69.refs_1_, bf16[4,512,256]{2,1,0:T(8,128)(2,1)S(1)} %shard_map.70.refs_2_, bf16[4,512,256]{2,1,0:T(8,128)(2,1)S(1)} %get-tuple-element.10.refs_3_), custom_call_target="tpu_custom_call" | custom-call | flops 1342177280 | bytes 1048576 | tf_op jit(solution)/shard_map/pallas_call | solution.py:26
  46.0 3.1 %collective-permute-start.3 = (f32[4,128,128]{2,1,0:T(8,128)S(1)}, f32[4,128,128]{2,1,0:T(8,128)S(1)}, u32[]{:S(2)}, u32[]{:S(2)}) collective-permute-start(f32[4,128,128]{2,1,0:T(8,128)S(1)} %shard_map.73), channel_id=1, source_target_pairs={{0,24},{4,12},{8,0},{12,20},{16,8},{20,28},{24,16},{28,4},{1,25},{... | collective-permute-start | bytes 786440 | tf_op jit(solution)/shard_map/ppermute | solution.py:205
  49.0 2.0 %shard_map.74.one_ref = f32[4,128,128]{2,1,0:T(8,128)S(1)} custom-call(s32[4,4,16,128]{3,2,1,0:T(8,128)S(1)} %bitcast.11, bf16[8,512,256]{2,1,0:T(8,128)(2,1)S(1)} %shard_map.69.refs_1_, bf16[4,512,256]{2,1,0:T(8,128)(2,1)S(1)} %shard_map.70.refs_2_, bf16[4,512,256]{2,1,0:T(8,128)(2,1)S(1)} %get-tuple-element.10.refs_3_), custom_call_target="tpu_custom_call" | custom-call | flops 1342177280 | bytes 1048576 | tf_op jit(solution)/shard_map/pallas_call | solution.py:26
  51.1 2.3 %collective-permute-done.4.two_ref = f32[4,128,128]{2,1,0:T(8,128)S(1)} collective-permute-done((f32[4,128,128]{2,1,0:T(8,128)S(1)}, f32[4,128,128]{2,1,0:T(8,128)S(1)}, u32[]{:S(2)}, u32[]{:S(2)}) %collective-permute-start.4) | collective-permute-done | bytes 262176 | tf_op jit(solution)/shard_map/ppermute | solution.py:205
  53.5 0.0 copy-start.1
  53.5 0.3 collective-permute-start.5
  53.7 2.0 %shard_map.72.refs_0_ = f32[4,128,128]{2,1,0:T(8,128)S(1)} custom-call(s32[4,4,16,128]{3,2,1,0:T(8,128)S(1)} %bitcast.12, bf16[8,512,256]{2,1,0:T(8,128)(2,1)S(1)} %shard_map.69.refs_1_, bf16[4,512,256]{2,1,0:T(8,128)(2,1)S(1)} %shard_map.70.refs_2_, bf16[4,512,256]{2,1,0:T(8,128)(2,1)S(1)} %get-tuple-element.10.refs_3_), custom_call_target="tpu_custom_call" | custom-call | flops 1342177280 | bytes 1048576 | tf_op jit(solution)/shard_map/pallas_call | solution.py:26
  55.8 5.5 %collective-permute-done.5.refs_2_ = f32[4,128,128]{2,1,0:T(8,128)S(1)} collective-permute-done((f32[4,128,128]{2,1,0:T(8,128)S(1)}, f32[4,128,128]{2,1,0:T(8,128)S(1)}, u32[]{:S(2)}, u32[]{:S(2)}) %collective-permute-start.5) | collective-permute-done | bytes 262176 | tf_op jit(solution)/shard_map/ppermute | solution.py:205
  61.4 1.3 %collective-permute-start.6 = (f32[128,128]{1,0:T(8,128)S(1)}, f32[128,128]{1,0:T(8,128)S(1)}, u32[]{:S(2)}, u32[]{:S(2)}) collective-permute-start(f32[128,128]{1,0:T(8,128)S(1)} %get-tuple-element.13), channel_id=1, source_target_pairs={{0,128},{32,160},{64,192},{96,224},{128,0},{160,32},{192,64},{224,... | collective-permute-start | bytes 196616 | tf_op jit(solution)/shard_map/ppermute | solution.py:285
  62.7 2.0 %collective-permute-start.7 = (f32[128,128]{1,0:T(8,128)S(1)}, f32[128,128]{1,0:T(8,128)S(1)}, u32[]{:S(2)}, u32[]{:S(2)}) collective-permute-start(f32[128,128]{1,0:T(8,128)S(1)} %get-tuple-element.14), channel_id=1, source_target_pairs={{0,64},{32,96},{64,128},{96,160},{128,192},{160,224},{192,0},{224,... | collective-permute-start | bytes 196616 | tf_op jit(solution)/shard_map/ppermute | solution.py:285
  64.7 2.2 %collective-permute-start.8 = (f32[128,128]{1,0:T(8,128)S(1)}, f32[128,128]{1,0:T(8,128)S(1)}, u32[]{:S(2)}, u32[]{:S(2)}) collective-permute-start(f32[128,128]{1,0:T(8,128)S(1)} %get-tuple-element.15), channel_id=1, source_target_pairs={{0,192},{32,224},{64,0},{96,32},{128,64},{160,96},{192,128},{224,1... | collective-permute-start | bytes 196616 | tf_op jit(solution)/shard_map/ppermute | solution.py:285
  66.8 3.4 %collective-permute-done.6.one_ref = f32[128,128]{1,0:T(8,128)S(1)} collective-permute-done((f32[128,128]{1,0:T(8,128)S(1)}, f32[128,128]{1,0:T(8,128)S(1)}, u32[]{:S(2)}, u32[]{:S(2)}) %collective-permute-start.6) | collective-permute-done | bytes 65568 | tf_op jit(solution)/shard_map/ppermute | solution.py:285
  70.2 1.4 %collective-permute-done.8.three_ref = f32[128,128]{1,0:T(8,128)S(1)} collective-permute-done((f32[128,128]{1,0:T(8,128)S(1)}, f32[128,128]{1,0:T(8,128)S(1)}, u32[]{:S(2)}, u32[]{:S(2)}) %collective-permute-start.8) | collective-permute-done | bytes 65568 | tf_op jit(solution)/shard_map/ppermute | solution.py:285
  71.6 0.7 shard_map.77
  72.3 0.7 collective-permute-start.11
  73.0 2.5 %collective-permute-start.10 = (f32[10,32]{1,0:T(8,128)S(1)}, f32[10,32]{1,0:T(8,128)S(1)}, u32[]{:S(2)}, u32[]{:S(2)}) collective-permute-start(f32[10,32]{1,0:T(8,128)S(1)} %get-tuple-element.17), channel_id=1, source_target_pairs={{0,1},{1,2},{2,3},{3,0},{4,5},{5,6},{6,7},{7,4},{8,9},{9,10},{10,1... | collective-permute-start | bytes 3848 | tf_op jit(solution)/shard_map/ppermute | solution.py:21
  75.5 0.0 collective-permute-start.9
  75.5 1.6 %collective-permute-done.11 = f32[10,32]{1,0:T(8,128)S(1)} collective-permute-done((f32[10,32]{1,0:T(8,128)S(1)}, f32[10,32]{1,0:T(8,128)S(1)}, u32[]{:S(2)}, u32[]{:S(2)}) %collective-permute-start.11) | collective-permute-done | bytes 1312 | tf_op jit(solution)/shard_map/ppermute | solution.py:21
  77.1 3.5 %collective-permute-done.9 = f32[10,32]{1,0:T(8,128)S(1)} collective-permute-done((f32[10,32]{1,0:T(8,128)S(1)}, f32[10,32]{1,0:T(8,128)S(1)}, u32[]{:S(2)}, u32[]{:S(2)}) %collective-permute-start.9) | collective-permute-done | bytes 1312 | tf_op jit(solution)/shard_map/ppermute | solution.py:21
  80.7 0.6 multiply_bitcast_fusion
  (9 shorter events, 0.1 us)
Async XLA Ops:
  0.6 15.2 %collective-permute-start.1 = (f32[4,512,128]{2,1,0:T(8,128)}, f32[4,512,128]{2,1,0:T(8,128)}, u32[]{:S(2)}, u32[]{:S(2)}) collective-permute-start(f32[4,512,128]{2,1,0:T(8,128)} %refs_0_.1), channel_id=1, source_target_pairs={{0,32},{4,228},{32,0},{36,68},{64,96},{68,36},{96,64},{100,132},{1... | collective-permute-start | bytes 3145736 | tf_op jit(solution)/shard_map/ppermute | solution.py:250
  2.6 27.6 %collective-permute-start = (f32[4,512,128]{2,1,0:T(8,128)}, f32[4,512,128]{2,1,0:T(8,128)}, u32[]{:S(2)}, u32[]{:S(2)}) collective-permute-start(f32[4,512,128]{2,1,0:T(8,128)} %refs_0_.1), channel_id=1, source_target_pairs={{0,4},{4,0},{1,5},{5,1},{2,6},{6,2},{3,7},{7,3},{8,12},{12,8},{9,1... | collective-permute-start | bytes 3145736 | tf_op jit(solution)/shard_map/ppermute | solution.py:21
  15.8 23.9 %collective-permute-start.2 = (f32[4,512,128]{2,1,0:T(8,128)}, f32[4,512,128]{2,1,0:T(8,128)}, u32[]{:S(2)}, u32[]{:S(2)}) collective-permute-start(f32[4,512,128]{2,1,0:T(8,128)} %collective-permute-done.1.refs_0_), channel_id=1, source_target_pairs={{0,4},{4,0},{1,5},{5,1},{2,6},{6,2},{3,7},{7,3},{8,12},{12,8},{9,1... | collective-permute-start | bytes 3145736 | tf_op jit(solution)/shard_map/ppermute | solution.py:21
  20.4 19.3 %all-to-all-start = ((s32[16,16,128]{2,1,0:T(8,128)}), s32[16,16,128]{2,1,0:T(8,128)S(1)}, u32[]{:S(2)}, u32[]{:S(2)}) async-start(s32[16,16,128]{2,1,0:T(8,128)} %bitcast.13), calls=%async_computation | async-start | bytes 262144 | tf_op jit(solution)/shard_map/all_to_all | solution.py:268
  28.7 1.6 %copy-start = (f32[4,512,128]{2,1,0:T(8,128)S(1)}, f32[4,512,128]{2,1,0:T(8,128)}, u32[]{:S(2)}) copy-start(f32[4,512,128]{2,1,0:T(8,128)} %refs_0_.1) | copy-start | bytes 3145732
  43.6 9.8 %collective-permute-start.4 = (f32[4,128,128]{2,1,0:T(8,128)S(1)}, f32[4,128,128]{2,1,0:T(8,128)S(1)}, u32[]{:S(2)}, u32[]{:S(2)}) collective-permute-start(f32[4,128,128]{2,1,0:T(8,128)S(1)} %get-tuple-element.11), channel_id=1, source_target_pairs={{0,8},{4,28},{8,16},{12,4},{16,24},{20,12},{24,0},{28,20},{1,9},{5... | collective-permute-start | bytes 786440 | tf_op jit(solution)/shard_map/ppermute | solution.py:205
  46.0 9.8 %collective-permute-start.3 = (f32[4,128,128]{2,1,0:T(8,128)S(1)}, f32[4,128,128]{2,1,0:T(8,128)S(1)}, u32[]{:S(2)}, u32[]{:S(2)}) collective-permute-start(f32[4,128,128]{2,1,0:T(8,128)S(1)} %shard_map.73), channel_id=1, source_target_pairs={{0,24},{4,12},{8,0},{12,20},{16,8},{20,28},{24,16},{28,4},{1,25},{... | collective-permute-start | bytes 786440 | tf_op jit(solution)/shard_map/ppermute | solution.py:205
  53.5 18.1 %copy-start.1 = (f32[32,128]{1,0:T(8,128)S(1)}, f32[32,128]{1,0:T(8,128)}, u32[]{:S(2)}) copy-start(f32[32,128]{1,0:T(8,128)} %dense_ref.1) | copy-start | bytes 49156
  53.5 7.8 %collective-permute-start.5 = (f32[4,128,128]{2,1,0:T(8,128)S(1)}, f32[4,128,128]{2,1,0:T(8,128)S(1)}, u32[]{:S(2)}, u32[]{:S(2)}) collective-permute-start(f32[4,128,128]{2,1,0:T(8,128)S(1)} %shard_map.75), channel_id=1, source_target_pairs={{0,8},{4,28},{8,16},{12,4},{16,24},{20,12},{24,0},{28,20},{1,9},{5... | collective-permute-start | bytes 786440 | tf_op jit(solution)/shard_map/ppermute | solution.py:205
  61.4 8.8 %collective-permute-start.6 = (f32[128,128]{1,0:T(8,128)S(1)}, f32[128,128]{1,0:T(8,128)S(1)}, u32[]{:S(2)}, u32[]{:S(2)}) collective-permute-start(f32[128,128]{1,0:T(8,128)S(1)} %get-tuple-element.13), channel_id=1, source_target_pairs={{0,128},{32,160},{64,192},{96,224},{128,0},{160,32},{192,64},{224,... | collective-permute-start | bytes 196616 | tf_op jit(solution)/shard_map/ppermute | solution.py:285
  62.7 7.5 %collective-permute-start.7 = (f32[128,128]{1,0:T(8,128)S(1)}, f32[128,128]{1,0:T(8,128)S(1)}, u32[]{:S(2)}, u32[]{:S(2)}) collective-permute-start(f32[128,128]{1,0:T(8,128)S(1)} %get-tuple-element.14), channel_id=1, source_target_pairs={{0,64},{32,96},{64,128},{96,160},{128,192},{160,224},{192,0},{224,... | collective-permute-start | bytes 196616 | tf_op jit(solution)/shard_map/ppermute | solution.py:285
  64.7 6.9 %collective-permute-start.8 = (f32[128,128]{1,0:T(8,128)S(1)}, f32[128,128]{1,0:T(8,128)S(1)}, u32[]{:S(2)}, u32[]{:S(2)}) collective-permute-start(f32[128,128]{1,0:T(8,128)S(1)} %get-tuple-element.15), channel_id=1, source_target_pairs={{0,192},{32,224},{64,0},{96,32},{128,64},{160,96},{192,128},{224,1... | collective-permute-start | bytes 196616 | tf_op jit(solution)/shard_map/ppermute | solution.py:285
  72.3 4.9 %collective-permute-start.11 = (f32[10,32]{1,0:T(8,128)S(1)}, f32[10,32]{1,0:T(8,128)S(1)}, u32[]{:S(2)}, u32[]{:S(2)}) collective-permute-start(f32[10,32]{1,0:T(8,128)S(1)} %get-tuple-element.17), channel_id=1, source_target_pairs={{0,3},{1,0},{2,1},{3,2},{4,7},{5,4},{6,5},{7,6},{8,11},{9,8},{10,9... | collective-permute-start | bytes 3848 | tf_op jit(solution)/shard_map/ppermute | solution.py:21
  73.0 4.1 %collective-permute-start.10 = (f32[10,32]{1,0:T(8,128)S(1)}, f32[10,32]{1,0:T(8,128)S(1)}, u32[]{:S(2)}, u32[]{:S(2)}) collective-permute-start(f32[10,32]{1,0:T(8,128)S(1)} %get-tuple-element.17), channel_id=1, source_target_pairs={{0,1},{1,2},{2,3},{3,0},{4,5},{5,6},{6,7},{7,4},{8,9},{9,10},{10,1... | collective-permute-start | bytes 3848 | tf_op jit(solution)/shard_map/ppermute | solution.py:21
  75.5 5.2 %collective-permute-start.9 = (f32[10,32]{1,0:T(8,128)S(1)}, f32[10,32]{1,0:T(8,128)S(1)}, u32[]{:S(2)}, u32[]{:S(2)}) collective-permute-start(f32[10,32]{1,0:T(8,128)S(1)} %get-tuple-element.17), channel_id=1, source_target_pairs={{0,2},{1,3},{2,0},{3,1},{4,6},{5,7},{6,4},{7,5},{8,10},{9,11},{10,... | collective-permute-start | bytes 3848 | tf_op jit(solution)/shard_map/ppermute | solution.py:21

commit v8 on v5

--- a/solution.py
+++ b/solution.py
@@ -116,9 +116,9 @@
 def bags_kernel(*refs, away, examples, count, raw):
     ids_ref, near_ref, part_ref, shared_ref, out_ref, *refs = refs
     if raw:
-        full_hbm = shared_ref
+        shared_hbm = shared_ref
         shared_ref, looked_ref, full_ref, sem = refs
-        copy = pltpu.make_async_copy(full_hbm, full_ref, sem)
+        copy = pltpu.make_async_copy(shared_hbm, full_ref, sem)
         copy.start()
     else:
         (looked_ref,) = refs
@@ -212,15 +212,14 @@
         out_ref[...] = ins[0][j] + ins[1][j] + ins[2][j]
 
 
-def close_kernel(own_ref, one_ref, two_ref, three_ref, dense_ref, pooled_ref, pairs_ref):
+def pairs_kernel(own_ref, one_ref, two_ref, three_ref, dense_ref, pairs_ref, summed_ref):
     examples = dense_ref.shape[0]
     pooled = own_ref[...] + one_ref[...] + two_ref[...] + three_ref[...]
+    summed_ref[...] = pooled
     tables = pooled.shape[0] // examples
     vectors = [dense_ref[...]]
     for t in range(tables):
-        one = pooled[t * examples : (t + 1) * examples]
-        pooled_ref[:, t, :] = one
-        vectors.append(one)
+        vectors.append(pooled[t * examples : (t + 1) * examples])
     lane = lax.broadcasted_iota(jnp.int32, dense_ref.shape, 1)
     pairs = jnp.zeros(dense_ref.shape, jnp.float32)
     place = 0
@@ -230,6 +229,12 @@
             pairs = jnp.where(lane == place, product, pairs)
             place += 1
     pairs_ref[...] = jnp.swapaxes(pairs, 0, 1)[: pairs_ref.shape[0]]
+
+
+def pooled_kernel(summed_ref, pooled_ref):
+    examples, tables = pooled_ref.shape[:2]
+    for t in range(tables):
+        pooled_ref[:, t, :] = summed_ref[t * examples : (t + 1) * examples]
 
 
 def body(embedding, tables, dense_features, slot_rows, slot_examples, slot_counts):
@@ -283,17 +288,23 @@
         for piece, by in ((over, 2), (up, 1), (down, 3))
     )
     pairs = count * (count + 1) // 2
-    pooled, products = local_kernel(
-        close_kernel,
+    products, summed = local_kernel(
+        pairs_kernel,
         (
-            jax.ShapeDtypeStruct((examples, count, width), jnp.float32),
             jax.ShapeDtypeStruct((pairs, examples), jnp.float32),
+            jax.ShapeDtypeStruct((count * examples, width), jnp.float32),
         ),
         (here, over, up, down, dense_features),
     )
+    pooled = local_kernel(
+        pooled_kernel,
+        jax.ShapeDtypeStruct((examples, count, width), jnp.float32),
+        (summed,),
+    )
     opposite = shifted(products, "y", 2)
-    beside = shifted(products, "y", 1) + shifted(products, "y", -1)
-    total = ((products + opposite) + beside) * embedding**-0.5
+    after = shifted(products, "y", 1)
+    before = shifted(products, "y", -1)
+    total = ((products + opposite) + (after + before)) * embedding**-0.5
     return pooled, total.T
 
 

time: 81 us -> 80.6 us (level)
    pallas_call x10 -> x11, Pallas kernels: 15 us -> 15.2 us  [local_kernel(): pl.pallas_call(kernel, in_specs=[HBM if k in in_hbm else VMEM for k in ra...]
  transfers between devices with their start and end apart: 13 -> 13, of which waited for: 8 -> 8; matrix products, arithmetic and copies ran while one was open for 0% -> 0% of each run, Pallas kernels for 14% -> 15%
where the time goes in v8:
time: 80.6 us; the launch traced here: 80.1 us
  waiting for transfers between devices  34.6 us (43%)
  starting transfers between devices  28.9 us (36%)
  Pallas kernels  15.2 us (19%)
    pallas_call x11, Pallas kernels, local_kernel(): pl.pallas_call(kernel, in_specs=[HBM if k in in_hbm else VMEM for k in ra...  15.2 us
    ppermute x1, waiting for transfers between devices, body(): part = lax.ppermute(tables, Z + ('c',), pairs)  9.7 us
    ppermute x5, starting transfers between devices, shifted(): lax.ppermute(value, axis, [(i, (i + by) % size) for i in range(size)])  9.58 us
    all_to_all x1, starting transfers between devices, body(): ids = lax.all_to_all(ids, ('zq', 'x'), 0, 0, tiled=True)  8.24 us
    ppermute x3, waiting for transfers between devices, by_core(): return lax.ppermute(value, ('x', 'c'), pairs)  7.87 us
    all_to_all x1, waiting for transfers between devices, body(): ids = lax.all_to_all(ids, ('zq', 'x'), 0, 0, tiled=True)  7.83 us
    ppermute x3, starting transfers between devices, body(): lax.ppermute(piece, Z, [(i, (i + parities * by) % depth) for i in range(d...  5.47 us
    ppermute x3, waiting for transfers between devices, body(): lax.ppermute(piece, Z, [(i, (i + parities * by) % depth) for i in range(d...  4.76 us
  transfers between devices with their start and end apart: 13, of which 8 were waited for; matrix products, arithmetic and copies ran while one was open for 0% of the time, Pallas kernels for 15%

profile of v8, /device:TPU:24, one launch (start us, length us, event | category | flops | bytes accessed | tf_op | source)
XLA Modules:
  0.0 80.1 jit_solution(9291083236808755944)
XLA Ops:
  0.6 2.0 %collective-permute-start.1 = (f32[4,512,128]{2,1,0:T(8,128)}, f32[4,512,128]{2,1,0:T(8,128)}, u32[]{:S(2)}, u32[]{:S(2)}) collective-permute-start(f32[4,512,128]{2,1,0:T(8,128)} %refs_0_.1), channel_id=1, source_target_pairs={{0,32},{4,228},{32,0},{36,68},{64,96},{68,36},{96,64},{100,132},{1... | collective-permute-start | bytes 3145736 | tf_op jit(solution)/shard_map/ppermute | solution.py:252
  2.6 3.5 %collective-permute-start = (f32[4,512,128]{2,1,0:T(8,128)}, f32[4,512,128]{2,1,0:T(8,128)}, u32[]{:S(2)}, u32[]{:S(2)}) collective-permute-start(f32[4,512,128]{2,1,0:T(8,128)} %refs_0_.1), channel_id=1, source_target_pairs={{0,4},{4,0},{1,5},{5,1},{2,6},{6,2},{3,7},{7,3},{8,12},{12,8},{9,1... | collective-permute-start | bytes 3145736 | tf_op jit(solution)/shard_map/ppermute | solution.py:21
  6.1 9.7 %collective-permute-done.1.refs_0_ = f32[4,512,128]{2,1,0:T(8,128)} collective-permute-done((f32[4,512,128]{2,1,0:T(8,128)}, f32[4,512,128]{2,1,0:T(8,128)}, u32[]{:S(2)}, u32[]{:S(2)}) %collective-permute-start.1) | collective-permute-done | bytes 1048608 | tf_op jit(solution)/shard_map/ppermute | solution.py:252
  15.8 2.8 %collective-permute-start.2 = (f32[4,512,128]{2,1,0:T(8,128)}, f32[4,512,128]{2,1,0:T(8,128)}, u32[]{:S(2)}, u32[]{:S(2)}) collective-permute-start(f32[4,512,128]{2,1,0:T(8,128)} %collective-permute-done.1.refs_0_), channel_id=1, source_target_pairs={{0,4},{4,0},{1,5},{5,1},{2,6},{6,2},{3,7},{7,3},{8,12},{12,8},{9,1... | collective-permute-start | bytes 3145736 | tf_op jit(solution)/shard_map/ppermute | solution.py:21
  18.6 1.8 %shard_map.68 = s32[4,4,16,128]{3,2,1,0:T(8,128)} custom-call(s32[4,64]{1,0:T(4,128)} %bitcast.16, s32[8,4,8,64]{3,2,1,0:T(8,128)} %bitcast.14, s32[8,4,8,64]{3,2,1,0:T(8,128)} %bitcast.15), custom_call_target="tpu_custom_call" | custom-call | flops 1048576 | bytes 1048576 | tf_op jit(solution)/shard_map/pallas_call | solution.py:26
  20.4 8.2 %all-to-all-start = ((s32[16,16,128]{2,1,0:T(8,128)}), s32[16,16,128]{2,1,0:T(8,128)S(1)}, u32[]{:S(2)}, u32[]{:S(2)}) async-start(s32[16,16,128]{2,1,0:T(8,128)} %bitcast.13), calls=%async_computation | async-start | bytes 262144 | tf_op jit(solution)/shard_map/all_to_all | solution.py:270
  28.7 0.0 copy-start
  28.7 1.5 %shard_map.70.refs_2_ = bf16[4,512,256]{2,1,0:T(8,128)(2,1)S(1)} custom-call(f32[4,512,128]{2,1,0:T(8,128)} %collective-permute-done.1.refs_0_), custom_call_target="tpu_custom_call" | custom-call | flops 1048576 | bytes 1048576 | tf_op jit(solution)/shard_map/pallas_call | solution.py:26
  30.2 1.7 %shard_map.69.refs_1_ = bf16[8,512,256]{2,1,0:T(8,128)(2,1)S(1)} custom-call(f32[4,512,128]{2,1,0:T(8,128)S(1)} %copy-done, f32[4,512,128]{2,1,0:T(8,128)} %collective-permute-done.refs_1_), custom_call_target="tpu_custom_call" | custom-call | flops 1048576 | bytes 1048576 | tf_op jit(solution)/shard_map/pallas_call | solution.py:26
  31.9 7.8 %all-to-all-done = s32[16,16,128]{2,1,0:T(8,128)S(1)} async-done(((s32[16,16,128]{2,1,0:T(8,128)}), s32[16,16,128]{2,1,0:T(8,128)S(1)}, u32[]{:S(2)}, u32[]{:S(2)}) %all-to-all-start) | async-done | bytes 131104 | tf_op jit(solution)/shard_map/all_to_all | solution.py:270
  39.7 3.2 %shard_map.71 = (f32[4,128,128]{2,1,0:T(8,128)S(1)}, bf16[4,512,256]{2,1,0:T(8,128)(2,1)S(1)}) custom-call(s32[4,4,16,128]{3,2,1,0:T(8,128)S(1)} %bitcast.9, bf16[8,512,256]{2,1,0:T(8,128)(2,1)S(1)} %shard_map.69.refs_1_, bf16[4,512,256]{2,1,0:T(8,128)(2,1)S(1)} %shard_map.70.refs_2_, f32[4,512,128]{2,1,0:T(8,128)} %collective-permute-done.2.refs_3_), custom_call_target="tpu_custom_call" | custom-call | flops 1342177280 | bytes 1048576 | tf_op jit(solution)/shard_map/pallas_call | solution.py:26
  42.9 0.3 collective-permute-start.4
  43.3 2.0 %shard_map.73 = f32[4,128,128]{2,1,0:T(8,128)S(1)} custom-call(s32[4,4,16,128]{3,2,1,0:T(8,128)S(1)} %bitcast.10, bf16[8,512,256]{2,1,0:T(8,128)(2,1)S(1)} %shard_map.69.refs_1_, bf16[4,512,256]{2,1,0:T(8,128)(2,1)S(1)} %shard_map.70.refs_2_, bf16[4,512,256]{2,1,0:T(8,128)(2,1)S(1)} %get-tuple-element.10.refs_3_), custom_call_target="tpu_custom_call" | custom-call | flops 1342177280 | bytes 1048576 | tf_op jit(solution)/shard_map/pallas_call | solution.py:26
  45.3 3.1 %collective-permute-start.3 = (f32[4,128,128]{2,1,0:T(8,128)S(1)}, f32[4,128,128]{2,1,0:T(8,128)S(1)}, u32[]{:S(2)}, u32[]{:S(2)}) collective-permute-start(f32[4,128,128]{2,1,0:T(8,128)S(1)} %shard_map.73), channel_id=1, source_target_pairs={{0,24},{4,12},{8,0},{12,20},{16,8},{20,28},{24,16},{28,4},{1,25},{... | collective-permute-start | bytes 786440 | tf_op jit(solution)/shard_map/ppermute | solution.py:202
  48.4 2.0 %shard_map.74.one_ref = f32[4,128,128]{2,1,0:T(8,128)S(1)} custom-call(s32[4,4,16,128]{3,2,1,0:T(8,128)S(1)} %bitcast.11, bf16[8,512,256]{2,1,0:T(8,128)(2,1)S(1)} %shard_map.69.refs_1_, bf16[4,512,256]{2,1,0:T(8,128)(2,1)S(1)} %shard_map.70.refs_2_, bf16[4,512,256]{2,1,0:T(8,128)(2,1)S(1)} %get-tuple-element.10.refs_3_), custom_call_target="tpu_custom_call" | custom-call | flops 1342177280 | bytes 1048576 | tf_op jit(solution)/shard_map/pallas_call | solution.py:26
  50.4 2.3 %collective-permute-done.4.two_ref = f32[4,128,128]{2,1,0:T(8,128)S(1)} collective-permute-done((f32[4,128,128]{2,1,0:T(8,128)S(1)}, f32[4,128,128]{2,1,0:T(8,128)S(1)}, u32[]{:S(2)}, u32[]{:S(2)}) %collective-permute-start.4) | collective-permute-done | bytes 262176 | tf_op jit(solution)/shard_map/ppermute | solution.py:202
  52.8 0.3 collective-permute-start.5
  53.1 2.0 %shard_map.72.refs_0_ = f32[4,128,128]{2,1,0:T(8,128)S(1)} custom-call(s32[4,4,16,128]{3,2,1,0:T(8,128)S(1)} %bitcast.12, bf16[8,512,256]{2,1,0:T(8,128)(2,1)S(1)} %shard_map.69.refs_1_, bf16[4,512,256]{2,1,0:T(8,128)(2,1)S(1)} %shard_map.70.refs_2_, bf16[4,512,256]{2,1,0:T(8,128)(2,1)S(1)} %get-tuple-element.10.refs_3_), custom_call_target="tpu_custom_call" | custom-call | flops 1342177280 | bytes 1048576 | tf_op jit(solution)/shard_map/pallas_call | solution.py:26
  55.1 5.5 %collective-permute-done.5.refs_2_ = f32[4,128,128]{2,1,0:T(8,128)S(1)} collective-permute-done((f32[4,128,128]{2,1,0:T(8,128)S(1)}, f32[4,128,128]{2,1,0:T(8,128)S(1)}, u32[]{:S(2)}, u32[]{:S(2)}) %collective-permute-start.5) | collective-permute-done | bytes 262176 | tf_op jit(solution)/shard_map/ppermute | solution.py:202
  60.7 1.3 %collective-permute-start.6 = (f32[128,128]{1,0:T(8,128)S(1)}, f32[128,128]{1,0:T(8,128)S(1)}, u32[]{:S(2)}, u32[]{:S(2)}) collective-permute-start(f32[128,128]{1,0:T(8,128)S(1)} %get-tuple-element.13), channel_id=1, source_target_pairs={{0,128},{32,160},{64,192},{96,224},{128,0},{160,32},{192,64},{224,... | collective-permute-start | bytes 196616 | tf_op jit(solution)/shard_map/ppermute | solution.py:287
  62.0 2.0 %collective-permute-start.7 = (f32[128,128]{1,0:T(8,128)S(1)}, f32[128,128]{1,0:T(8,128)S(1)}, u32[]{:S(2)}, u32[]{:S(2)}) collective-permute-start(f32[128,128]{1,0:T(8,128)S(1)} %get-tuple-element.14), channel_id=1, source_target_pairs={{0,64},{32,96},{64,128},{96,160},{128,192},{160,224},{192,0},{224,... | collective-permute-start | bytes 196616 | tf_op jit(solution)/shard_map/ppermute | solution.py:287
  64.0 2.2 %collective-permute-start.8 = (f32[128,128]{1,0:T(8,128)S(1)}, f32[128,128]{1,0:T(8,128)S(1)}, u32[]{:S(2)}, u32[]{:S(2)}) collective-permute-start(f32[128,128]{1,0:T(8,128)S(1)} %get-tuple-element.15), channel_id=1, source_target_pairs={{0,192},{32,224},{64,0},{96,32},{128,64},{160,96},{192,128},{224,1... | collective-permute-start | bytes 196616 | tf_op jit(solution)/shard_map/ppermute | solution.py:287
  66.1 3.4 %collective-permute-done.6.one_ref = f32[128,128]{1,0:T(8,128)S(1)} collective-permute-done((f32[128,128]{1,0:T(8,128)S(1)}, f32[128,128]{1,0:T(8,128)S(1)}, u32[]{:S(2)}, u32[]{:S(2)}) %collective-permute-start.6) | collective-permute-done | bytes 65568 | tf_op jit(solution)/shard_map/ppermute | solution.py:287
  69.5 1.4 %collective-permute-done.8.three_ref = f32[128,128]{1,0:T(8,128)S(1)} collective-permute-done((f32[128,128]{1,0:T(8,128)S(1)}, f32[128,128]{1,0:T(8,128)S(1)}, u32[]{:S(2)}, u32[]{:S(2)}) %collective-permute-start.8) | collective-permute-done | bytes 65568 | tf_op jit(solution)/shard_map/ppermute | solution.py:287
  70.9 0.2 shard_map.77
  71.1 0.8 collective-permute-start.11
  71.9 2.5 %collective-permute-start.10 = (f32[10,32]{1,0:T(8,128)S(1)}, f32[10,32]{1,0:T(8,128)S(1)}, u32[]{:S(2)}, u32[]{:S(2)}) collective-permute-start(f32[10,32]{1,0:T(8,128)S(1)} %get-tuple-element.17), channel_id=1, source_target_pairs={{0,1},{1,2},{2,3},{3,0},{4,5},{5,6},{6,7},{7,4},{8,9},{9,10},{10,1... | collective-permute-start | bytes 3848 | tf_op jit(solution)/shard_map/ppermute | solution.py:21
  74.3 0.0 collective-permute-start.9
  74.4 0.7 shard_map.78
  75.0 0.9 %collective-permute-done.11 = f32[10,32]{1,0:T(8,128)S(1)} collective-permute-done((f32[10,32]{1,0:T(8,128)S(1)}, f32[10,32]{1,0:T(8,128)S(1)}, u32[]{:S(2)}, u32[]{:S(2)}) %collective-permute-start.11) | collective-permute-done | bytes 1312 | tf_op jit(solution)/shard_map/ppermute | solution.py:21
  76.0 3.5 %collective-permute-done.9 = f32[10,32]{1,0:T(8,128)S(1)} collective-permute-done((f32[10,32]{1,0:T(8,128)S(1)}, f32[10,32]{1,0:T(8,128)S(1)}, u32[]{:S(2)}, u32[]{:S(2)}) %collective-permute-start.9) | collective-permute-done | bytes 1312 | tf_op jit(solution)/shard_map/ppermute | solution.py:21
  79.5 0.6 multiply_bitcast_fusion
  (10 shorter events, 0.1 us)
Async XLA Ops:
  0.6 15.2 %collective-permute-start.1 = (f32[4,512,128]{2,1,0:T(8,128)}, f32[4,512,128]{2,1,0:T(8,128)}, u32[]{:S(2)}, u32[]{:S(2)}) collective-permute-start(f32[4,512,128]{2,1,0:T(8,128)} %refs_0_.1), channel_id=1, source_target_pairs={{0,32},{4,228},{32,0},{36,68},{64,96},{68,36},{96,64},{100,132},{1... | collective-permute-start | bytes 3145736 | tf_op jit(solution)/shard_map/ppermute | solution.py:252
  2.6 27.6 %collective-permute-start = (f32[4,512,128]{2,1,0:T(8,128)}, f32[4,512,128]{2,1,0:T(8,128)}, u32[]{:S(2)}, u32[]{:S(2)}) collective-permute-start(f32[4,512,128]{2,1,0:T(8,128)} %refs_0_.1), channel_id=1, source_target_pairs={{0,4},{4,0},{1,5},{5,1},{2,6},{6,2},{3,7},{7,3},{8,12},{12,8},{9,1... | collective-permute-start | bytes 3145736 | tf_op jit(solution)/shard_map/ppermute | solution.py:21
  15.8 23.9 %collective-permute-start.2 = (f32[4,512,128]{2,1,0:T(8,128)}, f32[4,512,128]{2,1,0:T(8,128)}, u32[]{:S(2)}, u32[]{:S(2)}) collective-permute-start(f32[4,512,128]{2,1,0:T(8,128)} %collective-permute-done.1.refs_0_), channel_id=1, source_target_pairs={{0,4},{4,0},{1,5},{5,1},{2,6},{6,2},{3,7},{7,3},{8,12},{12,8},{9,1... | collective-permute-start | bytes 3145736 | tf_op jit(solution)/shard_map/ppermute | solution.py:21
  20.4 19.3 %all-to-all-start = ((s32[16,16,128]{2,1,0:T(8,128)}), s32[16,16,128]{2,1,0:T(8,128)S(1)}, u32[]{:S(2)}, u32[]{:S(2)}) async-start(s32[16,16,128]{2,1,0:T(8,128)} %bitcast.13), calls=%async_computation | async-start | bytes 262144 | tf_op jit(solution)/shard_map/all_to_all | solution.py:270
  28.7 1.6 %copy-start = (f32[4,512,128]{2,1,0:T(8,128)S(1)}, f32[4,512,128]{2,1,0:T(8,128)}, u32[]{:S(2)}) copy-start(f32[4,512,128]{2,1,0:T(8,128)} %refs_0_.1) | copy-start | bytes 3145732
  42.9 9.8 %collective-permute-start.4 = (f32[4,128,128]{2,1,0:T(8,128)S(1)}, f32[4,128,128]{2,1,0:T(8,128)S(1)}, u32[]{:S(2)}, u32[]{:S(2)}) collective-permute-start(f32[4,128,128]{2,1,0:T(8,128)S(1)} %get-tuple-element.11), channel_id=1, source_target_pairs={{0,8},{4,28},{8,16},{12,4},{16,24},{20,12},{24,0},{28,20},{1,9},{5... | collective-permute-start | bytes 786440 | tf_op jit(solution)/shard_map/ppermute | solution.py:202
  45.3 9.8 %collective-permute-start.3 = (f32[4,128,128]{2,1,0:T(8,128)S(1)}, f32[4,128,128]{2,1,0:T(8,128)S(1)}, u32[]{:S(2)}, u32[]{:S(2)}) collective-permute-start(f32[4,128,128]{2,1,0:T(8,128)S(1)} %shard_map.73), channel_id=1, source_target_pairs={{0,24},{4,12},{8,0},{12,20},{16,8},{20,28},{24,16},{28,4},{1,25},{... | collective-permute-start | bytes 786440 | tf_op jit(solution)/shard_map/ppermute | solution.py:202
  52.8 18.1 %copy-start.1 = (f32[32,128]{1,0:T(8,128)S(1)}, f32[32,128]{1,0:T(8,128)}, u32[]{:S(2)}) copy-start(f32[32,128]{1,0:T(8,128)} %dense_ref.1) | copy-start | bytes 49156
  52.8 7.8 %collective-permute-start.5 = (f32[4,128,128]{2,1,0:T(8,128)S(1)}, f32[4,128,128]{2,1,0:T(8,128)S(1)}, u32[]{:S(2)}, u32[]{:S(2)}) collective-permute-start(f32[4,128,128]{2,1,0:T(8,128)S(1)} %shard_map.75), channel_id=1, source_target_pairs={{0,8},{4,28},{8,16},{12,4},{16,24},{20,12},{24,0},{28,20},{1,9},{5... | collective-permute-start | bytes 786440 | tf_op jit(solution)/shard_map/ppermute | solution.py:202
  60.7 8.8 %collective-permute-start.6 = (f32[128,128]{1,0:T(8,128)S(1)}, f32[128,128]{1,0:T(8,128)S(1)}, u32[]{:S(2)}, u32[]{:S(2)}) collective-permute-start(f32[128,128]{1,0:T(8,128)S(1)} %get-tuple-element.13), channel_id=1, source_target_pairs={{0,128},{32,160},{64,192},{96,224},{128,0},{160,32},{192,64},{224,... | collective-permute-start | bytes 196616 | tf_op jit(solution)/shard_map/ppermute | solution.py:287
  62.0 7.5 %collective-permute-start.7 = (f32[128,128]{1,0:T(8,128)S(1)}, f32[128,128]{1,0:T(8,128)S(1)}, u32[]{:S(2)}, u32[]{:S(2)}) collective-permute-start(f32[128,128]{1,0:T(8,128)S(1)} %get-tuple-element.14), channel_id=1, source_target_pairs={{0,64},{32,96},{64,128},{96,160},{128,192},{160,224},{192,0},{224,... | collective-permute-start | bytes 196616 | tf_op jit(solution)/shard_map/ppermute | solution.py:287
  64.0 6.9 %collective-permute-start.8 = (f32[128,128]{1,0:T(8,128)S(1)}, f32[128,128]{1,0:T(8,128)S(1)}, u32[]{:S(2)}, u32[]{:S(2)}) collective-permute-start(f32[128,128]{1,0:T(8,128)S(1)} %get-tuple-element.15), channel_id=1, source_target_pairs={{0,192},{32,224},{64,0},{96,32},{128,64},{160,96},{192,128},{224,1... | collective-permute-start | bytes 196616 | tf_op jit(solution)/shard_map/ppermute | solution.py:287
  71.1 4.9 %collective-permute-start.11 = (f32[10,32]{1,0:T(8,128)S(1)}, f32[10,32]{1,0:T(8,128)S(1)}, u32[]{:S(2)}, u32[]{:S(2)}) collective-permute-start(f32[10,32]{1,0:T(8,128)S(1)} %get-tuple-element.17), channel_id=1, source_target_pairs={{0,3},{1,0},{2,1},{3,2},{4,7},{5,4},{6,5},{7,6},{8,11},{9,8},{10,9... | collective-permute-start | bytes 3848 | tf_op jit(solution)/shard_map/ppermute | solution.py:21
  71.9 4.1 %collective-permute-start.10 = (f32[10,32]{1,0:T(8,128)S(1)}, f32[10,32]{1,0:T(8,128)S(1)}, u32[]{:S(2)}, u32[]{:S(2)}) collective-permute-start(f32[10,32]{1,0:T(8,128)S(1)} %get-tuple-element.17), channel_id=1, source_target_pairs={{0,1},{1,2},{2,3},{3,0},{4,5},{5,6},{6,7},{7,4},{8,9},{9,10},{10,1... | collective-permute-start | bytes 3848 | tf_op jit(solution)/shard_map/ppermute | solution.py:21
  74.3 5.2 %collective-permute-start.9 = (f32[10,32]{1,0:T(8,128)S(1)}, f32[10,32]{1,0:T(8,128)S(1)}, u32[]{:S(2)}, u32[]{:S(2)}) collective-permute-start(f32[10,32]{1,0:T(8,128)S(1)} %get-tuple-element.17), channel_id=1, source_target_pairs={{0,2},{1,3},{2,0},{3,1},{4,6},{5,7},{6,4},{7,5},{8,10},{9,11},{10,... | collective-permute-start | bytes 3848 | tf_op jit(solution)/shard_map/ppermute | solution.py:21

commit v9 on v8

--- a/solution.py
+++ b/solution.py
@@ -113,13 +113,23 @@
     return jnp.where(mask, 1.0, 0.0).astype(jnp.bfloat16)
 
 
-def bags_kernel(*refs, away, examples, count, raw):
-    ids_ref, near_ref, part_ref, shared_ref, out_ref, *refs = refs
+def bags_kernel(*refs, away, examples, count, parts, raw):
+    ids_ref, near_ref, part_ref, shared_ref, *refs = refs
+    out_refs, refs = refs[: len(parts)], refs[len(parts) :]
     if raw:
         shared_hbm = shared_ref
-        shared_ref, looked_ref, full_ref, sem = refs
-        copy = pltpu.make_async_copy(shared_hbm, full_ref, sem)
-        copy.start()
+        shared_ref, looked_ref, full_ref, sems = refs
+        half = count // 2
+        copies = [
+            pltpu.make_async_copy(
+                shared_hbm.at[k * half : (k + 1) * half],
+                full_ref.at[k * half : (k + 1) * half],
+                sems.at[k],
+            )
+            for k in range(2)
+        ]
+        for copy in copies:
+            copy.start()
     else:
         (looked_ref,) = refs
     group, ring, messages, lanes = ids_ref.shape
@@ -151,41 +161,53 @@
         looked = jnp.dot(picks, ref[place], preferred_element_type=jnp.float32)
         looked_ref[t, o * group * slots : (o + 1) * group * slots, :] = looked.astype(jnp.bfloat16)
 
-    def pool(t):
+    def pool(t, out_ref, place):
         into = [one_hot(keys[o * count + t : o * count + t + 1] == key_iota) for o in range(owners)]
         total = jnp.dot(
             jnp.concatenate(into, axis=1), looked_ref[t], preferred_element_type=jnp.float32
         )
         summed = total[:, : wide // 2] + total[:, wide // 2 :]
-        out_ref[:, t * examples : (t + 1) * examples, :] = summed.reshape(
+        out_ref[:, place * examples : (place + 1) * examples, :] = summed.reshape(
             group, examples, wide // 2
         )
 
     early = owners - 1 if raw else 0
-    for t in range(count):
-        for o in range(early):
-            look(o, t)
+    for tables in parts:
+        for t in tables:
+            for o in range(early):
+                look(o, t)
+    for k, (tables, out_ref) in enumerate(zip(parts, out_refs)):
+        if raw:
+            copies[k].wait()
+        for place, t in enumerate(tables):
+            if raw:
+                split_into(shared_ref, t, full_ref[t])
+            for o in range(early, owners):
+                look(o, t)
+            pool(t, out_ref, place)
     if raw:
-        copy.wait()
-    for t in range(count):
-        if raw:
+        copies[1].wait()
+        for t in range(half, count):
             split_into(shared_ref, t, full_ref[t])
-        for o in range(early, owners):
-            look(o, t)
-        pool(t)
-
-
-def bags(ids, near, part, shared, away, examples, raw=False):
+
+
+def bags(ids, near, part, shared, away, examples, parts, raw=False):
     group, _, messages, lanes = ids.shape
     count, rows, wide = part.shape
-    work = messages * group * lanes // 2
-    out = jax.ShapeDtypeStruct((group, count * examples, wide // 2), jnp.float32)
+    tasks = sum(len(tables) for tables in parts)
+    work = messages // count * tasks * group * lanes // 2
+    out = tuple(
+        jax.ShapeDtypeStruct((group, len(tables) * examples, wide // 2), jnp.float32)
+        for tables in parts
+    )
     scratch = [pltpu.VMEM((count, messages // count * group * lanes // 2, wide), jnp.bfloat16)]
     if raw:
-        out = (out, jax.ShapeDtypeStruct(part.shape, part.dtype))
-        scratch += [pltpu.VMEM(shared.shape, jnp.float32), pltpu.SemaphoreType.DMA]
+        out += (jax.ShapeDtypeStruct(part.shape, part.dtype),)
+        scratch += [pltpu.VMEM(shared.shape, jnp.float32), pltpu.SemaphoreType.DMA((2,))]
     return local_kernel(
-        functools.partial(bags_kernel, away=away, examples=examples, count=count, raw=raw),
+        functools.partial(
+            bags_kernel, away=away, examples=examples, count=count, parts=parts, raw=raw
+        ),
         out,
         (ids, near, part, shared),
         flops=2 * work * wide * (rows + group * examples),
@@ -206,10 +228,11 @@
     out_ref[...] = one_ref[...] + two_ref[...]
 
 
-def join_kernel(*refs):
-    ins, outs = refs[:3], refs[3:]
-    for j, out_ref in enumerate(outs):
-        out_ref[...] = ins[0][j] + ins[1][j] + ins[2][j]
+def join_kernel(own_ref, soon_ref, low_ref, high_ref, *out_refs):
+    half = low_ref.shape[1]
+    for j, out_ref in enumerate(out_refs):
+        out_ref[:half] = own_ref[j, :half] + soon_ref[j, :half] + low_ref[j]
+        out_ref[half:] = own_ref[j, half:] + soon_ref[j, half:] + high_ref[j]
 
 
 def pairs_kernel(own_ref, one_ref, two_ref, three_ref, dense_ref, pairs_ref, summed_ref):
@@ -273,16 +296,26 @@
     near = split_tables(tables, other)
     part = split_tables(part)
 
-    far, shared = bags(ids, near, part, shared, (2, 2), examples, raw=True)
-    far = by_core(far, 1, ring)
-    soon = bags(ids, near, part, shared, (3, 1), examples)
+    low, high = tuple(range(count // 2)), tuple(range(count // 2, count))
+    whole = (low + high,)
+
+    far_low, shared = bags(ids, near, part, shared, (2, 2), examples, (low,), raw=True)
+    far_low = by_core(far_low, 1, ring)
+    (far_high,) = bags(ids, near, part, shared, (2, 2), examples, (high,))
+    far_high = by_core(far_high, 1, ring)
+    (soon,) = bags(ids, near, part, shared, (3, 1), examples, whole)
     soon = by_core(soon, -1, ring)
-    late = bags(ids, near, part, shared, (1, 3), examples)
-    late = local_kernel(add_kernel, jax.ShapeDtypeStruct(late.shape, late.dtype), (late, far))
-    late = by_core(late, 1, ring)
-    own = bags(ids, near, part, shared, (0, 0), examples)
+    late_low, late_high = bags(ids, near, part, shared, (1, 3), examples, (low, high))
+    piece = jax.ShapeDtypeStruct(late_low.shape, late_low.dtype)
+    late_low = local_kernel(add_kernel, piece, (late_low, far_low))
+    late_low = by_core(late_low, 1, ring)
+    late_high = local_kernel(add_kernel, piece, (late_high, far_high))
+    late_high = by_core(late_high, 1, ring)
+    (own,) = bags(ids, near, part, shared, (0, 0), examples, whole)
     block = jax.ShapeDtypeStruct(own.shape[1:], jnp.float32)
-    here, up, over, down = local_kernel(join_kernel, (block,) * group, (own, soon, late))
+    here, up, over, down = local_kernel(
+        join_kernel, (block,) * group, (own, soon, late_low, late_high)
+    )
     over, up, down = (
         lax.ppermute(piece, Z, [(i, (i + parities * by) % depth) for i in range(depth)])
         for piece, by in ((over, 2), (up, 1), (down, 3))

time: 80.6 us -> 78.8 us (0.978); the launches traced: 80.1 us -> 77.3 us
  waiting for transfers between devices: 34.6 us -> 30.9 us
    ppermute x3 -> x5, waiting for transfers between devices: 7.87 us -> 5.39 us  [by_core(): return lax.ppermute(value, ('x', 'c'), pairs)]
    ppermute x3, waiting for transfers between devices: 4.76 us -> 3.49 us  [body(): lax.ppermute(piece, Z, [(i, (i + parities * by) % depth) for i in range(d...]
    pallas_call x11 -> x13, Pallas kernels: 15.2 us -> 15.6 us  [local_kernel(): pl.pallas_call(kernel, in_specs=[HBM if k in in_hbm else VMEM for k in ra...]
    ppermute x3 -> x5, starting transfers between devices: 3.65 us -> 4.02 us  [by_core(): return lax.ppermute(value, ('x', 'c'), pairs)]
  transfers between devices with their start and end apart: 13 -> 15, of which waited for: 8 -> 11; matrix products, arithmetic and copies ran while one was open for 0% -> 0% of each run, Pallas kernels for 15% -> 15%
where the time goes in v9:
time: 78.8 us; the launch traced here: 77.3 us
  waiting for transfers between devices  30.9 us (39%)
  starting transfers between devices  29.5 us (37%)
  Pallas kernels  15.6 us (20%)
    pallas_call x13, Pallas kernels, local_kernel(): pl.pallas_call(kernel, in_specs=[HBM if k in in_hbm else VMEM for k in ra...  15.6 us
    ppermute x1, waiting for transfers between devices, body(): part = lax.ppermute(tables, Z + ('c',), pairs)  9.7 us
    ppermute x5, starting transfers between devices, shifted(): lax.ppermute(value, axis, [(i, (i + by) % size) for i in range(size)])  9.58 us
    all_to_all x1, starting transfers between devices, body(): ids = lax.all_to_all(ids, ('zq', 'x'), 0, 0, tiled=True)  8.24 us
    all_to_all x1, waiting for transfers between devices, body(): ids = lax.all_to_all(ids, ('zq', 'x'), 0, 0, tiled=True)  7.83 us
    ppermute x3, starting transfers between devices, body(): lax.ppermute(piece, Z, [(i, (i + parities * by) % depth) for i in range(d...  5.67 us
    ppermute x5, waiting for transfers between devices, by_core(): return lax.ppermute(value, ('x', 'c'), pairs)  5.39 us
    ppermute x5, waiting for transfers between devices, shifted(): lax.ppermute(value, axis, [(i, (i + by) % size) for i in range(size)])  4.47 us
  transfers between devices with their start and end apart: 15, of which 11 were waited for; matrix products, arithmetic and copies ran while one was open for 0% of the time, Pallas kernels for 15%

profile of v9, /device:TPU:24, one launch (start us, length us, event | category | flops | bytes accessed | tf_op | source)
XLA Modules:
  0.0 77.3 jit_solution(17180574829543290989)
XLA Ops:
  0.6 2.0 %collective-permute-start.1 = (f32[4,512,128]{2,1,0:T(8,128)}, f32[4,512,128]{2,1,0:T(8,128)}, u32[]{:S(2)}, u32[]{:S(2)}) collective-permute-start(f32[4,512,128]{2,1,0:T(8,128)} %refs_0_.1), channel_id=1, source_target_pairs={{0,32},{4,228},{32,0},{36,68},{64,96},{68,36},{96,64},{100,132},{1... | collective-permute-start | bytes 3145736 | tf_op jit(solution)/shard_map/ppermute | solution.py:275
  2.6 3.5 %collective-permute-start = (f32[4,512,128]{2,1,0:T(8,128)}, f32[4,512,128]{2,1,0:T(8,128)}, u32[]{:S(2)}, u32[]{:S(2)}) collective-permute-start(f32[4,512,128]{2,1,0:T(8,128)} %refs_0_.1), channel_id=1, source_target_pairs={{0,4},{4,0},{1,5},{5,1},{2,6},{6,2},{3,7},{7,3},{8,12},{12,8},{9,1... | collective-permute-start | bytes 3145736 | tf_op jit(solution)/shard_map/ppermute | solution.py:21
  6.1 9.7 %collective-permute-done.1.refs_0_ = f32[4,512,128]{2,1,0:T(8,128)} collective-permute-done((f32[4,512,128]{2,1,0:T(8,128)}, f32[4,512,128]{2,1,0:T(8,128)}, u32[]{:S(2)}, u32[]{:S(2)}) %collective-permute-start.1) | collective-permute-done | bytes 1048608 | tf_op jit(solution)/shard_map/ppermute | solution.py:275
  15.8 2.8 %collective-permute-start.2 = (f32[4,512,128]{2,1,0:T(8,128)}, f32[4,512,128]{2,1,0:T(8,128)}, u32[]{:S(2)}, u32[]{:S(2)}) collective-permute-start(f32[4,512,128]{2,1,0:T(8,128)} %collective-permute-done.1.refs_0_), channel_id=1, source_target_pairs={{0,4},{4,0},{1,5},{5,1},{2,6},{6,2},{3,7},{7,3},{8,12},{12,8},{9,1... | collective-permute-start | bytes 3145736 | tf_op jit(solution)/shard_map/ppermute | solution.py:21
  18.6 1.8 %shard_map.68 = s32[4,4,16,128]{3,2,1,0:T(8,128)} custom-call(s32[4,64]{1,0:T(4,128)} %bitcast.17, s32[8,4,8,64]{3,2,1,0:T(8,128)} %bitcast.15, s32[8,4,8,64]{3,2,1,0:T(8,128)} %bitcast.16), custom_call_target="tpu_custom_call" | custom-call | flops 1048576 | bytes 1048576 | tf_op jit(solution)/shard_map/pallas_call | solution.py:26
  20.4 8.2 %all-to-all-start = ((s32[16,16,128]{2,1,0:T(8,128)}), s32[16,16,128]{2,1,0:T(8,128)S(1)}, u32[]{:S(2)}, u32[]{:S(2)}) async-start(s32[16,16,128]{2,1,0:T(8,128)} %bitcast.14), calls=%async_computation | async-start | bytes 262144 | tf_op jit(solution)/shard_map/all_to_all | solution.py:293
  28.7 1.5 %shard_map.70.refs_2_ = bf16[4,512,256]{2,1,0:T(8,128)(2,1)S(1)} custom-call(f32[4,512,128]{2,1,0:T(8,128)} %collective-permute-done.1.refs_0_), custom_call_target="tpu_custom_call" | custom-call | flops 1048576 | bytes 1048576 | tf_op jit(solution)/shard_map/pallas_call | solution.py:26
  30.2 1.7 %shard_map.69.refs_1_ = bf16[8,512,256]{2,1,0:T(8,128)(2,1)S(1)} custom-call(f32[4,512,128]{2,1,0:T(8,128)S(1)} %copy-done, f32[4,512,128]{2,1,0:T(8,128)} %collective-permute-done.refs_1_), custom_call_target="tpu_custom_call" | custom-call | flops 1048576 | bytes 1048576 | tf_op jit(solution)/shard_map/pallas_call | solution.py:26
  31.9 7.8 %all-to-all-done = s32[16,16,128]{2,1,0:T(8,128)S(1)} async-done(((s32[16,16,128]{2,1,0:T(8,128)}), s32[16,16,128]{2,1,0:T(8,128)S(1)}, u32[]{:S(2)}, u32[]{:S(2)}) %all-to-all-start) | async-done | bytes 131104 | tf_op jit(solution)/shard_map/all_to_all | solution.py:293
  39.7 2.4 %shard_map.71 = (f32[4,64,128]{2,1,0:T(8,128)S(1)}, bf16[4,512,256]{2,1,0:T(8,128)(2,1)S(1)}) custom-call(s32[4,4,16,128]{3,2,1,0:T(8,128)S(1)} %bitcast.9, bf16[8,512,256]{2,1,0:T(8,128)(2,1)S(1)} %shard_map.69.refs_1_, bf16[4,512,256]{2,1,0:T(8,128)(2,1)S(1)} %shard_map.70.refs_2_, f32[4,512,128]{2,1,0:T(8,128)} %collective-permute-done.2.refs_3_), custom_call_target="tpu_custom_call" | custom-call | flops 671088640 | bytes 1048576 | tf_op jit(solution)/shard_map/pallas_call | solution.py:26
  42.1 1.2 %shard_map.76 = f32[4,64,128]{2,1,0:T(8,128)S(1)} custom-call(s32[4,4,16,128]{3,2,1,0:T(8,128)S(1)} %bitcast.10, bf16[8,512,256]{2,1,0:T(8,128)(2,1)S(1)} %shard_map.69.refs_1_, bf16[4,512,256]{2,1,0:T(8,128)(2,1)S(1)} %shard_map.70.refs_2_, bf16[4,512,256]{2,1,0:T(8,128)(2,1)S(1)} %get-tuple-element.12.refs_3_), custom_call_target="tpu_custom_call" | custom-call | flops 671088640 | bytes 1048576 | tf_op jit(solution)/shard_map/pallas_call | solution.py:26
  43.3 0.3 collective-permute-start.6
  43.7 1.3 %collective-permute-start.4 = (f32[4,64,128]{2,1,0:T(8,128)S(1)}, f32[4,64,128]{2,1,0:T(8,128)S(1)}, u32[]{:S(2)}, u32[]{:S(2)}) collective-permute-start(f32[4,64,128]{2,1,0:T(8,128)S(1)} %get-tuple-element.14), channel_id=1, source_target_pairs={{0,8},{4,28},{8,16},{12,4},{16,24},{20,12},{24,0},{28,20},{1,9},{5... | collective-permute-start | bytes 393224 | tf_op jit(solution)/shard_map/ppermute | solution.py:224
  44.9 2.0 %shard_map.73 = f32[4,128,128]{2,1,0:T(8,128)S(1)} custom-call(s32[4,4,16,128]{3,2,1,0:T(8,128)S(1)} %bitcast.11, bf16[8,512,256]{2,1,0:T(8,128)(2,1)S(1)} %shard_map.69.refs_1_, bf16[4,512,256]{2,1,0:T(8,128)(2,1)S(1)} %shard_map.70.refs_2_, bf16[4,512,256]{2,1,0:T(8,128)(2,1)S(1)} %get-tuple-element.12.refs_3_), custom_call_target="tpu_custom_call" | custom-call | flops 1342177280 | bytes 1048576 | tf_op jit(solution)/shard_map/pallas_call | solution.py:26
  46.9 2.1 %collective-permute-start.3 = (f32[4,128,128]{2,1,0:T(8,128)S(1)}, f32[4,128,128]{2,1,0:T(8,128)S(1)}, u32[]{:S(2)}, u32[]{:S(2)}) collective-permute-start(f32[4,128,128]{2,1,0:T(8,128)S(1)} %shard_map.73), channel_id=1, source_target_pairs={{0,24},{4,12},{8,0},{12,20},{16,8},{20,28},{24,16},{28,4},{1,25},{... | collective-permute-start | bytes 786440 | tf_op jit(solution)/shard_map/ppermute | solution.py:224
  49.0 2.0 %shard_map.74 = (f32[4,64,128]{2,1,0:T(8,128)S(1)}, f32[4,64,128]{2,1,0:T(8,128)S(1)}) custom-call(s32[4,4,16,128]{3,2,1,0:T(8,128)S(1)} %bitcast.12, bf16[8,512,256]{2,1,0:T(8,128)(2,1)S(1)} %shard_map.69.refs_1_, bf16[4,512,256]{2,1,0:T(8,128)(2,1)S(1)} %shard_map.70.refs_2_, bf16[4,512,256]{2,1,0:T(8,128)(2,1)S(1)} %get-tuple-element.12.refs_3_), custom_call_target="tpu_custom_call" | custom-call | flops 1342177280 | bytes 1048576 | tf_op jit(solution)/shard_map/pallas_call | solution.py:26
  51.2 1.3 %collective-permute-done.4.two_ref = f32[4,64,128]{2,1,0:T(8,128)S(1)} collective-permute-done((f32[4,64,128]{2,1,0:T(8,128)S(1)}, f32[4,64,128]{2,1,0:T(8,128)S(1)}, u32[]{:S(2)}, u32[]{:S(2)}) %collective-permute-start.4) | collective-permute-done | bytes 131104 | tf_op jit(solution)/shard_map/ppermute | solution.py:224
  52.7 2.0 %shard_map.72.own_ref = f32[4,128,128]{2,1,0:T(8,128)S(1)} custom-call(s32[4,4,16,128]{3,2,1,0:T(8,128)S(1)} %bitcast.13, bf16[8,512,256]{2,1,0:T(8,128)(2,1)S(1)} %shard_map.69.refs_1_, bf16[4,512,256]{2,1,0:T(8,128)(2,1)S(1)} %shard_map.70.refs_2_, bf16[4,512,256]{2,1,0:T(8,128)(2,1)S(1)} %get-tuple-element.12.refs_3_), custom_call_target="tpu_custom_call" | custom-call | flops 1342177280 | bytes 1048576 | tf_op jit(solution)/shard_map/pallas_call | solution.py:26
  54.8 0.8 collective-permute-done.3.soon_ref
  55.5 1.8 %collective-permute-done.7.high_ref = f32[4,64,128]{2,1,0:T(8,128)S(1)} collective-permute-done((f32[4,64,128]{2,1,0:T(8,128)S(1)}, f32[4,64,128]{2,1,0:T(8,128)S(1)}, u32[]{:S(2)}, u32[]{:S(2)}) %collective-permute-start.7) | collective-permute-done | bytes 131104 | tf_op jit(solution)/shard_map/ppermute | solution.py:224
  57.3 1.6 %collective-permute-done.5.low_ref = f32[4,64,128]{2,1,0:T(8,128)S(1)} collective-permute-done((f32[4,64,128]{2,1,0:T(8,128)S(1)}, f32[4,64,128]{2,1,0:T(8,128)S(1)}, u32[]{:S(2)}, u32[]{:S(2)}) %collective-permute-start.5) | collective-permute-done | bytes 131104 | tf_op jit(solution)/shard_map/ppermute | solution.py:224
  59.0 1.5 %collective-permute-start.8 = (f32[128,128]{1,0:T(8,128)S(1)}, f32[128,128]{1,0:T(8,128)S(1)}, u32[]{:S(2)}, u32[]{:S(2)}) collective-permute-start(f32[128,128]{1,0:T(8,128)S(1)} %get-tuple-element.17), channel_id=1, source_target_pairs={{0,128},{32,160},{64,192},{96,224},{128,0},{160,32},{192,64},{224,... | collective-permute-start | bytes 196616 | tf_op jit(solution)/shard_map/ppermute | solution.py:320
  60.5 2.2 %collective-permute-start.9 = (f32[128,128]{1,0:T(8,128)S(1)}, f32[128,128]{1,0:T(8,128)S(1)}, u32[]{:S(2)}, u32[]{:S(2)}) collective-permute-start(f32[128,128]{1,0:T(8,128)S(1)} %get-tuple-element.18), channel_id=1, source_target_pairs={{0,64},{32,96},{64,128},{96,160},{128,192},{160,224},{192,0},{224,... | collective-permute-start | bytes 196616 | tf_op jit(solution)/shard_map/ppermute | solution.py:320
  62.7 1.9 %collective-permute-start.10 = (f32[128,128]{1,0:T(8,128)S(1)}, f32[128,128]{1,0:T(8,128)S(1)}, u32[]{:S(2)}, u32[]{:S(2)}) collective-permute-start(f32[128,128]{1,0:T(8,128)S(1)} %get-tuple-element.19), channel_id=1, source_target_pairs={{0,192},{32,224},{64,0},{96,32},{128,64},{160,96},{192,128},{224,1... | collective-permute-start | bytes 196616 | tf_op jit(solution)/shard_map/ppermute | solution.py:320
  64.6 2.8 %collective-permute-done.8.one_ref = f32[128,128]{1,0:T(8,128)S(1)} collective-permute-done((f32[128,128]{1,0:T(8,128)S(1)}, f32[128,128]{1,0:T(8,128)S(1)}, u32[]{:S(2)}, u32[]{:S(2)}) %collective-permute-start.8) | collective-permute-done | bytes 65568 | tf_op jit(solution)/shard_map/ppermute | solution.py:320
  67.7 0.4 collective-permute-done.10.three_ref
  68.3 0.8 collective-permute-start.13
  69.1 2.5 %collective-permute-start.12 = (f32[10,32]{1,0:T(8,128)S(1)}, f32[10,32]{1,0:T(8,128)S(1)}, u32[]{:S(2)}, u32[]{:S(2)}) collective-permute-start(f32[10,32]{1,0:T(8,128)S(1)} %get-tuple-element.21), channel_id=1, source_target_pairs={{0,1},{1,2},{2,3},{3,0},{4,5},{5,6},{6,7},{7,4},{8,9},{9,10},{10,1... | collective-permute-start | bytes 3848 | tf_op jit(solution)/shard_map/ppermute | solution.py:21
  71.6 0.7 shard_map.80
  72.3 0.9 %collective-permute-done.13 = f32[10,32]{1,0:T(8,128)S(1)} collective-permute-done((f32[10,32]{1,0:T(8,128)S(1)}, f32[10,32]{1,0:T(8,128)S(1)}, u32[]{:S(2)}, u32[]{:S(2)}) %collective-permute-start.13) | collective-permute-done | bytes 1312 | tf_op jit(solution)/shard_map/ppermute | solution.py:21
  73.2 3.5 %collective-permute-done.11 = f32[10,32]{1,0:T(8,128)S(1)} collective-permute-done((f32[10,32]{1,0:T(8,128)S(1)}, f32[10,32]{1,0:T(8,128)S(1)}, u32[]{:S(2)}, u32[]{:S(2)}) %collective-permute-start.11) | collective-permute-done | bytes 1312 | tf_op jit(solution)/shard_map/ppermute | solution.py:21
  76.7 0.6 multiply_bitcast_fusion
  (16 shorter events, 1.0 us)
Async XLA Ops:
  0.6 15.2 %collective-permute-start.1 = (f32[4,512,128]{2,1,0:T(8,128)}, f32[4,512,128]{2,1,0:T(8,128)}, u32[]{:S(2)}, u32[]{:S(2)}) collective-permute-start(f32[4,512,128]{2,1,0:T(8,128)} %refs_0_.1), channel_id=1, source_target_pairs={{0,32},{4,228},{32,0},{36,68},{64,96},{68,36},{96,64},{100,132},{1... | collective-permute-start | bytes 3145736 | tf_op jit(solution)/shard_map/ppermute | solution.py:275
  2.6 27.6 %collective-permute-start = (f32[4,512,128]{2,1,0:T(8,128)}, f32[4,512,128]{2,1,0:T(8,128)}, u32[]{:S(2)}, u32[]{:S(2)}) collective-permute-start(f32[4,512,128]{2,1,0:T(8,128)} %refs_0_.1), channel_id=1, source_target_pairs={{0,4},{4,0},{1,5},{5,1},{2,6},{6,2},{3,7},{7,3},{8,12},{12,8},{9,1... | collective-permute-start | bytes 3145736 | tf_op jit(solution)/shard_map/ppermute | solution.py:21
  15.8 23.9 %collective-permute-start.2 = (f32[4,512,128]{2,1,0:T(8,128)}, f32[4,512,128]{2,1,0:T(8,128)}, u32[]{:S(2)}, u32[]{:S(2)}) collective-permute-start(f32[4,512,128]{2,1,0:T(8,128)} %collective-permute-done.1.refs_0_), channel_id=1, source_target_pairs={{0,4},{4,0},{1,5},{5,1},{2,6},{6,2},{3,7},{7,3},{8,12},{12,8},{9,1... | collective-permute-start | bytes 3145736 | tf_op jit(solution)/shard_map/ppermute | solution.py:21
  20.4 19.3 %all-to-all-start = ((s32[16,16,128]{2,1,0:T(8,128)}), s32[16,16,128]{2,1,0:T(8,128)S(1)}, u32[]{:S(2)}, u32[]{:S(2)}) async-start(s32[16,16,128]{2,1,0:T(8,128)} %bitcast.14), calls=%async_computation | async-start | bytes 262144 | tf_op jit(solution)/shard_map/all_to_all | solution.py:293
  28.6 1.6 %copy-start = (f32[4,512,128]{2,1,0:T(8,128)S(1)}, f32[4,512,128]{2,1,0:T(8,128)}, u32[]{:S(2)}) copy-start(f32[4,512,128]{2,1,0:T(8,128)} %refs_0_.1) | copy-start | bytes 3145732
  43.3 7.7 %collective-permute-start.6 = (f32[4,64,128]{2,1,0:T(8,128)S(1)}, f32[4,64,128]{2,1,0:T(8,128)S(1)}, u32[]{:S(2)}, u32[]{:S(2)}) collective-permute-start(f32[4,64,128]{2,1,0:T(8,128)S(1)} %shard_map.76), channel_id=1, source_target_pairs={{0,8},{4,28},{8,16},{12,4},{16,24},{20,12},{24,0},{28,20},{1,9},{5... | collective-permute-start | bytes 393224 | tf_op jit(solution)/shard_map/ppermute | solution.py:224
  43.7 8.8 %collective-permute-start.4 = (f32[4,64,128]{2,1,0:T(8,128)S(1)}, f32[4,64,128]{2,1,0:T(8,128)S(1)}, u32[]{:S(2)}, u32[]{:S(2)}) collective-permute-start(f32[4,64,128]{2,1,0:T(8,128)S(1)} %get-tuple-element.14), channel_id=1, source_target_pairs={{0,8},{4,28},{8,16},{12,4},{16,24},{20,12},{24,0},{28,20},{1,9},{5... | collective-permute-start | bytes 393224 | tf_op jit(solution)/shard_map/ppermute | solution.py:224
  46.9 8.6 %collective-permute-start.3 = (f32[4,128,128]{2,1,0:T(8,128)S(1)}, f32[4,128,128]{2,1,0:T(8,128)S(1)}, u32[]{:S(2)}, u32[]{:S(2)}) collective-permute-start(f32[4,128,128]{2,1,0:T(8,128)S(1)} %shard_map.73), channel_id=1, source_target_pairs={{0,24},{4,12},{8,0},{12,20},{16,8},{20,28},{24,16},{28,4},{1,25},{... | collective-permute-start | bytes 786440 | tf_op jit(solution)/shard_map/ppermute | solution.py:224
  51.1 6.3 %collective-permute-start.7 = (f32[4,64,128]{2,1,0:T(8,128)S(1)}, f32[4,64,128]{2,1,0:T(8,128)S(1)}, u32[]{:S(2)}, u32[]{:S(2)}) collective-permute-start(f32[4,64,128]{2,1,0:T(8,128)S(1)} %shard_map.77), channel_id=1, source_target_pairs={{0,8},{4,28},{8,16},{12,4},{16,24},{20,12},{24,0},{28,20},{1,9},{5... | collective-permute-start | bytes 393224 | tf_op jit(solution)/shard_map/ppermute | solution.py:224
  52.5 15.7 %copy-start.1 = (f32[32,128]{1,0:T(8,128)S(1)}, f32[32,128]{1,0:T(8,128)}, u32[]{:S(2)}) copy-start(f32[32,128]{1,0:T(8,128)} %dense_ref.1) | copy-start | bytes 49156
  52.5 6.4 %collective-permute-start.5 = (f32[4,64,128]{2,1,0:T(8,128)S(1)}, f32[4,64,128]{2,1,0:T(8,128)S(1)}, u32[]{:S(2)}, u32[]{:S(2)}) collective-permute-start(f32[4,64,128]{2,1,0:T(8,128)S(1)} %shard_map.75), channel_id=1, source_target_pairs={{0,8},{4,28},{8,16},{12,4},{16,24},{20,12},{24,0},{28,20},{1,9},{5... | collective-permute-start | bytes 393224 | tf_op jit(solution)/shard_map/ppermute | solution.py:224
  59.0 8.4 %collective-permute-start.8 = (f32[128,128]{1,0:T(8,128)S(1)}, f32[128,128]{1,0:T(8,128)S(1)}, u32[]{:S(2)}, u32[]{:S(2)}) collective-permute-start(f32[128,128]{1,0:T(8,128)S(1)} %get-tuple-element.17), channel_id=1, source_target_pairs={{0,128},{32,160},{64,192},{96,224},{128,0},{160,32},{192,64},{224,... | collective-permute-start | bytes 196616 | tf_op jit(solution)/shard_map/ppermute | solution.py:320
  60.5 7.2 %collective-permute-start.9 = (f32[128,128]{1,0:T(8,128)S(1)}, f32[128,128]{1,0:T(8,128)S(1)}, u32[]{:S(2)}, u32[]{:S(2)}) collective-permute-start(f32[128,128]{1,0:T(8,128)S(1)} %get-tuple-element.18), channel_id=1, source_target_pairs={{0,64},{32,96},{64,128},{96,160},{128,192},{160,224},{192,0},{224,... | collective-permute-start | bytes 196616 | tf_op jit(solution)/shard_map/ppermute | solution.py:320
  62.7 5.4 %collective-permute-start.10 = (f32[128,128]{1,0:T(8,128)S(1)}, f32[128,128]{1,0:T(8,128)S(1)}, u32[]{:S(2)}, u32[]{:S(2)}) collective-permute-start(f32[128,128]{1,0:T(8,128)S(1)} %get-tuple-element.19), channel_id=1, source_target_pairs={{0,192},{32,224},{64,0},{96,32},{128,64},{160,96},{192,128},{224,1... | collective-permute-start | bytes 196616 | tf_op jit(solution)/shard_map/ppermute | solution.py:320
  68.3 4.9 %collective-permute-start.13 = (f32[10,32]{1,0:T(8,128)S(1)}, f32[10,32]{1,0:T(8,128)S(1)}, u32[]{:S(2)}, u32[]{:S(2)}) collective-permute-start(f32[10,32]{1,0:T(8,128)S(1)} %get-tuple-element.21), channel_id=1, source_target_pairs={{0,3},{1,0},{2,1},{3,2},{4,7},{5,4},{6,5},{7,6},{8,11},{9,8},{10,9... | collective-permute-start | bytes 3848 | tf_op jit(solution)/shard_map/ppermute | solution.py:21
  69.1 4.1 %collective-permute-start.12 = (f32[10,32]{1,0:T(8,128)S(1)}, f32[10,32]{1,0:T(8,128)S(1)}, u32[]{:S(2)}, u32[]{:S(2)}) collective-permute-start(f32[10,32]{1,0:T(8,128)S(1)} %get-tuple-element.21), channel_id=1, source_target_pairs={{0,1},{1,2},{2,3},{3,0},{4,5},{5,6},{6,7},{7,4},{8,9},{9,10},{10,1... | collective-permute-start | bytes 3848 | tf_op jit(solution)/shard_map/ppermute | solution.py:21
  71.6 5.2 %collective-permute-start.11 = (f32[10,32]{1,0:T(8,128)S(1)}, f32[10,32]{1,0:T(8,128)S(1)}, u32[]{:S(2)}, u32[]{:S(2)}) collective-permute-start(f32[10,32]{1,0:T(8,128)S(1)} %get-tuple-element.21), channel_id=1, source_target_pairs={{0,2},{1,3},{2,0},{3,1},{4,6},{5,7},{6,4},{7,5},{8,10},{9,11},{10,... | collective-permute-start | bytes 3848 | tf_op jit(solution)/shard_map/ppermute | solution.py:21

commit v10 on v9

--- a/solution.py
+++ b/solution.py
@@ -113,7 +113,7 @@
     return jnp.where(mask, 1.0, 0.0).astype(jnp.bfloat16)
 
 
-def bags_kernel(*refs, away, examples, count, parts, raw):
+def bags_kernel(*refs, examples, count, parts, raw):
     ids_ref, near_ref, part_ref, shared_ref, *refs = refs
     out_refs, refs = refs[: len(parts)], refs[len(parts) :]
     if raw:
@@ -137,14 +137,20 @@
     owners = messages // count
     slots = lanes // 2
     core = lax.axis_index("c")
-    chosen = away[0] + core * (away[1] - away[0])
-    column = lax.rem(lax.axis_index("x") + chosen, ring)
+    aways = tuple(dict.fromkeys(away for away, _ in parts))
     depth = lax.axis_index("zq")
     row_iota = lax.broadcasted_iota(jnp.int32, (slots, rows), 1)
     key_iota = lax.broadcasted_iota(jnp.int32, (group * examples, group * slots), 0)
-    ids = [ids_ref[lax.rem(depth + j, group), column] for j in range(group)]
-    columns = jnp.swapaxes(jnp.concatenate(ids, axis=0), 0, 1)
-    keys = jnp.concatenate([ids[j][:, slots:] + j * examples for j in range(group)], axis=1)
+    columns, keys = [], []
+    for away in aways:
+        chosen = away[0] + core * (away[1] - away[0])
+        column = lax.rem(lax.axis_index("x") + chosen, ring)
+        ids = [ids_ref[lax.rem(depth + j, group), column] for j in range(group)]
+        columns.append(jnp.swapaxes(jnp.concatenate(ids, axis=0), 0, 1))
+        keys.append(
+            jnp.concatenate([ids[j][:, slots:] + j * examples for j in range(group)], axis=1)
+        )
+    block = group * slots
 
     def look(o, t):
         ref, place = ((near_ref, t), (near_ref, count + t), (part_ref, t), (shared_ref, t))[o]
@@ -152,19 +158,25 @@
         picks = jnp.concatenate(
             [
                 one_hot(
-                    columns[:slots, j * messages + message : j * messages + message + 1] == row_iota
+                    one[:slots, j * messages + message : j * messages + message + 1] == row_iota
                 )
+                for one in columns
                 for j in range(group)
             ],
             axis=0,
         )
         looked = jnp.dot(picks, ref[place], preferred_element_type=jnp.float32)
-        looked_ref[t, o * group * slots : (o + 1) * group * slots, :] = looked.astype(jnp.bfloat16)
-
-    def pool(t, out_ref, place):
-        into = [one_hot(keys[o * count + t : o * count + t + 1] == key_iota) for o in range(owners)]
+        for k in range(len(aways)):
+            looked_ref[k, t, o * block : (o + 1) * block, :] = looked[
+                k * block : (k + 1) * block
+            ].astype(jnp.bfloat16)
+
+    def pool(k, t, out_ref, place):
+        into = [
+            one_hot(keys[k][o * count + t : o * count + t + 1] == key_iota) for o in range(owners)
+        ]
         total = jnp.dot(
-            jnp.concatenate(into, axis=1), looked_ref[t], preferred_element_type=jnp.float32
+            jnp.concatenate(into, axis=1), looked_ref[k, t], preferred_element_type=jnp.float32
         )
         summed = total[:, : wide // 2] + total[:, wide // 2 :]
         out_ref[:, place * examples : (place + 1) * examples, :] = summed.reshape(
@@ -172,46 +184,48 @@
         )
 
     early = owners - 1 if raw else 0
-    for tables in parts:
-        for t in tables:
-            for o in range(early):
-                look(o, t)
-    for k, (tables, out_ref) in enumerate(zip(parts, out_refs)):
+    tables = tuple(dict.fromkeys(t for _, chosen in parts for t in chosen))
+    for t in tables:
+        for o in range(early):
+            look(o, t)
+    if raw:
+        copies[0].wait()
+    for t in tables:
         if raw:
-            copies[k].wait()
-        for place, t in enumerate(tables):
-            if raw:
-                split_into(shared_ref, t, full_ref[t])
-            for o in range(early, owners):
-                look(o, t)
-            pool(t, out_ref, place)
+            split_into(shared_ref, t, full_ref[t])
+        for o in range(early, owners):
+            look(o, t)
+        for (away, chosen), out_ref in zip(parts, out_refs):
+            if t in chosen:
+                pool(aways.index(away), t, out_ref, chosen.index(t))
     if raw:
         copies[1].wait()
         for t in range(half, count):
             split_into(shared_ref, t, full_ref[t])
 
 
-def bags(ids, near, part, shared, away, examples, parts, raw=False):
+def bags(ids, near, part, shared, examples, parts, raw=False):
     group, _, messages, lanes = ids.shape
     count, rows, wide = part.shape
-    tasks = sum(len(tables) for tables in parts)
+    tasks = sum(len(tables) for _, tables in parts)
     work = messages // count * tasks * group * lanes // 2
     out = tuple(
         jax.ShapeDtypeStruct((group, len(tables) * examples, wide // 2), jnp.float32)
-        for tables in parts
-    )
-    scratch = [pltpu.VMEM((count, messages // count * group * lanes // 2, wide), jnp.bfloat16)]
+        for _, tables in parts
+    )
+    chunks = len(set(away for away, _ in parts))
+    scratch = [
+        pltpu.VMEM((chunks, count, messages // count * group * lanes // 2, wide), jnp.bfloat16)
+    ]
     if raw:
         out += (jax.ShapeDtypeStruct(part.shape, part.dtype),)
         scratch += [pltpu.VMEM(shared.shape, jnp.float32), pltpu.SemaphoreType.DMA((2,))]
     return local_kernel(
-        functools.partial(
-            bags_kernel, away=away, examples=examples, count=count, parts=parts, raw=raw
-        ),
+        functools.partial(bags_kernel, examples=examples, count=count, parts=parts, raw=raw),
         out,
         (ids, near, part, shared),
         flops=2 * work * wide * (rows + group * examples),
-        vmem=16 << 20,
+        vmem=20 << 20,
         scratch=scratch,
         in_hbm=(3,) if raw else (),
     )
@@ -297,21 +311,22 @@
     part = split_tables(part)
 
     low, high = tuple(range(count // 2)), tuple(range(count // 2, count))
-    whole = (low + high,)
-
-    far_low, shared = bags(ids, near, part, shared, (2, 2), examples, (low,), raw=True)
+    whole = low + high
+
+    far_low, shared = bags(ids, near, part, shared, examples, (((2, 2), low),), raw=True)
     far_low = by_core(far_low, 1, ring)
-    (far_high,) = bags(ids, near, part, shared, (2, 2), examples, (high,))
+    (far_high,) = bags(ids, near, part, shared, examples, (((2, 2), high),))
     far_high = by_core(far_high, 1, ring)
-    (soon,) = bags(ids, near, part, shared, (3, 1), examples, whole)
+    soon, late_low, late_high = bags(
+        ids, near, part, shared, examples, (((3, 1), whole), ((1, 3), low), ((1, 3), high))
+    )
     soon = by_core(soon, -1, ring)
-    late_low, late_high = bags(ids, near, part, shared, (1, 3), examples, (low, high))
     piece = jax.ShapeDtypeStruct(late_low.shape, late_low.dtype)
     late_low = local_kernel(add_kernel, piece, (late_low, far_low))
     late_low = by_core(late_low, 1, ring)
     late_high = local_kernel(add_kernel, piece, (late_high, far_high))
     late_high = by_core(late_high, 1, ring)
-    (own,) = bags(ids, near, part, shared, (0, 0), examples, whole)
+    (own,) = bags(ids, near, part, shared, examples, (((0, 0), whole),))
     block = jax.ShapeDtypeStruct(own.shape[1:], jnp.float32)
     here, up, over, down = local_kernel(
         join_kernel, (block,) * group, (own, soon, late_low, late_high)

time: 78.8 us -> 78.9 us (level); the launches traced: 77.3 us -> 78.3 us
  waiting for transfers between devices: 30.9 us -> 32.1 us
  Pallas kernels: 15.6 us -> 14.7 us
    pallas_call x13 -> x12, Pallas kernels: 15.6 us -> 14.7 us  [local_kernel(): pl.pallas_call(kernel, in_specs=[HBM if k in in_hbm else VMEM for k in ra...]
    ppermute x3, waiting for transfers between devices: 3.49 us -> 4.36 us  [body(): lax.ppermute(piece, Z, [(i, (i + parities * by) % depth) for i in range(d...]
  transfers between devices with their start and end apart: 15 -> 15, of which waited for: 11 -> 10; matrix products, arithmetic and copies ran while one was open for 0% -> 0% of each run, Pallas kernels for 15% -> 14%
where the time goes in v10:
time: 78.9 us; the launch traced here: 78.3 us
  waiting for transfers between devices  32.1 us (41%)
  starting transfers between devices  30.1 us (38%)
  Pallas kernels  14.7 us (19%)
    pallas_call x12, Pallas kernels, local_kernel(): pl.pallas_call(kernel, in_specs=[HBM if k in in_hbm else VMEM for k in ra...  14.7 us
    ppermute x1, waiting for transfers between devices, body(): part = lax.ppermute(tables, Z + ('c',), pairs)  9.7 us
    ppermute x5, starting transfers between devices, shifted(): lax.ppermute(value, axis, [(i, (i + by) % size) for i in range(size)])  9.58 us
    all_to_all x1, starting transfers between devices, body(): ids = lax.all_to_all(ids, ('zq', 'x'), 0, 0, tiled=True)  8.24 us
    all_to_all x1, waiting for transfers between devices, body(): ids = lax.all_to_all(ids, ('zq', 'x'), 0, 0, tiled=True)  7.83 us
    ppermute x5, waiting for transfers between devices, by_core(): return lax.ppermute(value, ('x', 'c'), pairs)  5.77 us
    ppermute x3, starting transfers between devices, body(): lax.ppermute(piece, Z, [(i, (i + parities * by) % depth) for i in range(d...  5.67 us
    ppermute x5, starting transfers between devices, by_core(): return lax.ppermute(value, ('x', 'c'), pairs)  4.61 us
  transfers between devices with their start and end apart: 15, of which 10 were waited for; matrix products, arithmetic and copies ran while one was open for 0% of the time, Pallas kernels for 14%

profile of v10, /device:TPU:24, one launch (start us, length us, event | category | flops | bytes accessed | tf_op | source)
XLA Modules:
  0.0 78.3 jit_solution(12471646581340054903)
XLA Ops:
  0.6 2.0 %collective-permute-start.1 = (f32[4,512,128]{2,1,0:T(8,128)}, f32[4,512,128]{2,1,0:T(8,128)}, u32[]{:S(2)}, u32[]{:S(2)}) collective-permute-start(f32[4,512,128]{2,1,0:T(8,128)} %refs_0_.1), channel_id=1, source_target_pairs={{0,32},{4,228},{32,0},{36,68},{64,96},{68,36},{96,64},{100,132},{1... | collective-permute-start | bytes 3145736 | tf_op jit(solution)/shard_map/ppermute | solution.py:289
  2.6 3.5 %collective-permute-start = (f32[4,512,128]{2,1,0:T(8,128)}, f32[4,512,128]{2,1,0:T(8,128)}, u32[]{:S(2)}, u32[]{:S(2)}) collective-permute-start(f32[4,512,128]{2,1,0:T(8,128)} %refs_0_.1), channel_id=1, source_target_pairs={{0,4},{4,0},{1,5},{5,1},{2,6},{6,2},{3,7},{7,3},{8,12},{12,8},{9,1... | collective-permute-start | bytes 3145736 | tf_op jit(solution)/shard_map/ppermute | solution.py:21
  6.1 9.7 %collective-permute-done.1.refs_0_ = f32[4,512,128]{2,1,0:T(8,128)} collective-permute-done((f32[4,512,128]{2,1,0:T(8,128)}, f32[4,512,128]{2,1,0:T(8,128)}, u32[]{:S(2)}, u32[]{:S(2)}) %collective-permute-start.1) | collective-permute-done | bytes 1048608 | tf_op jit(solution)/shard_map/ppermute | solution.py:289
  15.8 2.8 %collective-permute-start.2 = (f32[4,512,128]{2,1,0:T(8,128)}, f32[4,512,128]{2,1,0:T(8,128)}, u32[]{:S(2)}, u32[]{:S(2)}) collective-permute-start(f32[4,512,128]{2,1,0:T(8,128)} %collective-permute-done.1.refs_0_), channel_id=1, source_target_pairs={{0,4},{4,0},{1,5},{5,1},{2,6},{6,2},{3,7},{7,3},{8,12},{12,8},{9,1... | collective-permute-start | bytes 3145736 | tf_op jit(solution)/shard_map/ppermute | solution.py:21
  18.6 1.8 %shard_map.68 = s32[4,4,16,128]{3,2,1,0:T(8,128)} custom-call(s32[4,64]{1,0:T(4,128)} %bitcast.16, s32[8,4,8,64]{3,2,1,0:T(8,128)} %bitcast.14, s32[8,4,8,64]{3,2,1,0:T(8,128)} %bitcast.15), custom_call_target="tpu_custom_call" | custom-call | flops 1048576 | bytes 1048576 | tf_op jit(solution)/shard_map/pallas_call | solution.py:26
  20.4 8.2 %all-to-all-start = ((s32[16,16,128]{2,1,0:T(8,128)}), s32[16,16,128]{2,1,0:T(8,128)S(1)}, u32[]{:S(2)}, u32[]{:S(2)}) async-start(s32[16,16,128]{2,1,0:T(8,128)} %bitcast.13), calls=%async_computation | async-start | bytes 262144 | tf_op jit(solution)/shard_map/all_to_all | solution.py:307
  28.7 1.5 %shard_map.70.refs_2_ = bf16[4,512,256]{2,1,0:T(8,128)(2,1)S(1)} custom-call(f32[4,512,128]{2,1,0:T(8,128)} %collective-permute-done.1.refs_0_), custom_call_target="tpu_custom_call" | custom-call | flops 1048576 | bytes 1048576 | tf_op jit(solution)/shard_map/pallas_call | solution.py:26
  30.2 1.7 %shard_map.69.refs_1_ = bf16[8,512,256]{2,1,0:T(8,128)(2,1)S(1)} custom-call(f32[4,512,128]{2,1,0:T(8,128)S(1)} %copy-done, f32[4,512,128]{2,1,0:T(8,128)} %collective-permute-done.refs_1_), custom_call_target="tpu_custom_call" | custom-call | flops 1048576 | bytes 1048576 | tf_op jit(solution)/shard_map/pallas_call | solution.py:26
  31.9 7.8 %all-to-all-done = s32[16,16,128]{2,1,0:T(8,128)S(1)} async-done(((s32[16,16,128]{2,1,0:T(8,128)}), s32[16,16,128]{2,1,0:T(8,128)S(1)}, u32[]{:S(2)}, u32[]{:S(2)}) %all-to-all-start) | async-done | bytes 131104 | tf_op jit(solution)/shard_map/all_to_all | solution.py:307
  39.7 2.4 %shard_map.71 = (f32[4,64,128]{2,1,0:T(8,128)S(1)}, bf16[4,512,256]{2,1,0:T(8,128)(2,1)S(1)}) custom-call(s32[4,4,16,128]{3,2,1,0:T(8,128)S(1)} %bitcast.9, bf16[8,512,256]{2,1,0:T(8,128)(2,1)S(1)} %shard_map.69.refs_1_, bf16[4,512,256]{2,1,0:T(8,128)(2,1)S(1)} %shard_map.70.refs_2_, f32[4,512,128]{2,1,0:T(8,128)} %collective-permute-done.2.refs_3_), custom_call_target="tpu_custom_call" | custom-call | flops 671088640 | bytes 1048576 | tf_op jit(solution)/shard_map/pallas_call | solution.py:26
  42.1 1.2 %shard_map.75 = f32[4,64,128]{2,1,0:T(8,128)S(1)} custom-call(s32[4,4,16,128]{3,2,1,0:T(8,128)S(1)} %bitcast.10, bf16[8,512,256]{2,1,0:T(8,128)(2,1)S(1)} %shard_map.69.refs_1_, bf16[4,512,256]{2,1,0:T(8,128)(2,1)S(1)} %shard_map.70.refs_2_, bf16[4,512,256]{2,1,0:T(8,128)(2,1)S(1)} %get-tuple-element.13.refs_3_), custom_call_target="tpu_custom_call" | custom-call | flops 671088640 | bytes 1048576 | tf_op jit(solution)/shard_map/pallas_call | solution.py:26
  43.3 0.3 collective-permute-start.6
  43.7 1.3 %collective-permute-start.4 = (f32[4,64,128]{2,1,0:T(8,128)S(1)}, f32[4,64,128]{2,1,0:T(8,128)S(1)}, u32[]{:S(2)}, u32[]{:S(2)}) collective-permute-start(f32[4,64,128]{2,1,0:T(8,128)S(1)} %get-tuple-element.16), channel_id=1, source_target_pairs={{0,8},{4,28},{8,16},{12,4},{16,24},{20,12},{24,0},{28,20},{1,9},{5... | collective-permute-start | bytes 393224 | tf_op jit(solution)/shard_map/ppermute | solution.py:238
  44.9 3.2 %shard_map.73 = (f32[4,128,128]{2,1,0:T(8,128)S(1)}, f32[4,64,128]{2,1,0:T(8,128)S(1)}, f32[4,64,128]{2,1,0:T(8,128)S(1)}) custom-call(s32[4,4,16,128]{3,2,1,0:T(8,128)S(1)} %bitcast.11, bf16[8,512,256]{2,1,0:T(8,128)(2,1)S(1)} %shard_map.69.refs_1_, bf16[4,512,256]{2,1,0:T(8,128)(2,1)S(1)} %shard_map.70.refs_2_, ...), custom_call_target="tpu_custom_call" | custom-call | flops 2684354560 | bytes 1048576 | tf_op jit(solution)/shard_map/pallas_call | solution.py:26
  48.1 2.1 %collective-permute-start.3 = (f32[4,128,128]{2,1,0:T(8,128)S(1)}, f32[4,128,128]{2,1,0:T(8,128)S(1)}, u32[]{:S(2)}, u32[]{:S(2)}) collective-permute-start(f32[4,128,128]{2,1,0:T(8,128)S(1)} %get-tuple-element.14), channel_id=1, source_target_pairs={{0,24},{4,12},{8,0},{12,20},{16,8},{20,28},{24,16},{28,4},{1,25},{... | collective-permute-start | bytes 786440 | tf_op jit(solution)/shard_map/ppermute | solution.py:238
  50.1 1.2 %collective-permute-done.4.two_ref = f32[4,64,128]{2,1,0:T(8,128)S(1)} collective-permute-done((f32[4,64,128]{2,1,0:T(8,128)S(1)}, f32[4,64,128]{2,1,0:T(8,128)S(1)}, u32[]{:S(2)}, u32[]{:S(2)}) %collective-permute-start.4) | collective-permute-done | bytes 131104 | tf_op jit(solution)/shard_map/ppermute | solution.py:238
  51.5 0.9 %collective-permute-start.7 = (f32[4,64,128]{2,1,0:T(8,128)S(1)}, f32[4,64,128]{2,1,0:T(8,128)S(1)}, u32[]{:S(2)}, u32[]{:S(2)}) collective-permute-start(f32[4,64,128]{2,1,0:T(8,128)S(1)} %shard_map.76), channel_id=1, source_target_pairs={{0,8},{4,28},{8,16},{12,4},{16,24},{20,12},{24,0},{28,20},{1,9},{5... | collective-permute-start | bytes 393224 | tf_op jit(solution)/shard_map/ppermute | solution.py:238
  52.3 2.0 %shard_map.72.own_ref = f32[4,128,128]{2,1,0:T(8,128)S(1)} custom-call(s32[4,4,16,128]{3,2,1,0:T(8,128)S(1)} %bitcast.12, bf16[8,512,256]{2,1,0:T(8,128)(2,1)S(1)} %shard_map.69.refs_1_, bf16[4,512,256]{2,1,0:T(8,128)(2,1)S(1)} %shard_map.70.refs_2_, bf16[4,512,256]{2,1,0:T(8,128)(2,1)S(1)} %get-tuple-element.13.refs_3_), custom_call_target="tpu_custom_call" | custom-call | flops 1342177280 | bytes 1048576 | tf_op jit(solution)/shard_map/pallas_call | solution.py:26
  54.4 1.6 %collective-permute-done.3.soon_ref = f32[4,128,128]{2,1,0:T(8,128)S(1)} collective-permute-done((f32[4,128,128]{2,1,0:T(8,128)S(1)}, f32[4,128,128]{2,1,0:T(8,128)S(1)}, u32[]{:S(2)}, u32[]{:S(2)}) %collective-permute-start.3) | collective-permute-done | bytes 262176 | tf_op jit(solution)/shard_map/ppermute | solution.py:238
  55.9 1.6 %collective-permute-done.5.low_ref = f32[4,64,128]{2,1,0:T(8,128)S(1)} collective-permute-done((f32[4,64,128]{2,1,0:T(8,128)S(1)}, f32[4,64,128]{2,1,0:T(8,128)S(1)}, u32[]{:S(2)}, u32[]{:S(2)}) %collective-permute-start.5) | collective-permute-done | bytes 131104 | tf_op jit(solution)/shard_map/ppermute | solution.py:238
  57.6 1.4 %collective-permute-done.7.high_ref = f32[4,64,128]{2,1,0:T(8,128)S(1)} collective-permute-done((f32[4,64,128]{2,1,0:T(8,128)S(1)}, f32[4,64,128]{2,1,0:T(8,128)S(1)}, u32[]{:S(2)}, u32[]{:S(2)}) %collective-permute-start.7) | collective-permute-done | bytes 131104 | tf_op jit(solution)/shard_map/ppermute | solution.py:238
  59.0 1.5 %collective-permute-start.8 = (f32[128,128]{1,0:T(8,128)S(1)}, f32[128,128]{1,0:T(8,128)S(1)}, u32[]{:S(2)}, u32[]{:S(2)}) collective-permute-start(f32[128,128]{1,0:T(8,128)S(1)} %get-tuple-element.19), channel_id=1, source_target_pairs={{0,128},{32,160},{64,192},{96,224},{128,0},{160,32},{192,64},{224,... | collective-permute-start | bytes 196616 | tf_op jit(solution)/shard_map/ppermute | solution.py:335
  60.6 1.8 %collective-permute-start.9 = (f32[128,128]{1,0:T(8,128)S(1)}, f32[128,128]{1,0:T(8,128)S(1)}, u32[]{:S(2)}, u32[]{:S(2)}) collective-permute-start(f32[128,128]{1,0:T(8,128)S(1)} %get-tuple-element.20), channel_id=1, source_target_pairs={{0,64},{32,96},{64,128},{96,160},{128,192},{160,224},{192,0},{224,... | collective-permute-start | bytes 196616 | tf_op jit(solution)/shard_map/ppermute | solution.py:335
  62.4 2.3 %collective-permute-start.10 = (f32[128,128]{1,0:T(8,128)S(1)}, f32[128,128]{1,0:T(8,128)S(1)}, u32[]{:S(2)}, u32[]{:S(2)}) collective-permute-start(f32[128,128]{1,0:T(8,128)S(1)} %get-tuple-element.21), channel_id=1, source_target_pairs={{0,192},{32,224},{64,0},{96,32},{128,64},{160,96},{192,128},{224,1... | collective-permute-start | bytes 196616 | tf_op jit(solution)/shard_map/ppermute | solution.py:335
  64.7 3.5 %collective-permute-done.8.one_ref = f32[128,128]{1,0:T(8,128)S(1)} collective-permute-done((f32[128,128]{1,0:T(8,128)S(1)}, f32[128,128]{1,0:T(8,128)S(1)}, u32[]{:S(2)}, u32[]{:S(2)}) %collective-permute-start.8) | collective-permute-done | bytes 65568 | tf_op jit(solution)/shard_map/ppermute | solution.py:335
  68.2 0.9 %collective-permute-done.10.three_ref = f32[128,128]{1,0:T(8,128)S(1)} collective-permute-done((f32[128,128]{1,0:T(8,128)S(1)}, f32[128,128]{1,0:T(8,128)S(1)}, u32[]{:S(2)}, u32[]{:S(2)}) %collective-permute-start.10) | collective-permute-done | bytes 65568 | tf_op jit(solution)/shard_map/ppermute | solution.py:335
  69.2 0.8 collective-permute-start.13
  70.0 2.5 %collective-permute-start.12 = (f32[10,32]{1,0:T(8,128)S(1)}, f32[10,32]{1,0:T(8,128)S(1)}, u32[]{:S(2)}, u32[]{:S(2)}) collective-permute-start(f32[10,32]{1,0:T(8,128)S(1)} %get-tuple-element.23), channel_id=1, source_target_pairs={{0,1},{1,2},{2,3},{3,0},{4,5},{5,6},{6,7},{7,4},{8,9},{9,10},{10,1... | collective-permute-start | bytes 3848 | tf_op jit(solution)/shard_map/ppermute | solution.py:21
  72.5 0.7 shard_map.79
  73.2 0.9 %collective-permute-done.13 = f32[10,32]{1,0:T(8,128)S(1)} collective-permute-done((f32[10,32]{1,0:T(8,128)S(1)}, f32[10,32]{1,0:T(8,128)S(1)}, u32[]{:S(2)}, u32[]{:S(2)}) %collective-permute-start.13) | collective-permute-done | bytes 1312 | tf_op jit(solution)/shard_map/ppermute | solution.py:21
  74.1 3.5 %collective-permute-done.11 = f32[10,32]{1,0:T(8,128)S(1)} collective-permute-done((f32[10,32]{1,0:T(8,128)S(1)}, f32[10,32]{1,0:T(8,128)S(1)}, u32[]{:S(2)}, u32[]{:S(2)}) %collective-permute-start.11) | collective-permute-done | bytes 1312 | tf_op jit(solution)/shard_map/ppermute | solution.py:21
  77.7 0.6 multiply_bitcast_fusion
  (15 shorter events, 0.4 us)
Async XLA Ops:
  0.6 15.2 %collective-permute-start.1 = (f32[4,512,128]{2,1,0:T(8,128)}, f32[4,512,128]{2,1,0:T(8,128)}, u32[]{:S(2)}, u32[]{:S(2)}) collective-permute-start(f32[4,512,128]{2,1,0:T(8,128)} %refs_0_.1), channel_id=1, source_target_pairs={{0,32},{4,228},{32,0},{36,68},{64,96},{68,36},{96,64},{100,132},{1... | collective-permute-start | bytes 3145736 | tf_op jit(solution)/shard_map/ppermute | solution.py:289
  2.6 27.6 %collective-permute-start = (f32[4,512,128]{2,1,0:T(8,128)}, f32[4,512,128]{2,1,0:T(8,128)}, u32[]{:S(2)}, u32[]{:S(2)}) collective-permute-start(f32[4,512,128]{2,1,0:T(8,128)} %refs_0_.1), channel_id=1, source_target_pairs={{0,4},{4,0},{1,5},{5,1},{2,6},{6,2},{3,7},{7,3},{8,12},{12,8},{9,1... | collective-permute-start | bytes 3145736 | tf_op jit(solution)/shard_map/ppermute | solution.py:21
  15.8 23.9 %collective-permute-start.2 = (f32[4,512,128]{2,1,0:T(8,128)}, f32[4,512,128]{2,1,0:T(8,128)}, u32[]{:S(2)}, u32[]{:S(2)}) collective-permute-start(f32[4,512,128]{2,1,0:T(8,128)} %collective-permute-done.1.refs_0_), channel_id=1, source_target_pairs={{0,4},{4,0},{1,5},{5,1},{2,6},{6,2},{3,7},{7,3},{8,12},{12,8},{9,1... | collective-permute-start | bytes 3145736 | tf_op jit(solution)/shard_map/ppermute | solution.py:21
  20.4 19.3 %all-to-all-start = ((s32[16,16,128]{2,1,0:T(8,128)}), s32[16,16,128]{2,1,0:T(8,128)S(1)}, u32[]{:S(2)}, u32[]{:S(2)}) async-start(s32[16,16,128]{2,1,0:T(8,128)} %bitcast.13), calls=%async_computation | async-start | bytes 262144 | tf_op jit(solution)/shard_map/all_to_all | solution.py:307
  28.6 1.6 %copy-start = (f32[4,512,128]{2,1,0:T(8,128)S(1)}, f32[4,512,128]{2,1,0:T(8,128)}, u32[]{:S(2)}) copy-start(f32[4,512,128]{2,1,0:T(8,128)} %refs_0_.1) | copy-start | bytes 3145732
  43.3 8.1 %collective-permute-start.6 = (f32[4,64,128]{2,1,0:T(8,128)S(1)}, f32[4,64,128]{2,1,0:T(8,128)S(1)}, u32[]{:S(2)}, u32[]{:S(2)}) collective-permute-start(f32[4,64,128]{2,1,0:T(8,128)S(1)} %shard_map.75), channel_id=1, source_target_pairs={{0,8},{4,28},{8,16},{12,4},{16,24},{20,12},{24,0},{28,20},{1,9},{5... | collective-permute-start | bytes 393224 | tf_op jit(solution)/shard_map/ppermute | solution.py:238
  43.7 7.6 %collective-permute-start.4 = (f32[4,64,128]{2,1,0:T(8,128)S(1)}, f32[4,64,128]{2,1,0:T(8,128)S(1)}, u32[]{:S(2)}, u32[]{:S(2)}) collective-permute-start(f32[4,64,128]{2,1,0:T(8,128)S(1)} %get-tuple-element.16), channel_id=1, source_target_pairs={{0,8},{4,28},{8,16},{12,4},{16,24},{20,12},{24,0},{28,20},{1,9},{5... | collective-permute-start | bytes 393224 | tf_op jit(solution)/shard_map/ppermute | solution.py:238
  48.1 7.9 %collective-permute-start.3 = (f32[4,128,128]{2,1,0:T(8,128)S(1)}, f32[4,128,128]{2,1,0:T(8,128)S(1)}, u32[]{:S(2)}, u32[]{:S(2)}) collective-permute-start(f32[4,128,128]{2,1,0:T(8,128)S(1)} %get-tuple-element.14), channel_id=1, source_target_pairs={{0,24},{4,12},{8,0},{12,20},{16,8},{20,28},{24,16},{28,4},{1,25},{... | collective-permute-start | bytes 786440 | tf_op jit(solution)/shard_map/ppermute | solution.py:238
  51.3 6.3 %collective-permute-start.5 = (f32[4,64,128]{2,1,0:T(8,128)S(1)}, f32[4,64,128]{2,1,0:T(8,128)S(1)}, u32[]{:S(2)}, u32[]{:S(2)}) collective-permute-start(f32[4,64,128]{2,1,0:T(8,128)S(1)} %shard_map.74), channel_id=1, source_target_pairs={{0,8},{4,28},{8,16},{12,4},{16,24},{20,12},{24,0},{28,20},{1,9},{5... | collective-permute-start | bytes 393224 | tf_op jit(solution)/shard_map/ppermute | solution.py:238
  51.4 17.6 %copy-start.1 = (f32[32,128]{1,0:T(8,128)S(1)}, f32[32,128]{1,0:T(8,128)}, u32[]{:S(2)}) copy-start(f32[32,128]{1,0:T(8,128)} %dense_ref.1) | copy-start | bytes 49156
  51.5 7.5 %collective-permute-start.7 = (f32[4,64,128]{2,1,0:T(8,128)S(1)}, f32[4,64,128]{2,1,0:T(8,128)S(1)}, u32[]{:S(2)}, u32[]{:S(2)}) collective-permute-start(f32[4,64,128]{2,1,0:T(8,128)S(1)} %shard_map.76), channel_id=1, source_target_pairs={{0,8},{4,28},{8,16},{12,4},{16,24},{20,12},{24,0},{28,20},{1,9},{5... | collective-permute-start | bytes 393224 | tf_op jit(solution)/shard_map/ppermute | solution.py:238
  59.0 9.1 %collective-permute-start.8 = (f32[128,128]{1,0:T(8,128)S(1)}, f32[128,128]{1,0:T(8,128)S(1)}, u32[]{:S(2)}, u32[]{:S(2)}) collective-permute-start(f32[128,128]{1,0:T(8,128)S(1)} %get-tuple-element.19), channel_id=1, source_target_pairs={{0,128},{32,160},{64,192},{96,224},{128,0},{160,32},{192,64},{224,... | collective-permute-start | bytes 196616 | tf_op jit(solution)/shard_map/ppermute | solution.py:335
  60.6 7.6 %collective-permute-start.9 = (f32[128,128]{1,0:T(8,128)S(1)}, f32[128,128]{1,0:T(8,128)S(1)}, u32[]{:S(2)}, u32[]{:S(2)}) collective-permute-start(f32[128,128]{1,0:T(8,128)S(1)} %get-tuple-element.20), channel_id=1, source_target_pairs={{0,64},{32,96},{64,128},{96,160},{128,192},{160,224},{192,0},{224,... | collective-permute-start | bytes 196616 | tf_op jit(solution)/shard_map/ppermute | solution.py:335
  62.4 6.7 %collective-permute-start.10 = (f32[128,128]{1,0:T(8,128)S(1)}, f32[128,128]{1,0:T(8,128)S(1)}, u32[]{:S(2)}, u32[]{:S(2)}) collective-permute-start(f32[128,128]{1,0:T(8,128)S(1)} %get-tuple-element.21), channel_id=1, source_target_pairs={{0,192},{32,224},{64,0},{96,32},{128,64},{160,96},{192,128},{224,1... | collective-permute-start | bytes 196616 | tf_op jit(solution)/shard_map/ppermute | solution.py:335
  69.2 4.9 %collective-permute-start.13 = (f32[10,32]{1,0:T(8,128)S(1)}, f32[10,32]{1,0:T(8,128)S(1)}, u32[]{:S(2)}, u32[]{:S(2)}) collective-permute-start(f32[10,32]{1,0:T(8,128)S(1)} %get-tuple-element.23), channel_id=1, source_target_pairs={{0,3},{1,0},{2,1},{3,2},{4,7},{5,4},{6,5},{7,6},{8,11},{9,8},{10,9... | collective-permute-start | bytes 3848 | tf_op jit(solution)/shard_map/ppermute | solution.py:21
  70.0 4.1 %collective-permute-start.12 = (f32[10,32]{1,0:T(8,128)S(1)}, f32[10,32]{1,0:T(8,128)S(1)}, u32[]{:S(2)}, u32[]{:S(2)}) collective-permute-start(f32[10,32]{1,0:T(8,128)S(1)} %get-tuple-element.23), channel_id=1, source_target_pairs={{0,1},{1,2},{2,3},{3,0},{4,5},{5,6},{6,7},{7,4},{8,9},{9,10},{10,1... | collective-permute-start | bytes 3848 | tf_op jit(solution)/shard_map/ppermute | solution.py:21
  72.5 5.2 %collective-permute-start.11 = (f32[10,32]{1,0:T(8,128)S(1)}, f32[10,32]{1,0:T(8,128)S(1)}, u32[]{:S(2)}, u32[]{:S(2)}) collective-permute-start(f32[10,32]{1,0:T(8,128)S(1)} %get-tuple-element.23), channel_id=1, source_target_pairs={{0,2},{1,3},{2,0},{3,1},{4,6},{5,7},{6,4},{7,5},{8,10},{9,11},{10,... | collective-permute-start | bytes 3848 | tf_op jit(solution)/shard_map/ppermute | solution.py:21

commit v11 on v10

--- a/solution.py
+++ b/solution.py
@@ -331,10 +331,12 @@
     here, up, over, down = local_kernel(
         join_kernel, (block,) * group, (own, soon, late_low, late_high)
     )
-    over, up, down = (
-        lax.ppermute(piece, Z, [(i, (i + parities * by) % depth) for i in range(depth)])
-        for piece, by in ((over, 2), (up, 1), (down, 3))
-    )
+    moves = []
+    for piece, by in ((up, 1), (down, 3), (over, 2)):
+        moves.append(
+            lax.ppermute(piece, Z, [(i, (i + parities * by) % depth) for i in range(depth)])
+        )
+    up, down, over = moves
     pairs = count * (count + 1) // 2
     products, summed = local_kernel(
         pairs_kernel,

time: 78.9 us -> 78.9 us (level)
  no operation moved by 1% of the time
where the time goes in v11:
time: 78.9 us; the launch traced here: 78.3 us
  waiting for transfers between devices  32.1 us (41%)
  starting transfers between devices  30.1 us (38%)
  Pallas kernels  14.7 us (19%)
    pallas_call x12, Pallas kernels, local_kernel(): pl.pallas_call(kernel, in_specs=[HBM if k in in_hbm else VMEM for k in ra...  14.7 us
    ppermute x1, waiting for transfers between devices, body(): part = lax.ppermute(tables, Z + ('c',), pairs)  9.7 us
    ppermute x5, starting transfers between devices, shifted(): lax.ppermute(value, axis, [(i, (i + by) % size) for i in range(size)])  9.58 us
    all_to_all x1, starting transfers between devices, body(): ids = lax.all_to_all(ids, ('zq', 'x'), 0, 0, tiled=True)  8.24 us
    all_to_all x1, waiting for transfers between devices, body(): ids = lax.all_to_all(ids, ('zq', 'x'), 0, 0, tiled=True)  7.83 us
    ppermute x5, waiting for transfers between devices, by_core(): return lax.ppermute(value, ('x', 'c'), pairs)  5.77 us
    ppermute x3, starting transfers between devices, body(): lax.ppermute(piece, Z, [(i, (i + parities * by) % depth) for i in range(d...  5.67 us
    ppermute x5, starting transfers between devices, by_core(): return lax.ppermute(value, ('x', 'c'), pairs)  4.61 us
  transfers between devices with their start and end apart: 15, of which 10 were waited for; matrix products, arithmetic and copies ran while one was open for 0% of the time, Pallas kernels for 14%

profile of v11, /device:TPU:24, one launch (start us, length us, event | category | flops | bytes accessed | tf_op | source)
XLA Modules:
  0.0 78.3 jit_solution(12471646581340054903)
XLA Ops:
  0.6 2.0 %collective-permute-start.1 = (f32[4,512,128]{2,1,0:T(8,128)}, f32[4,512,128]{2,1,0:T(8,128)}, u32[]{:S(2)}, u32[]{:S(2)}) collective-permute-start(f32[4,512,128]{2,1,0:T(8,128)} %refs_0_.1), channel_id=1, source_target_pairs={{0,32},{4,228},{32,0},{36,68},{64,96},{68,36},{96,64},{100,132},{1... | collective-permute-start | bytes 3145736 | tf_op jit(solution)/shard_map/ppermute | solution.py:289
  2.6 3.5 %collective-permute-start = (f32[4,512,128]{2,1,0:T(8,128)}, f32[4,512,128]{2,1,0:T(8,128)}, u32[]{:S(2)}, u32[]{:S(2)}) collective-permute-start(f32[4,512,128]{2,1,0:T(8,128)} %refs_0_.1), channel_id=1, source_target_pairs={{0,4},{4,0},{1,5},{5,1},{2,6},{6,2},{3,7},{7,3},{8,12},{12,8},{9,1... | collective-permute-start | bytes 3145736 | tf_op jit(solution)/shard_map/ppermute | solution.py:21
  6.1 9.7 %collective-permute-done.1.refs_0_ = f32[4,512,128]{2,1,0:T(8,128)} collective-permute-done((f32[4,512,128]{2,1,0:T(8,128)}, f32[4,512,128]{2,1,0:T(8,128)}, u32[]{:S(2)}, u32[]{:S(2)}) %collective-permute-start.1) | collective-permute-done | bytes 1048608 | tf_op jit(solution)/shard_map/ppermute | solution.py:289
  15.8 2.8 %collective-permute-start.2 = (f32[4,512,128]{2,1,0:T(8,128)}, f32[4,512,128]{2,1,0:T(8,128)}, u32[]{:S(2)}, u32[]{:S(2)}) collective-permute-start(f32[4,512,128]{2,1,0:T(8,128)} %collective-permute-done.1.refs_0_), channel_id=1, source_target_pairs={{0,4},{4,0},{1,5},{5,1},{2,6},{6,2},{3,7},{7,3},{8,12},{12,8},{9,1... | collective-permute-start | bytes 3145736 | tf_op jit(solution)/shard_map/ppermute | solution.py:21
  18.6 1.8 %shard_map.68 = s32[4,4,16,128]{3,2,1,0:T(8,128)} custom-call(s32[4,64]{1,0:T(4,128)} %bitcast.16, s32[8,4,8,64]{3,2,1,0:T(8,128)} %bitcast.14, s32[8,4,8,64]{3,2,1,0:T(8,128)} %bitcast.15), custom_call_target="tpu_custom_call" | custom-call | flops 1048576 | bytes 1048576 | tf_op jit(solution)/shard_map/pallas_call | solution.py:26
  20.4 8.2 %all-to-all-start = ((s32[16,16,128]{2,1,0:T(8,128)}), s32[16,16,128]{2,1,0:T(8,128)S(1)}, u32[]{:S(2)}, u32[]{:S(2)}) async-start(s32[16,16,128]{2,1,0:T(8,128)} %bitcast.13), calls=%async_computation | async-start | bytes 262144 | tf_op jit(solution)/shard_map/all_to_all | solution.py:307
  28.7 1.5 %shard_map.70.refs_2_ = bf16[4,512,256]{2,1,0:T(8,128)(2,1)S(1)} custom-call(f32[4,512,128]{2,1,0:T(8,128)} %collective-permute-done.1.refs_0_), custom_call_target="tpu_custom_call" | custom-call | flops 1048576 | bytes 1048576 | tf_op jit(solution)/shard_map/pallas_call | solution.py:26
  30.2 1.7 %shard_map.69.refs_1_ = bf16[8,512,256]{2,1,0:T(8,128)(2,1)S(1)} custom-call(f32[4,512,128]{2,1,0:T(8,128)S(1)} %copy-done, f32[4,512,128]{2,1,0:T(8,128)} %collective-permute-done.refs_1_), custom_call_target="tpu_custom_call" | custom-call | flops 1048576 | bytes 1048576 | tf_op jit(solution)/shard_map/pallas_call | solution.py:26
  31.9 7.8 %all-to-all-done = s32[16,16,128]{2,1,0:T(8,128)S(1)} async-done(((s32[16,16,128]{2,1,0:T(8,128)}), s32[16,16,128]{2,1,0:T(8,128)S(1)}, u32[]{:S(2)}, u32[]{:S(2)}) %all-to-all-start) | async-done | bytes 131104 | tf_op jit(solution)/shard_map/all_to_all | solution.py:307
  39.7 2.4 %shard_map.71 = (f32[4,64,128]{2,1,0:T(8,128)S(1)}, bf16[4,512,256]{2,1,0:T(8,128)(2,1)S(1)}) custom-call(s32[4,4,16,128]{3,2,1,0:T(8,128)S(1)} %bitcast.9, bf16[8,512,256]{2,1,0:T(8,128)(2,1)S(1)} %shard_map.69.refs_1_, bf16[4,512,256]{2,1,0:T(8,128)(2,1)S(1)} %shard_map.70.refs_2_, f32[4,512,128]{2,1,0:T(8,128)} %collective-permute-done.2.refs_3_), custom_call_target="tpu_custom_call" | custom-call | flops 671088640 | bytes 1048576 | tf_op jit(solution)/shard_map/pallas_call | solution.py:26
  42.1 1.2 %shard_map.75 = f32[4,64,128]{2,1,0:T(8,128)S(1)} custom-call(s32[4,4,16,128]{3,2,1,0:T(8,128)S(1)} %bitcast.10, bf16[8,512,256]{2,1,0:T(8,128)(2,1)S(1)} %shard_map.69.refs_1_, bf16[4,512,256]{2,1,0:T(8,128)(2,1)S(1)} %shard_map.70.refs_2_, bf16[4,512,256]{2,1,0:T(8,128)(2,1)S(1)} %get-tuple-element.13.refs_3_), custom_call_target="tpu_custom_call" | custom-call | flops 671088640 | bytes 1048576 | tf_op jit(solution)/shard_map/pallas_call | solution.py:26
  43.3 0.3 collective-permute-start.6
  43.7 1.3 %collective-permute-start.4 = (f32[4,64,128]{2,1,0:T(8,128)S(1)}, f32[4,64,128]{2,1,0:T(8,128)S(1)}, u32[]{:S(2)}, u32[]{:S(2)}) collective-permute-start(f32[4,64,128]{2,1,0:T(8,128)S(1)} %get-tuple-element.16), channel_id=1, source_target_pairs={{0,8},{4,28},{8,16},{12,4},{16,24},{20,12},{24,0},{28,20},{1,9},{5... | collective-permute-start | bytes 393224 | tf_op jit(solution)/shard_map/ppermute | solution.py:238
  44.9 3.2 %shard_map.73 = (f32[4,128,128]{2,1,0:T(8,128)S(1)}, f32[4,64,128]{2,1,0:T(8,128)S(1)}, f32[4,64,128]{2,1,0:T(8,128)S(1)}) custom-call(s32[4,4,16,128]{3,2,1,0:T(8,128)S(1)} %bitcast.11, bf16[8,512,256]{2,1,0:T(8,128)(2,1)S(1)} %shard_map.69.refs_1_, bf16[4,512,256]{2,1,0:T(8,128)(2,1)S(1)} %shard_map.70.refs_2_, ...), custom_call_target="tpu_custom_call" | custom-call | flops 2684354560 | bytes 1048576 | tf_op jit(solution)/shard_map/pallas_call | solution.py:26
  48.1 2.1 %collective-permute-start.3 = (f32[4,128,128]{2,1,0:T(8,128)S(1)}, f32[4,128,128]{2,1,0:T(8,128)S(1)}, u32[]{:S(2)}, u32[]{:S(2)}) collective-permute-start(f32[4,128,128]{2,1,0:T(8,128)S(1)} %get-tuple-element.14), channel_id=1, source_target_pairs={{0,24},{4,12},{8,0},{12,20},{16,8},{20,28},{24,16},{28,4},{1,25},{... | collective-permute-start | bytes 786440 | tf_op jit(solution)/shard_map/ppermute | solution.py:238
  50.1 1.2 %collective-permute-done.4.two_ref = f32[4,64,128]{2,1,0:T(8,128)S(1)} collective-permute-done((f32[4,64,128]{2,1,0:T(8,128)S(1)}, f32[4,64,128]{2,1,0:T(8,128)S(1)}, u32[]{:S(2)}, u32[]{:S(2)}) %collective-permute-start.4) | collective-permute-done | bytes 131104 | tf_op jit(solution)/shard_map/ppermute | solution.py:238
  51.5 0.9 %collective-permute-start.7 = (f32[4,64,128]{2,1,0:T(8,128)S(1)}, f32[4,64,128]{2,1,0:T(8,128)S(1)}, u32[]{:S(2)}, u32[]{:S(2)}) collective-permute-start(f32[4,64,128]{2,1,0:T(8,128)S(1)} %shard_map.76), channel_id=1, source_target_pairs={{0,8},{4,28},{8,16},{12,4},{16,24},{20,12},{24,0},{28,20},{1,9},{5... | collective-permute-start | bytes 393224 | tf_op jit(solution)/shard_map/ppermute | solution.py:238
  52.3 2.0 %shard_map.72.own_ref = f32[4,128,128]{2,1,0:T(8,128)S(1)} custom-call(s32[4,4,16,128]{3,2,1,0:T(8,128)S(1)} %bitcast.12, bf16[8,512,256]{2,1,0:T(8,128)(2,1)S(1)} %shard_map.69.refs_1_, bf16[4,512,256]{2,1,0:T(8,128)(2,1)S(1)} %shard_map.70.refs_2_, bf16[4,512,256]{2,1,0:T(8,128)(2,1)S(1)} %get-tuple-element.13.refs_3_), custom_call_target="tpu_custom_call" | custom-call | flops 1342177280 | bytes 1048576 | tf_op jit(solution)/shard_map/pallas_call | solution.py:26
  54.4 1.6 %collective-permute-done.3.soon_ref = f32[4,128,128]{2,1,0:T(8,128)S(1)} collective-permute-done((f32[4,128,128]{2,1,0:T(8,128)S(1)}, f32[4,128,128]{2,1,0:T(8,128)S(1)}, u32[]{:S(2)}, u32[]{:S(2)}) %collective-permute-start.3) | collective-permute-done | bytes 262176 | tf_op jit(solution)/shard_map/ppermute | solution.py:238
  55.9 1.6 %collective-permute-done.5.low_ref = f32[4,64,128]{2,1,0:T(8,128)S(1)} collective-permute-done((f32[4,64,128]{2,1,0:T(8,128)S(1)}, f32[4,64,128]{2,1,0:T(8,128)S(1)}, u32[]{:S(2)}, u32[]{:S(2)}) %collective-permute-start.5) | collective-permute-done | bytes 131104 | tf_op jit(solution)/shard_map/ppermute | solution.py:238
  57.6 1.4 %collective-permute-done.7.high_ref = f32[4,64,128]{2,1,0:T(8,128)S(1)} collective-permute-done((f32[4,64,128]{2,1,0:T(8,128)S(1)}, f32[4,64,128]{2,1,0:T(8,128)S(1)}, u32[]{:S(2)}, u32[]{:S(2)}) %collective-permute-start.7) | collective-permute-done | bytes 131104 | tf_op jit(solution)/shard_map/ppermute | solution.py:238
  59.0 1.5 %collective-permute-start.8 = (f32[128,128]{1,0:T(8,128)S(1)}, f32[128,128]{1,0:T(8,128)S(1)}, u32[]{:S(2)}, u32[]{:S(2)}) collective-permute-start(f32[128,128]{1,0:T(8,128)S(1)} %get-tuple-element.19), channel_id=1, source_target_pairs={{0,128},{32,160},{64,192},{96,224},{128,0},{160,32},{192,64},{224,... | collective-permute-start | bytes 196616 | tf_op jit(solution)/shard_map/ppermute | solution.py:337
  60.6 1.8 %collective-permute-start.9 = (f32[128,128]{1,0:T(8,128)S(1)}, f32[128,128]{1,0:T(8,128)S(1)}, u32[]{:S(2)}, u32[]{:S(2)}) collective-permute-start(f32[128,128]{1,0:T(8,128)S(1)} %get-tuple-element.20), channel_id=1, source_target_pairs={{0,64},{32,96},{64,128},{96,160},{128,192},{160,224},{192,0},{224,... | collective-permute-start | bytes 196616 | tf_op jit(solution)/shard_map/ppermute | solution.py:337
  62.4 2.3 %collective-permute-start.10 = (f32[128,128]{1,0:T(8,128)S(1)}, f32[128,128]{1,0:T(8,128)S(1)}, u32[]{:S(2)}, u32[]{:S(2)}) collective-permute-start(f32[128,128]{1,0:T(8,128)S(1)} %get-tuple-element.21), channel_id=1, source_target_pairs={{0,192},{32,224},{64,0},{96,32},{128,64},{160,96},{192,128},{224,1... | collective-permute-start | bytes 196616 | tf_op jit(solution)/shard_map/ppermute | solution.py:337
  64.7 3.5 %collective-permute-done.8.one_ref = f32[128,128]{1,0:T(8,128)S(1)} collective-permute-done((f32[128,128]{1,0:T(8,128)S(1)}, f32[128,128]{1,0:T(8,128)S(1)}, u32[]{:S(2)}, u32[]{:S(2)}) %collective-permute-start.8) | collective-permute-done | bytes 65568 | tf_op jit(solution)/shard_map/ppermute | solution.py:337
  68.2 0.9 %collective-permute-done.10.three_ref = f32[128,128]{1,0:T(8,128)S(1)} collective-permute-done((f32[128,128]{1,0:T(8,128)S(1)}, f32[128,128]{1,0:T(8,128)S(1)}, u32[]{:S(2)}, u32[]{:S(2)}) %collective-permute-start.10) | collective-permute-done | bytes 65568 | tf_op jit(solution)/shard_map/ppermute | solution.py:337
  69.2 0.8 collective-permute-start.13
  70.0 2.5 %collective-permute-start.12 = (f32[10,32]{1,0:T(8,128)S(1)}, f32[10,32]{1,0:T(8,128)S(1)}, u32[]{:S(2)}, u32[]{:S(2)}) collective-permute-start(f32[10,32]{1,0:T(8,128)S(1)} %get-tuple-element.23), channel_id=1, source_target_pairs={{0,1},{1,2},{2,3},{3,0},{4,5},{5,6},{6,7},{7,4},{8,9},{9,10},{10,1... | collective-permute-start | bytes 3848 | tf_op jit(solution)/shard_map/ppermute | solution.py:21
  72.5 0.7 shard_map.79
  73.2 0.9 %collective-permute-done.13 = f32[10,32]{1,0:T(8,128)S(1)} collective-permute-done((f32[10,32]{1,0:T(8,128)S(1)}, f32[10,32]{1,0:T(8,128)S(1)}, u32[]{:S(2)}, u32[]{:S(2)}) %collective-permute-start.13) | collective-permute-done | bytes 1312 | tf_op jit(solution)/shard_map/ppermute | solution.py:21
  74.1 3.5 %collective-permute-done.11 = f32[10,32]{1,0:T(8,128)S(1)} collective-permute-done((f32[10,32]{1,0:T(8,128)S(1)}, f32[10,32]{1,0:T(8,128)S(1)}, u32[]{:S(2)}, u32[]{:S(2)}) %collective-permute-start.11) | collective-permute-done | bytes 1312 | tf_op jit(solution)/shard_map/ppermute | solution.py:21
  77.7 0.6 multiply_bitcast_fusion
  (15 shorter events, 0.4 us)
Async XLA Ops:
  0.6 15.2 %collective-permute-start.1 = (f32[4,512,128]{2,1,0:T(8,128)}, f32[4,512,128]{2,1,0:T(8,128)}, u32[]{:S(2)}, u32[]{:S(2)}) collective-permute-start(f32[4,512,128]{2,1,0:T(8,128)} %refs_0_.1), channel_id=1, source_target_pairs={{0,32},{4,228},{32,0},{36,68},{64,96},{68,36},{96,64},{100,132},{1... | collective-permute-start | bytes 3145736 | tf_op jit(solution)/shard_map/ppermute | solution.py:289
  2.6 27.6 %collective-permute-start = (f32[4,512,128]{2,1,0:T(8,128)}, f32[4,512,128]{2,1,0:T(8,128)}, u32[]{:S(2)}, u32[]{:S(2)}) collective-permute-start(f32[4,512,128]{2,1,0:T(8,128)} %refs_0_.1), channel_id=1, source_target_pairs={{0,4},{4,0},{1,5},{5,1},{2,6},{6,2},{3,7},{7,3},{8,12},{12,8},{9,1... | collective-permute-start | bytes 3145736 | tf_op jit(solution)/shard_map/ppermute | solution.py:21
  15.8 23.9 %collective-permute-start.2 = (f32[4,512,128]{2,1,0:T(8,128)}, f32[4,512,128]{2,1,0:T(8,128)}, u32[]{:S(2)}, u32[]{:S(2)}) collective-permute-start(f32[4,512,128]{2,1,0:T(8,128)} %collective-permute-done.1.refs_0_), channel_id=1, source_target_pairs={{0,4},{4,0},{1,5},{5,1},{2,6},{6,2},{3,7},{7,3},{8,12},{12,8},{9,1... | collective-permute-start | bytes 3145736 | tf_op jit(solution)/shard_map/ppermute | solution.py:21
  20.4 19.3 %all-to-all-start = ((s32[16,16,128]{2,1,0:T(8,128)}), s32[16,16,128]{2,1,0:T(8,128)S(1)}, u32[]{:S(2)}, u32[]{:S(2)}) async-start(s32[16,16,128]{2,1,0:T(8,128)} %bitcast.13), calls=%async_computation | async-start | bytes 262144 | tf_op jit(solution)/shard_map/all_to_all | solution.py:307
  28.6 1.6 %copy-start = (f32[4,512,128]{2,1,0:T(8,128)S(1)}, f32[4,512,128]{2,1,0:T(8,128)}, u32[]{:S(2)}) copy-start(f32[4,512,128]{2,1,0:T(8,128)} %refs_0_.1) | copy-start | bytes 3145732
  43.3 8.1 %collective-permute-start.6 = (f32[4,64,128]{2,1,0:T(8,128)S(1)}, f32[4,64,128]{2,1,0:T(8,128)S(1)}, u32[]{:S(2)}, u32[]{:S(2)}) collective-permute-start(f32[4,64,128]{2,1,0:T(8,128)S(1)} %shard_map.75), channel_id=1, source_target_pairs={{0,8},{4,28},{8,16},{12,4},{16,24},{20,12},{24,0},{28,20},{1,9},{5... | collective-permute-start | bytes 393224 | tf_op jit(solution)/shard_map/ppermute | solution.py:238
  43.7 7.6 %collective-permute-start.4 = (f32[4,64,128]{2,1,0:T(8,128)S(1)}, f32[4,64,128]{2,1,0:T(8,128)S(1)}, u32[]{:S(2)}, u32[]{:S(2)}) collective-permute-start(f32[4,64,128]{2,1,0:T(8,128)S(1)} %get-tuple-element.16), channel_id=1, source_target_pairs={{0,8},{4,28},{8,16},{12,4},{16,24},{20,12},{24,0},{28,20},{1,9},{5... | collective-permute-start | bytes 393224 | tf_op jit(solution)/shard_map/ppermute | solution.py:238
  48.1 7.9 %collective-permute-start.3 = (f32[4,128,128]{2,1,0:T(8,128)S(1)}, f32[4,128,128]{2,1,0:T(8,128)S(1)}, u32[]{:S(2)}, u32[]{:S(2)}) collective-permute-start(f32[4,128,128]{2,1,0:T(8,128)S(1)} %get-tuple-element.14), channel_id=1, source_target_pairs={{0,24},{4,12},{8,0},{12,20},{16,8},{20,28},{24,16},{28,4},{1,25},{... | collective-permute-start | bytes 786440 | tf_op jit(solution)/shard_map/ppermute | solution.py:238
  51.3 6.3 %collective-permute-start.5 = (f32[4,64,128]{2,1,0:T(8,128)S(1)}, f32[4,64,128]{2,1,0:T(8,128)S(1)}, u32[]{:S(2)}, u32[]{:S(2)}) collective-permute-start(f32[4,64,128]{2,1,0:T(8,128)S(1)} %shard_map.74), channel_id=1, source_target_pairs={{0,8},{4,28},{8,16},{12,4},{16,24},{20,12},{24,0},{28,20},{1,9},{5... | collective-permute-start | bytes 393224 | tf_op jit(solution)/shard_map/ppermute | solution.py:238
  51.4 17.6 %copy-start.1 = (f32[32,128]{1,0:T(8,128)S(1)}, f32[32,128]{1,0:T(8,128)}, u32[]{:S(2)}) copy-start(f32[32,128]{1,0:T(8,128)} %dense_ref.1) | copy-start | bytes 49156
  51.5 7.5 %collective-permute-start.7 = (f32[4,64,128]{2,1,0:T(8,128)S(1)}, f32[4,64,128]{2,1,0:T(8,128)S(1)}, u32[]{:S(2)}, u32[]{:S(2)}) collective-permute-start(f32[4,64,128]{2,1,0:T(8,128)S(1)} %shard_map.76), channel_id=1, source_target_pairs={{0,8},{4,28},{8,16},{12,4},{16,24},{20,12},{24,0},{28,20},{1,9},{5... | collective-permute-start | bytes 393224 | tf_op jit(solution)/shard_map/ppermute | solution.py:238
  59.0 9.1 %collective-permute-start.8 = (f32[128,128]{1,0:T(8,128)S(1)}, f32[128,128]{1,0:T(8,128)S(1)}, u32[]{:S(2)}, u32[]{:S(2)}) collective-permute-start(f32[128,128]{1,0:T(8,128)S(1)} %get-tuple-element.19), channel_id=1, source_target_pairs={{0,128},{32,160},{64,192},{96,224},{128,0},{160,32},{192,64},{224,... | collective-permute-start | bytes 196616 | tf_op jit(solution)/shard_map/ppermute | solution.py:337
  60.6 7.6 %collective-permute-start.9 = (f32[128,128]{1,0:T(8,128)S(1)}, f32[128,128]{1,0:T(8,128)S(1)}, u32[]{:S(2)}, u32[]{:S(2)}) collective-permute-start(f32[128,128]{1,0:T(8,128)S(1)} %get-tuple-element.20), channel_id=1, source_target_pairs={{0,64},{32,96},{64,128},{96,160},{128,192},{160,224},{192,0},{224,... | collective-permute-start | bytes 196616 | tf_op jit(solution)/shard_map/ppermute | solution.py:337
  62.4 6.7 %collective-permute-start.10 = (f32[128,128]{1,0:T(8,128)S(1)}, f32[128,128]{1,0:T(8,128)S(1)}, u32[]{:S(2)}, u32[]{:S(2)}) collective-permute-start(f32[128,128]{1,0:T(8,128)S(1)} %get-tuple-element.21), channel_id=1, source_target_pairs={{0,192},{32,224},{64,0},{96,32},{128,64},{160,96},{192,128},{224,1... | collective-permute-start | bytes 196616 | tf_op jit(solution)/shard_map/ppermute | solution.py:337
  69.2 4.9 %collective-permute-start.13 = (f32[10,32]{1,0:T(8,128)S(1)}, f32[10,32]{1,0:T(8,128)S(1)}, u32[]{:S(2)}, u32[]{:S(2)}) collective-permute-start(f32[10,32]{1,0:T(8,128)S(1)} %get-tuple-element.23), channel_id=1, source_target_pairs={{0,3},{1,0},{2,1},{3,2},{4,7},{5,4},{6,5},{7,6},{8,11},{9,8},{10,9... | collective-permute-start | bytes 3848 | tf_op jit(solution)/shard_map/ppermute | solution.py:21
  70.0 4.1 %collective-permute-start.12 = (f32[10,32]{1,0:T(8,128)S(1)}, f32[10,32]{1,0:T(8,128)S(1)}, u32[]{:S(2)}, u32[]{:S(2)}) collective-permute-start(f32[10,32]{1,0:T(8,128)S(1)} %get-tuple-element.23), channel_id=1, source_target_pairs={{0,1},{1,2},{2,3},{3,0},{4,5},{5,6},{6,7},{7,4},{8,9},{9,10},{10,1... | collective-permute-start | bytes 3848 | tf_op jit(solution)/shard_map/ppermute | solution.py:21
  72.5 5.2 %collective-permute-start.11 = (f32[10,32]{1,0:T(8,128)S(1)}, f32[10,32]{1,0:T(8,128)S(1)}, u32[]{:S(2)}, u32[]{:S(2)}) collective-permute-start(f32[10,32]{1,0:T(8,128)S(1)} %get-tuple-element.23), channel_id=1, source_target_pairs={{0,2},{1,3},{2,0},{3,1},{4,6},{5,7},{6,4},{7,5},{8,10},{9,11},{10,... | collective-permute-start | bytes 3848 | tf_op jit(solution)/shard_map/ppermute | solution.py:21

commit v12 on v10

--- a/solution.py
+++ b/solution.py
@@ -155,20 +155,22 @@
     def look(o, t):
         ref, place = ((near_ref, t), (near_ref, count + t), (part_ref, t), (shared_ref, t))[o]
         message = o * count + t
+        active = [k for k, a in enumerate(aways) if any(a == b and t in c for b, c in parts)]
         picks = jnp.concatenate(
             [
                 one_hot(
-                    one[:slots, j * messages + message : j * messages + message + 1] == row_iota
+                    columns[k][:slots, j * messages + message : j * messages + message + 1]
+                    == row_iota
                 )
-                for one in columns
+                for k in active
                 for j in range(group)
             ],
             axis=0,
         )
         looked = jnp.dot(picks, ref[place], preferred_element_type=jnp.float32)
-        for k in range(len(aways)):
+        for n, k in enumerate(active):
             looked_ref[k, t, o * block : (o + 1) * block, :] = looked[
-                k * block : (k + 1) * block
+                n * block : (n + 1) * block
             ].astype(jnp.bfloat16)
 
     def pool(k, t, out_ref, place):
@@ -315,12 +317,10 @@
 
     far_low, shared = bags(ids, near, part, shared, examples, (((2, 2), low),), raw=True)
     far_low = by_core(far_low, 1, ring)
-    (far_high,) = bags(ids, near, part, shared, examples, (((2, 2), high),))
+    far_high, soon = bags(ids, near, part, shared, examples, (((2, 2), high), ((3, 1), whole)))
     far_high = by_core(far_high, 1, ring)
-    soon, late_low, late_high = bags(
-        ids, near, part, shared, examples, (((3, 1), whole), ((1, 3), low), ((1, 3), high))
-    )
     soon = by_core(soon, -1, ring)
+    late_low, late_high = bags(ids, near, part, shared, examples, (((1, 3), low), ((1, 3), high)))
     piece = jax.ShapeDtypeStruct(late_low.shape, late_low.dtype)
     late_low = local_kernel(add_kernel, piece, (late_low, far_low))
     late_low = by_core(late_low, 1, ring)

time: 78.9 us -> 79.1 us (level)
  transfers between devices with their start and end apart: 15 -> 15, of which waited for: 10 -> 10; matrix products, arithmetic and copies ran while one was open for 0% -> 0% of each run, Pallas kernels for 14% -> 16%
where the time goes in v12:
time: 79.1 us; the launch traced here: 78.5 us
  waiting for transfers between devices  32.7 us (41%)
  starting transfers between devices  29.5 us (37%)
  Pallas kernels  14.9 us (19%)
    pallas_call x12, Pallas kernels, local_kernel(): pl.pallas_call(kernel, in_specs=[HBM if k in in_hbm else VMEM for k in ra...  14.9 us
    ppermute x1, waiting for transfers between devices, body(): part = lax.ppermute(tables, Z + ('c',), pairs)  9.7 us
    ppermute x5, starting transfers between devices, shifted(): lax.ppermute(value, axis, [(i, (i + by) % size) for i in range(size)])  9.58 us
    all_to_all x1, starting transfers between devices, body(): ids = lax.all_to_all(ids, ('zq', 'x'), 0, 0, tiled=True)  8.24 us
    all_to_all x1, waiting for transfers between devices, body(): ids = lax.all_to_all(ids, ('zq', 'x'), 0, 0, tiled=True)  7.83 us
    ppermute x5, waiting for transfers between devices, by_core(): return lax.ppermute(value, ('x', 'c'), pairs)  6.26 us
    ppermute x3, starting transfers between devices, body(): lax.ppermute(piece, Z, [(i, (i + parities * by) % depth) for i in range(d...  5.58 us
    ppermute x5, waiting for transfers between devices, shifted(): lax.ppermute(value, axis, [(i, (i + by) % size) for i in range(size)])  4.46 us
  transfers between devices with their start and end apart: 15, of which 10 were waited for; matrix products, arithmetic and copies ran while one was open for 0% of the time, Pallas kernels for 16%

profile of v12, /device:TPU:24, one launch (start us, length us, event | category | flops | bytes accessed | tf_op | source)
XLA Modules:
  0.0 78.5 jit_solution(18051011583836207961)
XLA Ops:
  0.6 2.0 %collective-permute-start.1 = (f32[4,512,128]{2,1,0:T(8,128)}, f32[4,512,128]{2,1,0:T(8,128)}, u32[]{:S(2)}, u32[]{:S(2)}) collective-permute-start(f32[4,512,128]{2,1,0:T(8,128)} %refs_0_.1), channel_id=1, source_target_pairs={{0,32},{4,228},{32,0},{36,68},{64,96},{68,36},{96,64},{100,132},{1... | collective-permute-start | bytes 3145736 | tf_op jit(solution)/shard_map/ppermute | solution.py:291
  2.6 3.5 %collective-permute-start = (f32[4,512,128]{2,1,0:T(8,128)}, f32[4,512,128]{2,1,0:T(8,128)}, u32[]{:S(2)}, u32[]{:S(2)}) collective-permute-start(f32[4,512,128]{2,1,0:T(8,128)} %refs_0_.1), channel_id=1, source_target_pairs={{0,4},{4,0},{1,5},{5,1},{2,6},{6,2},{3,7},{7,3},{8,12},{12,8},{9,1... | collective-permute-start | bytes 3145736 | tf_op jit(solution)/shard_map/ppermute | solution.py:21
  6.1 9.7 %collective-permute-done.1.refs_0_ = f32[4,512,128]{2,1,0:T(8,128)} collective-permute-done((f32[4,512,128]{2,1,0:T(8,128)}, f32[4,512,128]{2,1,0:T(8,128)}, u32[]{:S(2)}, u32[]{:S(2)}) %collective-permute-start.1) | collective-permute-done | bytes 1048608 | tf_op jit(solution)/shard_map/ppermute | solution.py:291
  15.8 2.8 %collective-permute-start.2 = (f32[4,512,128]{2,1,0:T(8,128)}, f32[4,512,128]{2,1,0:T(8,128)}, u32[]{:S(2)}, u32[]{:S(2)}) collective-permute-start(f32[4,512,128]{2,1,0:T(8,128)} %collective-permute-done.1.refs_0_), channel_id=1, source_target_pairs={{0,4},{4,0},{1,5},{5,1},{2,6},{6,2},{3,7},{7,3},{8,12},{12,8},{9,1... | collective-permute-start | bytes 3145736 | tf_op jit(solution)/shard_map/ppermute | solution.py:21
  18.6 1.8 %shard_map.68 = s32[4,4,16,128]{3,2,1,0:T(8,128)} custom-call(s32[4,64]{1,0:T(4,128)} %bitcast.16, s32[8,4,8,64]{3,2,1,0:T(8,128)} %bitcast.14, s32[8,4,8,64]{3,2,1,0:T(8,128)} %bitcast.15), custom_call_target="tpu_custom_call" | custom-call | flops 1048576 | bytes 1048576 | tf_op jit(solution)/shard_map/pallas_call | solution.py:26
  20.4 8.2 %all-to-all-start = ((s32[16,16,128]{2,1,0:T(8,128)}), s32[16,16,128]{2,1,0:T(8,128)S(1)}, u32[]{:S(2)}, u32[]{:S(2)}) async-start(s32[16,16,128]{2,1,0:T(8,128)} %bitcast.13), calls=%async_computation | async-start | bytes 262144 | tf_op jit(solution)/shard_map/all_to_all | solution.py:309
  28.7 1.5 %shard_map.70.refs_2_ = bf16[4,512,256]{2,1,0:T(8,128)(2,1)S(1)} custom-call(f32[4,512,128]{2,1,0:T(8,128)} %collective-permute-done.1.refs_0_), custom_call_target="tpu_custom_call" | custom-call | flops 1048576 | bytes 1048576 | tf_op jit(solution)/shard_map/pallas_call | solution.py:26
  30.2 1.7 %shard_map.69.refs_1_ = bf16[8,512,256]{2,1,0:T(8,128)(2,1)S(1)} custom-call(f32[4,512,128]{2,1,0:T(8,128)S(1)} %copy-done, f32[4,512,128]{2,1,0:T(8,128)} %collective-permute-done.refs_1_), custom_call_target="tpu_custom_call" | custom-call | flops 1048576 | bytes 1048576 | tf_op jit(solution)/shard_map/pallas_call | solution.py:26
  31.9 7.8 %all-to-all-done = s32[16,16,128]{2,1,0:T(8,128)S(1)} async-done(((s32[16,16,128]{2,1,0:T(8,128)}), s32[16,16,128]{2,1,0:T(8,128)S(1)}, u32[]{:S(2)}, u32[]{:S(2)}) %all-to-all-start) | async-done | bytes 131104 | tf_op jit(solution)/shard_map/all_to_all | solution.py:309
  39.7 2.4 %shard_map.71 = (f32[4,64,128]{2,1,0:T(8,128)S(1)}, bf16[4,512,256]{2,1,0:T(8,128)(2,1)S(1)}) custom-call(s32[4,4,16,128]{3,2,1,0:T(8,128)S(1)} %bitcast.9, bf16[8,512,256]{2,1,0:T(8,128)(2,1)S(1)} %shard_map.69.refs_1_, bf16[4,512,256]{2,1,0:T(8,128)(2,1)S(1)} %shard_map.70.refs_2_, f32[4,512,128]{2,1,0:T(8,128)} %collective-permute-done.2.refs_3_), custom_call_target="tpu_custom_call" | custom-call | flops 671088640 | bytes 1048576 | tf_op jit(solution)/shard_map/pallas_call | solution.py:26
  42.1 0.3 collective-permute-start.4
  42.4 2.6 %shard_map.73 = (f32[4,64,128]{2,1,0:T(8,128)S(1)}, f32[4,128,128]{2,1,0:T(8,128)S(1)}) custom-call(s32[4,4,16,128]{3,2,1,0:T(8,128)S(1)} %bitcast.10, bf16[8,512,256]{2,1,0:T(8,128)(2,1)S(1)} %shard_map.69.refs_1_, bf16[4,512,256]{2,1,0:T(8,128)(2,1)S(1)} %shard_map.70.refs_2_, bf16[4,512,256]{2,1,0:T(8,128)(2,1)S(1)} %get-tuple-element.14.refs_3_), custom_call_target="tpu_custom_call" | custom-call | flops 2013265920 | bytes 1048576 | tf_op jit(solution)/shard_map/pallas_call | solution.py:26
  45.0 1.3 %collective-permute-start.6 = (f32[4,64,128]{2,1,0:T(8,128)S(1)}, f32[4,64,128]{2,1,0:T(8,128)S(1)}, u32[]{:S(2)}, u32[]{:S(2)}) collective-permute-start(f32[4,64,128]{2,1,0:T(8,128)S(1)} %get-tuple-element.19), channel_id=1, source_target_pairs={{0,8},{4,28},{8,16},{12,4},{16,24},{20,12},{24,0},{28,20},{1,9},{5... | collective-permute-start | bytes 393224 | tf_op jit(solution)/shard_map/ppermute | solution.py:240
  46.4 2.0 %collective-permute-start.3 = (f32[4,128,128]{2,1,0:T(8,128)S(1)}, f32[4,128,128]{2,1,0:T(8,128)S(1)}, u32[]{:S(2)}, u32[]{:S(2)}) collective-permute-start(f32[4,128,128]{2,1,0:T(8,128)S(1)} %get-tuple-element.15), channel_id=1, source_target_pairs={{0,24},{4,12},{8,0},{12,20},{16,8},{20,28},{24,16},{28,4},{1,25},{... | collective-permute-start | bytes 786440 | tf_op jit(solution)/shard_map/ppermute | solution.py:240
  48.4 2.0 %shard_map.74 = (f32[4,64,128]{2,1,0:T(8,128)S(1)}, f32[4,64,128]{2,1,0:T(8,128)S(1)}) custom-call(s32[4,4,16,128]{3,2,1,0:T(8,128)S(1)} %bitcast.11, bf16[8,512,256]{2,1,0:T(8,128)(2,1)S(1)} %shard_map.69.refs_1_, bf16[4,512,256]{2,1,0:T(8,128)(2,1)S(1)} %shard_map.70.refs_2_, bf16[4,512,256]{2,1,0:T(8,128)(2,1)S(1)} %get-tuple-element.14.refs_3_), custom_call_target="tpu_custom_call" | custom-call | flops 1342177280 | bytes 1048576 | tf_op jit(solution)/shard_map/pallas_call | solution.py:26
  50.5 2.2 %collective-permute-done.6.two_ref = f32[4,64,128]{2,1,0:T(8,128)S(1)} collective-permute-done((f32[4,64,128]{2,1,0:T(8,128)S(1)}, f32[4,64,128]{2,1,0:T(8,128)S(1)}, u32[]{:S(2)}, u32[]{:S(2)}) %collective-permute-start.6) | collective-permute-done | bytes 131104 | tf_op jit(solution)/shard_map/ppermute | solution.py:240
  52.7 0.3 collective-permute-start.7
  53.0 2.0 %shard_map.72.own_ref = f32[4,128,128]{2,1,0:T(8,128)S(1)} custom-call(s32[4,4,16,128]{3,2,1,0:T(8,128)S(1)} %bitcast.12, bf16[8,512,256]{2,1,0:T(8,128)(2,1)S(1)} %shard_map.69.refs_1_, bf16[4,512,256]{2,1,0:T(8,128)(2,1)S(1)} %shard_map.70.refs_2_, bf16[4,512,256]{2,1,0:T(8,128)(2,1)S(1)} %get-tuple-element.14.refs_3_), custom_call_target="tpu_custom_call" | custom-call | flops 1342177280 | bytes 1048576 | tf_op jit(solution)/shard_map/pallas_call | solution.py:26
  55.1 1.6 %collective-permute-done.5.low_ref = f32[4,64,128]{2,1,0:T(8,128)S(1)} collective-permute-done((f32[4,64,128]{2,1,0:T(8,128)S(1)}, f32[4,64,128]{2,1,0:T(8,128)S(1)}, u32[]{:S(2)}, u32[]{:S(2)}) %collective-permute-start.5) | collective-permute-done | bytes 131104 | tf_op jit(solution)/shard_map/ppermute | solution.py:240
  56.7 2.5 %collective-permute-done.7.high_ref = f32[4,64,128]{2,1,0:T(8,128)S(1)} collective-permute-done((f32[4,64,128]{2,1,0:T(8,128)S(1)}, f32[4,64,128]{2,1,0:T(8,128)S(1)}, u32[]{:S(2)}, u32[]{:S(2)}) %collective-permute-start.7) | collective-permute-done | bytes 131104 | tf_op jit(solution)/shard_map/ppermute | solution.py:240
  59.2 1.4 %collective-permute-start.8 = (f32[128,128]{1,0:T(8,128)S(1)}, f32[128,128]{1,0:T(8,128)S(1)}, u32[]{:S(2)}, u32[]{:S(2)}) collective-permute-start(f32[128,128]{1,0:T(8,128)S(1)} %get-tuple-element.21), channel_id=1, source_target_pairs={{0,128},{32,160},{64,192},{96,224},{128,0},{160,32},{192,64},{224,... | collective-permute-start | bytes 196616 | tf_op jit(solution)/shard_map/ppermute | solution.py:335
  60.6 2.5 %collective-permute-start.9 = (f32[128,128]{1,0:T(8,128)S(1)}, f32[128,128]{1,0:T(8,128)S(1)}, u32[]{:S(2)}, u32[]{:S(2)}) collective-permute-start(f32[128,128]{1,0:T(8,128)S(1)} %get-tuple-element.22), channel_id=1, source_target_pairs={{0,64},{32,96},{64,128},{96,160},{128,192},{160,224},{192,0},{224,... | collective-permute-start | bytes 196616 | tf_op jit(solution)/shard_map/ppermute | solution.py:335
  63.2 1.6 %collective-permute-start.10 = (f32[128,128]{1,0:T(8,128)S(1)}, f32[128,128]{1,0:T(8,128)S(1)}, u32[]{:S(2)}, u32[]{:S(2)}) collective-permute-start(f32[128,128]{1,0:T(8,128)S(1)} %get-tuple-element.23), channel_id=1, source_target_pairs={{0,192},{32,224},{64,0},{96,32},{128,64},{160,96},{192,128},{224,1... | collective-permute-start | bytes 196616 | tf_op jit(solution)/shard_map/ppermute | solution.py:335
  64.8 2.9 %collective-permute-done.8.one_ref = f32[128,128]{1,0:T(8,128)S(1)} collective-permute-done((f32[128,128]{1,0:T(8,128)S(1)}, f32[128,128]{1,0:T(8,128)S(1)}, u32[]{:S(2)}, u32[]{:S(2)}) %collective-permute-start.8) | collective-permute-done | bytes 65568 | tf_op jit(solution)/shard_map/ppermute | solution.py:335
  67.8 1.4 %collective-permute-done.10.three_ref = f32[128,128]{1,0:T(8,128)S(1)} collective-permute-done((f32[128,128]{1,0:T(8,128)S(1)}, f32[128,128]{1,0:T(8,128)S(1)}, u32[]{:S(2)}, u32[]{:S(2)}) %collective-permute-start.10) | collective-permute-done | bytes 65568 | tf_op jit(solution)/shard_map/ppermute | solution.py:335
  69.2 0.2 shard_map.78
  69.4 0.8 collective-permute-start.13
  70.2 2.5 %collective-permute-start.12 = (f32[10,32]{1,0:T(8,128)S(1)}, f32[10,32]{1,0:T(8,128)S(1)}, u32[]{:S(2)}, u32[]{:S(2)}) collective-permute-start(f32[10,32]{1,0:T(8,128)S(1)} %get-tuple-element.25), channel_id=1, source_target_pairs={{0,1},{1,2},{2,3},{3,0},{4,5},{5,6},{6,7},{7,4},{8,9},{9,10},{10,1... | collective-permute-start | bytes 3848 | tf_op jit(solution)/shard_map/ppermute | solution.py:21
  72.7 0.7 shard_map.79
  73.4 0.9 %collective-permute-done.13 = f32[10,32]{1,0:T(8,128)S(1)} collective-permute-done((f32[10,32]{1,0:T(8,128)S(1)}, f32[10,32]{1,0:T(8,128)S(1)}, u32[]{:S(2)}, u32[]{:S(2)}) %collective-permute-start.13) | collective-permute-done | bytes 1312 | tf_op jit(solution)/shard_map/ppermute | solution.py:21
  74.3 3.5 %collective-permute-done.11 = f32[10,32]{1,0:T(8,128)S(1)} collective-permute-done((f32[10,32]{1,0:T(8,128)S(1)}, f32[10,32]{1,0:T(8,128)S(1)}, u32[]{:S(2)}, u32[]{:S(2)}) %collective-permute-start.11) | collective-permute-done | bytes 1312 | tf_op jit(solution)/shard_map/ppermute | solution.py:21
  77.8 0.6 multiply_bitcast_fusion
  (15 shorter events, 0.4 us)
Async XLA Ops:
  0.6 15.2 %collective-permute-start.1 = (f32[4,512,128]{2,1,0:T(8,128)}, f32[4,512,128]{2,1,0:T(8,128)}, u32[]{:S(2)}, u32[]{:S(2)}) collective-permute-start(f32[4,512,128]{2,1,0:T(8,128)} %refs_0_.1), channel_id=1, source_target_pairs={{0,32},{4,228},{32,0},{36,68},{64,96},{68,36},{96,64},{100,132},{1... | collective-permute-start | bytes 3145736 | tf_op jit(solution)/shard_map/ppermute | solution.py:291
  2.6 27.6 %collective-permute-start = (f32[4,512,128]{2,1,0:T(8,128)}, f32[4,512,128]{2,1,0:T(8,128)}, u32[]{:S(2)}, u32[]{:S(2)}) collective-permute-start(f32[4,512,128]{2,1,0:T(8,128)} %refs_0_.1), channel_id=1, source_target_pairs={{0,4},{4,0},{1,5},{5,1},{2,6},{6,2},{3,7},{7,3},{8,12},{12,8},{9,1... | collective-permute-start | bytes 3145736 | tf_op jit(solution)/shard_map/ppermute | solution.py:21
  15.8 23.9 %collective-permute-start.2 = (f32[4,512,128]{2,1,0:T(8,128)}, f32[4,512,128]{2,1,0:T(8,128)}, u32[]{:S(2)}, u32[]{:S(2)}) collective-permute-start(f32[4,512,128]{2,1,0:T(8,128)} %collective-permute-done.1.refs_0_), channel_id=1, source_target_pairs={{0,4},{4,0},{1,5},{5,1},{2,6},{6,2},{3,7},{7,3},{8,12},{12,8},{9,1... | collective-permute-start | bytes 3145736 | tf_op jit(solution)/shard_map/ppermute | solution.py:21
  20.4 19.3 %all-to-all-start = ((s32[16,16,128]{2,1,0:T(8,128)}), s32[16,16,128]{2,1,0:T(8,128)S(1)}, u32[]{:S(2)}, u32[]{:S(2)}) async-start(s32[16,16,128]{2,1,0:T(8,128)} %bitcast.13), calls=%async_computation | async-start | bytes 262144 | tf_op jit(solution)/shard_map/all_to_all | solution.py:309
  28.7 1.6 %copy-start = (f32[4,512,128]{2,1,0:T(8,128)S(1)}, f32[4,512,128]{2,1,0:T(8,128)}, u32[]{:S(2)}) copy-start(f32[4,512,128]{2,1,0:T(8,128)} %refs_0_.1) | copy-start | bytes 3145732
  42.1 8.3 %collective-permute-start.4 = (f32[4,64,128]{2,1,0:T(8,128)S(1)}, f32[4,64,128]{2,1,0:T(8,128)S(1)}, u32[]{:S(2)}, u32[]{:S(2)}) collective-permute-start(f32[4,64,128]{2,1,0:T(8,128)S(1)} %get-tuple-element.17), channel_id=1, source_target_pairs={{0,8},{4,28},{8,16},{12,4},{16,24},{20,12},{24,0},{28,20},{1,9},{5... | collective-permute-start | bytes 393224 | tf_op jit(solution)/shard_map/ppermute | solution.py:240
  45.0 7.7 %collective-permute-start.6 = (f32[4,64,128]{2,1,0:T(8,128)S(1)}, f32[4,64,128]{2,1,0:T(8,128)S(1)}, u32[]{:S(2)}, u32[]{:S(2)}) collective-permute-start(f32[4,64,128]{2,1,0:T(8,128)S(1)} %get-tuple-element.19), channel_id=1, source_target_pairs={{0,8},{4,28},{8,16},{12,4},{16,24},{20,12},{24,0},{28,20},{1,9},{5... | collective-permute-start | bytes 393224 | tf_op jit(solution)/shard_map/ppermute | solution.py:240
  46.4 8.7 %collective-permute-start.3 = (f32[4,128,128]{2,1,0:T(8,128)S(1)}, f32[4,128,128]{2,1,0:T(8,128)S(1)}, u32[]{:S(2)}, u32[]{:S(2)}) collective-permute-start(f32[4,128,128]{2,1,0:T(8,128)S(1)} %get-tuple-element.15), channel_id=1, source_target_pairs={{0,24},{4,12},{8,0},{12,20},{16,8},{20,28},{24,16},{28,4},{1,25},{... | collective-permute-start | bytes 786440 | tf_op jit(solution)/shard_map/ppermute | solution.py:240
  50.4 6.3 %collective-permute-start.5 = (f32[4,64,128]{2,1,0:T(8,128)S(1)}, f32[4,64,128]{2,1,0:T(8,128)S(1)}, u32[]{:S(2)}, u32[]{:S(2)}) collective-permute-start(f32[4,64,128]{2,1,0:T(8,128)S(1)} %shard_map.75), channel_id=1, source_target_pairs={{0,8},{4,28},{8,16},{12,4},{16,24},{20,12},{24,0},{28,20},{1,9},{5... | collective-permute-start | bytes 393224 | tf_op jit(solution)/shard_map/ppermute | solution.py:240
  52.7 16.5 %copy-start.1 = (f32[32,128]{1,0:T(8,128)S(1)}, f32[32,128]{1,0:T(8,128)}, u32[]{:S(2)}) copy-start(f32[32,128]{1,0:T(8,128)} %dense_ref.1) | copy-start | bytes 49156
  52.7 6.4 %collective-permute-start.7 = (f32[4,64,128]{2,1,0:T(8,128)S(1)}, f32[4,64,128]{2,1,0:T(8,128)S(1)}, u32[]{:S(2)}, u32[]{:S(2)}) collective-permute-start(f32[4,64,128]{2,1,0:T(8,128)S(1)} %shard_map.76), channel_id=1, source_target_pairs={{0,8},{4,28},{8,16},{12,4},{16,24},{20,12},{24,0},{28,20},{1,9},{5... | collective-permute-start | bytes 393224 | tf_op jit(solution)/shard_map/ppermute | solution.py:240
  59.2 8.5 %collective-permute-start.8 = (f32[128,128]{1,0:T(8,128)S(1)}, f32[128,128]{1,0:T(8,128)S(1)}, u32[]{:S(2)}, u32[]{:S(2)}) collective-permute-start(f32[128,128]{1,0:T(8,128)S(1)} %get-tuple-element.21), channel_id=1, source_target_pairs={{0,128},{32,160},{64,192},{96,224},{128,0},{160,32},{192,64},{224,... | collective-permute-start | bytes 196616 | tf_op jit(solution)/shard_map/ppermute | solution.py:335
  60.6 7.2 %collective-permute-start.9 = (f32[128,128]{1,0:T(8,128)S(1)}, f32[128,128]{1,0:T(8,128)S(1)}, u32[]{:S(2)}, u32[]{:S(2)}) collective-permute-start(f32[128,128]{1,0:T(8,128)S(1)} %get-tuple-element.22), channel_id=1, source_target_pairs={{0,64},{32,96},{64,128},{96,160},{128,192},{160,224},{192,0},{224,... | collective-permute-start | bytes 196616 | tf_op jit(solution)/shard_map/ppermute | solution.py:335
  63.2 6.1 %collective-permute-start.10 = (f32[128,128]{1,0:T(8,128)S(1)}, f32[128,128]{1,0:T(8,128)S(1)}, u32[]{:S(2)}, u32[]{:S(2)}) collective-permute-start(f32[128,128]{1,0:T(8,128)S(1)} %get-tuple-element.23), channel_id=1, source_target_pairs={{0,192},{32,224},{64,0},{96,32},{128,64},{160,96},{192,128},{224,1... | collective-permute-start | bytes 196616 | tf_op jit(solution)/shard_map/ppermute | solution.py:335
  69.4 4.9 %collective-permute-start.13 = (f32[10,32]{1,0:T(8,128)S(1)}, f32[10,32]{1,0:T(8,128)S(1)}, u32[]{:S(2)}, u32[]{:S(2)}) collective-permute-start(f32[10,32]{1,0:T(8,128)S(1)} %get-tuple-element.25), channel_id=1, source_target_pairs={{0,3},{1,0},{2,1},{3,2},{4,7},{5,4},{6,5},{7,6},{8,11},{9,8},{10,9... | collective-permute-start | bytes 3848 | tf_op jit(solution)/shard_map/ppermute | solution.py:21
  70.2 4.1 %collective-permute-start.12 = (f32[10,32]{1,0:T(8,128)S(1)}, f32[10,32]{1,0:T(8,128)S(1)}, u32[]{:S(2)}, u32[]{:S(2)}) collective-permute-start(f32[10,32]{1,0:T(8,128)S(1)} %get-tuple-element.25), channel_id=1, source_target_pairs={{0,1},{1,2},{2,3},{3,0},{4,5},{5,6},{6,7},{7,4},{8,9},{9,10},{10,1... | collective-permute-start | bytes 3848 | tf_op jit(solution)/shard_map/ppermute | solution.py:21
  72.7 5.2 %collective-permute-start.11 = (f32[10,32]{1,0:T(8,128)S(1)}, f32[10,32]{1,0:T(8,128)S(1)}, u32[]{:S(2)}, u32[]{:S(2)}) collective-permute-start(f32[10,32]{1,0:T(8,128)S(1)} %get-tuple-element.25), channel_id=1, source_target_pairs={{0,2},{1,3},{2,0},{3,1},{4,6},{5,7},{6,4},{7,5},{8,10},{9,11},{10,... | collective-permute-start | bytes 3848 | tf_op jit(solution)/shard_map/ppermute | solution.py:21

commit v13 on v10

--- a/solution.py
+++ b/solution.py
@@ -113,25 +113,10 @@
     return jnp.where(mask, 1.0, 0.0).astype(jnp.bfloat16)
 
 
-def bags_kernel(*refs, examples, count, parts, raw):
+def bags_kernel(*refs, examples, count, parts):
     ids_ref, near_ref, part_ref, shared_ref, *refs = refs
     out_refs, refs = refs[: len(parts)], refs[len(parts) :]
-    if raw:
-        shared_hbm = shared_ref
-        shared_ref, looked_ref, full_ref, sems = refs
-        half = count // 2
-        copies = [
-            pltpu.make_async_copy(
-                shared_hbm.at[k * half : (k + 1) * half],
-                full_ref.at[k * half : (k + 1) * half],
-                sems.at[k],
-            )
-            for k in range(2)
-        ]
-        for copy in copies:
-            copy.start()
-    else:
-        (looked_ref,) = refs
+    (looked_ref,) = refs
     group, ring, messages, lanes = ids_ref.shape
     rows, wide = near_ref.shape[1:]
     owners = messages // count
@@ -183,28 +168,15 @@
             group, examples, wide // 2
         )
 
-    early = owners - 1 if raw else 0
-    tables = tuple(dict.fromkeys(t for _, chosen in parts for t in chosen))
-    for t in tables:
-        for o in range(early):
-            look(o, t)
-    if raw:
-        copies[0].wait()
-    for t in tables:
-        if raw:
-            split_into(shared_ref, t, full_ref[t])
-        for o in range(early, owners):
+    for t in dict.fromkeys(t for _, chosen in parts for t in chosen):
+        for o in range(owners):
             look(o, t)
         for (away, chosen), out_ref in zip(parts, out_refs):
             if t in chosen:
                 pool(aways.index(away), t, out_ref, chosen.index(t))
-    if raw:
-        copies[1].wait()
-        for t in range(half, count):
-            split_into(shared_ref, t, full_ref[t])
-
-
-def bags(ids, near, part, shared, examples, parts, raw=False):
+
+
+def bags(ids, near, part, shared, examples, parts):
     group, _, messages, lanes = ids.shape
     count, rows, wide = part.shape
     tasks = sum(len(tables) for _, tables in parts)
@@ -217,18 +189,74 @@
     scratch = [
         pltpu.VMEM((chunks, count, messages // count * group * lanes // 2, wide), jnp.bfloat16)
     ]
-    if raw:
-        out += (jax.ShapeDtypeStruct(part.shape, part.dtype),)
-        scratch += [pltpu.VMEM(shared.shape, jnp.float32), pltpu.SemaphoreType.DMA((2,))]
     return local_kernel(
-        functools.partial(bags_kernel, examples=examples, count=count, parts=parts, raw=raw),
+        functools.partial(bags_kernel, examples=examples, count=count, parts=parts),
         out,
         (ids, near, part, shared),
         flops=2 * work * wide * (rows + group * examples),
         vmem=20 << 20,
         scratch=scratch,
-        in_hbm=(3,) if raw else (),
-    )
+    )
+
+
+def far_chunk(ids_ref, examples):
+    group, ring, _, lanes = ids_ref.shape
+    column = lax.rem(lax.axis_index("x") + ring // 2, ring)
+    depth = lax.axis_index("zq")
+    ids = [ids_ref[lax.rem(depth + j, group), column] for j in range(group)]
+    columns = jnp.swapaxes(jnp.concatenate(ids, axis=0), 0, 1)[: lanes // 2]
+    keys = jnp.concatenate([ids[j][:, lanes // 2 :] + j * examples for j in range(group)], axis=1)
+    return columns, keys
+
+
+def far_look(ids_ref, columns, message, table):
+    group, _, messages, lanes = ids_ref.shape
+    row_iota = lax.broadcasted_iota(jnp.int32, (lanes // 2, table.shape[0]), 1)
+    picks = jnp.concatenate(
+        [
+            one_hot(columns[:, j * messages + message : j * messages + message + 1] == row_iota)
+            for j in range(group)
+        ],
+        axis=0,
+    )
+    looked = jnp.dot(picks, table, preferred_element_type=jnp.float32)
+    return looked.astype(jnp.bfloat16)
+
+
+def far_look_kernel(
+    ids_ref, near_ref, part_ref, shared_hbm, looked_ref, shared_ref, full_ref, sem, *, examples
+):
+    copy = pltpu.make_async_copy(shared_hbm, full_ref, sem)
+    copy.start()
+    count = part_ref.shape[0]
+    block = ids_ref.shape[0] * ids_ref.shape[3] // 2
+    columns, _ = far_chunk(ids_ref, examples)
+    for t in range(count):
+        for o, ref in enumerate((near_ref.at[t], near_ref.at[count + t], part_ref.at[t])):
+            looked_ref[t, o * block : (o + 1) * block, :] = far_look(
+                ids_ref, columns, o * count + t, ref[...]
+            )
+    copy.wait()
+    for t in range(count):
+        split_into(shared_ref, t, full_ref[t])
+
+
+def far_pool_kernel(ids_ref, shared_ref, looked_ref, out_ref, *, examples, tables):
+    group, _, messages, lanes = ids_ref.shape
+    count, _, wide = shared_ref.shape
+    owners = messages // count
+    columns, keys = far_chunk(ids_ref, examples)
+    key_iota = lax.broadcasted_iota(jnp.int32, (group * examples, group * lanes // 2), 0)
+    for place, t in enumerate(tables):
+        last = far_look(ids_ref, columns, (owners - 1) * count + t, shared_ref[t])
+        into = [one_hot(keys[o * count + t : o * count + t + 1] == key_iota) for o in range(owners)]
+        total = jnp.dot(
+            jnp.concatenate(into[:-1], axis=1), looked_ref[t], preferred_element_type=jnp.float32
+        ) + jnp.dot(into[-1], last, preferred_element_type=jnp.float32)
+        summed = total[:, : wide // 2] + total[:, wide // 2 :]
+        out_ref[:, place * examples : (place + 1) * examples, :] = summed.reshape(
+            group, examples, wide // 2
+        )
 
 
 def by_core(value, by, ring):
@@ -275,7 +303,7 @@
 
 
 def body(embedding, tables, dense_features, slot_rows, slot_examples, slot_counts):
-    count, _, width = tables.shape
+    count, rows, width = tables.shape
     examples = dense_features.shape[0]
     capacity = slot_rows.shape[3]
     group, parities, ring, cores = (lax.axis_size(a) for a in ROWS)
@@ -313,9 +341,31 @@
     low, high = tuple(range(count // 2)), tuple(range(count // 2, count))
     whole = low + high
 
-    far_low, shared = bags(ids, near, part, shared, examples, (((2, 2), low),), raw=True)
+    block = group * capacity
+    looked, shared = local_kernel(
+        functools.partial(far_look_kernel, examples=examples),
+        (
+            jax.ShapeDtypeStruct((count, (2 * cores - 1) * block, 2 * width), jnp.bfloat16),
+            jax.ShapeDtypeStruct(part.shape, part.dtype),
+        ),
+        (ids, near, part, shared),
+        flops=2 * 3 * cores * count * block * rows * width,
+        vmem=16 << 20,
+        scratch=[pltpu.VMEM(shared.shape, jnp.float32), pltpu.SemaphoreType.DMA],
+        in_hbm=(3,),
+    )
+
+    def far_pool(tables):
+        return local_kernel(
+            functools.partial(far_pool_kernel, examples=examples, tables=tables),
+            jax.ShapeDtypeStruct((group, len(tables) * examples, width), jnp.float32),
+            (ids, shared, looked),
+            flops=4 * len(tables) * block * rows * width,
+        )
+
+    far_low = far_pool(low)
     far_low = by_core(far_low, 1, ring)
-    (far_high,) = bags(ids, near, part, shared, examples, (((2, 2), high),))
+    far_high = far_pool(high)
     far_high = by_core(far_high, 1, ring)
     soon, late_low, late_high = bags(
         ids, near, part, shared, examples, (((3, 1), whole), ((1, 3), low), ((1, 3), high))
@@ -327,9 +377,9 @@
     late_high = local_kernel(add_kernel, piece, (late_high, far_high))
     late_high = by_core(late_high, 1, ring)
     (own,) = bags(ids, near, part, shared, examples, (((0, 0), whole),))
-    block = jax.ShapeDtypeStruct(own.shape[1:], jnp.float32)
+    final = jax.ShapeDtypeStruct(own.shape[1:], jnp.float32)
     here, up, over, down = local_kernel(
-        join_kernel, (block,) * group, (own, soon, late_low, late_high)
+        join_kernel, (final,) * group, (own, soon, late_low, late_high)
     )
     over, up, down = (
         lax.ppermute(piece, Z, [(i, (i + parities * by) % depth) for i in range(depth)])

time: 78.9 us -> 77.2 us (0.978)
    pallas_call x12 -> x13, Pallas kernels: 14.7 us -> 14.1 us  [local_kernel(): pl.pallas_call(kernel, in_specs=[HBM if k in in_hbm else VMEM for k in ra...]
  transfers between devices with their start and end apart: 15 -> 15, of which waited for: 10 -> 11; matrix products, arithmetic and copies ran while one was open for 0% -> 0% of each run, Pallas kernels for 14% -> 14%
where the time goes in v13:
time: 77.2 us; the launch traced here: 76.7 us
  waiting for transfers between devices  31.5 us (41%)
  starting transfers between devices  29.7 us (38%)
  Pallas kernels  14.1 us (18%)
    pallas_call x13, Pallas kernels, local_kernel(): pl.pallas_call(kernel, in_specs=[HBM if k in in_hbm else VMEM for k in ra...  14.1 us
    ppermute x1, waiting for transfers between devices, body(): part = lax.ppermute(tables, Z + ('c',), pairs)  9.7 us
    ppermute x5, starting transfers between devices, shifted(): lax.ppermute(value, axis, [(i, (i + by) % size) for i in range(size)])  9.58 us
    all_to_all x1, starting transfers between devices, body(): ids = lax.all_to_all(ids, ('zq', 'x'), 0, 0, tiled=True)  8.24 us
    all_to_all x1, waiting for transfers between devices, body(): ids = lax.all_to_all(ids, ('zq', 'x'), 0, 0, tiled=True)  7.83 us
    ppermute x3, starting transfers between devices, body(): lax.ppermute(piece, Z, [(i, (i + parities * by) % depth) for i in range(d...  5.74 us
    ppermute x5, waiting for transfers between devices, by_core(): return lax.ppermute(value, ('x', 'c'), pairs)  5.08 us
    ppermute x5, waiting for transfers between devices, shifted(): lax.ppermute(value, axis, [(i, (i + by) % size) for i in range(size)])  4.46 us
  transfers between devices with their start and end apart: 15, of which 11 were waited for; matrix products, arithmetic and copies ran while one was open for 0% of the time, Pallas kernels for 14%

profile of v13, /device:TPU:24, one launch (start us, length us, event | category | flops | bytes accessed | tf_op | source)
XLA Modules:
  0.0 76.7 jit_solution(2109103569929160475)
XLA Ops:
  0.6 2.0 %collective-permute-start.1 = (f32[4,512,128]{2,1,0:T(8,128)}, f32[4,512,128]{2,1,0:T(8,128)}, u32[]{:S(2)}, u32[]{:S(2)}) collective-permute-start(f32[4,512,128]{2,1,0:T(8,128)} %refs_0_.1), channel_id=1, source_target_pairs={{0,32},{4,228},{32,0},{36,68},{64,96},{68,36},{96,64},{100,132},{1... | collective-permute-start | bytes 3145736 | tf_op jit(solution)/shard_map/ppermute | solution.py:317
  2.6 3.5 %collective-permute-start = (f32[4,512,128]{2,1,0:T(8,128)}, f32[4,512,128]{2,1,0:T(8,128)}, u32[]{:S(2)}, u32[]{:S(2)}) collective-permute-start(f32[4,512,128]{2,1,0:T(8,128)} %refs_0_.1), channel_id=1, source_target_pairs={{0,4},{4,0},{1,5},{5,1},{2,6},{6,2},{3,7},{7,3},{8,12},{12,8},{9,1... | collective-permute-start | bytes 3145736 | tf_op jit(solution)/shard_map/ppermute | solution.py:21
  6.1 9.7 %collective-permute-done.1.refs_0_ = f32[4,512,128]{2,1,0:T(8,128)} collective-permute-done((f32[4,512,128]{2,1,0:T(8,128)}, f32[4,512,128]{2,1,0:T(8,128)}, u32[]{:S(2)}, u32[]{:S(2)}) %collective-permute-start.1) | collective-permute-done | bytes 1048608 | tf_op jit(solution)/shard_map/ppermute | solution.py:317
  15.8 2.8 %collective-permute-start.2 = (f32[4,512,128]{2,1,0:T(8,128)}, f32[4,512,128]{2,1,0:T(8,128)}, u32[]{:S(2)}, u32[]{:S(2)}) collective-permute-start(f32[4,512,128]{2,1,0:T(8,128)} %collective-permute-done.1.refs_0_), channel_id=1, source_target_pairs={{0,4},{4,0},{1,5},{5,1},{2,6},{6,2},{3,7},{7,3},{8,12},{12,8},{9,1... | collective-permute-start | bytes 3145736 | tf_op jit(solution)/shard_map/ppermute | solution.py:21
  18.6 1.8 %shard_map.68 = s32[4,4,16,128]{3,2,1,0:T(8,128)} custom-call(s32[4,64]{1,0:T(4,128)} %bitcast.17, s32[8,4,8,64]{3,2,1,0:T(8,128)} %bitcast.15, s32[8,4,8,64]{3,2,1,0:T(8,128)} %bitcast.16), custom_call_target="tpu_custom_call" | custom-call | flops 1048576 | bytes 1048576 | tf_op jit(solution)/shard_map/pallas_call | solution.py:26
  20.4 8.2 %all-to-all-start = ((s32[16,16,128]{2,1,0:T(8,128)}), s32[16,16,128]{2,1,0:T(8,128)S(1)}, u32[]{:S(2)}, u32[]{:S(2)}) async-start(s32[16,16,128]{2,1,0:T(8,128)} %bitcast.14), calls=%async_computation | async-start | bytes 262144 | tf_op jit(solution)/shard_map/all_to_all | solution.py:335
  28.7 1.5 %shard_map.70.part_ref.refs_2_ = bf16[4,512,256]{2,1,0:T(8,128)(2,1)S(1)} custom-call(f32[4,512,128]{2,1,0:T(8,128)} %collective-permute-done.1.refs_0_), custom_call_target="tpu_custom_call" | custom-call | flops 1048576 | bytes 1048576 | tf_op jit(solution)/shard_map/pallas_call | solution.py:26
  30.2 1.7 %shard_map.69.near_ref.refs_1_ = bf16[8,512,256]{2,1,0:T(8,128)(2,1)S(1)} custom-call(f32[4,512,128]{2,1,0:T(8,128)S(1)} %copy-done, f32[4,512,128]{2,1,0:T(8,128)} %collective-permute-done.refs_1_), custom_call_target="tpu_custom_call" | custom-call | flops 1048576 | bytes 1048576 | tf_op jit(solution)/shard_map/pallas_call | solution.py:26
  31.9 7.8 %all-to-all-done = s32[16,16,128]{2,1,0:T(8,128)S(1)} async-done(((s32[16,16,128]{2,1,0:T(8,128)}), s32[16,16,128]{2,1,0:T(8,128)S(1)}, u32[]{:S(2)}, u32[]{:S(2)}) %all-to-all-start) | async-done | bytes 131104 | tf_op jit(solution)/shard_map/all_to_all | solution.py:335
  39.7 1.5 %shard_map.71 = (bf16[4,768,256]{2,1,0:T(8,128)(2,1)S(1)}, bf16[4,512,256]{2,1,0:T(8,128)(2,1)S(1)}) custom-call(s32[4,4,16,128]{3,2,1,0:T(8,128)S(1)} %bitcast.9, bf16[8,512,256]{2,1,0:T(8,128)(2,1)S(1)} %shard_map.69.near_ref.refs_1_, bf16[4,512,256]{2,1,0:T(8,128)(2,1)S(1)} %shard_map.70.part_ref.refs_2_, f32[4,512,128]{2,1,0:T(8,128)} %collective-permute-done.2.shared_hbm), custom_call_target="tpu_custom_call" | custom-call | flops 805306368 | bytes 1048576 | tf_op jit(solution)/shard_map/pallas_call | solution.py:26
  41.2 0.8 %shard_map.76 = f32[4,64,128]{2,1,0:T(8,128)S(1)} custom-call(s32[4,4,16,128]{3,2,1,0:T(8,128)S(1)} %bitcast.10, bf16[4,512,256]{2,1,0:T(8,128)(2,1)S(1)} %get-tuple-element.13.refs_3_.shared_ref, bf16[4,768,256]{2,1,0:T(8,128)(2,1)S(1)} %get-tuple-element.16.looked_ref), custom_call_target="tpu_custom_call" | custom-call | flops 134217728 | bytes 1048576 | tf_op jit(solution)/shard_map/pallas_call | solution.py:26
  42.0 0.8 %shard_map.74 = f32[4,64,128]{2,1,0:T(8,128)S(1)} custom-call(s32[4,4,16,128]{3,2,1,0:T(8,128)S(1)} %bitcast.11, bf16[4,512,256]{2,1,0:T(8,128)(2,1)S(1)} %get-tuple-element.13.refs_3_.shared_ref, bf16[4,768,256]{2,1,0:T(8,128)(2,1)S(1)} %get-tuple-element.16.looked_ref), custom_call_target="tpu_custom_call" | custom-call | flops 134217728 | bytes 1048576 | tf_op jit(solution)/shard_map/pallas_call | solution.py:26
  43.1 1.3 %collective-permute-start.6 = (f32[4,64,128]{2,1,0:T(8,128)S(1)}, f32[4,64,128]{2,1,0:T(8,128)S(1)}, u32[]{:S(2)}, u32[]{:S(2)}) collective-permute-start(f32[4,64,128]{2,1,0:T(8,128)S(1)} %shard_map.76), channel_id=1, source_target_pairs={{0,8},{4,28},{8,16},{12,4},{16,24},{20,12},{24,0},{28,20},{1,9},{5... | collective-permute-start | bytes 393224 | tf_op jit(solution)/shard_map/ppermute | solution.py:266
  44.4 3.2 %shard_map.73 = (f32[4,128,128]{2,1,0:T(8,128)S(1)}, f32[4,64,128]{2,1,0:T(8,128)S(1)}, f32[4,64,128]{2,1,0:T(8,128)S(1)}) custom-call(s32[4,4,16,128]{3,2,1,0:T(8,128)S(1)} %bitcast.12, bf16[8,512,256]{2,1,0:T(8,128)(2,1)S(1)} %shard_map.69.near_ref.refs_1_, bf16[4,512,256]{2,1,0:T(8,128)(2,1)S(1)} %shard_map.70.part_ref.refs_2_, ...), custom_call_target="tpu_custom_call" | custom-call | flops 2684354560 | bytes 1048576 | tf_op jit(solution)/shard_map/pallas_call | solution.py:26
  47.5 2.1 %collective-permute-start.3 = (f32[4,128,128]{2,1,0:T(8,128)S(1)}, f32[4,128,128]{2,1,0:T(8,128)S(1)}, u32[]{:S(2)}, u32[]{:S(2)}) collective-permute-start(f32[4,128,128]{2,1,0:T(8,128)S(1)} %get-tuple-element.14), channel_id=1, source_target_pairs={{0,24},{4,12},{8,0},{12,20},{16,8},{20,28},{24,16},{28,4},{1,25},{... | collective-permute-start | bytes 786440 | tf_op jit(solution)/shard_map/ppermute | solution.py:266
  49.7 1.0 %collective-permute-done.6.two_ref = f32[4,64,128]{2,1,0:T(8,128)S(1)} collective-permute-done((f32[4,64,128]{2,1,0:T(8,128)S(1)}, f32[4,64,128]{2,1,0:T(8,128)S(1)}, u32[]{:S(2)}, u32[]{:S(2)}) %collective-permute-start.6) | collective-permute-done | bytes 131104 | tf_op jit(solution)/shard_map/ppermute | solution.py:266
  51.2 2.0 %shard_map.72.own_ref = f32[4,128,128]{2,1,0:T(8,128)S(1)} custom-call(s32[4,4,16,128]{3,2,1,0:T(8,128)S(1)} %bitcast.13, bf16[8,512,256]{2,1,0:T(8,128)(2,1)S(1)} %shard_map.69.near_ref.refs_1_, bf16[4,512,256]{2,1,0:T(8,128)(2,1)S(1)} %shard_map.70.part_ref.refs_2_, bf16[4,512,256]{2,1,0:T(8,128)(2,1)S(1)} %get-tuple-element.13.refs_3_.shared_ref), custom_call_target="tpu_custom_call" | custom-call | flops 1342177280 | bytes 1048576 | tf_op jit(solution)/shard_map/pallas_call | solution.py:26
  53.2 2.2 %collective-permute-done.3.soon_ref = f32[4,128,128]{2,1,0:T(8,128)S(1)} collective-permute-done((f32[4,128,128]{2,1,0:T(8,128)S(1)}, f32[4,128,128]{2,1,0:T(8,128)S(1)}, u32[]{:S(2)}, u32[]{:S(2)}) %collective-permute-start.3) | collective-permute-done | bytes 262176 | tf_op jit(solution)/shard_map/ppermute | solution.py:266
  55.4 0.5 collective-permute-done.5.low_ref
  55.9 1.4 %collective-permute-done.7.high_ref = f32[4,64,128]{2,1,0:T(8,128)S(1)} collective-permute-done((f32[4,64,128]{2,1,0:T(8,128)S(1)}, f32[4,64,128]{2,1,0:T(8,128)S(1)}, u32[]{:S(2)}, u32[]{:S(2)}) %collective-permute-start.7) | collective-permute-done | bytes 131104 | tf_op jit(solution)/shard_map/ppermute | solution.py:266
  57.3 1.6 %collective-permute-start.8 = (f32[128,128]{1,0:T(8,128)S(1)}, f32[128,128]{1,0:T(8,128)S(1)}, u32[]{:S(2)}, u32[]{:S(2)}) collective-permute-start(f32[128,128]{1,0:T(8,128)S(1)} %get-tuple-element.19), channel_id=1, source_target_pairs={{0,128},{32,160},{64,192},{96,224},{128,0},{160,32},{192,64},{224,... | collective-permute-start | bytes 196616 | tf_op jit(solution)/shard_map/ppermute | solution.py:385
  58.9 2.4 %collective-permute-start.9 = (f32[128,128]{1,0:T(8,128)S(1)}, f32[128,128]{1,0:T(8,128)S(1)}, u32[]{:S(2)}, u32[]{:S(2)}) collective-permute-start(f32[128,128]{1,0:T(8,128)S(1)} %get-tuple-element.20), channel_id=1, source_target_pairs={{0,64},{32,96},{64,128},{96,160},{128,192},{160,224},{192,0},{224,... | collective-permute-start | bytes 196616 | tf_op jit(solution)/shard_map/ppermute | solution.py:385
  61.3 1.8 %collective-permute-start.10 = (f32[128,128]{1,0:T(8,128)S(1)}, f32[128,128]{1,0:T(8,128)S(1)}, u32[]{:S(2)}, u32[]{:S(2)}) collective-permute-start(f32[128,128]{1,0:T(8,128)S(1)} %get-tuple-element.21), channel_id=1, source_target_pairs={{0,192},{32,224},{64,0},{96,32},{128,64},{160,96},{192,128},{224,1... | collective-permute-start | bytes 196616 | tf_op jit(solution)/shard_map/ppermute | solution.py:385
  63.1 2.7 %collective-permute-done.8.one_ref = f32[128,128]{1,0:T(8,128)S(1)} collective-permute-done((f32[128,128]{1,0:T(8,128)S(1)}, f32[128,128]{1,0:T(8,128)S(1)}, u32[]{:S(2)}, u32[]{:S(2)}) %collective-permute-start.8) | collective-permute-done | bytes 65568 | tf_op jit(solution)/shard_map/ppermute | solution.py:385
  65.8 0.4 collective-permute-done.9.two_ref
  66.2 1.3 %collective-permute-done.10.three_ref = f32[128,128]{1,0:T(8,128)S(1)} collective-permute-done((f32[128,128]{1,0:T(8,128)S(1)}, f32[128,128]{1,0:T(8,128)S(1)}, u32[]{:S(2)}, u32[]{:S(2)}) %collective-permute-start.10) | collective-permute-done | bytes 65568 | tf_op jit(solution)/shard_map/ppermute | solution.py:385
  67.7 0.8 collective-permute-start.13
  68.4 2.5 %collective-permute-start.12 = (f32[10,32]{1,0:T(8,128)S(1)}, f32[10,32]{1,0:T(8,128)S(1)}, u32[]{:S(2)}, u32[]{:S(2)}) collective-permute-start(f32[10,32]{1,0:T(8,128)S(1)} %get-tuple-element.23), channel_id=1, source_target_pairs={{0,1},{1,2},{2,3},{3,0},{4,5},{5,6},{6,7},{7,4},{8,9},{9,10},{10,1... | collective-permute-start | bytes 3848 | tf_op jit(solution)/shard_map/ppermute | solution.py:21
  71.0 0.7 shard_map.80
  71.6 0.9 %collective-permute-done.13 = f32[10,32]{1,0:T(8,128)S(1)} collective-permute-done((f32[10,32]{1,0:T(8,128)S(1)}, f32[10,32]{1,0:T(8,128)S(1)}, u32[]{:S(2)}, u32[]{:S(2)}) %collective-permute-start.13) | collective-permute-done | bytes 1312 | tf_op jit(solution)/shard_map/ppermute | solution.py:21
  72.6 3.5 %collective-permute-done.11 = f32[10,32]{1,0:T(8,128)S(1)} collective-permute-done((f32[10,32]{1,0:T(8,128)S(1)}, f32[10,32]{1,0:T(8,128)S(1)}, u32[]{:S(2)}, u32[]{:S(2)}) %collective-permute-start.11) | collective-permute-done | bytes 1312 | tf_op jit(solution)/shard_map/ppermute | solution.py:21
  76.1 0.6 multiply_bitcast_fusion
  (16 shorter events, 1.2 us)
Async XLA Ops:
  0.6 15.2 %collective-permute-start.1 = (f32[4,512,128]{2,1,0:T(8,128)}, f32[4,512,128]{2,1,0:T(8,128)}, u32[]{:S(2)}, u32[]{:S(2)}) collective-permute-start(f32[4,512,128]{2,1,0:T(8,128)} %refs_0_.1), channel_id=1, source_target_pairs={{0,32},{4,228},{32,0},{36,68},{64,96},{68,36},{96,64},{100,132},{1... | collective-permute-start | bytes 3145736 | tf_op jit(solution)/shard_map/ppermute | solution.py:317
  2.6 27.6 %collective-permute-start = (f32[4,512,128]{2,1,0:T(8,128)}, f32[4,512,128]{2,1,0:T(8,128)}, u32[]{:S(2)}, u32[]{:S(2)}) collective-permute-start(f32[4,512,128]{2,1,0:T(8,128)} %refs_0_.1), channel_id=1, source_target_pairs={{0,4},{4,0},{1,5},{5,1},{2,6},{6,2},{3,7},{7,3},{8,12},{12,8},{9,1... | collective-permute-start | bytes 3145736 | tf_op jit(solution)/shard_map/ppermute | solution.py:21
  15.8 23.9 %collective-permute-start.2 = (f32[4,512,128]{2,1,0:T(8,128)}, f32[4,512,128]{2,1,0:T(8,128)}, u32[]{:S(2)}, u32[]{:S(2)}) collective-permute-start(f32[4,512,128]{2,1,0:T(8,128)} %collective-permute-done.1.refs_0_), channel_id=1, source_target_pairs={{0,4},{4,0},{1,5},{5,1},{2,6},{6,2},{3,7},{7,3},{8,12},{12,8},{9,1... | collective-permute-start | bytes 3145736 | tf_op jit(solution)/shard_map/ppermute | solution.py:21
  20.4 19.3 %all-to-all-start = ((s32[16,16,128]{2,1,0:T(8,128)}), s32[16,16,128]{2,1,0:T(8,128)S(1)}, u32[]{:S(2)}, u32[]{:S(2)}) async-start(s32[16,16,128]{2,1,0:T(8,128)} %bitcast.14), calls=%async_computation | async-start | bytes 262144 | tf_op jit(solution)/shard_map/all_to_all | solution.py:335
  28.6 1.6 %copy-start = (f32[4,512,128]{2,1,0:T(8,128)S(1)}, f32[4,512,128]{2,1,0:T(8,128)}, u32[]{:S(2)}) copy-start(f32[4,512,128]{2,1,0:T(8,128)} %refs_0_.1) | copy-start | bytes 3145732
  42.8 6.8 %collective-permute-start.4 = (f32[4,64,128]{2,1,0:T(8,128)S(1)}, f32[4,64,128]{2,1,0:T(8,128)S(1)}, u32[]{:S(2)}, u32[]{:S(2)}) collective-permute-start(f32[4,64,128]{2,1,0:T(8,128)S(1)} %shard_map.74), channel_id=1, source_target_pairs={{0,8},{4,28},{8,16},{12,4},{16,24},{20,12},{24,0},{28,20},{1,9},{5... | collective-permute-start | bytes 393224 | tf_op jit(solution)/shard_map/ppermute | solution.py:266
  43.1 7.6 %collective-permute-start.6 = (f32[4,64,128]{2,1,0:T(8,128)S(1)}, f32[4,64,128]{2,1,0:T(8,128)S(1)}, u32[]{:S(2)}, u32[]{:S(2)}) collective-permute-start(f32[4,64,128]{2,1,0:T(8,128)S(1)} %shard_map.76), channel_id=1, source_target_pairs={{0,8},{4,28},{8,16},{12,4},{16,24},{20,12},{24,0},{28,20},{1,9},{5... | collective-permute-start | bytes 393224 | tf_op jit(solution)/shard_map/ppermute | solution.py:266
  47.5 7.9 %collective-permute-start.3 = (f32[4,128,128]{2,1,0:T(8,128)S(1)}, f32[4,128,128]{2,1,0:T(8,128)S(1)}, u32[]{:S(2)}, u32[]{:S(2)}) collective-permute-start(f32[4,128,128]{2,1,0:T(8,128)S(1)} %get-tuple-element.14), channel_id=1, source_target_pairs={{0,24},{4,12},{8,0},{12,20},{16,8},{20,28},{24,16},{28,4},{1,25},{... | collective-permute-start | bytes 786440 | tf_op jit(solution)/shard_map/ppermute | solution.py:266
  49.6 6.3 %collective-permute-start.5 = (f32[4,64,128]{2,1,0:T(8,128)S(1)}, f32[4,64,128]{2,1,0:T(8,128)S(1)}, u32[]{:S(2)}, u32[]{:S(2)}) collective-permute-start(f32[4,64,128]{2,1,0:T(8,128)S(1)} %shard_map.75), channel_id=1, source_target_pairs={{0,8},{4,28},{8,16},{12,4},{16,24},{20,12},{24,0},{28,20},{1,9},{5... | collective-permute-start | bytes 393224 | tf_op jit(solution)/shard_map/ppermute | solution.py:266
  50.8 16.7 %copy-start.1 = (f32[32,128]{1,0:T(8,128)S(1)}, f32[32,128]{1,0:T(8,128)}, u32[]{:S(2)}) copy-start(f32[32,128]{1,0:T(8,128)} %dense_ref.1) | copy-start | bytes 49156
  50.8 6.5 %collective-permute-start.7 = (f32[4,64,128]{2,1,0:T(8,128)S(1)}, f32[4,64,128]{2,1,0:T(8,128)S(1)}, u32[]{:S(2)}, u32[]{:S(2)}) collective-permute-start(f32[4,64,128]{2,1,0:T(8,128)S(1)} %shard_map.77), channel_id=1, source_target_pairs={{0,8},{4,28},{8,16},{12,4},{16,24},{20,12},{24,0},{28,20},{1,9},{5... | collective-permute-start | bytes 393224 | tf_op jit(solution)/shard_map/ppermute | solution.py:266
  57.3 8.5 %collective-permute-start.8 = (f32[128,128]{1,0:T(8,128)S(1)}, f32[128,128]{1,0:T(8,128)S(1)}, u32[]{:S(2)}, u32[]{:S(2)}) collective-permute-start(f32[128,128]{1,0:T(8,128)S(1)} %get-tuple-element.19), channel_id=1, source_target_pairs={{0,128},{32,160},{64,192},{96,224},{128,0},{160,32},{192,64},{224,... | collective-permute-start | bytes 196616 | tf_op jit(solution)/shard_map/ppermute | solution.py:385
  58.9 7.2 %collective-permute-start.9 = (f32[128,128]{1,0:T(8,128)S(1)}, f32[128,128]{1,0:T(8,128)S(1)}, u32[]{:S(2)}, u32[]{:S(2)}) collective-permute-start(f32[128,128]{1,0:T(8,128)S(1)} %get-tuple-element.20), channel_id=1, source_target_pairs={{0,64},{32,96},{64,128},{96,160},{128,192},{160,224},{192,0},{224,... | collective-permute-start | bytes 196616 | tf_op jit(solution)/shard_map/ppermute | solution.py:385
  61.3 6.2 %collective-permute-start.10 = (f32[128,128]{1,0:T(8,128)S(1)}, f32[128,128]{1,0:T(8,128)S(1)}, u32[]{:S(2)}, u32[]{:S(2)}) collective-permute-start(f32[128,128]{1,0:T(8,128)S(1)} %get-tuple-element.21), channel_id=1, source_target_pairs={{0,192},{32,224},{64,0},{96,32},{128,64},{160,96},{192,128},{224,1... | collective-permute-start | bytes 196616 | tf_op jit(solution)/shard_map/ppermute | solution.py:385
  67.7 4.9 %collective-permute-start.13 = (f32[10,32]{1,0:T(8,128)S(1)}, f32[10,32]{1,0:T(8,128)S(1)}, u32[]{:S(2)}, u32[]{:S(2)}) collective-permute-start(f32[10,32]{1,0:T(8,128)S(1)} %get-tuple-element.23), channel_id=1, source_target_pairs={{0,3},{1,0},{2,1},{3,2},{4,7},{5,4},{6,5},{7,6},{8,11},{9,8},{10,9... | collective-permute-start | bytes 3848 | tf_op jit(solution)/shard_map/ppermute | solution.py:21
  68.4 4.1 %collective-permute-start.12 = (f32[10,32]{1,0:T(8,128)S(1)}, f32[10,32]{1,0:T(8,128)S(1)}, u32[]{:S(2)}, u32[]{:S(2)}) collective-permute-start(f32[10,32]{1,0:T(8,128)S(1)} %get-tuple-element.23), channel_id=1, source_target_pairs={{0,1},{1,2},{2,3},{3,0},{4,5},{5,6},{6,7},{7,4},{8,9},{9,10},{10,1... | collective-permute-start | bytes 3848 | tf_op jit(solution)/shard_map/ppermute | solution.py:21
  70.9 5.2 %collective-permute-start.11 = (f32[10,32]{1,0:T(8,128)S(1)}, f32[10,32]{1,0:T(8,128)S(1)}, u32[]{:S(2)}, u32[]{:S(2)}) collective-permute-start(f32[10,32]{1,0:T(8,128)S(1)} %get-tuple-element.23), channel_id=1, source_target_pairs={{0,2},{1,3},{2,0},{3,1},{4,6},{5,7},{6,4},{7,5},{8,10},{9,11},{10,... | collective-permute-start | bytes 3848 | tf_op jit(solution)/shard_map/ppermute | solution.py:21

commit v14 on v13

--- a/solution.py
+++ b/solution.py
@@ -272,9 +272,14 @@
 
 def join_kernel(own_ref, soon_ref, low_ref, high_ref, *out_refs):
     half = low_ref.shape[1]
-    for j, out_ref in enumerate(out_refs):
+    odd = lax.rem(lax.axis_index("zq"), 2)
+    for j, out_ref in zip((0, 2, 3 - 2 * odd, 1 + 2 * odd), out_refs):
         out_ref[:half] = own_ref[j, :half] + soon_ref[j, :half] + low_ref[j]
         out_ref[half:] = own_ref[j, half:] + soon_ref[j, half:] + high_ref[j]
+
+
+def swapped(value, axis, partner):
+    return lax.ppermute(value, axis, [(i, partner(i)) for i in range(lax.axis_size(axis))])
 
 
 def pairs_kernel(own_ref, one_ref, two_ref, three_ref, dense_ref, pairs_ref, summed_ref):
@@ -367,10 +372,9 @@
     far_low = by_core(far_low, 1, ring)
     far_high = far_pool(high)
     far_high = by_core(far_high, 1, ring)
-    soon, late_low, late_high = bags(
-        ids, near, part, shared, examples, (((3, 1), whole), ((1, 3), low), ((1, 3), high))
-    )
+    (soon,) = bags(ids, near, part, shared, examples, (((3, 1), whole),))
     soon = by_core(soon, -1, ring)
+    late_low, late_high = bags(ids, near, part, shared, examples, (((1, 3), low), ((1, 3), high)))
     piece = jax.ShapeDtypeStruct(late_low.shape, late_low.dtype)
     late_low = local_kernel(add_kernel, piece, (late_low, far_low))
     late_low = by_core(late_low, 1, ring)
@@ -378,13 +382,12 @@
     late_high = by_core(late_high, 1, ring)
     (own,) = bags(ids, near, part, shared, examples, (((0, 0), whole),))
     final = jax.ShapeDtypeStruct(own.shape[1:], jnp.float32)
-    here, up, over, down = local_kernel(
+    here, *others = local_kernel(
         join_kernel, (final,) * group, (own, soon, late_low, late_high)
     )
-    over, up, down = (
-        lax.ppermute(piece, Z, [(i, (i + parities * by) % depth) for i in range(depth)])
-        for piece, by in ((over, 2), (up, 1), (down, 3))
-    )
+    partners = (lambda i: i ^ 2, lambda i: 3 - i, lambda i: i ^ 1)
+    for k, partner in enumerate(partners):
+        others[k] = swapped(others[k], "zq", partner)
     pairs = count * (count + 1) // 2
     products, summed = local_kernel(
         pairs_kernel,
@@ -392,17 +395,17 @@
             jax.ShapeDtypeStruct((pairs, examples), jnp.float32),
             jax.ShapeDtypeStruct((count * examples, width), jnp.float32),
         ),
-        (here, over, up, down, dense_features),
+        (here, *others, dense_features),
     )
     pooled = local_kernel(
         pooled_kernel,
         jax.ShapeDtypeStruct((examples, count, width), jnp.float32),
         (summed,),
     )
-    opposite = shifted(products, "y", 2)
-    after = shifted(products, "y", 1)
-    before = shifted(products, "y", -1)
-    total = ((products + opposite) + (after + before)) * embedding**-0.5
+    got = []
+    for partner in partners:
+        got.append(swapped(products, "y", partner))
+    total = ((products + got[0]) + (got[1] + got[2])) * embedding**-0.5
     return pooled, total.T
 
 

time: 77.2 us -> 79.4 us (1.028); the launches traced: 76.7 us -> 78.1 us
  starting transfers between devices: 29.7 us -> 31.3 us
  waiting for transfers between devices: 31.5 us -> 30.4 us
  Pallas kernels: 14.1 us -> 15 us
    ppermute x3 -> x6, starting transfers between devices: 5.74 us -> 10.7 us  [swapped(): lax.ppermute(value, axis, [(i, partner(i)) for i in range(lax.axis_size(a...]
    ppermute x5 -> x2, waiting for transfers between devices: 4.46 us -> 0.01 us  [shifted(): lax.ppermute(value, axis, [(i, (i + by) % size) for i in range(size)])]
    ppermute x5 -> x2, starting transfers between devices: 9.58 us -> 6.3 us  [shifted(): lax.ppermute(value, axis, [(i, (i + by) % size) for i in range(size)])]
    ppermute x3 -> x6, waiting for transfers between devices: 4.43 us -> 6.29 us  [swapped(): lax.ppermute(value, axis, [(i, partner(i)) for i in range(lax.axis_size(a...]
    ppermute x5, waiting for transfers between devices: 5.08 us -> 6.6 us  [by_core(): return lax.ppermute(value, ('x', 'c'), pairs)]
    pallas_call x13 -> x14, Pallas kernels: 14.1 us -> 15 us  [local_kernel(): pl.pallas_call(kernel, in_specs=[HBM if k in in_hbm else VMEM for k in ra...]
  transfers between devices with their start and end apart: 15 -> 15, of which waited for: 11 -> 10; matrix products, arithmetic and copies ran while one was open for 0% -> 0% of each run, Pallas kernels for 14% -> 15%
where the time goes in v14:
time: 79.4 us; the launch traced here: 78.1 us
  starting transfers between devices  31.3 us (39%)
  waiting for transfers between devices  30.4 us (38%)
  Pallas kernels  15 us (19%)
    pallas_call x14, Pallas kernels, local_kernel(): pl.pallas_call(kernel, in_specs=[HBM if k in in_hbm else VMEM for k in ra...  15 us
    ppermute x6, starting transfers between devices, swapped(): lax.ppermute(value, axis, [(i, partner(i)) for i in range(lax.axis_size(a...  10.7 us
    ppermute x1, waiting for transfers between devices, body(): part = lax.ppermute(tables, Z + ('c',), pairs)  9.7 us
    all_to_all x1, starting transfers between devices, body(): ids = lax.all_to_all(ids, ('zq', 'x'), 0, 0, tiled=True)  8.24 us
    all_to_all x1, waiting for transfers between devices, body(): ids = lax.all_to_all(ids, ('zq', 'x'), 0, 0, tiled=True)  7.83 us
    ppermute x5, waiting for transfers between devices, by_core(): return lax.ppermute(value, ('x', 'c'), pairs)  6.6 us
    ppermute x2, starting transfers between devices, shifted(): lax.ppermute(value, axis, [(i, (i + by) % size) for i in range(size)])  6.3 us
    ppermute x6, waiting for transfers between devices, swapped(): lax.ppermute(value, axis, [(i, partner(i)) for i in range(lax.axis_size(a...  6.29 us
  transfers between devices with their start and end apart: 15, of which 10 were waited for; matrix products, arithmetic and copies ran while one was open for 0% of the time, Pallas kernels for 15%

profile of v14, /device:TPU:24, one launch (start us, length us, event | category | flops | bytes accessed | tf_op | source)
XLA Modules:
  0.0 78.1 jit_solution(5175000000405688790)
XLA Ops:
  0.6 2.0 %collective-permute-start.1 = (f32[4,512,128]{2,1,0:T(8,128)}, f32[4,512,128]{2,1,0:T(8,128)}, u32[]{:S(2)}, u32[]{:S(2)}) collective-permute-start(f32[4,512,128]{2,1,0:T(8,128)} %refs_0_.1), channel_id=1, source_target_pairs={{0,32},{4,228},{32,0},{36,68},{64,96},{68,36},{96,64},{100,132},{1... | collective-permute-start | bytes 3145736 | tf_op jit(solution)/shard_map/ppermute | solution.py:322
  2.6 3.5 %collective-permute-start = (f32[4,512,128]{2,1,0:T(8,128)}, f32[4,512,128]{2,1,0:T(8,128)}, u32[]{:S(2)}, u32[]{:S(2)}) collective-permute-start(f32[4,512,128]{2,1,0:T(8,128)} %refs_0_.1), channel_id=1, source_target_pairs={{0,4},{4,0},{1,5},{5,1},{2,6},{6,2},{3,7},{7,3},{8,12},{12,8},{9,1... | collective-permute-start | bytes 3145736 | tf_op jit(solution)/shard_map/ppermute | solution.py:21
  6.1 9.7 %collective-permute-done.1.refs_0_ = f32[4,512,128]{2,1,0:T(8,128)} collective-permute-done((f32[4,512,128]{2,1,0:T(8,128)}, f32[4,512,128]{2,1,0:T(8,128)}, u32[]{:S(2)}, u32[]{:S(2)}) %collective-permute-start.1) | collective-permute-done | bytes 1048608 | tf_op jit(solution)/shard_map/ppermute | solution.py:322
  15.8 2.8 %collective-permute-start.2 = (f32[4,512,128]{2,1,0:T(8,128)}, f32[4,512,128]{2,1,0:T(8,128)}, u32[]{:S(2)}, u32[]{:S(2)}) collective-permute-start(f32[4,512,128]{2,1,0:T(8,128)} %collective-permute-done.1.refs_0_), channel_id=1, source_target_pairs={{0,4},{4,0},{1,5},{5,1},{2,6},{6,2},{3,7},{7,3},{8,12},{12,8},{9,1... | collective-permute-start | bytes 3145736 | tf_op jit(solution)/shard_map/ppermute | solution.py:21
  18.6 1.8 %shard_map.68 = s32[4,4,16,128]{3,2,1,0:T(8,128)} custom-call(s32[4,64]{1,0:T(4,128)} %bitcast.18, s32[8,4,8,64]{3,2,1,0:T(8,128)} %bitcast.16, s32[8,4,8,64]{3,2,1,0:T(8,128)} %bitcast.17), custom_call_target="tpu_custom_call" | custom-call | flops 1048576 | bytes 1048576 | tf_op jit(solution)/shard_map/pallas_call | solution.py:26
  20.4 8.2 %all-to-all-start = ((s32[16,16,128]{2,1,0:T(8,128)}), s32[16,16,128]{2,1,0:T(8,128)S(1)}, u32[]{:S(2)}, u32[]{:S(2)}) async-start(s32[16,16,128]{2,1,0:T(8,128)} %bitcast.15), calls=%async_computation | async-start | bytes 262144 | tf_op jit(solution)/shard_map/all_to_all | solution.py:340
  28.7 1.5 %shard_map.70.part_ref.refs_2_ = bf16[4,512,256]{2,1,0:T(8,128)(2,1)S(1)} custom-call(f32[4,512,128]{2,1,0:T(8,128)} %collective-permute-done.1.refs_0_), custom_call_target="tpu_custom_call" | custom-call | flops 1048576 | bytes 1048576 | tf_op jit(solution)/shard_map/pallas_call | solution.py:26
  30.2 1.7 %shard_map.69.near_ref.refs_1_ = bf16[8,512,256]{2,1,0:T(8,128)(2,1)S(1)} custom-call(f32[4,512,128]{2,1,0:T(8,128)S(1)} %copy-done, f32[4,512,128]{2,1,0:T(8,128)} %collective-permute-done.refs_1_), custom_call_target="tpu_custom_call" | custom-call | flops 1048576 | bytes 1048576 | tf_op jit(solution)/shard_map/pallas_call | solution.py:26
  31.9 7.8 %all-to-all-done = s32[16,16,128]{2,1,0:T(8,128)S(1)} async-done(((s32[16,16,128]{2,1,0:T(8,128)}), s32[16,16,128]{2,1,0:T(8,128)S(1)}, u32[]{:S(2)}, u32[]{:S(2)}) %all-to-all-start) | async-done | bytes 131104 | tf_op jit(solution)/shard_map/all_to_all | solution.py:340
  39.7 1.5 %shard_map.71 = (bf16[4,768,256]{2,1,0:T(8,128)(2,1)S(1)}, bf16[4,512,256]{2,1,0:T(8,128)(2,1)S(1)}) custom-call(s32[4,4,16,128]{3,2,1,0:T(8,128)S(1)} %bitcast.9, bf16[8,512,256]{2,1,0:T(8,128)(2,1)S(1)} %shard_map.69.near_ref.refs_1_, bf16[4,512,256]{2,1,0:T(8,128)(2,1)S(1)} %shard_map.70.part_ref.refs_2_, f32[4,512,128]{2,1,0:T(8,128)} %collective-permute-done.2.shared_hbm), custom_call_target="tpu_custom_call" | custom-call | flops 805306368 | bytes 1048576 | tf_op jit(solution)/shard_map/pallas_call | solution.py:26
  41.2 0.8 %shard_map.77 = f32[4,64,128]{2,1,0:T(8,128)S(1)} custom-call(s32[4,4,16,128]{3,2,1,0:T(8,128)S(1)} %bitcast.10, bf16[4,512,256]{2,1,0:T(8,128)(2,1)S(1)} %get-tuple-element.12.refs_3_.shared_ref, bf16[4,768,256]{2,1,0:T(8,128)(2,1)S(1)} %get-tuple-element.14.looked_ref), custom_call_target="tpu_custom_call" | custom-call | flops 134217728 | bytes 1048576 | tf_op jit(solution)/shard_map/pallas_call | solution.py:26
  42.0 0.8 %shard_map.75 = f32[4,64,128]{2,1,0:T(8,128)S(1)} custom-call(s32[4,4,16,128]{3,2,1,0:T(8,128)S(1)} %bitcast.11, bf16[4,512,256]{2,1,0:T(8,128)(2,1)S(1)} %get-tuple-element.12.refs_3_.shared_ref, bf16[4,768,256]{2,1,0:T(8,128)(2,1)S(1)} %get-tuple-element.14.looked_ref), custom_call_target="tpu_custom_call" | custom-call | flops 134217728 | bytes 1048576 | tf_op jit(solution)/shard_map/pallas_call | solution.py:26
  43.1 1.3 %collective-permute-start.6 = (f32[4,64,128]{2,1,0:T(8,128)S(1)}, f32[4,64,128]{2,1,0:T(8,128)S(1)}, u32[]{:S(2)}, u32[]{:S(2)}) collective-permute-start(f32[4,64,128]{2,1,0:T(8,128)S(1)} %shard_map.77), channel_id=1, source_target_pairs={{0,8},{4,28},{8,16},{12,4},{16,24},{20,12},{24,0},{28,20},{1,9},{5... | collective-permute-start | bytes 393224 | tf_op jit(solution)/shard_map/ppermute | solution.py:266
  44.4 2.0 %shard_map.73 = f32[4,128,128]{2,1,0:T(8,128)S(1)} custom-call(s32[4,4,16,128]{3,2,1,0:T(8,128)S(1)} %bitcast.12, bf16[8,512,256]{2,1,0:T(8,128)(2,1)S(1)} %shard_map.69.near_ref.refs_1_, bf16[4,512,256]{2,1,0:T(8,128)(2,1)S(1)} %shard_map.70.part_ref.refs_2_, bf16[4,512,256]{2,1,0:T(8,128)(2,1)S(1)} %get-tuple-element.12.refs_3_.shared_ref), custom_call_target="tpu_custom_call" | custom-call | flops 1342177280 | bytes 1048576 | tf_op jit(solution)/shard_map/pallas_call | solution.py:26
  46.4 2.1 %collective-permute-start.3 = (f32[4,128,128]{2,1,0:T(8,128)S(1)}, f32[4,128,128]{2,1,0:T(8,128)S(1)}, u32[]{:S(2)}, u32[]{:S(2)}) collective-permute-start(f32[4,128,128]{2,1,0:T(8,128)S(1)} %shard_map.73), channel_id=1, source_target_pairs={{0,24},{4,12},{8,0},{12,20},{16,8},{20,28},{24,16},{28,4},{1,25},{... | collective-permute-start | bytes 786440 | tf_op jit(solution)/shard_map/ppermute | solution.py:266
  48.5 2.0 %shard_map.74 = (f32[4,64,128]{2,1,0:T(8,128)S(1)}, f32[4,64,128]{2,1,0:T(8,128)S(1)}) custom-call(s32[4,4,16,128]{3,2,1,0:T(8,128)S(1)} %bitcast.13, bf16[8,512,256]{2,1,0:T(8,128)(2,1)S(1)} %shard_map.69.near_ref.refs_1_, bf16[4,512,256]{2,1,0:T(8,128)(2,1)S(1)} %shard_map.70.part_ref.refs_2_, bf16[4,512,256]{2,1,0:T(8,128)(2,1)S(1)} %get-tuple-element.12.refs_3_.shared_ref), custom_call_target="tpu_custom_call" | custom-call | flops 1342177280 | bytes 1048576 | tf_op jit(solution)/shard_map/pallas_call | solution.py:26
  50.5 1.4 %collective-permute-done.6.two_ref = f32[4,64,128]{2,1,0:T(8,128)S(1)} collective-permute-done((f32[4,64,128]{2,1,0:T(8,128)S(1)}, f32[4,64,128]{2,1,0:T(8,128)S(1)}, u32[]{:S(2)}, u32[]{:S(2)}) %collective-permute-start.6) | collective-permute-done | bytes 131104 | tf_op jit(solution)/shard_map/ppermute | solution.py:266
  52.3 2.0 %shard_map.72.own_ref = f32[4,128,128]{2,1,0:T(8,128)S(1)} custom-call(s32[4,4,16,128]{3,2,1,0:T(8,128)S(1)} %bitcast.14, bf16[8,512,256]{2,1,0:T(8,128)(2,1)S(1)} %shard_map.69.near_ref.refs_1_, bf16[4,512,256]{2,1,0:T(8,128)(2,1)S(1)} %shard_map.70.part_ref.refs_2_, bf16[4,512,256]{2,1,0:T(8,128)(2,1)S(1)} %get-tuple-element.12.refs_3_.shared_ref), custom_call_target="tpu_custom_call" | custom-call | flops 1342177280 | bytes 1048576 | tf_op jit(solution)/shard_map/pallas_call | solution.py:26
  54.4 0.6 collective-permute-done.3.soon_ref
  55.0 3.2 %collective-permute-done.7.high_ref = f32[4,64,128]{2,1,0:T(8,128)S(1)} collective-permute-done((f32[4,64,128]{2,1,0:T(8,128)S(1)}, f32[4,64,128]{2,1,0:T(8,128)S(1)}, u32[]{:S(2)}, u32[]{:S(2)}) %collective-permute-start.7) | collective-permute-done | bytes 131104 | tf_op jit(solution)/shard_map/ppermute | solution.py:266
  58.2 1.4 %collective-permute-done.5.low_ref = f32[4,64,128]{2,1,0:T(8,128)S(1)} collective-permute-done((f32[4,64,128]{2,1,0:T(8,128)S(1)}, f32[4,64,128]{2,1,0:T(8,128)S(1)}, u32[]{:S(2)}, u32[]{:S(2)}) %collective-permute-start.5) | collective-permute-done | bytes 131104 | tf_op jit(solution)/shard_map/ppermute | solution.py:266
  59.6 1.5 %collective-permute-start.8 = (f32[128,128]{1,0:T(8,128)S(1)}, f32[128,128]{1,0:T(8,128)S(1)}, u32[]{:S(2)}, u32[]{:S(2)}) collective-permute-start(f32[128,128]{1,0:T(8,128)S(1)} %get-tuple-element.17), channel_id=1, source_target_pairs={{0,128},{64,192},{128,0},{192,64},{1,129},{65,193},{129,1},{193,65... | collective-permute-start | bytes 196616 | tf_op jit(solution)/shard_map/ppermute | solution.py:282
  61.2 3.0 %collective-permute-start.9 = (f32[128,128]{1,0:T(8,128)S(1)}, f32[128,128]{1,0:T(8,128)S(1)}, u32[]{:S(2)}, u32[]{:S(2)}) collective-permute-start(f32[128,128]{1,0:T(8,128)S(1)} %get-tuple-element.18), channel_id=1, source_target_pairs={{0,192},{64,128},{128,64},{192,0},{1,193},{65,129},{129,65},{193,1... | collective-permute-start | bytes 196616 | tf_op jit(solution)/shard_map/ppermute | solution.py:282
  64.1 2.1 %collective-permute-start.10 = (f32[128,128]{1,0:T(8,128)S(1)}, f32[128,128]{1,0:T(8,128)S(1)}, u32[]{:S(2)}, u32[]{:S(2)}) collective-permute-start(f32[128,128]{1,0:T(8,128)S(1)} %get-tuple-element.19), channel_id=1, source_target_pairs={{0,64},{64,0},{128,192},{192,128},{1,65},{65,1},{129,193},{193,129... | collective-permute-start | bytes 196616 | tf_op jit(solution)/shard_map/ppermute | solution.py:282
  66.2 2.3 %collective-permute-done.8.one_ref = f32[128,128]{1,0:T(8,128)S(1)} collective-permute-done((f32[128,128]{1,0:T(8,128)S(1)}, f32[128,128]{1,0:T(8,128)S(1)}, u32[]{:S(2)}, u32[]{:S(2)}) %collective-permute-start.8) | collective-permute-done | bytes 65568 | tf_op jit(solution)/shard_map/ppermute | solution.py:282
  68.5 1.8 %collective-permute-done.10.three_ref = f32[128,128]{1,0:T(8,128)S(1)} collective-permute-done((f32[128,128]{1,0:T(8,128)S(1)}, f32[128,128]{1,0:T(8,128)S(1)}, u32[]{:S(2)}, u32[]{:S(2)}) %collective-permute-start.10) | collective-permute-done | bytes 65568 | tf_op jit(solution)/shard_map/ppermute | solution.py:282
  70.5 0.8 collective-permute-start.13
  71.3 1.1 %collective-permute-start.12 = (f32[10,32]{1,0:T(8,128)S(1)}, f32[10,32]{1,0:T(8,128)S(1)}, u32[]{:S(2)}, u32[]{:S(2)}) collective-permute-start(f32[10,32]{1,0:T(8,128)S(1)} %get-tuple-element.21), channel_id=1, source_target_pairs={{0,3},{1,2},{2,1},{3,0},{4,7},{5,6},{6,5},{7,4},{8,11},{9,10},{10,... | collective-permute-start | bytes 3848 | tf_op jit(solution)/shard_map/ppermute | solution.py:282
  72.3 2.3 %collective-permute-start.11 = (f32[10,32]{1,0:T(8,128)S(1)}, f32[10,32]{1,0:T(8,128)S(1)}, u32[]{:S(2)}, u32[]{:S(2)}) collective-permute-start(f32[10,32]{1,0:T(8,128)S(1)} %get-tuple-element.21), channel_id=1, source_target_pairs={{0,2},{1,3},{2,0},{3,1},{4,6},{5,7},{6,4},{7,5},{8,10},{9,11},{10,... | collective-permute-start | bytes 3848 | tf_op jit(solution)/shard_map/ppermute | solution.py:282
  74.6 0.7 shard_map.81
  75.3 0.8 %collective-permute-done.12 = f32[10,32]{1,0:T(8,128)S(1)} collective-permute-done((f32[10,32]{1,0:T(8,128)S(1)}, f32[10,32]{1,0:T(8,128)S(1)}, u32[]{:S(2)}, u32[]{:S(2)}) %collective-permute-start.12) | collective-permute-done | bytes 1312 | tf_op jit(solution)/shard_map/ppermute | solution.py:282
  76.1 1.4 %collective-permute-done.11 = f32[10,32]{1,0:T(8,128)S(1)} collective-permute-done((f32[10,32]{1,0:T(8,128)S(1)}, f32[10,32]{1,0:T(8,128)S(1)}, u32[]{:S(2)}, u32[]{:S(2)}) %collective-permute-start.11) | collective-permute-done | bytes 1312 | tf_op jit(solution)/shard_map/ppermute | solution.py:282
  (17 shorter events, 1.6 us)
Async XLA Ops:
  0.6 15.2 %collective-permute-start.1 = (f32[4,512,128]{2,1,0:T(8,128)}, f32[4,512,128]{2,1,0:T(8,128)}, u32[]{:S(2)}, u32[]{:S(2)}) collective-permute-start(f32[4,512,128]{2,1,0:T(8,128)} %refs_0_.1), channel_id=1, source_target_pairs={{0,32},{4,228},{32,0},{36,68},{64,96},{68,36},{96,64},{100,132},{1... | collective-permute-start | bytes 3145736 | tf_op jit(solution)/shard_map/ppermute | solution.py:322
  2.6 27.6 %collective-permute-start = (f32[4,512,128]{2,1,0:T(8,128)}, f32[4,512,128]{2,1,0:T(8,128)}, u32[]{:S(2)}, u32[]{:S(2)}) collective-permute-start(f32[4,512,128]{2,1,0:T(8,128)} %refs_0_.1), channel_id=1, source_target_pairs={{0,4},{4,0},{1,5},{5,1},{2,6},{6,2},{3,7},{7,3},{8,12},{12,8},{9,1... | collective-permute-start | bytes 3145736 | tf_op jit(solution)/shard_map/ppermute | solution.py:21
  15.8 23.9 %collective-permute-start.2 = (f32[4,512,128]{2,1,0:T(8,128)}, f32[4,512,128]{2,1,0:T(8,128)}, u32[]{:S(2)}, u32[]{:S(2)}) collective-permute-start(f32[4,512,128]{2,1,0:T(8,128)} %collective-permute-done.1.refs_0_), channel_id=1, source_target_pairs={{0,4},{4,0},{1,5},{5,1},{2,6},{6,2},{3,7},{7,3},{8,12},{12,8},{9,1... | collective-permute-start | bytes 3145736 | tf_op jit(solution)/shard_map/ppermute | solution.py:21
  20.4 19.3 %all-to-all-start = ((s32[16,16,128]{2,1,0:T(8,128)}), s32[16,16,128]{2,1,0:T(8,128)S(1)}, u32[]{:S(2)}, u32[]{:S(2)}) async-start(s32[16,16,128]{2,1,0:T(8,128)} %bitcast.15), calls=%async_computation | async-start | bytes 262144 | tf_op jit(solution)/shard_map/all_to_all | solution.py:340
  28.6 1.6 %copy-start = (f32[4,512,128]{2,1,0:T(8,128)S(1)}, f32[4,512,128]{2,1,0:T(8,128)}, u32[]{:S(2)}) copy-start(f32[4,512,128]{2,1,0:T(8,128)} %refs_0_.1) | copy-start | bytes 3145732
  42.8 9.2 %collective-permute-start.4 = (f32[4,64,128]{2,1,0:T(8,128)S(1)}, f32[4,64,128]{2,1,0:T(8,128)S(1)}, u32[]{:S(2)}, u32[]{:S(2)}) collective-permute-start(f32[4,64,128]{2,1,0:T(8,128)S(1)} %shard_map.75), channel_id=1, source_target_pairs={{0,8},{4,28},{8,16},{12,4},{16,24},{20,12},{24,0},{28,20},{1,9},{5... | collective-permute-start | bytes 393224 | tf_op jit(solution)/shard_map/ppermute | solution.py:266
  43.1 8.8 %collective-permute-start.6 = (f32[4,64,128]{2,1,0:T(8,128)S(1)}, f32[4,64,128]{2,1,0:T(8,128)S(1)}, u32[]{:S(2)}, u32[]{:S(2)}) collective-permute-start(f32[4,64,128]{2,1,0:T(8,128)S(1)} %shard_map.77), channel_id=1, source_target_pairs={{0,8},{4,28},{8,16},{12,4},{16,24},{20,12},{24,0},{28,20},{1,9},{5... | collective-permute-start | bytes 393224 | tf_op jit(solution)/shard_map/ppermute | solution.py:266
  46.4 8.6 %collective-permute-start.3 = (f32[4,128,128]{2,1,0:T(8,128)S(1)}, f32[4,128,128]{2,1,0:T(8,128)S(1)}, u32[]{:S(2)}, u32[]{:S(2)}) collective-permute-start(f32[4,128,128]{2,1,0:T(8,128)S(1)} %shard_map.73), channel_id=1, source_target_pairs={{0,24},{4,12},{8,0},{12,20},{16,8},{20,28},{24,16},{28,4},{1,25},{... | collective-permute-start | bytes 786440 | tf_op jit(solution)/shard_map/ppermute | solution.py:266
  51.9 6.3 %collective-permute-start.7 = (f32[4,64,128]{2,1,0:T(8,128)S(1)}, f32[4,64,128]{2,1,0:T(8,128)S(1)}, u32[]{:S(2)}, u32[]{:S(2)}) collective-permute-start(f32[4,64,128]{2,1,0:T(8,128)S(1)} %shard_map.78), channel_id=1, source_target_pairs={{0,8},{4,28},{8,16},{12,4},{16,24},{20,12},{24,0},{28,20},{1,9},{5... | collective-permute-start | bytes 393224 | tf_op jit(solution)/shard_map/ppermute | solution.py:266
  52.0 18.3 %copy-start.1 = (f32[32,128]{1,0:T(8,128)S(1)}, f32[32,128]{1,0:T(8,128)}, u32[]{:S(2)}) copy-start(f32[32,128]{1,0:T(8,128)} %dense_ref.1) | copy-start | bytes 49156
  52.0 7.5 %collective-permute-start.5 = (f32[4,64,128]{2,1,0:T(8,128)S(1)}, f32[4,64,128]{2,1,0:T(8,128)S(1)}, u32[]{:S(2)}, u32[]{:S(2)}) collective-permute-start(f32[4,64,128]{2,1,0:T(8,128)S(1)} %shard_map.76), channel_id=1, source_target_pairs={{0,8},{4,28},{8,16},{12,4},{16,24},{20,12},{24,0},{28,20},{1,9},{5... | collective-permute-start | bytes 393224 | tf_op jit(solution)/shard_map/ppermute | solution.py:266
  59.6 8.9 %collective-permute-start.8 = (f32[128,128]{1,0:T(8,128)S(1)}, f32[128,128]{1,0:T(8,128)S(1)}, u32[]{:S(2)}, u32[]{:S(2)}) collective-permute-start(f32[128,128]{1,0:T(8,128)S(1)} %get-tuple-element.17), channel_id=1, source_target_pairs={{0,128},{64,192},{128,0},{192,64},{1,129},{65,193},{129,1},{193,65... | collective-permute-start | bytes 196616 | tf_op jit(solution)/shard_map/ppermute | solution.py:282
  61.2 7.3 %collective-permute-start.9 = (f32[128,128]{1,0:T(8,128)S(1)}, f32[128,128]{1,0:T(8,128)S(1)}, u32[]{:S(2)}, u32[]{:S(2)}) collective-permute-start(f32[128,128]{1,0:T(8,128)S(1)} %get-tuple-element.18), channel_id=1, source_target_pairs={{0,192},{64,128},{128,64},{192,0},{1,193},{65,129},{129,65},{193,1... | collective-permute-start | bytes 196616 | tf_op jit(solution)/shard_map/ppermute | solution.py:282
  64.1 6.2 %collective-permute-start.10 = (f32[128,128]{1,0:T(8,128)S(1)}, f32[128,128]{1,0:T(8,128)S(1)}, u32[]{:S(2)}, u32[]{:S(2)}) collective-permute-start(f32[128,128]{1,0:T(8,128)S(1)} %get-tuple-element.19), channel_id=1, source_target_pairs={{0,64},{64,0},{128,192},{192,128},{1,65},{65,1},{129,193},{193,129... | collective-permute-start | bytes 196616 | tf_op jit(solution)/shard_map/ppermute | solution.py:282
  70.5 4.8 %collective-permute-start.13 = (f32[10,32]{1,0:T(8,128)S(1)}, f32[10,32]{1,0:T(8,128)S(1)}, u32[]{:S(2)}, u32[]{:S(2)}) collective-permute-start(f32[10,32]{1,0:T(8,128)S(1)} %get-tuple-element.21), channel_id=1, source_target_pairs={{0,1},{1,0},{2,3},{3,2},{4,5},{5,4},{6,7},{7,6},{8,9},{9,8},{10,11... | collective-permute-start | bytes 3848 | tf_op jit(solution)/shard_map/ppermute | solution.py:282
  71.3 4.9 %collective-permute-start.12 = (f32[10,32]{1,0:T(8,128)S(1)}, f32[10,32]{1,0:T(8,128)S(1)}, u32[]{:S(2)}, u32[]{:S(2)}) collective-permute-start(f32[10,32]{1,0:T(8,128)S(1)} %get-tuple-element.21), channel_id=1, source_target_pairs={{0,3},{1,2},{2,1},{3,0},{4,7},{5,6},{6,5},{7,4},{8,11},{9,10},{10,... | collective-permute-start | bytes 3848 | tf_op jit(solution)/shard_map/ppermute | solution.py:282
  72.3 5.2 %collective-permute-start.11 = (f32[10,32]{1,0:T(8,128)S(1)}, f32[10,32]{1,0:T(8,128)S(1)}, u32[]{:S(2)}, u32[]{:S(2)}) collective-permute-start(f32[10,32]{1,0:T(8,128)S(1)} %get-tuple-element.21), channel_id=1, source_target_pairs={{0,2},{1,3},{2,0},{3,1},{4,6},{5,7},{6,4},{7,5},{8,10},{9,11},{10,... | collective-permute-start | bytes 3848 | tf_op jit(solution)/shard_map/ppermute | solution.py:282

commit v15 on v14

--- a/solution.py
+++ b/solution.py
@@ -273,7 +273,7 @@
 def join_kernel(own_ref, soon_ref, low_ref, high_ref, *out_refs):
     half = low_ref.shape[1]
     odd = lax.rem(lax.axis_index("zq"), 2)
-    for j, out_ref in zip((0, 2, 3 - 2 * odd, 1 + 2 * odd), out_refs):
+    for j, out_ref in zip((0, 2, 1 + 2 * odd, 3 - 2 * odd), out_refs):
         out_ref[:half] = own_ref[j, :half] + soon_ref[j, :half] + low_ref[j]
         out_ref[half:] = own_ref[j, half:] + soon_ref[j, half:] + high_ref[j]
 
@@ -372,9 +372,10 @@
     far_low = by_core(far_low, 1, ring)
     far_high = far_pool(high)
     far_high = by_core(far_high, 1, ring)
-    (soon,) = bags(ids, near, part, shared, examples, (((3, 1), whole),))
+    soon, late_low, late_high = bags(
+        ids, near, part, shared, examples, (((3, 1), whole), ((1, 3), low), ((1, 3), high))
+    )
     soon = by_core(soon, -1, ring)
-    late_low, late_high = bags(ids, near, part, shared, examples, (((1, 3), low), ((1, 3), high)))
     piece = jax.ShapeDtypeStruct(late_low.shape, late_low.dtype)
     late_low = local_kernel(add_kernel, piece, (late_low, far_low))
     late_low = by_core(late_low, 1, ring)
@@ -386,7 +387,7 @@
         join_kernel, (final,) * group, (own, soon, late_low, late_high)
     )
     partners = (lambda i: i ^ 2, lambda i: 3 - i, lambda i: i ^ 1)
-    for k, partner in enumerate(partners):
+    for k, partner in enumerate((partners[0], partners[2], partners[1])):
         others[k] = swapped(others[k], "zq", partner)
     pairs = count * (count + 1) // 2
     products, summed = local_kernel(

time: 79.4 us -> 77.7 us (0.979)
  the two profiles are of different devices: /device:TPU:24 before, /device:TPU:32 now
where the time goes in v15:
time: 77.7 us; the launch traced here: 77.4 us
  waiting for transfers between devices  34.5 us (44%)
  starting transfers between devices  27.4 us (35%)
  Pallas kernels  14.1 us (18%)
    pallas_call x13, Pallas kernels, local_kernel(): pl.pallas_call(kernel, in_specs=[HBM if k in in_hbm else VMEM for k in ra...  14.1 us
    ppermute x1, waiting for transfers between devices, body(): part = lax.ppermute(tables, Z + ('c',), pairs)  13.3 us
    ppermute x6, starting transfers between devices, swapped(): lax.ppermute(value, axis, [(i, partner(i)) for i in range(lax.axis_size(a...  11.1 us
    all_to_all x1, starting transfers between devices, body(): ids = lax.all_to_all(ids, ('zq', 'x'), 0, 0, tiled=True)  10.1 us
    ppermute x6, waiting for transfers between devices, swapped(): lax.ppermute(value, axis, [(i, partner(i)) for i in range(lax.axis_size(a...  8.5 us
    all_to_all x1, waiting for transfers between devices, body(): ids = lax.all_to_all(ids, ('zq', 'x'), 0, 0, tiled=True)  7.74 us
    ppermute x5, waiting for transfers between devices, by_core(): return lax.ppermute(value, ('x', 'c'), pairs)  4.98 us
    ppermute x5, starting transfers between devices, by_core(): return lax.ppermute(value, ('x', 'c'), pairs)  4.26 us
  transfers between devices with their start and end apart: 15, of which 10 were waited for; matrix products, arithmetic and copies ran while one was open for 0% of the time, Pallas kernels for 14%

profile of v15, /device:TPU:32, one launch (start us, length us, event | category | flops | bytes accessed | tf_op | source)
XLA Modules:
  0.0 77.4 jit_solution(12576456671872199414)
XLA Ops:
  0.6 1.9 %collective-permute-start.1 = (f32[4,512,128]{2,1,0:T(8,128)}, f32[4,512,128]{2,1,0:T(8,128)}, u32[]{:S(2)}, u32[]{:S(2)}) collective-permute-start(f32[4,512,128]{2,1,0:T(8,128)} %refs_0_.1), channel_id=1, source_target_pairs={{0,32},{4,228},{32,0},{36,68},{64,96},{68,36},{96,64},{100,132},{1... | collective-permute-start | bytes 3145736 | tf_op jit(solution)/shard_map/ppermute | solution.py:322
  2.5 13.3 %collective-permute-done.1.refs_0_ = f32[4,512,128]{2,1,0:T(8,128)} collective-permute-done((f32[4,512,128]{2,1,0:T(8,128)}, f32[4,512,128]{2,1,0:T(8,128)}, u32[]{:S(2)}, u32[]{:S(2)}) %collective-permute-start.1) | collective-permute-done | bytes 1048608 | tf_op jit(solution)/shard_map/ppermute | solution.py:322
  15.8 1.8 %shard_map.68 = s32[4,4,16,128]{3,2,1,0:T(8,128)} custom-call(s32[4,64]{1,0:T(4,128)} %bitcast.17, s32[8,4,8,64]{3,2,1,0:T(8,128)} %bitcast.15, s32[8,4,8,64]{3,2,1,0:T(8,128)} %bitcast.16), custom_call_target="tpu_custom_call" | custom-call | flops 1048576 | bytes 1048576 | tf_op jit(solution)/shard_map/pallas_call | solution.py:26
  17.6 10.1 %all-to-all-start = ((s32[16,16,128]{2,1,0:T(8,128)}), s32[16,16,128]{2,1,0:T(8,128)S(1)}, u32[]{:S(2)}, u32[]{:S(2)}) async-start(s32[16,16,128]{2,1,0:T(8,128)} %bitcast.14), calls=%async_computation | async-start | bytes 262144 | tf_op jit(solution)/shard_map/all_to_all | solution.py:340
  27.8 1.5 %shard_map.70.part_ref.refs_2_ = bf16[4,512,256]{2,1,0:T(8,128)(2,1)S(1)} custom-call(f32[4,512,128]{2,1,0:T(8,128)} %collective-permute-done.1.refs_0_), custom_call_target="tpu_custom_call" | custom-call | flops 1048576 | bytes 1048576 | tf_op jit(solution)/shard_map/pallas_call | solution.py:26
  29.3 1.7 %shard_map.69.near_ref.refs_1_ = bf16[8,512,256]{2,1,0:T(8,128)(2,1)S(1)} custom-call(f32[4,512,128]{2,1,0:T(8,128)S(1)} %copy-done, f32[4,512,128]{2,1,0:T(8,128)} %collective-permute-done.refs_1_), custom_call_target="tpu_custom_call" | custom-call | flops 1048576 | bytes 1048576 | tf_op jit(solution)/shard_map/pallas_call | solution.py:26
  31.0 7.7 %all-to-all-done = s32[16,16,128]{2,1,0:T(8,128)S(1)} async-done(((s32[16,16,128]{2,1,0:T(8,128)}), s32[16,16,128]{2,1,0:T(8,128)S(1)}, u32[]{:S(2)}, u32[]{:S(2)}) %all-to-all-start) | async-done | bytes 131104 | tf_op jit(solution)/shard_map/all_to_all | solution.py:340
  38.7 1.5 %shard_map.71 = (bf16[4,768,256]{2,1,0:T(8,128)(2,1)S(1)}, bf16[4,512,256]{2,1,0:T(8,128)(2,1)S(1)}) custom-call(s32[4,4,16,128]{3,2,1,0:T(8,128)S(1)} %bitcast.9, bf16[8,512,256]{2,1,0:T(8,128)(2,1)S(1)} %shard_map.69.near_ref.refs_1_, bf16[4,512,256]{2,1,0:T(8,128)(2,1)S(1)} %shard_map.70.part_ref.refs_2_, f32[4,512,128]{2,1,0:T(8,128)} %collective-permute-done.2.shared_hbm), custom_call_target="tpu_custom_call" | custom-call | flops 805306368 | bytes 1048576 | tf_op jit(solution)/shard_map/pallas_call | solution.py:26
  40.2 0.8 %shard_map.76 = f32[4,64,128]{2,1,0:T(8,128)S(1)} custom-call(s32[4,4,16,128]{3,2,1,0:T(8,128)S(1)} %bitcast.10, bf16[4,512,256]{2,1,0:T(8,128)(2,1)S(1)} %get-tuple-element.13.refs_3_.shared_ref, bf16[4,768,256]{2,1,0:T(8,128)(2,1)S(1)} %get-tuple-element.16.looked_ref), custom_call_target="tpu_custom_call" | custom-call | flops 134217728 | bytes 1048576 | tf_op jit(solution)/shard_map/pallas_call | solution.py:26
  41.0 0.8 %shard_map.74 = f32[4,64,128]{2,1,0:T(8,128)S(1)} custom-call(s32[4,4,16,128]{3,2,1,0:T(8,128)S(1)} %bitcast.11, bf16[4,512,256]{2,1,0:T(8,128)(2,1)S(1)} %get-tuple-element.13.refs_3_.shared_ref, bf16[4,768,256]{2,1,0:T(8,128)(2,1)S(1)} %get-tuple-element.16.looked_ref), custom_call_target="tpu_custom_call" | custom-call | flops 134217728 | bytes 1048576 | tf_op jit(solution)/shard_map/pallas_call | solution.py:26
  41.8 0.3 collective-permute-start.4
  42.1 1.3 %collective-permute-start.6 = (f32[4,64,128]{2,1,0:T(8,128)S(1)}, f32[4,64,128]{2,1,0:T(8,128)S(1)}, u32[]{:S(2)}, u32[]{:S(2)}) collective-permute-start(f32[4,64,128]{2,1,0:T(8,128)S(1)} %shard_map.76), channel_id=1, source_target_pairs={{0,8},{4,28},{8,16},{12,4},{16,24},{20,12},{24,0},{28,20},{1,9},{5... | collective-permute-start | bytes 393224 | tf_op jit(solution)/shard_map/ppermute | solution.py:266
  43.4 3.2 %shard_map.73 = (f32[4,128,128]{2,1,0:T(8,128)S(1)}, f32[4,64,128]{2,1,0:T(8,128)S(1)}, f32[4,64,128]{2,1,0:T(8,128)S(1)}) custom-call(s32[4,4,16,128]{3,2,1,0:T(8,128)S(1)} %bitcast.12, bf16[8,512,256]{2,1,0:T(8,128)(2,1)S(1)} %shard_map.69.near_ref.refs_1_, bf16[4,512,256]{2,1,0:T(8,128)(2,1)S(1)} %shard_map.70.part_ref.refs_2_, ...), custom_call_target="tpu_custom_call" | custom-call | flops 2684354560 | bytes 1048576 | tf_op jit(solution)/shard_map/pallas_call | solution.py:26
  46.5 2.1 %collective-permute-start.3 = (f32[4,128,128]{2,1,0:T(8,128)S(1)}, f32[4,128,128]{2,1,0:T(8,128)S(1)}, u32[]{:S(2)}, u32[]{:S(2)}) collective-permute-start(f32[4,128,128]{2,1,0:T(8,128)S(1)} %get-tuple-element.14), channel_id=1, source_target_pairs={{0,24},{4,12},{8,0},{12,20},{16,8},{20,28},{24,16},{28,4},{1,25},{... | collective-permute-start | bytes 786440 | tf_op jit(solution)/shard_map/ppermute | solution.py:266
  48.8 0.9 %collective-permute-done.6.two_ref = f32[4,64,128]{2,1,0:T(8,128)S(1)} collective-permute-done((f32[4,64,128]{2,1,0:T(8,128)S(1)}, f32[4,64,128]{2,1,0:T(8,128)S(1)}, u32[]{:S(2)}, u32[]{:S(2)}) %collective-permute-start.6) | collective-permute-done | bytes 131104 | tf_op jit(solution)/shard_map/ppermute | solution.py:266
  49.7 0.5 collective-permute-start.7
  50.2 2.0 %shard_map.72.own_ref = f32[4,128,128]{2,1,0:T(8,128)S(1)} custom-call(s32[4,4,16,128]{3,2,1,0:T(8,128)S(1)} %bitcast.13, bf16[8,512,256]{2,1,0:T(8,128)(2,1)S(1)} %shard_map.69.near_ref.refs_1_, bf16[4,512,256]{2,1,0:T(8,128)(2,1)S(1)} %shard_map.70.part_ref.refs_2_, bf16[4,512,256]{2,1,0:T(8,128)(2,1)S(1)} %get-tuple-element.13.refs_3_.shared_ref), custom_call_target="tpu_custom_call" | custom-call | flops 1342177280 | bytes 1048576 | tf_op jit(solution)/shard_map/pallas_call | solution.py:26
  52.2 2.2 %collective-permute-done.3.soon_ref = f32[4,128,128]{2,1,0:T(8,128)S(1)} collective-permute-done((f32[4,128,128]{2,1,0:T(8,128)S(1)}, f32[4,128,128]{2,1,0:T(8,128)S(1)}, u32[]{:S(2)}, u32[]{:S(2)}) %collective-permute-start.3) | collective-permute-done | bytes 262176 | tf_op jit(solution)/shard_map/ppermute | solution.py:266
  54.4 0.5 collective-permute-done.5.low_ref
  54.9 1.4 %collective-permute-done.7.high_ref = f32[4,64,128]{2,1,0:T(8,128)S(1)} collective-permute-done((f32[4,64,128]{2,1,0:T(8,128)S(1)}, f32[4,64,128]{2,1,0:T(8,128)S(1)}, u32[]{:S(2)}, u32[]{:S(2)}) %collective-permute-start.7) | collective-permute-done | bytes 131104 | tf_op jit(solution)/shard_map/ppermute | solution.py:266
  56.3 1.5 %collective-permute-start.8 = (f32[128,128]{1,0:T(8,128)S(1)}, f32[128,128]{1,0:T(8,128)S(1)}, u32[]{:S(2)}, u32[]{:S(2)}) collective-permute-start(f32[128,128]{1,0:T(8,128)S(1)} %get-tuple-element.19), channel_id=1, source_target_pairs={{0,128},{64,192},{128,0},{192,64},{1,129},{65,193},{129,1},{193,65... | collective-permute-start | bytes 196616 | tf_op jit(solution)/shard_map/ppermute | solution.py:282
  57.8 2.8 %collective-permute-start.9 = (f32[128,128]{1,0:T(8,128)S(1)}, f32[128,128]{1,0:T(8,128)S(1)}, u32[]{:S(2)}, u32[]{:S(2)}) collective-permute-start(f32[128,128]{1,0:T(8,128)S(1)} %get-tuple-element.20), channel_id=1, source_target_pairs={{0,64},{64,0},{128,192},{192,128},{1,65},{65,1},{129,193},{193,129... | collective-permute-start | bytes 196616 | tf_op jit(solution)/shard_map/ppermute | solution.py:282
  60.6 2.3 %collective-permute-start.10 = (f32[128,128]{1,0:T(8,128)S(1)}, f32[128,128]{1,0:T(8,128)S(1)}, u32[]{:S(2)}, u32[]{:S(2)}) collective-permute-start(f32[128,128]{1,0:T(8,128)S(1)} %get-tuple-element.21), channel_id=1, source_target_pairs={{0,192},{64,128},{128,64},{192,0},{1,193},{65,129},{129,65},{193,1... | collective-permute-start | bytes 196616 | tf_op jit(solution)/shard_map/ppermute | solution.py:282
  62.9 2.3 %collective-permute-done.8.one_ref = f32[128,128]{1,0:T(8,128)S(1)} collective-permute-done((f32[128,128]{1,0:T(8,128)S(1)}, f32[128,128]{1,0:T(8,128)S(1)}, u32[]{:S(2)}, u32[]{:S(2)}) %collective-permute-start.8) | collective-permute-done | bytes 65568 | tf_op jit(solution)/shard_map/ppermute | solution.py:282
  65.2 2.4 %collective-permute-done.10.three_ref = f32[128,128]{1,0:T(8,128)S(1)} collective-permute-done((f32[128,128]{1,0:T(8,128)S(1)}, f32[128,128]{1,0:T(8,128)S(1)}, u32[]{:S(2)}, u32[]{:S(2)}) %collective-permute-start.10) | collective-permute-done | bytes 65568 | tf_op jit(solution)/shard_map/ppermute | solution.py:282
  67.8 1.6 %collective-permute-start.13 = (f32[10,32]{1,0:T(8,128)S(1)}, f32[10,32]{1,0:T(8,128)S(1)}, u32[]{:S(2)}, u32[]{:S(2)}) collective-permute-start(f32[10,32]{1,0:T(8,128)S(1)} %get-tuple-element.23), channel_id=1, source_target_pairs={{0,1},{1,0},{2,3},{3,2},{4,5},{5,4},{6,7},{7,6},{8,9},{9,8},{10,11... | collective-permute-start | bytes 3848 | tf_op jit(solution)/shard_map/ppermute | solution.py:282
  69.5 2.2 %collective-permute-start.12 = (f32[10,32]{1,0:T(8,128)S(1)}, f32[10,32]{1,0:T(8,128)S(1)}, u32[]{:S(2)}, u32[]{:S(2)}) collective-permute-start(f32[10,32]{1,0:T(8,128)S(1)} %get-tuple-element.23), channel_id=1, source_target_pairs={{0,3},{1,2},{2,1},{3,0},{4,7},{5,6},{6,5},{7,4},{8,11},{9,10},{10,... | collective-permute-start | bytes 3848 | tf_op jit(solution)/shard_map/ppermute | solution.py:282
  71.6 0.7 collective-permute-start.11
  72.4 0.7 shard_map.80
  73.0 1.3 %collective-permute-done.12 = f32[10,32]{1,0:T(8,128)S(1)} collective-permute-done((f32[10,32]{1,0:T(8,128)S(1)}, f32[10,32]{1,0:T(8,128)S(1)}, u32[]{:S(2)}, u32[]{:S(2)}) %collective-permute-start.12) | collective-permute-done | bytes 1312 | tf_op jit(solution)/shard_map/ppermute | solution.py:282
  74.3 2.5 %collective-permute-done.11 = f32[10,32]{1,0:T(8,128)S(1)} collective-permute-done((f32[10,32]{1,0:T(8,128)S(1)}, f32[10,32]{1,0:T(8,128)S(1)}, u32[]{:S(2)}, u32[]{:S(2)}) %collective-permute-start.11) | collective-permute-done | bytes 1312 | tf_op jit(solution)/shard_map/ppermute | solution.py:282
  76.8 0.6 multiply_bitcast_fusion
  (16 shorter events, 0.4 us)
Async XLA Ops:
  0.6 15.2 %collective-permute-start.1 = (f32[4,512,128]{2,1,0:T(8,128)}, f32[4,512,128]{2,1,0:T(8,128)}, u32[]{:S(2)}, u32[]{:S(2)}) collective-permute-start(f32[4,512,128]{2,1,0:T(8,128)} %refs_0_.1), channel_id=1, source_target_pairs={{0,32},{4,228},{32,0},{36,68},{64,96},{68,36},{96,64},{100,132},{1... | collective-permute-start | bytes 3145736 | tf_op jit(solution)/shard_map/ppermute | solution.py:322
  2.5 26.8 %collective-permute-start = (f32[4,512,128]{2,1,0:T(8,128)}, f32[4,512,128]{2,1,0:T(8,128)}, u32[]{:S(2)}, u32[]{:S(2)}) collective-permute-start(f32[4,512,128]{2,1,0:T(8,128)} %refs_0_.1), channel_id=1, source_target_pairs={{0,4},{4,0},{1,5},{5,1},{2,6},{6,2},{3,7},{7,3},{8,12},{12,8},{9,1... | collective-permute-start | bytes 3145736 | tf_op jit(solution)/shard_map/ppermute | solution.py:21
  15.8 22.9 %collective-permute-start.2 = (f32[4,512,128]{2,1,0:T(8,128)}, f32[4,512,128]{2,1,0:T(8,128)}, u32[]{:S(2)}, u32[]{:S(2)}) collective-permute-start(f32[4,512,128]{2,1,0:T(8,128)} %collective-permute-done.1.refs_0_), channel_id=1, source_target_pairs={{0,4},{4,0},{1,5},{5,1},{2,6},{6,2},{3,7},{7,3},{8,12},{12,8},{9,1... | collective-permute-start | bytes 3145736 | tf_op jit(solution)/shard_map/ppermute | solution.py:21
  17.6 21.1 %all-to-all-start = ((s32[16,16,128]{2,1,0:T(8,128)}), s32[16,16,128]{2,1,0:T(8,128)S(1)}, u32[]{:S(2)}, u32[]{:S(2)}) async-start(s32[16,16,128]{2,1,0:T(8,128)} %bitcast.14), calls=%async_computation | async-start | bytes 262144 | tf_op jit(solution)/shard_map/all_to_all | solution.py:340
  27.7 1.6 %copy-start = (f32[4,512,128]{2,1,0:T(8,128)S(1)}, f32[4,512,128]{2,1,0:T(8,128)}, u32[]{:S(2)}) copy-start(f32[4,512,128]{2,1,0:T(8,128)} %refs_0_.1) | copy-start | bytes 3145732
  41.8 6.8 %collective-permute-start.4 = (f32[4,64,128]{2,1,0:T(8,128)S(1)}, f32[4,64,128]{2,1,0:T(8,128)S(1)}, u32[]{:S(2)}, u32[]{:S(2)}) collective-permute-start(f32[4,64,128]{2,1,0:T(8,128)S(1)} %shard_map.74), channel_id=1, source_target_pairs={{0,8},{4,28},{8,16},{12,4},{16,24},{20,12},{24,0},{28,20},{1,9},{5... | collective-permute-start | bytes 393224 | tf_op jit(solution)/shard_map/ppermute | solution.py:266
  42.1 7.5 %collective-permute-start.6 = (f32[4,64,128]{2,1,0:T(8,128)S(1)}, f32[4,64,128]{2,1,0:T(8,128)S(1)}, u32[]{:S(2)}, u32[]{:S(2)}) collective-permute-start(f32[4,64,128]{2,1,0:T(8,128)S(1)} %shard_map.76), channel_id=1, source_target_pairs={{0,8},{4,28},{8,16},{12,4},{16,24},{20,12},{24,0},{28,20},{1,9},{5... | collective-permute-start | bytes 393224 | tf_op jit(solution)/shard_map/ppermute | solution.py:266
  46.5 7.9 %collective-permute-start.3 = (f32[4,128,128]{2,1,0:T(8,128)S(1)}, f32[4,128,128]{2,1,0:T(8,128)S(1)}, u32[]{:S(2)}, u32[]{:S(2)}) collective-permute-start(f32[4,128,128]{2,1,0:T(8,128)S(1)} %get-tuple-element.14), channel_id=1, source_target_pairs={{0,24},{4,12},{8,0},{12,20},{16,8},{20,28},{24,16},{28,4},{1,25},{... | collective-permute-start | bytes 786440 | tf_op jit(solution)/shard_map/ppermute | solution.py:266
  48.6 6.3 %collective-permute-start.5 = (f32[4,64,128]{2,1,0:T(8,128)S(1)}, f32[4,64,128]{2,1,0:T(8,128)S(1)}, u32[]{:S(2)}, u32[]{:S(2)}) collective-permute-start(f32[4,64,128]{2,1,0:T(8,128)S(1)} %shard_map.75), channel_id=1, source_target_pairs={{0,8},{4,28},{8,16},{12,4},{16,24},{20,12},{24,0},{28,20},{1,9},{5... | collective-permute-start | bytes 393224 | tf_op jit(solution)/shard_map/ppermute | solution.py:266
  49.7 18.0 %copy-start.1 = (f32[32,128]{1,0:T(8,128)S(1)}, f32[32,128]{1,0:T(8,128)}, u32[]{:S(2)}) copy-start(f32[32,128]{1,0:T(8,128)} %dense_ref.1) | copy-start | bytes 49156
  49.7 6.6 %collective-permute-start.7 = (f32[4,64,128]{2,1,0:T(8,128)S(1)}, f32[4,64,128]{2,1,0:T(8,128)S(1)}, u32[]{:S(2)}, u32[]{:S(2)}) collective-permute-start(f32[4,64,128]{2,1,0:T(8,128)S(1)} %shard_map.77), channel_id=1, source_target_pairs={{0,8},{4,28},{8,16},{12,4},{16,24},{20,12},{24,0},{28,20},{1,9},{5... | collective-permute-start | bytes 393224 | tf_op jit(solution)/shard_map/ppermute | solution.py:266
  56.3 8.9 %collective-permute-start.8 = (f32[128,128]{1,0:T(8,128)S(1)}, f32[128,128]{1,0:T(8,128)S(1)}, u32[]{:S(2)}, u32[]{:S(2)}) collective-permute-start(f32[128,128]{1,0:T(8,128)S(1)} %get-tuple-element.19), channel_id=1, source_target_pairs={{0,128},{64,192},{128,0},{192,64},{1,129},{65,193},{129,1},{193,65... | collective-permute-start | bytes 196616 | tf_op jit(solution)/shard_map/ppermute | solution.py:282
  57.8 7.4 %collective-permute-start.9 = (f32[128,128]{1,0:T(8,128)S(1)}, f32[128,128]{1,0:T(8,128)S(1)}, u32[]{:S(2)}, u32[]{:S(2)}) collective-permute-start(f32[128,128]{1,0:T(8,128)S(1)} %get-tuple-element.20), channel_id=1, source_target_pairs={{0,64},{64,0},{128,192},{192,128},{1,65},{65,1},{129,193},{193,129... | collective-permute-start | bytes 196616 | tf_op jit(solution)/shard_map/ppermute | solution.py:282
  60.6 7.1 %collective-permute-start.10 = (f32[128,128]{1,0:T(8,128)S(1)}, f32[128,128]{1,0:T(8,128)S(1)}, u32[]{:S(2)}, u32[]{:S(2)}) collective-permute-start(f32[128,128]{1,0:T(8,128)S(1)} %get-tuple-element.21), channel_id=1, source_target_pairs={{0,192},{64,128},{128,64},{192,0},{1,193},{65,129},{129,65},{193,1... | collective-permute-start | bytes 196616 | tf_op jit(solution)/shard_map/ppermute | solution.py:282
  67.8 5.2 %collective-permute-start.13 = (f32[10,32]{1,0:T(8,128)S(1)}, f32[10,32]{1,0:T(8,128)S(1)}, u32[]{:S(2)}, u32[]{:S(2)}) collective-permute-start(f32[10,32]{1,0:T(8,128)S(1)} %get-tuple-element.23), channel_id=1, source_target_pairs={{0,1},{1,0},{2,3},{3,2},{4,5},{5,4},{6,7},{7,6},{8,9},{9,8},{10,11... | collective-permute-start | bytes 3848 | tf_op jit(solution)/shard_map/ppermute | solution.py:282
  69.5 4.9 %collective-permute-start.12 = (f32[10,32]{1,0:T(8,128)S(1)}, f32[10,32]{1,0:T(8,128)S(1)}, u32[]{:S(2)}, u32[]{:S(2)}) collective-permute-start(f32[10,32]{1,0:T(8,128)S(1)} %get-tuple-element.23), channel_id=1, source_target_pairs={{0,3},{1,2},{2,1},{3,0},{4,7},{5,6},{6,5},{7,4},{8,11},{9,10},{10,... | collective-permute-start | bytes 3848 | tf_op jit(solution)/shard_map/ppermute | solution.py:282
  71.6 5.2 %collective-permute-start.11 = (f32[10,32]{1,0:T(8,128)S(1)}, f32[10,32]{1,0:T(8,128)S(1)}, u32[]{:S(2)}, u32[]{:S(2)}) collective-permute-start(f32[10,32]{1,0:T(8,128)S(1)} %get-tuple-element.23), channel_id=1, source_target_pairs={{0,2},{1,3},{2,0},{3,1},{4,6},{5,7},{6,4},{7,5},{8,10},{9,11},{10,... | collective-permute-start | bytes 3848 | tf_op jit(solution)/shard_map/ppermute | solution.py:282
